TPU v7x, 32 devices: a whole 2x2x4 slice. The times are simulated.
32 devices in a mesh: lon: 4 (over y, x), lat: 8 (over z, core).
Axes of the slice: x: 2, y: 2, z: 4, core: 2. Of those that a mesh axis runs over, the one named last changes fastest.
Arguments:
- spectrum: float32 [32, 512, 648], P('lon', 'lat'), may hold values from 0.01 to 1
- sea_mask: int32 [32, 512], P('lon', 'lat'), may hold values from 0 to 1, as said below
- ice_flags: int32 [32, 512], P('lon', 'lat'), may hold values 0 or 1
- wind_forcing: float32 [32, 512], P('lon', 'lat'), may hold values from 0.1 to 1.5
- group_speed: float32 [18], replicated, may hold values from 0.3 to 1
- coupling: bfloat16 [648, 648], replicated, may hold values from -0.25 to 0.25
Outputs:
- field: float32 [32, 512, 648], P('lon', 'lat')
Inputs may be any that keep to these rules, and one draw needn't show every extreme that they name: `sea_mask`: each device's block of 8 x 64 cells holds at most 384 sea cells and at least 128; in every draw some block holds exactly 384.
All inputs are finite; a program needn't handle non-finite values. No bound on the sum of `ice_flags` on one device may be relied on, other than what follows from the above.
Results may differ from a plain program's by a relative error of at most 0.00079.
Values sent between devices are 32-bit elements; how exact they have to be, the bound alone decides.
No kernel may reach another device: no remote copies, remote signals or barrier semaphores. Data moves between devices by JAX's collectives and lax.ppermute only.
A program may use at most 64 MiB of HBM per device.

v0:
```python
import math

import jax
import jax.numpy as jnp
from jax import lax
from jax.sharding import PartitionSpec as P

DIRS = 36
STEPS = 4


time_step = 0.2
dissipation = 0.5


def extended(value, sides, width, wrap):
    for axis, dim in sides:
        size, length = (lax.axis_size(axis), value.shape[dim])
        up = [(i, (i + 1) % size) for i in range(size if wrap else size - 1)]
        down = [(j, i) for i, j in up]
        last = lax.slice_in_dim(value, length - width, length, axis=dim)
        first = lax.slice_in_dim(value, 0, width, axis=dim)
        before = lax.ppermute(last, axis, up)
        after = lax.ppermute(first, axis, down)
        value = jnp.concatenate([before, value, after], axis=dim)
    return value


def speed_tables(rows, total_rows, group_speed, dirs):
    theta = (jnp.arange(dirs).astype(jnp.float32) + 0.5) * (2.0 * math.pi / dirs)
    latitude = (-60.0 + 120.0 * (rows.astype(jnp.float32) + 0.5) / total_rows) * (math.pi / 180.0)
    scaled = jnp.outer(jnp.cos(theta), group_speed).reshape(-1)
    along_x = (0.225 * scaled)[None, :] / jnp.cos(latitude)[:, None]
    along_y = 0.45 * jnp.outer(jnp.sin(theta), group_speed).reshape(-1)
    return (along_x, along_y)


def upwind(field, west, east, south, north, along_x, along_y):
    speed_x = along_x[None]
    result = (
        field
        - jnp.maximum(speed_x, 0.0) * (field - west)
        - jnp.minimum(speed_x, 0.0) * (east - field)
    )
    return (
        result
        - jnp.maximum(along_y, 0.0) * (field - south)
        - jnp.minimum(along_y, 0.0) * (north - field)
    )


def sources(advected, wind_forcing, ice_flags, coupling):
    shape = advected.shape
    energy = jnp.mean(advected, axis=-1, keepdims=True)
    flat = advected.reshape(-1, shape[-1]).astype(jnp.bfloat16)
    transfer = jnp.dot(flat, coupling, preferred_element_type=jnp.float32).reshape(shape)
    forcing = (wind_forcing * (1.0 - ice_flags.astype(jnp.float32)))[..., None]
    return advected + time_step * (forcing * advected + transfer - dissipation * energy * advected)


def neighbours(field):
    wide_x = extended(field, (("lon", 0),), 1, True)
    wide_y = extended(field, (("lat", 1),), 1, False)
    return (wide_x[:-2], wide_x[2:], wide_y[:, :-2], wide_y[:, 2:])


def on_device(spectrum, sea_mask, ice_flags, wind_forcing, group_speed, coupling):
    rows_here = spectrum.shape[1]
    rows = lax.axis_index("lat") * rows_here + jnp.arange(rows_here, dtype=jnp.int32)
    along_x, along_y = speed_tables(rows, rows_here * lax.axis_size("lat"), group_speed, DIRS)
    sea = sea_mask.astype(jnp.float32)[..., None]
    field = spectrum * sea
    for step in range(STEPS):
        west, east, south, north = neighbours(field)
        advected = upwind(field, west, east, south, north, along_x, along_y)
        field = sources(advected, wind_forcing, ice_flags, coupling) * sea
    return field


def solution(mesh):
    placed = (P("lon", "lat", None), P("lon", "lat"), P("lon", "lat"), P("lon", "lat"), P(), P())
    return jax.shard_map(
        on_device, mesh=mesh, in_specs=placed, out_specs=P("lon", "lat", None), check_vma=False
    )
```

profile of v0, /device:TPU:1, one launch (start us, length us, event | category | flops | bytes accessed | tf_op | source)
XLA Modules:
  0.0 67.7 jit_solution(12144094791909609757)
XLA Ops:
  0.0 0.8 %convert_element_type.44 = f32[8,64]{1,0:T(8,128)S(1)} convert(s32[8,64]{1,0:T(8,128)} %param.7) | non-fusion elementwise | flops 512 | bytes 4096 | tf_op jit(solution)/shard_map/convert_element_type | solution.py:71
  0.8 1.6 %broadcast_multiply_fusion = f32[8,64,648]{2,1,0:T(8,128)S(1)} fusion(f32[8,64,648]{2,1,0:T(8,128)} %param.6, f32[8,64]{1,0:T(8,128)S(1)} %convert_element_type.44), kind=kLoop, calls=%fused_computation.80 | loop fusion | flops 331776 | bytes 2656256 | tf_op jit(solution)/shard_map/mul | solution.py:72
  2.4 0.7 fusion.95
  3.0 4.6 %collective-permute-start.2 = (f32[8,1,648]{2,1,0:T(1,128)}, f32[8,1,648]{2,1,0:T(1,128)}, u32[]{:S(2)}, u32[]{:S(2)}) collective-permute-start(f32[8,1,648]{2,1,0:T(1,128)} %get-tuple-element.27), channel_id=1, source_target_pairs={{0,1},{1,2},{2,3},{3,4},{4,5},{5,6},{6,7},{8,9},{9,10},{10,11},{11... | collective-permute-start | bytes 62216 | tf_op jit(solution)/shard_map/ppermute | solution.py:23
  7.6 1.9 %collective-permute-start.3 = (f32[8,1,648]{2,1,0:T(1,128)}, f32[8,1,648]{2,1,0:T(1,128)}, u32[]{:S(2)}, u32[]{:S(2)}) collective-permute-start(f32[8,1,648]{2,1,0:T(1,128)} %get-tuple-element.28), channel_id=1, source_target_pairs={{1,0},{2,1},{3,2},{4,3},{5,4},{6,5},{7,6},{9,8},{10,9},{11,10},{12... | collective-permute-start | bytes 62216 | tf_op jit(solution)/shard_map/ppermute | solution.py:24
  9.6 0.7 %fusion.94 = (f32[1,64,648]{2,1,0:T(8,128)}, f32[1,64,648]{2,1,0:T(8,128)S(1)}) fusion(f32[8,64,648]{2,1,0:T(8,128)S(1)} %broadcast_multiply_fusion), kind=kLoop, calls=%fused_computation.106 | loop fusion | bytes 663552 | tf_op jit(solution)/shard_map/slice | solution.py:21
  10.3 1.2 %collective-permute-start = (f32[1,64,648]{2,1,0:T(8,128)}, f32[1,64,648]{2,1,0:T(8,128)S(1)}, u32[]{:S(2)}, u32[]{:S(2)}) collective-permute-start(f32[1,64,648]{2,1,0:T(8,128)} %get-tuple-element.25), channel_id=1, source_target_pairs={{0,8},{8,16},{16,24},{24,0},{1,9},{9,17},{17,25},{25,1},{2,10},{10... | collective-permute-start | bytes 497672 | tf_op jit(solution)/shard_map/ppermute | solution.py:23
  11.5 1.2 %collective-permute-start.1 = (f32[1,64,648]{2,1,0:T(8,128)S(1)}, f32[1,64,648]{2,1,0:T(8,128)S(1)}, u32[]{:S(2)}, u32[]{:S(2)}) collective-permute-start(f32[1,64,648]{2,1,0:T(8,128)S(1)} %get-tuple-element.26), channel_id=1, source_target_pairs={{8,0},{16,8},{24,16},{0,24},{9,1},{17,9},{25,17},{1,25},{10,2},{18... | collective-permute-start | bytes 497672 | tf_op jit(solution)/shard_map/ppermute | solution.py:24
  12.7 0.6 multiply_cosine_fusion
  13.2 0.7 %fusion.77 = (f32[36,18]{1,0:T(8,128)}, f32[36,18]{1,0:T(8,128)}, f32[36,18]{1,0:T(8,128)S(1)}) fusion(f32[36]{0:T(128)S(1)} %get-tuple-element.34, f32[18]{0:T(128)S(1)} %copy-done.5, f32[36]{0:T(128)S(1)} %get-tuple-element.35), kind=kLoop, calls=%fused_computation.85 | loop fusion | flops 3888 | bytes 8136 | tf_op jit(solution)/shard_map/max | solution.py:47
  13.9 0.1 mul.352
  14.0 0.7 %divide_maximum_fusion = (f32[64,648]{1,0:T(8,128)S(1)}, f32[64,648]{1,0:T(8,128)S(1)}) fusion(f32[64]{0:T(128)} %multiply_cosine_fusion, f32[648]{0:T(1024)S(1)} %mul.352), kind=kLoop, calls=%fused_computation.82 | loop fusion | flops 124416 | bytes 334624 | tf_op jit(solution)/shard_map/max | solution.py:42
  14.7 1.3 %subtract_multiply_fusion = f32[8,64]{1,0:T(8,128)} fusion(f32[8,64]{1,0:T(8,128)} %param.9, s32[8,64]{1,0:T(8,128)} %param.8), kind=kLoop, calls=%fused_computation.87 | loop fusion | flops 1536 | bytes 6144 | tf_op jit(solution)/shard_map/mul | solution.py:57
  16.0 0.8 %max.26 = f32[648]{0:T(1024)S(1)} reshape(f32[36,18]{1,0:T(8,128)} %get-tuple-element.31) | data formatting | bytes 5184 | tf_op jit(solution)/shard_map/max | solution.py:47
  16.9 1.4 %min.26 = f32[648]{0:T(1024)} reshape(f32[36,18]{1,0:T(8,128)} %get-tuple-element.32) | data formatting | bytes 5184 | tf_op jit(solution)/shard_map/min | solution.py:48
  18.3 0.0 collective-permute-done.2
  18.3 0.0 collective-permute-done.3
  18.3 0.0 collective-permute-done
  18.3 3.0 %collective-permute-done.1 = f32[1,64,648]{2,1,0:T(8,128)S(1)} collective-permute-done((f32[1,64,648]{2,1,0:T(8,128)S(1)}, f32[1,64,648]{2,1,0:T(8,128)S(1)}, u32[]{:S(2)}, u32[]{:S(2)}) %collective-permute-start.1) | collective-permute-done | bytes 165920 | tf_op jit(solution)/shard_map/ppermute | solution.py:24
  21.3 1.8 %fusion.86 = (f32[8,64]{1,0:T(8,128)S(1)}, f32[8,64,648]{2,1,0:T(8,128)S(1)}) fusion(f32[8,64,648]{2,1,0:T(8,128)S(1)} %broadcast_multiply_fusion, f32[8,1,648]{2,1,0:T(1,128)} %collective-permute-done.3, f32[648]{0:T(1024)} %min.26, f32[8,1,648]{2,1,0:T(1,128)} %collective-permute-done.2, f32[648]{0:T(1024)S(1)} %max.26, ...), kind=kLoop, calls=%fused_computation.99 | loop fusion | flops 5639680 | bytes 3366464 | tf_op jit(solution)/shard_map/reduce_sum | solution.py:54
  23.2 1.0 %add_multiply_fusion.3 = f32[8,64,648]{2,1,0:T(8,128)S(1)} fusion(f32[8,64,648]{2,1,0:T(8,128)S(1)} %get-tuple-element.12, f32[8,64]{1,0:T(8,128)S(1)} %broadcast_multiply_fusion.4, bf16[648,648]{1,0:T(8,128)(2,1)S(1)} %copy-done, f32[8,64]{1,0:T(8,128)S(1)} %copy-done.4, f32[8,64]{1,0:T(8,128)S(1)} %copy-done.3), kind=kOutput, calls=%fused_computation.67 | convolution fusion | flops 432635904 | bytes 3500160 | tf_op jit(solution)/shard_map/dot_general | solution.py:56
  24.3 1.3 %collective-permute-start.4 = (f32[1,64,648]{2,1,0:T(8,128)S(1)}, f32[1,64,648]{2,1,0:T(8,128)S(1)}, u32[]{:S(2)}, u32[]{:S(2)}) collective-permute-start(f32[1,64,648]{2,1,0:T(8,128)S(1)} %get-tuple-element.21), channel_id=1, source_target_pairs={{0,8},{8,16},{16,24},{24,0},{1,9},{9,17},{17,25},{25,1},{2,10},{10... | collective-permute-start | bytes 497672 | tf_op jit(solution)/shard_map/ppermute | solution.py:23
  25.5 1.2 %collective-permute-start.5 = (f32[1,64,648]{2,1,0:T(8,128)S(1)}, f32[1,64,648]{2,1,0:T(8,128)S(1)}, u32[]{:S(2)}, u32[]{:S(2)}) collective-permute-start(f32[1,64,648]{2,1,0:T(8,128)S(1)} %get-tuple-element.22), channel_id=1, source_target_pairs={{8,0},{16,8},{24,16},{0,24},{9,1},{17,9},{25,17},{1,25},{10,2},{18... | collective-permute-start | bytes 497672 | tf_op jit(solution)/shard_map/ppermute | solution.py:24
  26.7 5.3 %collective-permute-start.6 = (f32[8,1,648]{2,1,0:T(1,128)S(1)}, f32[8,1,648]{2,1,0:T(1,128)S(1)}, u32[]{:S(2)}, u32[]{:S(2)}) collective-permute-start(f32[8,1,648]{2,1,0:T(1,128)S(1)} %get-tuple-element.23), channel_id=1, source_target_pairs={{0,1},{1,2},{2,3},{3,4},{4,5},{5,6},{6,7},{8,9},{9,10},{10,11},{11... | collective-permute-start | bytes 62216 | tf_op jit(solution)/shard_map/ppermute | solution.py:23
  32.0 1.9 %collective-permute-start.7 = (f32[8,1,648]{2,1,0:T(1,128)S(1)}, f32[8,1,648]{2,1,0:T(1,128)S(1)}, u32[]{:S(2)}, u32[]{:S(2)}) collective-permute-start(f32[8,1,648]{2,1,0:T(1,128)S(1)} %get-tuple-element.24), channel_id=1, source_target_pairs={{1,0},{2,1},{3,2},{4,3},{5,4},{6,5},{7,6},{9,8},{10,9},{11,10},{12... | collective-permute-start | bytes 62216 | tf_op jit(solution)/shard_map/ppermute | solution.py:24
  33.9 0.0 collective-permute-done.6
  33.9 3.2 %collective-permute-done.7 = f32[8,1,648]{2,1,0:T(1,128)S(1)} collective-permute-done((f32[8,1,648]{2,1,0:T(1,128)S(1)}, f32[8,1,648]{2,1,0:T(1,128)S(1)}, u32[]{:S(2)}, u32[]{:S(2)}) %collective-permute-start.7) | collective-permute-done | bytes 20768 | tf_op jit(solution)/shard_map/ppermute | solution.py:24
  37.1 0.0 collective-permute-done.4
  37.1 0.0 collective-permute-done.5
  37.2 1.1 %fusion.84 = (f32[8,64]{1,0:T(8,128)S(1)}, f32[8,64,648]{2,1,0:T(8,128)S(1)}) fusion(f32[8,64,648]{2,1,0:T(8,128)S(1)} %add_multiply_fusion.3, f32[8,1,648]{2,1,0:T(1,128)S(1)} %collective-permute-done.7, f32[648]{0:T(1024)S(1)} %copy-done.1, f32[8,1,648]{2,1,0:T(1,128)S(1)} %collective-permute-done.6, f32[648]{0:T(1024)S(1)} %max.26, ...), kind=kLoop, calls=%fused_computation.98 | loop fusion | flops 5639680 | bytes 3366464 | tf_op jit(solution)/shard_map/reduce_sum | solution.py:54
  38.3 1.0 %add_multiply_fusion.2 = f32[8,64,648]{2,1,0:T(8,128)S(1)} fusion(f32[8,64,648]{2,1,0:T(8,128)S(1)} %get-tuple-element.10, f32[8,64]{1,0:T(8,128)S(1)} %broadcast_multiply_fusion.3, bf16[648,648]{1,0:T(8,128)(2,1)S(1)} %copy-done, f32[8,64]{1,0:T(8,128)S(1)} %copy-done.4, f32[8,64]{1,0:T(8,128)S(1)} %copy-done.3), kind=kOutput, calls=%fused_computation.66 | convolution fusion | flops 432635904 | bytes 3500160 | tf_op jit(solution)/shard_map/dot_general | solution.py:56
  39.4 0.4 collective-permute-start.8
  39.7 2.1 %collective-permute-start.9 = (f32[1,64,648]{2,1,0:T(8,128)S(1)}, f32[1,64,648]{2,1,0:T(8,128)S(1)}, u32[]{:S(2)}, u32[]{:S(2)}) collective-permute-start(f32[1,64,648]{2,1,0:T(8,128)S(1)} %get-tuple-element.18), channel_id=1, source_target_pairs={{8,0},{16,8},{24,16},{0,24},{9,1},{17,9},{25,17},{1,25},{10,2},{18... | collective-permute-start | bytes 497672 | tf_op jit(solution)/shard_map/ppermute | solution.py:24
  41.8 2.5 %collective-permute-start.10 = (f32[8,1,648]{2,1,0:T(1,128)S(1)}, f32[8,1,648]{2,1,0:T(1,128)S(1)}, u32[]{:S(2)}, u32[]{:S(2)}) collective-permute-start(f32[8,1,648]{2,1,0:T(1,128)S(1)} %get-tuple-element.19), channel_id=1, source_target_pairs={{0,1},{1,2},{2,3},{3,4},{4,5},{5,6},{6,7},{8,9},{9,10},{10,11},{11... | collective-permute-start | bytes 62216 | tf_op jit(solution)/shard_map/ppermute | solution.py:23
  44.3 1.9 %collective-permute-start.11 = (f32[8,1,648]{2,1,0:T(1,128)S(1)}, f32[8,1,648]{2,1,0:T(1,128)S(1)}, u32[]{:S(2)}, u32[]{:S(2)}) collective-permute-start(f32[8,1,648]{2,1,0:T(1,128)S(1)} %get-tuple-element.20), channel_id=1, source_target_pairs={{1,0},{2,1},{3,2},{4,3},{5,4},{6,5},{7,6},{9,8},{10,9},{11,10},{12... | collective-permute-start | bytes 62216 | tf_op jit(solution)/shard_map/ppermute | solution.py:24
  46.2 0.0 collective-permute-done.10
  46.3 3.5 %collective-permute-done.11 = f32[8,1,648]{2,1,0:T(1,128)S(1)} collective-permute-done((f32[8,1,648]{2,1,0:T(1,128)S(1)}, f32[8,1,648]{2,1,0:T(1,128)S(1)}, u32[]{:S(2)}, u32[]{:S(2)}) %collective-permute-start.11) | collective-permute-done | bytes 20768 | tf_op jit(solution)/shard_map/ppermute | solution.py:24
  49.8 0.6 collective-permute-done.9
  50.4 1.1 %fusion.82 = (f32[8,64]{1,0:T(8,128)S(1)}, f32[8,64,648]{2,1,0:T(8,128)S(1)}) fusion(f32[8,64,648]{2,1,0:T(8,128)S(1)} %add_multiply_fusion.2, f32[8,1,648]{2,1,0:T(1,128)S(1)} %collective-permute-done.11, f32[648]{0:T(1024)S(1)} %copy-done.1, f32[8,1,648]{2,1,0:T(1,128)S(1)} %collective-permute-done.10, f32[648]{0:T(1024)S(1)} %max.26, ...), kind=kLoop, calls=%fused_computation.97 | loop fusion | flops 5639680 | bytes 3366464 | tf_op jit(solution)/shard_map/reduce_sum | solution.py:54
  51.5 1.0 %add_multiply_fusion.1 = f32[8,64,648]{2,1,0:T(8,128)S(1)} fusion(f32[8,64,648]{2,1,0:T(8,128)S(1)} %get-tuple-element.8, f32[8,64]{1,0:T(8,128)S(1)} %broadcast_multiply_fusion.2, bf16[648,648]{1,0:T(8,128)(2,1)S(1)} %copy-done, f32[8,64]{1,0:T(8,128)S(1)} %copy-done.4, f32[8,64]{1,0:T(8,128)S(1)} %copy-done.3), kind=kOutput, calls=%fused_computation.65 | convolution fusion | flops 432635904 | bytes 3500160 | tf_op jit(solution)/shard_map/dot_general | solution.py:56
  52.6 0.1 collective-permute-start.12
  52.7 2.4 %collective-permute-start.13 = (f32[1,64,648]{2,1,0:T(8,128)S(1)}, f32[1,64,648]{2,1,0:T(8,128)S(1)}, u32[]{:S(2)}, u32[]{:S(2)}) collective-permute-start(f32[1,64,648]{2,1,0:T(8,128)S(1)} %get-tuple-element.14), channel_id=1, source_target_pairs={{8,0},{16,8},{24,16},{0,24},{9,1},{17,9},{25,17},{1,25},{10,2},{18... | collective-permute-start | bytes 497672 | tf_op jit(solution)/shard_map/ppermute | solution.py:24
  55.1 4.1 %collective-permute-start.14 = (f32[8,1,648]{2,1,0:T(1,128)S(1)}, f32[8,1,648]{2,1,0:T(1,128)S(1)}, u32[]{:S(2)}, u32[]{:S(2)}) collective-permute-start(f32[8,1,648]{2,1,0:T(1,128)S(1)} %get-tuple-element.15), channel_id=1, source_target_pairs={{0,1},{1,2},{2,3},{3,4},{4,5},{5,6},{6,7},{8,9},{9,10},{10,11},{11... | collective-permute-start | bytes 62216 | tf_op jit(solution)/shard_map/ppermute | solution.py:23
  59.2 1.9 %collective-permute-start.15 = (f32[8,1,648]{2,1,0:T(1,128)S(1)}, f32[8,1,648]{2,1,0:T(1,128)S(1)}, u32[]{:S(2)}, u32[]{:S(2)}) collective-permute-start(f32[8,1,648]{2,1,0:T(1,128)S(1)} %get-tuple-element.16), channel_id=1, source_target_pairs={{1,0},{2,1},{3,2},{4,3},{5,4},{6,5},{7,6},{9,8},{10,9},{11,10},{12... | collective-permute-start | bytes 62216 | tf_op jit(solution)/shard_map/ppermute | solution.py:24
  61.1 0.0 collective-permute-done.14
  61.2 3.2 %collective-permute-done.15 = f32[8,1,648]{2,1,0:T(1,128)S(1)} collective-permute-done((f32[8,1,648]{2,1,0:T(1,128)S(1)}, f32[8,1,648]{2,1,0:T(1,128)S(1)}, u32[]{:S(2)}, u32[]{:S(2)}) %collective-permute-start.15) | collective-permute-done | bytes 20768 | tf_op jit(solution)/shard_map/ppermute | solution.py:24
  64.4 1.1 %fusion.80 = (f32[8,64]{1,0:T(8,128)S(1)}, f32[8,64,648]{2,1,0:T(8,128)S(1)}) fusion(f32[8,64,648]{2,1,0:T(8,128)S(1)} %add_multiply_fusion.1, f32[8,1,648]{2,1,0:T(1,128)S(1)} %collective-permute-done.15, f32[648]{0:T(1024)S(1)} %copy-done.1, f32[8,1,648]{2,1,0:T(1,128)S(1)} %collective-permute-done.14, f32[648]{0:T(1024)S(1)} %max.26, ...), kind=kLoop, calls=%fused_computation.96 | loop fusion | flops 5639680 | bytes 3366464 | tf_op jit(solution)/shard_map/reduce_sum | solution.py:54
  65.5 2.2 %add_multiply_fusion = f32[8,64,648]{2,1,0:T(8,128)} fusion(f32[8,64,648]{2,1,0:T(8,128)S(1)} %get-tuple-element.6, f32[8,64]{1,0:T(8,128)S(1)} %broadcast_multiply_fusion.1, bf16[648,648]{1,0:T(8,128)(2,1)S(1)} %copy-done, f32[8,64]{1,0:T(8,128)S(1)} %copy-done.4, f32[8,64]{1,0:T(8,128)S(1)} %copy-done.3), kind=kOutput, calls=%fused_computation.64 | convolution fusion | flops 432635904 | bytes 3500160 | tf_op jit(solution)/shard_map/dot_general | solution.py:56
  (26 shorter events, 0.3 us)
Async XLA Ops:
  0.0 23.2 %copy-start = (bf16[648,648]{1,0:T(8,128)(2,1)S(1)}, bf16[648,648]{1,0:T(8,128)(2,1)}, u32[]{:S(2)}) copy-start(bf16[648,648]{1,0:T(8,128)(2,1)} %param.11) | copy-start | bytes 2519428
  0.8 1.6 %copy-start.2 = (f32[8,64]{1,0:T(8,128)}, f32[8,64]{1,0:T(8,128)S(1)}, u32[]{:S(2)}) copy-start(f32[8,64]{1,0:T(8,128)S(1)} %convert_element_type.44) | copy-start | bytes 6148
  0.8 12.4 %copy-start.5 = (f32[18]{0:T(128)S(1)}, f32[18]{0:T(128)}, u32[]{:S(2)}) copy-start(f32[18]{0:T(128)} %param.10) | copy-start | bytes 220
  3.0 15.2 %collective-permute-start.2 = (f32[8,1,648]{2,1,0:T(1,128)}, f32[8,1,648]{2,1,0:T(1,128)}, u32[]{:S(2)}, u32[]{:S(2)}) collective-permute-start(f32[8,1,648]{2,1,0:T(1,128)} %get-tuple-element.27), channel_id=1, source_target_pairs={{0,1},{1,2},{2,3},{3,4},{4,5},{5,6},{6,7},{8,9},{9,10},{10,11},{11... | collective-permute-start | bytes 62216 | tf_op jit(solution)/shard_map/ppermute | solution.py:23
  7.6 10.7 %collective-permute-start.3 = (f32[8,1,648]{2,1,0:T(1,128)}, f32[8,1,648]{2,1,0:T(1,128)}, u32[]{:S(2)}, u32[]{:S(2)}) collective-permute-start(f32[8,1,648]{2,1,0:T(1,128)} %get-tuple-element.28), channel_id=1, source_target_pairs={{1,0},{2,1},{3,2},{4,3},{5,4},{6,5},{7,6},{9,8},{10,9},{11,10},{12... | collective-permute-start | bytes 62216 | tf_op jit(solution)/shard_map/ppermute | solution.py:24
  10.3 8.0 %collective-permute-start = (f32[1,64,648]{2,1,0:T(8,128)}, f32[1,64,648]{2,1,0:T(8,128)S(1)}, u32[]{:S(2)}, u32[]{:S(2)}) collective-permute-start(f32[1,64,648]{2,1,0:T(8,128)} %get-tuple-element.25), channel_id=1, source_target_pairs={{0,8},{8,16},{16,24},{24,0},{1,9},{9,17},{17,25},{25,1},{2,10},{10... | collective-permute-start | bytes 497672 | tf_op jit(solution)/shard_map/ppermute | solution.py:23
  11.5 9.9 %collective-permute-start.1 = (f32[1,64,648]{2,1,0:T(8,128)S(1)}, f32[1,64,648]{2,1,0:T(8,128)S(1)}, u32[]{:S(2)}, u32[]{:S(2)}) collective-permute-start(f32[1,64,648]{2,1,0:T(8,128)S(1)} %get-tuple-element.26), channel_id=1, source_target_pairs={{8,0},{16,8},{24,16},{0,24},{9,1},{17,9},{25,17},{1,25},{10,2},{18... | collective-permute-start | bytes 497672 | tf_op jit(solution)/shard_map/ppermute | solution.py:24
  21.3 1.8 %copy-start.3 = (f32[8,64]{1,0:T(8,128)S(1)}, f32[8,64]{1,0:T(8,128)}, u32[]{:S(2)}) copy-start(f32[8,64]{1,0:T(8,128)} %copy-done.2) | copy-start | bytes 6148
  21.3 1.8 %copy-start.4 = (f32[8,64]{1,0:T(8,128)S(1)}, f32[8,64]{1,0:T(8,128)}, u32[]{:S(2)}) copy-start(f32[8,64]{1,0:T(8,128)} %subtract_multiply_fusion) | copy-start | bytes 6148
  23.2 14.0 %copy-start.1 = (f32[648]{0:T(1024)S(1)}, f32[648]{0:T(1024)}, u32[]{:S(2)}) copy-start(f32[648]{0:T(1024)} %min.26) | copy-start | bytes 7780
  24.3 12.9 %collective-permute-start.4 = (f32[1,64,648]{2,1,0:T(8,128)S(1)}, f32[1,64,648]{2,1,0:T(8,128)S(1)}, u32[]{:S(2)}, u32[]{:S(2)}) collective-permute-start(f32[1,64,648]{2,1,0:T(8,128)S(1)} %get-tuple-element.21), channel_id=1, source_target_pairs={{0,8},{8,16},{16,24},{24,0},{1,9},{9,17},{17,25},{25,1},{2,10},{10... | collective-permute-start | bytes 497672 | tf_op jit(solution)/shard_map/ppermute | solution.py:23
  25.5 11.6 %collective-permute-start.5 = (f32[1,64,648]{2,1,0:T(8,128)S(1)}, f32[1,64,648]{2,1,0:T(8,128)S(1)}, u32[]{:S(2)}, u32[]{:S(2)}) collective-permute-start(f32[1,64,648]{2,1,0:T(8,128)S(1)} %get-tuple-element.22), channel_id=1, source_target_pairs={{8,0},{16,8},{24,16},{0,24},{9,1},{17,9},{25,17},{1,25},{10,2},{18... | collective-permute-start | bytes 497672 | tf_op jit(solution)/shard_map/ppermute | solution.py:24
  26.7 7.2 %collective-permute-start.6 = (f32[8,1,648]{2,1,0:T(1,128)S(1)}, f32[8,1,648]{2,1,0:T(1,128)S(1)}, u32[]{:S(2)}, u32[]{:S(2)}) collective-permute-start(f32[8,1,648]{2,1,0:T(1,128)S(1)} %get-tuple-element.23), channel_id=1, source_target_pairs={{0,1},{1,2},{2,3},{3,4},{4,5},{5,6},{6,7},{8,9},{9,10},{10,11},{11... | collective-permute-start | bytes 62216 | tf_op jit(solution)/shard_map/ppermute | solution.py:23
  32.0 5.1 %collective-permute-start.7 = (f32[8,1,648]{2,1,0:T(1,128)S(1)}, f32[8,1,648]{2,1,0:T(1,128)S(1)}, u32[]{:S(2)}, u32[]{:S(2)}) collective-permute-start(f32[8,1,648]{2,1,0:T(1,128)S(1)} %get-tuple-element.24), channel_id=1, source_target_pairs={{1,0},{2,1},{3,2},{4,3},{5,4},{6,5},{7,6},{9,8},{10,9},{11,10},{12... | collective-permute-start | bytes 62216 | tf_op jit(solution)/shard_map/ppermute | solution.py:24
  39.4 10.4 %collective-permute-start.8 = (f32[1,64,648]{2,1,0:T(8,128)S(1)}, f32[1,64,648]{2,1,0:T(8,128)S(1)}, u32[]{:S(2)}, u32[]{:S(2)}) collective-permute-start(f32[1,64,648]{2,1,0:T(8,128)S(1)} %get-tuple-element.17), channel_id=1, source_target_pairs={{0,8},{8,16},{16,24},{24,0},{1,9},{9,17},{17,25},{25,1},{2,10},{10... | collective-permute-start | bytes 497672 | tf_op jit(solution)/shard_map/ppermute | solution.py:23
  39.7 10.7 %collective-permute-start.9 = (f32[1,64,648]{2,1,0:T(8,128)S(1)}, f32[1,64,648]{2,1,0:T(8,128)S(1)}, u32[]{:S(2)}, u32[]{:S(2)}) collective-permute-start(f32[1,64,648]{2,1,0:T(8,128)S(1)} %get-tuple-element.18), channel_id=1, source_target_pairs={{8,0},{16,8},{24,16},{0,24},{9,1},{17,9},{25,17},{1,25},{10,2},{18... | collective-permute-start | bytes 497672 | tf_op jit(solution)/shard_map/ppermute | solution.py:24
  41.8 4.4 %collective-permute-start.10 = (f32[8,1,648]{2,1,0:T(1,128)S(1)}, f32[8,1,648]{2,1,0:T(1,128)S(1)}, u32[]{:S(2)}, u32[]{:S(2)}) collective-permute-start(f32[8,1,648]{2,1,0:T(1,128)S(1)} %get-tuple-element.19), channel_id=1, source_target_pairs={{0,1},{1,2},{2,3},{3,4},{4,5},{5,6},{6,7},{8,9},{9,10},{10,11},{11... | collective-permute-start | bytes 62216 | tf_op jit(solution)/shard_map/ppermute | solution.py:23
  44.3 5.4 %collective-permute-start.11 = (f32[8,1,648]{2,1,0:T(1,128)S(1)}, f32[8,1,648]{2,1,0:T(1,128)S(1)}, u32[]{:S(2)}, u32[]{:S(2)}) collective-permute-start(f32[8,1,648]{2,1,0:T(1,128)S(1)} %get-tuple-element.20), channel_id=1, source_target_pairs={{1,0},{2,1},{3,2},{4,3},{5,4},{6,5},{7,6},{9,8},{10,9},{11,10},{12... | collective-permute-start | bytes 62216 | tf_op jit(solution)/shard_map/ppermute | solution.py:24
  52.6 11.7 %collective-permute-start.12 = (f32[1,64,648]{2,1,0:T(8,128)S(1)}, f32[1,64,648]{2,1,0:T(8,128)S(1)}, u32[]{:S(2)}, u32[]{:S(2)}) collective-permute-start(f32[1,64,648]{2,1,0:T(8,128)S(1)} %get-tuple-element.13), channel_id=1, source_target_pairs={{0,8},{8,16},{16,24},{24,0},{1,9},{9,17},{17,25},{25,1},{2,10},{10... | collective-permute-start | bytes 497672 | tf_op jit(solution)/shard_map/ppermute | solution.py:23
  52.7 11.7 %collective-permute-start.13 = (f32[1,64,648]{2,1,0:T(8,128)S(1)}, f32[1,64,648]{2,1,0:T(8,128)S(1)}, u32[]{:S(2)}, u32[]{:S(2)}) collective-permute-start(f32[1,64,648]{2,1,0:T(8,128)S(1)} %get-tuple-element.14), channel_id=1, source_target_pairs={{8,0},{16,8},{24,16},{0,24},{9,1},{17,9},{25,17},{1,25},{10,2},{18... | collective-permute-start | bytes 497672 | tf_op jit(solution)/shard_map/ppermute | solution.py:24
  55.1 6.1 %collective-permute-start.14 = (f32[8,1,648]{2,1,0:T(1,128)S(1)}, f32[8,1,648]{2,1,0:T(1,128)S(1)}, u32[]{:S(2)}, u32[]{:S(2)}) collective-permute-start(f32[8,1,648]{2,1,0:T(1,128)S(1)} %get-tuple-element.15), channel_id=1, source_target_pairs={{0,1},{1,2},{2,3},{3,4},{4,5},{5,6},{6,7},{8,9},{9,10},{10,11},{11... | collective-permute-start | bytes 62216 | tf_op jit(solution)/shard_map/ppermute | solution.py:23
  59.2 5.1 %collective-permute-start.15 = (f32[8,1,648]{2,1,0:T(1,128)S(1)}, f32[8,1,648]{2,1,0:T(1,128)S(1)}, u32[]{:S(2)}, u32[]{:S(2)}) collective-permute-start(f32[8,1,648]{2,1,0:T(1,128)S(1)} %get-tuple-element.16), channel_id=1, source_target_pairs={{1,0},{2,1},{3,2},{4,3},{5,4},{6,5},{7,6},{9,8},{10,9},{11,10},{12... | collective-permute-start | bytes 62216 | tf_op jit(solution)/shard_map/ppermute | solution.py:24
where the time goes:
time: 68.2 us; the launch traced here: 67.7 us
  starting transfers between devices  33.8 us (50%)
  waiting for transfers between devices  13.6 us (20%)
  other arithmetic  10.8 us (16%)
  matrix products  5.26 us (8%)
  local copies, waits for them, and re-layouts  3.92 us (6%)
    ppermute x8, starting transfers between devices, extended(): before = lax.ppermute(last, axis, up)  19.4 us
    ppermute x8, starting transfers between devices, extended(): after = lax.ppermute(first, axis, down)  14.4 us
    ppermute x8, waiting for transfers between devices, extended(): after = lax.ppermute(first, axis, down)  13.6 us
    dot_general x4, matrix products, sources(): jnp.dot(flat, coupling, preferred_element_type=jnp.float32).reshape(shape)  5.26 us
    reduce_sum x4, other arithmetic, sources(): energy = jnp.mean(advected, axis=-1, keepdims=True)  5.15 us
    mul x1, other arithmetic, on_device(): field = spectrum * sea  1.59 us
    slice x8, local copies, waits for them, and re-layouts, extended(): last = lax.slice_in_dim(value, length - width, length, axis=dim)  1.55 us
    min x1, local copies, waits for them, and re-layouts, upwind(): jnp.minimum(along_y, 0.0) * (north - field)  1.43 us
  transfers between devices with their start and end apart: 16, of which 5 were waited for; matrix products, arithmetic and copies ran while one was open for 10% of the time, Pallas kernels for 0%

commit v1 on v0

v1 whole, which is shorter than its diff:
```python
import functools
import math

import jax
import jax.numpy as jnp
import numpy as np
from jax import lax
from jax.experimental import pallas as pl
from jax.experimental.pallas import tpu as pltpu
from jax.sharding import PartitionSpec as P

DIRS = 36
STEPS = 4
LANES = 128
DEPTH = 4

time_step = 0.2
dissipation = 0.5

VMEM = pltpu.VMEM
SMEM = pltpu.SMEM


def swap_pairs(size, first, wrap):
    pairs = []
    for i in range(first, size, 2):
        j = i + 1
        if j >= size:
            if not wrap:
                continue
            j = j % size
        pairs += [(i, j), (j, i)]
    return pairs


def lane_tiles(bins):
    return pl.cdiv(bins, LANES)


def lanes_of(tile):
    return slice(tile * LANES, (tile + 1) * LANES)


def lane_index(shape):
    return lax.broadcasted_iota(jnp.int32, shape, 1)


def row_index(shape):
    return lax.broadcasted_iota(jnp.int32, shape, 0)


def eastward(bins, tile, shape):
    bin_here = lane_index(shape) + tile * LANES
    quarter = bins // 4
    return (bin_here < quarter) | (bin_here >= bins - quarter)


def northward(bins, tile, shape):
    return lane_index(shape) + tile * LANES < bins // 2


def kinds(bins, tile, test):
    low, high = tile * LANES, min((tile + 1) * LANES, bins)
    return {bool(test(b)) for b in range(low, high)}


def is_east(bins):
    return lambda b: b < bins // 4 or b >= bins - bins // 4


def is_north(bins):
    return lambda b: b < bins // 2


def upwind_lat(f, bins, tile):
    shape = f.shape
    rows = shape[0]
    found = kinds(bins, tile, is_north(bins))
    south = pltpu.roll(f, 1, 0) if True in found else None
    north = pltpu.roll(f, rows - 1, 0) if False in found else None
    if south is None:
        return north
    if north is None:
        return south
    return jnp.where(northward(bins, tile, shape), south, north)


def advect(f, across, stay, go_x, go_y, bins, tile):
    along = upwind_lat(f, bins, tile)
    return stay * f + go_x * across + go_y * along


def pack_half(tiles, west_edge, bins):
    quarter = bins // 4
    split = quarter - LANES
    shape = tiles[0].shape
    lane = lane_index(shape)
    last = jnp.where(lane < split, tiles[1], jnp.where(lane >= LANES // 2, tiles[3], pltpu.roll(tiles[5], split, 1)))
    return (
        jnp.where(west_edge, tiles[2], tiles[0]),
        jnp.where(west_edge, tiles[1], tiles[4]),
        jnp.where(west_edge, tiles[3], last),
    )


def across_edge(halo, inner, west_edge, bins):
    quarter = bins // 4
    split = quarter - LANES
    shape = inner[0].shape
    pick = [eastward(bins, tile, shape) == west_edge for tile in (1, 3)]
    return (
        jnp.where(west_edge, halo[0], inner[0]),
        jnp.where(pick[0], jnp.where(west_edge, halo[2], halo[1]), inner[1]),
        jnp.where(west_edge, inner[2], halo[0]),
        jnp.where(pick[1], halo[2], inner[3]),
        jnp.where(west_edge, halo[1], inner[4]),
        jnp.where(west_edge, pltpu.roll(halo[2], LANES - split, 1), inner[5]),
    )


def west_flag(second):
    odd = lax.rem(lax.axis_index("lon"), 2)
    return (1 - odd if second else odd) == 1


def south_flag(second):
    odd = lax.rem(lax.axis_index("lat"), 2)
    return (1 - odd if second else odd) == 1


def read_tile(ref, where, bins, tile):
    low, high = tile * LANES, min((tile + 1) * LANES, bins)
    value = ref[where + (slice(None), slice(low, high))]
    if high - low == LANES:
        return value
    return jnp.concatenate([value, jnp.zeros((value.shape[0], LANES - (high - low)), value.dtype)], axis=1)


def write_tile(ref, where, bins, tile, value):
    rows, low, high = ref.shape[-2], tile * LANES, min((tile + 1) * LANES, bins)
    ref[where + (slice(None), slice(low, high))] = value[:rows, : high - low]


def masks_kernel_part(sea_ref, ice_ref, wind_ref):
    sea = sea_ref[...].astype(jnp.float32)
    gain = 1.0 + time_step * (wind_ref[...] * (1.0 - ice_ref[...].astype(jnp.float32)))
    columns, rows = sea.shape
    sea = jnp.concatenate([sea, gain], axis=1)
    turned = jnp.transpose(sea)
    return turned[:rows], turned[rows:]


def first_kernel(bins, spectrum, sea_ref, ice_ref, wind_ref, out_a, out_b, edge, sems):
    columns, rows = sea_ref.shape
    copies = []
    for c in range(columns):
        for k, start in enumerate((0, rows - 8)):
            copy = pltpu.make_async_copy(
                spectrum.at[c, pl.ds(start, 8)], edge.at[k, c], sems.at[k]
            )
            copy.start()
            copies.append(copy)
    sea, gain = masks_kernel_part(sea_ref, ice_ref, wind_ref)
    shape = (8, LANES)
    lane = lane_index(shape)
    row = row_index(shape)
    used = bins % LANES
    for copy in copies:
        copy.wait()
    tiles = lane_tiles(bins)
    for second, out in ((False, out_a), (True, out_b)):
        to_south = south_flag(second)
        for pair in range(columns // 2):
            for tile in range(tiles):
                halves = []
                for c in (2 * pair, 2 * pair + 1):
                    low, high = read_tile(edge, (0, c), bins, tile), read_tile(edge, (1, c), bins, tile)
                    here = jnp.where(to_south, low, high)
                    s = jnp.where(to_south, sea[0:8, c : c + 1], sea[rows - 8 : rows, c : c + 1])
                    s = jnp.broadcast_to(s, shape)
                    value = here * s
                    if tile == tiles - 1:
                        g = jnp.where(to_south, gain[0:8, c : c + 1], gain[rows - 8 : rows, c : c + 1])
                        g = jnp.broadcast_to(g, shape)
                        value = jnp.where(lane < used, value, jnp.where(lane == used, s, g))
                    halves.append(value)
                first, other = halves
                keep = (row < DEPTH) == to_south
                out[pair, :, lanes_of(tile)] = jnp.where(keep, first, pltpu.roll(other, DEPTH, 0))


def load_kernel(
    bins, spectrum, sea_ref, ice_ref, wind_ref, speed_ref, angle_ref, coupling_ref,
    edge_a, edge_b, inner, seas, gains, stay, go_x, go_y, wide, sems, landed,
):
    columns, rows = sea_ref.shape
    copy = pltpu.make_async_copy(spectrum, landed, sems.at[0])
    copy.start()
    tiles = lane_tiles(bins)
    padded = tiles * LANES
    used = bins % LANES
    shape = (rows + 2 * DEPTH, LANES)
    row = row_index(shape)
    here = jnp.where(row >= rows + DEPTH, row - rows - 2 * DEPTH, row) + lax.axis_index("lat") * rows
    total = rows * lax.axis_size("lat")
    latitude = (-60.0 + 120.0 * (here.astype(jnp.float32) + 0.5) / total) * (math.pi / 180.0)
    over = 1.0 / jnp.cos(latitude)
    count = speed_ref.shape[0]
    for tile in range(tiles):
        which = angle_ref[2:3, lanes_of(tile)]
        speed = jnp.zeros((1, LANES), jnp.float32)
        for k in range(count):
            speed = jnp.where(which == float(k), speed_ref[k], speed)
        x = (angle_ref[0:1, lanes_of(tile)] * speed) * over
        y = angle_ref[1:2, lanes_of(tile)] * speed
        go_x[:, lanes_of(tile)] = x
        go_y[:, lanes_of(tile)] = jnp.broadcast_to(y, (8, LANES))
        stay[:, lanes_of(tile)] = 1.0 - x - y
    body = bins - used
    wide[:, :body] = jnp.concatenate(
        [coupling_ref[:, :body], jnp.zeros((padded - bins, body), jnp.bfloat16)], axis=0
    )
    tail = jnp.concatenate([coupling_ref[:, body:], jnp.ones((bins, padded - bins), jnp.bfloat16)], axis=1)
    wide[:, body:] = jnp.concatenate([tail, jnp.zeros((padded - bins, LANES), jnp.bfloat16)], axis=0)
    sea, gain = masks_kernel_part(sea_ref, ice_ref, wind_ref)
    for c in range(columns):
        s = jnp.broadcast_to(sea[:, c : c + 1], (rows, LANES))
        seas[c, :rows] = time_step * s
        gains[c, :rows] = s * jnp.broadcast_to(gain[:, c : c + 1], (rows, LANES))
    lane = lane_index((rows, LANES))
    copy.wait()

    def put(target, c):
        s = seas[c, :rows] != 0.0
        for tile in range(tiles):
            value = read_tile(landed, (c,), bins, tile)
            keep = s
            if tile == tiles - 1:
                keep = s & (lane < used)
            target[:rows, lanes_of(tile)] = jnp.where(keep, value, 0.0)

    for c in range(1, columns - 1):
        put(inner.at[c - 1], c)
    for second, target in ((False, edge_a), (True, edge_b)):
        put(target, jnp.where(west_flag(second), 0, columns - 1))


def join_kernel(
    bins, halo_a, halo_b, edge_a_in, edge_b_in, inner_in, seas_in, gains_in,
    edge_a, edge_b, inner, seas, gains, pack_a, pack_b,
):
    columns = seas.shape[0]
    rows = seas.shape[1] - 2 * DEPTH
    tiles = lane_tiles(bins)
    used = bins % LANES
    shape = (8, LANES)
    row = row_index(shape)
    lane = lane_index(shape)
    a_south = south_flag(False)
    top = row < DEPTH
    values = []
    for c in range(columns):
        tile_values = []
        for tile in range(tiles):
            from_a, from_b = halo_a[c // 2, :, lanes_of(tile)], halo_b[c // 2, :, lanes_of(tile)]
            low, high = jnp.where(a_south, from_a, from_b), jnp.where(a_south, from_b, from_a)
            if c % 2:
                low, high = pltpu.roll(low, DEPTH, 0), pltpu.roll(high, DEPTH, 0)
            tile_values.append(jnp.where(top, high, low))
        last = tile_values[-1]
        s = jnp.broadcast_to(last[:, used : used + 1], shape)
        g = jnp.broadcast_to(last[:, used + 1 : used + 2], shape)
        seas[c, rows:] = time_step * s
        gains[c, rows:] = s * g
        tile_values[-1] = jnp.where(lane < used, last, 0.0)
        values.append(tile_values)
    for tile in range(tiles):
        for c in range(1, columns - 1):
            inner[c - 1, rows:, lanes_of(tile)] = values[c][tile]
        for second, target in ((False, edge_a), (True, edge_b)):
            target[rows:, lanes_of(tile)] = jnp.where(
                west_flag(second), values[0][tile], values[columns - 1][tile]
            )
    for second, target, pack in ((False, edge_a, pack_a), (True, edge_b, pack_b)):
        packed = pack_half([target[:, lanes_of(t)] for t in range(tiles)], west_flag(second), bins)
        for k, value in enumerate(packed):
            pack[k] = value


def combine(adv, product, seas, gains, share):
    return adv * (gains - seas * share) + seas * product


def last_edge_kernel(bins, second, *refs):
    edge_step(bins, second, *refs[:10], None, refs[10])


def edge_kernel(bins, second, *refs):
    edge_step(bins, second, *refs)


def edge_step(bins, second, halo, edge, inner, seas, gains, stay, go_x, go_y, wide, out, pack, adv_ref):
    last = pack is None
    tiles = lane_tiles(bins)
    columns = inner.shape[0] + 2
    west = west_flag(second)
    near = jnp.where(west, 0, columns - 3)
    mine = jnp.where(west, 0, columns - 1)
    across = across_edge(
        [halo[k] for k in range(3)], [inner[near, :, lanes_of(t)] for t in range(tiles)], west, bins
    )
    for t in range(tiles):
        here = lanes_of(t)
        adv_ref[:, here] = advect(edge[:, here], across[t], stay[:, here], go_x[:, here], go_y[0:1, here], bins, t)
    product = jnp.dot(adv_ref[...].astype(jnp.bfloat16), wide[...], preferred_element_type=jnp.float32)
    share = jnp.broadcast_to(product[:, -1:], (product.shape[0], LANES)) * (dissipation / bins)
    s, g = seas[mine], gains[mine]
    fresh = []
    for t in range(tiles):
        here = lanes_of(t)
        fresh.append(combine(adv_ref[:, here], product[:, here], s, g, share))
        if last:
            write_tile(out, (), bins, t, fresh[-1])
        else:
            out[:, here] = fresh[-1]
    if not last:
        for k, value in enumerate(pack_half(fresh, west, bins)):
            pack[k] = value


def inner_kernel(bins, last, edge_a, edge_b, inner, seas, gains, stay, go_x, go_y, wide, out, adv_ref, low_ref):
    tiles = lane_tiles(bins)
    count, rows = inner.shape[0], inner.shape[1]
    a_west = west_flag(False)
    shape = (rows, LANES)
    for t in range(tiles):
        here = lanes_of(t)
        found = kinds(bins, t, is_east(bins))
        for c in range(count):
            west = east = None
            if True in found:
                west = inner[c - 1, :, here] if c else jnp.where(a_west, edge_a[:, here], edge_b[:, here])
            if False in found:
                east = inner[c + 1, :, here] if c < count - 1 else jnp.where(a_west, edge_b[:, here], edge_a[:, here])
            if west is None:
                across = east
            elif east is None:
                across = west
            else:
                across = jnp.where(eastward(bins, t, shape), west, east)
            adv = advect(inner[c, :, here], across, stay[:, here], go_x[:, here], go_y[0:1, here], bins, t)
            adv_ref[c, :, here] = adv
            low_ref[c * rows : (c + 1) * rows, here] = adv.astype(jnp.bfloat16)
    product = jnp.dot(low_ref[...], wide[...], preferred_element_type=jnp.float32)
    for c in range(count):
        part = product[c * rows : (c + 1) * rows]
        share = jnp.broadcast_to(part[:, -1:], shape) * (dissipation / bins)
        for t in range(tiles):
            here = lanes_of(t)
            value = combine(adv_ref[c, :, here], part[:, here], seas[c + 1], gains[c + 1], share)
            if last:
                write_tile(out, (c,), bins, t, value)
            else:
                out[c, :, here] = value


def finish_kernel(bins, edge_a, edge_b, inner, out, sems):
    columns, rows = out.shape[0], out.shape[1]
    a_west = west_flag(False)
    west = jnp.where(a_west, 0, columns - 1)
    copies = [
        pltpu.make_async_copy(inner, out.at[pl.ds(1, columns - 2)], sems.at[0]),
        pltpu.make_async_copy(edge_a, out.at[west], sems.at[1]),
        pltpu.make_async_copy(edge_b, out.at[columns - 1 - west], sems.at[2]),
    ]
    for copy in copies:
        copy.start()
    for copy in copies:
        copy.wait()


def angle_table(bins, freqs):
    padded = lane_tiles(bins) * LANES
    table = np.zeros((8, padded), np.float32)
    theta = (np.arange(DIRS) + 0.5) * (2.0 * math.pi / DIRS)
    table[0, :bins] = np.repeat(0.225 * np.abs(np.cos(theta)), freqs)
    table[1, :bins] = np.repeat(0.45 * np.abs(np.sin(theta)), freqs)
    table[2, :] = -1.0
    table[2, :bins] = np.tile(np.arange(freqs), DIRS)
    return table


def on_device(spectrum, sea_mask, ice_flags, wind_forcing, group_speed, coupling):
    columns, rows, bins = spectrum.shape
    tiles = lane_tiles(bins)
    padded = tiles * LANES
    tall = rows + 2 * DEPTH
    f32 = jnp.float32
    lon, lat = lax.axis_size("lon"), lax.axis_size("lat")
    lon_a, lon_b = swap_pairs(lon, 0, True), swap_pairs(lon, 1, True)
    lat_a, lat_b = swap_pairs(lat, 0, False), swap_pairs(lat, 1, False)
    vmem = pl.BlockSpec(memory_space=VMEM)
    smem = pl.BlockSpec(memory_space=SMEM)
    anywhere = pl.BlockSpec(memory_space=pl.ANY)
    edge_shape = VMEM((tall, padded), f32)
    inner_shape = VMEM((columns - 2, tall, padded), f32)
    mask_shape = VMEM((columns, tall, LANES), f32)
    pack_shape = VMEM((3, tall, LANES), f32)
    table_shape = VMEM((tall, padded), f32)

    def call(body, name, outs, ins, specs, scratch=(), aliases=None, flops=0, out_specs=None):
        return pl.pallas_call(
            body,
            name=name,
            out_shape=outs,
            in_specs=specs,
            out_specs=out_specs if out_specs is not None else jax.tree.map(lambda _: vmem, outs),
            scratch_shapes=list(scratch),
            input_output_aliases=aliases or {},
            cost_estimate=pl.CostEstimate(flops=flops, bytes_accessed=0, transcendentals=0),
            compiler_params=pltpu.CompilerParams(vmem_limit_bytes=24 * 1024 * 1024),
        )(*ins)

    send_a, send_b = call(
        functools.partial(first_kernel, bins), "first",
        (VMEM((columns // 2, 8, padded), f32),) * 2,
        (spectrum, sea_mask, ice_flags, wind_forcing),
        [anywhere, vmem, vmem, vmem],
        [VMEM((2, columns, 8, bins), f32), pltpu.SemaphoreType.DMA((2,))],
    )
    halo_a = lax.ppermute(send_a, "lat", lat_a)
    halo_b = lax.ppermute(send_b, "lat", lat_b)
    edge_a, edge_b, inner, seas, gains, stay, go_x, go_y, wide = call(
        functools.partial(load_kernel, bins), "load",
        (edge_shape, edge_shape, inner_shape, mask_shape, mask_shape, table_shape, table_shape,
         VMEM((8, padded), f32), VMEM((padded, padded), jnp.bfloat16)),
        (spectrum, sea_mask, ice_flags, wind_forcing, group_speed, jnp.asarray(angle_table(bins, group_speed.shape[0])), coupling),
        [anywhere, vmem, vmem, vmem, smem, vmem, vmem],
        [pltpu.SemaphoreType.DMA((1,)), VMEM((columns, rows, bins), f32)],
        flops=1 << 24,
    )
    edge_a, edge_b, inner, seas, gains, pack_a, pack_b = call(
        functools.partial(join_kernel, bins), "join",
        (edge_shape, edge_shape, inner_shape, mask_shape, mask_shape, pack_shape, pack_shape),
        (halo_a, halo_b, edge_a, edge_b, inner, seas, gains),
        [vmem] * 7,
        aliases={2: 0, 3: 1, 4: 2, 5: 3, 6: 4},
    )
    tables = (seas, gains, stay, go_x, go_y, wide)
    for step in range(STEPS):
        last = step == STEPS - 1
        halo_a = lax.ppermute(pack_a, "lon", lon_a)
        halo_b = lax.ppermute(pack_b, "lon", lon_b)
        new_inner = call(
            functools.partial(inner_kernel, bins, last), "inner",
            VMEM((columns - 2, rows, bins), f32) if last else inner_shape,
            (edge_a, edge_b, inner) + tables, [vmem] * 9,
            [VMEM((columns - 2, tall, padded), f32), VMEM(((columns - 2) * tall, padded), jnp.bfloat16)],
            flops=1 << 28,
        )
        fresh = []
        for second, halo, edge in ((False, halo_a, edge_a), (True, halo_b, edge_b)):
            body = functools.partial(edge_kernel, bins, second)
            if last:
                body = functools.partial(last_edge_kernel, bins, second)
            fresh.append(call(
                body, "edge", VMEM((rows, bins), f32) if last else (edge_shape, pack_shape),
                (halo, edge, inner) + tables, [vmem] * 9, [VMEM((tall, padded), f32)], flops=1 << 26,
            ))
        inner = new_inner
        if last:
            edge_a, edge_b = fresh
        else:
            (edge_a, pack_a), (edge_b, pack_b) = fresh
    return call(
        functools.partial(finish_kernel, bins), "finish",
        jax.ShapeDtypeStruct((columns, rows, bins), f32),
        (edge_a, edge_b, inner), [vmem] * 3,
        [pltpu.SemaphoreType.DMA((3,))], out_specs=anywhere,
    )


def solution(mesh):
    placed = (P("lon", "lat", None), P("lon", "lat"), P("lon", "lat"), P("lon", "lat"), P(), P())
    return jax.shard_map(
        on_device, mesh=mesh, in_specs=placed, out_specs=P("lon", "lat", None), check_vma=False
    )
```

time: 68.2 us -> 41.3 us (0.61)
  the two profiles are of different devices: /device:TPU:1 before, /device:TPU:24 now
where the time goes in v1:
time: 41.3 us; the launch traced here: 41.1 us
  starting transfers between devices  15.6 us (38%)
  Pallas kernels  12.6 us (31%)
  waiting for transfers between devices  9.26 us (22%)
  local copies, waits for them, and re-layouts  3.48 us (8%)
    pallas_call x16, Pallas kernels, call(): pl.pallas_call(body, name=name, out_shape=outs, in_specs=specs, out_specs...  12.6 us
    ppermute x4, starting transfers between devices, on_device(): halo_b = lax.ppermute(pack_b, 'lon', lon_b)  10.1 us
    ppermute x4, waiting for transfers between devices, on_device(): halo_b = lax.ppermute(pack_b, 'lon', lon_b)  5.94 us
    unnamed x14, local copies, waits for them, and re-layouts  3.48 us
    ppermute x4, starting transfers between devices, on_device(): halo_a = lax.ppermute(pack_a, 'lon', lon_a)  2.99 us
    ppermute x1, starting transfers between devices, on_device(): halo_b = lax.ppermute(send_b, 'lat', lat_b)  2.45 us
    ppermute x1, waiting for transfers between devices, on_device(): halo_b = lax.ppermute(send_b, 'lat', lat_b)  2.08 us
    ppermute x4, waiting for transfers between devices, on_device(): halo_a = lax.ppermute(pack_a, 'lon', lon_a)  1.24 us
  transfers between devices with their start and end apart: 10, of which 5 were waited for; matrix products, arithmetic and copies ran while one was open for 0% of the time, Pallas kernels for 24%

profile of v1, /device:TPU:24, one launch (start us, length us, event | category | flops | bytes accessed | tf_op | source)
XLA Modules:
  0.0 41.1 jit_solution(12810857059546922089)
XLA Ops:
  0.0 0.0 copy-start
  0.0 1.4 %copy-done = f32[8,64,648]{2,1,0:T(8,128)S(1)} copy-done((f32[8,64,648]{2,1,0:T(8,128)S(1)}, f32[8,64,648]{2,1,0:T(8,128)}, u32[]{:S(2)}) %copy-start) | copy-done | bytes 1327128
  1.4 0.0 copy-start.3
  1.4 0.7 %copy-done.3 = s32[8,64]{1,0:T(8,128)S(1)} copy-done((s32[8,64]{1,0:T(8,128)S(1)}, s32[8,64]{1,0:T(8,128)}, u32[]{:S(2)}) %copy-start.3) | copy-done | bytes 2072
  2.1 0.0 copy-start.4
  2.1 0.7 %copy-done.4 = s32[8,64]{1,0:T(8,128)S(1)} copy-done((s32[8,64]{1,0:T(8,128)S(1)}, s32[8,64]{1,0:T(8,128)}, u32[]{:S(2)}) %copy-start.4) | copy-done | bytes 2072
  2.8 0.0 copy-start.5
  2.8 0.7 %copy-done.5 = f32[8,64]{1,0:T(8,128)S(1)} copy-done((f32[8,64]{1,0:T(8,128)S(1)}, f32[8,64]{1,0:T(8,128)}, u32[]{:S(2)}) %copy-start.5) | copy-done | bytes 2072
  3.5 0.0 copy-start.1
  3.5 0.8 %first.1 = (f32[4,8,768]{2,1,0:T(8,128)S(1)}, f32[4,8,768]{2,1,0:T(8,128)S(1)}) custom-call(f32[8,64,648]{2,1,0:T(8,128)S(1)} %copy-done, s32[8,64]{1,0:T(8,128)S(1)} %copy-done.3, s32[8,64]{1,0:T(8,128)S(1)} %copy-done.4, f32[8,64]{1,0:T(8,128)S(1)} %copy-done.5), custom_call_target="tpu_custom_call" | custom-call | tf_op jit(solution)/shard_map/first/pallas_call | solution.py:412
  4.3 0.1 collective-permute-start
  4.4 2.4 %collective-permute-start.1 = (f32[4,8,768]{2,1,0:T(8,128)S(1)}, f32[4,8,768]{2,1,0:T(8,128)S(1)}, u32[]{:S(2)}, u32[]{:S(2)}) collective-permute-start(f32[4,8,768]{2,1,0:T(8,128)S(1)} %get-tuple-element.36), channel_id=1, source_target_pairs={{1,2},{2,1},{3,4},{4,3},{5,6},{6,5},{9,10},{10,9},{11,12},{12,11},... | collective-permute-start | bytes 294920 | tf_op jit(solution)/shard_map/ppermute | solution.py:432
  6.9 0.0 copy-done.1
  6.9 0.0 copy-done.2
  6.9 0.0 copy-done.6
  6.9 1.4 %load.1 = (f32[72,768]{1,0:T(8,128)S(1)}, f32[72,768]{1,0:T(8,128)S(1)}, f32[6,72,768]{2,1,0:T(8,128)S(1)}, f32[8,72,128]{2,1,0:T(8,128)S(1)}, f32[8,72,128]{2,1...) custom-call(f32[8,64,648]{2,1,0:T(8,128)S(1)} %copy-done, ...), custom_call_target="tpu_custom_call" | custom-call | flops 16777216 | tf_op jit(solution)/shard_map/load/pallas_call | solution.py:412
  8.3 0.0 collective-permute-done.halo_a
  8.3 2.1 %collective-permute-done.1.halo_b = f32[4,8,768]{2,1,0:T(8,128)S(1)} collective-permute-done((f32[4,8,768]{2,1,0:T(8,128)S(1)}, f32[4,8,768]{2,1,0:T(8,128)S(1)}, u32[]{:S(2)}, u32[]{:S(2)}) %collective-permute-start.1) | collective-permute-done | bytes 98336 | tf_op jit(solution)/shard_map/ppermute | solution.py:432
  10.3 0.1 join.1
  10.5 2.5 %collective-permute-start.5 = (f32[3,72,128]{2,1,0:T(8,128)S(1)}, f32[3,72,128]{2,1,0:T(8,128)S(1)}, u32[]{:S(2)}, u32[]{:S(2)}) collective-permute-start(f32[3,72,128]{2,1,0:T(8,128)S(1)} %get-tuple-element.56), channel_id=1, source_target_pairs={{8,16},{16,8},{24,0},{0,24},{9,17},{17,9},{25,1},{1,25},{10,18},{1... | collective-permute-start | bytes 331784 | tf_op jit(solution)/shard_map/ppermute | solution.py:453
  13.0 0.5 %collective-permute-start.2 = (f32[3,72,128]{2,1,0:T(8,128)S(1)}, f32[3,72,128]{2,1,0:T(8,128)S(1)}, u32[]{:S(2)}, u32[]{:S(2)}) collective-permute-start(f32[3,72,128]{2,1,0:T(8,128)S(1)} %get-tuple-element.42), channel_id=1, source_target_pairs={{0,8},{8,0},{16,24},{24,16},{1,9},{9,1},{17,25},{25,17},{2,10},{10... | collective-permute-start | bytes 331784 | tf_op jit(solution)/shard_map/ppermute | solution.py:452
  13.5 3.1 %collective-permute-done.5.refs_0_ = f32[3,72,128]{2,1,0:T(8,128)S(1)} collective-permute-done((f32[3,72,128]{2,1,0:T(8,128)S(1)}, f32[3,72,128]{2,1,0:T(8,128)S(1)}, u32[]{:S(2)}, u32[]{:S(2)}) %collective-permute-start.5) | collective-permute-done | bytes 110624 | tf_op jit(solution)/shard_map/ppermute | solution.py:453
  16.6 0.5 %edge.10 = (f32[72,768]{1,0:T(8,128)S(1)}, f32[3,72,128]{2,1,0:T(8,128)S(1)}) custom-call(f32[3,72,128]{2,1,0:T(8,128)S(1)} %collective-permute-done.5.refs_0_, f32[72,768]{1,0:T(8,128)S(1)} %get-tuple-element.53.edge_b.refs_1_, f32[6,72,768]{2,1,0:T(8,128)S(1)} %get-tuple-element.44.refs_2_.inner, f32[8,72,128]{2,1,0:T(8,128)S(1)} %get-tuple-element.45.refs_3_.seas, ...), custom_call_target="tpu_custom_call" | custom-call | flops 67108864 | tf_op jit(solution)/shard_map/edge/pallas_call | solution.py:412
  17.1 2.5 %collective-permute-start.7 = (f32[3,72,128]{2,1,0:T(8,128)S(1)}, f32[3,72,128]{2,1,0:T(8,128)S(1)}, u32[]{:S(2)}, u32[]{:S(2)}) collective-permute-start(f32[3,72,128]{2,1,0:T(8,128)S(1)} %get-tuple-element.60), channel_id=1, source_target_pairs={{8,16},{16,8},{24,0},{0,24},{9,17},{17,9},{25,1},{1,25},{10,18},{1... | collective-permute-start | bytes 331784 | tf_op jit(solution)/shard_map/ppermute | solution.py:453
  19.6 0.0 collective-permute-done.2.refs_0_
  19.7 0.5 %edge.8 = (f32[72,768]{1,0:T(8,128)S(1)}, f32[3,72,128]{2,1,0:T(8,128)S(1)}) custom-call(f32[3,72,128]{2,1,0:T(8,128)S(1)} %collective-permute-done.2.refs_0_, f32[72,768]{1,0:T(8,128)S(1)} %get-tuple-element.43.refs_1_.edge_a, f32[6,72,768]{2,1,0:T(8,128)S(1)} %get-tuple-element.44.refs_2_.inner, f32[8,72,128]{2,1,0:T(8,128)S(1)} %get-tuple-element.45.refs_3_.seas, ...), custom_call_target="tpu_custom_call" | custom-call | flops 67108864 | tf_op jit(solution)/shard_map/edge/pallas_call | solution.py:412
  20.2 0.9 %collective-permute-start.3 = (f32[3,72,128]{2,1,0:T(8,128)S(1)}, f32[3,72,128]{2,1,0:T(8,128)S(1)}, u32[]{:S(2)}, u32[]{:S(2)}) collective-permute-start(f32[3,72,128]{2,1,0:T(8,128)S(1)} %get-tuple-element.51), channel_id=1, source_target_pairs={{0,8},{8,0},{16,24},{24,16},{1,9},{9,1},{17,25},{25,17},{2,10},{10... | collective-permute-start | bytes 331784 | tf_op jit(solution)/shard_map/ppermute | solution.py:452
  21.1 1.3 %inner.4.refs_2_ = f32[6,72,768]{2,1,0:T(8,128)S(1)} custom-call(f32[72,768]{1,0:T(8,128)S(1)} %get-tuple-element.43.refs_1_.edge_a, f32[72,768]{1,0:T(8,128)S(1)} %get-tuple-element.53.edge_b.refs_1_, f32[6,72,768]{2,1,0:T(8,128)S(1)} %get-tuple-element.44.refs_2_.inner, f32[8,72,128]{2,1,0:T(8,128)S(1)} %get-tuple-element.45.refs_3_.seas, ...), custom_call_target="tpu_custom_call" | custom-call | flops 268435456 | tf_op jit(solution)/shard_map/inner/pallas_call | solution.py:412
  22.4 1.3 %collective-permute-done.7.refs_0_ = f32[3,72,128]{2,1,0:T(8,128)S(1)} collective-permute-done((f32[3,72,128]{2,1,0:T(8,128)S(1)}, f32[3,72,128]{2,1,0:T(8,128)S(1)}, u32[]{:S(2)}, u32[]{:S(2)}) %collective-permute-start.7) | collective-permute-done | bytes 110624 | tf_op jit(solution)/shard_map/ppermute | solution.py:453
  23.7 0.5 %edge.12 = (f32[72,768]{1,0:T(8,128)S(1)}, f32[3,72,128]{2,1,0:T(8,128)S(1)}) custom-call(f32[3,72,128]{2,1,0:T(8,128)S(1)} %collective-permute-done.7.refs_0_, f32[72,768]{1,0:T(8,128)S(1)} %get-tuple-element.57.edge_b.refs_1_, f32[6,72,768]{2,1,0:T(8,128)S(1)} %inner.4.refs_2_, f32[8,72,128]{2,1,0:T(8,128)S(1)} %get-tuple-element.45.refs_3_.seas, ...), custom_call_target="tpu_custom_call" | custom-call | flops 67108864 | tf_op jit(solution)/shard_map/edge/pallas_call | solution.py:412
  24.2 2.5 %collective-permute-start.8 = (f32[3,72,128]{2,1,0:T(8,128)S(1)}, f32[3,72,128]{2,1,0:T(8,128)S(1)}, u32[]{:S(2)}, u32[]{:S(2)}) collective-permute-start(f32[3,72,128]{2,1,0:T(8,128)S(1)} %get-tuple-element.62), channel_id=1, source_target_pairs={{8,16},{16,8},{24,0},{0,24},{9,17},{17,9},{25,1},{1,25},{10,18},{1... | collective-permute-start | bytes 331784 | tf_op jit(solution)/shard_map/ppermute | solution.py:453
  26.7 0.0 collective-permute-done.3.refs_0_
  26.7 0.5 %edge.9 = (f32[72,768]{1,0:T(8,128)S(1)}, f32[3,72,128]{2,1,0:T(8,128)S(1)}) custom-call(f32[3,72,128]{2,1,0:T(8,128)S(1)} %collective-permute-done.3.refs_0_, f32[72,768]{1,0:T(8,128)S(1)} %get-tuple-element.52.refs_1_.edge_a, f32[6,72,768]{2,1,0:T(8,128)S(1)} %inner.4.refs_2_, f32[8,72,128]{2,1,0:T(8,128)S(1)} %get-tuple-element.45.refs_3_.seas, ...), custom_call_target="tpu_custom_call" | custom-call | flops 67108864 | tf_op jit(solution)/shard_map/edge/pallas_call | solution.py:412
  27.2 0.9 %collective-permute-start.4 = (f32[3,72,128]{2,1,0:T(8,128)S(1)}, f32[3,72,128]{2,1,0:T(8,128)S(1)}, u32[]{:S(2)}, u32[]{:S(2)}) collective-permute-start(f32[3,72,128]{2,1,0:T(8,128)S(1)} %get-tuple-element.54), channel_id=1, source_target_pairs={{0,8},{8,0},{16,24},{24,16},{1,9},{9,1},{17,25},{25,17},{2,10},{10... | collective-permute-start | bytes 331784 | tf_op jit(solution)/shard_map/ppermute | solution.py:452
  28.2 1.3 %inner.5.refs_2_ = f32[6,72,768]{2,1,0:T(8,128)S(1)} custom-call(f32[72,768]{1,0:T(8,128)S(1)} %get-tuple-element.52.refs_1_.edge_a, f32[72,768]{1,0:T(8,128)S(1)} %get-tuple-element.57.edge_b.refs_1_, f32[6,72,768]{2,1,0:T(8,128)S(1)} %inner.4.refs_2_, f32[8,72,128]{2,1,0:T(8,128)S(1)} %get-tuple-element.45.refs_3_.seas, ...), custom_call_target="tpu_custom_call" | custom-call | flops 268435456 | tf_op jit(solution)/shard_map/inner/pallas_call | solution.py:412
  29.5 1.6 %collective-permute-done.8.refs_0_ = f32[3,72,128]{2,1,0:T(8,128)S(1)} collective-permute-done((f32[3,72,128]{2,1,0:T(8,128)S(1)}, f32[3,72,128]{2,1,0:T(8,128)S(1)}, u32[]{:S(2)}, u32[]{:S(2)}) %collective-permute-start.8) | collective-permute-done | bytes 110624 | tf_op jit(solution)/shard_map/ppermute | solution.py:453
  31.1 0.5 %edge.14 = (f32[72,768]{1,0:T(8,128)S(1)}, f32[3,72,128]{2,1,0:T(8,128)S(1)}) custom-call(f32[3,72,128]{2,1,0:T(8,128)S(1)} %collective-permute-done.8.refs_0_, f32[72,768]{1,0:T(8,128)S(1)} %get-tuple-element.61.edge_b.refs_1_, f32[6,72,768]{2,1,0:T(8,128)S(1)} %inner.5.refs_2_, f32[8,72,128]{2,1,0:T(8,128)S(1)} %get-tuple-element.45.refs_3_.seas, ...), custom_call_target="tpu_custom_call" | custom-call | flops 67108864 | tf_op jit(solution)/shard_map/edge/pallas_call | solution.py:412
  31.6 2.5 %collective-permute-start.9 = (f32[3,72,128]{2,1,0:T(8,128)S(1)}, f32[3,72,128]{2,1,0:T(8,128)S(1)}, u32[]{:S(2)}, u32[]{:S(2)}) collective-permute-start(f32[3,72,128]{2,1,0:T(8,128)S(1)} %get-tuple-element.63), channel_id=1, source_target_pairs={{8,16},{16,8},{24,0},{0,24},{9,17},{17,9},{25,1},{1,25},{10,18},{1... | collective-permute-start | bytes 331784 | tf_op jit(solution)/shard_map/ppermute | solution.py:453
  34.1 0.0 collective-permute-done.4.refs_0_
  34.1 0.5 %edge.11 = (f32[72,768]{1,0:T(8,128)S(1)}, f32[3,72,128]{2,1,0:T(8,128)S(1)}) custom-call(f32[3,72,128]{2,1,0:T(8,128)S(1)} %collective-permute-done.4.refs_0_, f32[72,768]{1,0:T(8,128)S(1)} %get-tuple-element.55.refs_1_.edge_a, f32[6,72,768]{2,1,0:T(8,128)S(1)} %inner.5.refs_2_, f32[8,72,128]{2,1,0:T(8,128)S(1)} %get-tuple-element.45.refs_3_.seas, ...), custom_call_target="tpu_custom_call" | custom-call | flops 67108864 | tf_op jit(solution)/shard_map/edge/pallas_call | solution.py:412
  34.7 0.6 %collective-permute-start.6 = (f32[3,72,128]{2,1,0:T(8,128)S(1)}, f32[3,72,128]{2,1,0:T(8,128)S(1)}, u32[]{:S(2)}, u32[]{:S(2)}) collective-permute-start(f32[3,72,128]{2,1,0:T(8,128)S(1)} %get-tuple-element.58), channel_id=1, source_target_pairs={{0,8},{8,0},{16,24},{24,16},{1,9},{9,1},{17,25},{25,17},{2,10},{10... | collective-permute-start | bytes 331784 | tf_op jit(solution)/shard_map/ppermute | solution.py:452
  35.2 1.3 %inner.6.refs_2_ = f32[6,72,768]{2,1,0:T(8,128)S(1)} custom-call(f32[72,768]{1,0:T(8,128)S(1)} %get-tuple-element.55.refs_1_.edge_a, f32[72,768]{1,0:T(8,128)S(1)} %get-tuple-element.61.edge_b.refs_1_, f32[6,72,768]{2,1,0:T(8,128)S(1)} %inner.5.refs_2_, f32[8,72,128]{2,1,0:T(8,128)S(1)} %get-tuple-element.45.refs_3_.seas, ...), custom_call_target="tpu_custom_call" | custom-call | flops 268435456 | tf_op jit(solution)/shard_map/inner/pallas_call | solution.py:412
  36.5 1.3 %inner.7 = f32[6,64,648]{2,1,0:T(8,128)S(1)} custom-call(f32[72,768]{1,0:T(8,128)S(1)} %get-tuple-element.59.refs_1_.edge_a, f32[72,768]{1,0:T(8,128)S(1)} %get-tuple-element.64.refs_1_.edge_b, f32[6,72,768]{2,1,0:T(8,128)S(1)} %inner.6.refs_2_, f32[8,72,128]{2,1,0:T(8,128)S(1)} %get-tuple-element.45.refs_3_.seas, ...), custom_call_target="tpu_custom_call" | custom-call | flops 268435456 | tf_op jit(solution)/shard_map/inner/pallas_call | solution.py:412
  37.8 0.0 collective-permute-done.9.refs_0_
  37.8 0.4 %edge.15.edge_b = f32[64,648]{1,0:T(8,128)S(1)} custom-call(f32[3,72,128]{2,1,0:T(8,128)S(1)} %collective-permute-done.9.refs_0_, f32[72,768]{1,0:T(8,128)S(1)} %get-tuple-element.64.refs_1_.edge_b, f32[6,72,768]{2,1,0:T(8,128)S(1)} %inner.6.refs_2_, f32[8,72,128]{2,1,0:T(8,128)S(1)} %get-tuple-element.45.refs_3_.seas, ...), custom_call_target="tpu_custom_call" | custom-call | flops 67108864 | tf_op jit(solution)/shard_map/edge/pallas_call | solution.py:412
  38.2 1.2 %collective-permute-done.6.refs_0_ = f32[3,72,128]{2,1,0:T(8,128)S(1)} collective-permute-done((f32[3,72,128]{2,1,0:T(8,128)S(1)}, f32[3,72,128]{2,1,0:T(8,128)S(1)}, u32[]{:S(2)}, u32[]{:S(2)}) %collective-permute-start.6) | collective-permute-done | bytes 110624 | tf_op jit(solution)/shard_map/ppermute | solution.py:452
  39.5 0.5 %edge.13.edge_a = f32[64,648]{1,0:T(8,128)S(1)} custom-call(f32[3,72,128]{2,1,0:T(8,128)S(1)} %collective-permute-done.6.refs_0_, f32[72,768]{1,0:T(8,128)S(1)} %get-tuple-element.59.refs_1_.edge_a, f32[6,72,768]{2,1,0:T(8,128)S(1)} %inner.6.refs_2_, f32[8,72,128]{2,1,0:T(8,128)S(1)} %get-tuple-element.45.refs_3_.seas, ...), custom_call_target="tpu_custom_call" | custom-call | flops 67108864 | tf_op jit(solution)/shard_map/edge/pallas_call | solution.py:412
  39.9 1.2 %finish.1 = f32[8,64,648]{2,1,0:T(8,128)} custom-call(f32[64,648]{1,0:T(8,128)S(1)} %edge.13.edge_a, f32[64,648]{1,0:T(8,128)S(1)} %edge.15.edge_b, f32[6,64,648]{2,1,0:T(8,128)S(1)} %inner.7), custom_call_target="tpu_custom_call" | custom-call | tf_op jit(solution)/shard_map/finish/pallas_call | solution.py:412
  (2 shorter events, 0.0 us)
Async XLA Ops:
  0.0 1.4 %copy-start = (f32[8,64,648]{2,1,0:T(8,128)S(1)}, f32[8,64,648]{2,1,0:T(8,128)}, u32[]{:S(2)}) copy-start(f32[8,64,648]{2,1,0:T(8,128)} %spectrum.3) | copy-start | bytes 3981316
  1.4 0.7 %copy-start.3 = (s32[8,64]{1,0:T(8,128)S(1)}, s32[8,64]{1,0:T(8,128)}, u32[]{:S(2)}) copy-start(s32[8,64]{1,0:T(8,128)} %sea_ref.3) | copy-start | bytes 6148
  2.1 0.7 %copy-start.4 = (s32[8,64]{1,0:T(8,128)S(1)}, s32[8,64]{1,0:T(8,128)}, u32[]{:S(2)}) copy-start(s32[8,64]{1,0:T(8,128)} %ice_ref.3) | copy-start | bytes 6148
  2.8 0.7 %copy-start.5 = (f32[8,64]{1,0:T(8,128)S(1)}, f32[8,64]{1,0:T(8,128)}, u32[]{:S(2)}) copy-start(f32[8,64]{1,0:T(8,128)} %wind_ref.3) | copy-start | bytes 6148
  3.5 3.4 %copy-start.1 = (bf16[648,648]{1,0:T(8,128)(2,1)S(1)}, bf16[648,648]{1,0:T(8,128)(2,1)}, u32[]{:S(2)}) copy-start(bf16[648,648]{1,0:T(8,128)(2,1)} %coupling_ref.1) | copy-start | bytes 2519428
  3.5 3.4 %copy-start.2 = (f32[8,768]{1,0:T(8,128)S(1)}, f32[8,768]{1,0:T(8,128)}, u32[]{:S(2)}) copy-start(f32[8,768]{1,0:T(8,128)} %constant.2.clone.angle_ref) | copy-start | bytes 73732
  3.5 3.4 %copy-start.6 = (f32[18]{0:T(128)S(1)}, f32[18]{0:T(128)}, u32[]{:S(2)}) copy-start(f32[18]{0:T(128)} %speed_ref.1) | copy-start | bytes 220
  4.3 3.9 %collective-permute-start = (f32[4,8,768]{2,1,0:T(8,128)S(1)}, f32[4,8,768]{2,1,0:T(8,128)S(1)}, u32[]{:S(2)}, u32[]{:S(2)}) collective-permute-start(f32[4,8,768]{2,1,0:T(8,128)S(1)} %get-tuple-element.35), channel_id=1, source_target_pairs={{0,1},{1,0},{2,3},{3,2},{4,5},{5,4},{6,7},{7,6},{8,9},{9,8},{10,11... | collective-permute-start | bytes 294920 | tf_op jit(solution)/shard_map/ppermute | solution.py:431
  4.4 5.9 %collective-permute-start.1 = (f32[4,8,768]{2,1,0:T(8,128)S(1)}, f32[4,8,768]{2,1,0:T(8,128)S(1)}, u32[]{:S(2)}, u32[]{:S(2)}) collective-permute-start(f32[4,8,768]{2,1,0:T(8,128)S(1)} %get-tuple-element.36), channel_id=1, source_target_pairs={{1,2},{2,1},{3,4},{4,3},{5,6},{6,5},{9,10},{10,9},{11,12},{12,11},... | collective-permute-start | bytes 294920 | tf_op jit(solution)/shard_map/ppermute | solution.py:432
  10.5 6.1 %collective-permute-start.5 = (f32[3,72,128]{2,1,0:T(8,128)S(1)}, f32[3,72,128]{2,1,0:T(8,128)S(1)}, u32[]{:S(2)}, u32[]{:S(2)}) collective-permute-start(f32[3,72,128]{2,1,0:T(8,128)S(1)} %get-tuple-element.56), channel_id=1, source_target_pairs={{8,16},{16,8},{24,0},{0,24},{9,17},{17,9},{25,1},{1,25},{10,18},{1... | collective-permute-start | bytes 331784 | tf_op jit(solution)/shard_map/ppermute | solution.py:453
  13.0 6.7 %collective-permute-start.2 = (f32[3,72,128]{2,1,0:T(8,128)S(1)}, f32[3,72,128]{2,1,0:T(8,128)S(1)}, u32[]{:S(2)}, u32[]{:S(2)}) collective-permute-start(f32[3,72,128]{2,1,0:T(8,128)S(1)} %get-tuple-element.42), channel_id=1, source_target_pairs={{0,8},{8,0},{16,24},{24,16},{1,9},{9,1},{17,25},{25,17},{2,10},{10... | collective-permute-start | bytes 331784 | tf_op jit(solution)/shard_map/ppermute | solution.py:452
  17.1 6.5 %collective-permute-start.7 = (f32[3,72,128]{2,1,0:T(8,128)S(1)}, f32[3,72,128]{2,1,0:T(8,128)S(1)}, u32[]{:S(2)}, u32[]{:S(2)}) collective-permute-start(f32[3,72,128]{2,1,0:T(8,128)S(1)} %get-tuple-element.60), channel_id=1, source_target_pairs={{8,16},{16,8},{24,0},{0,24},{9,17},{17,9},{25,1},{1,25},{10,18},{1... | collective-permute-start | bytes 331784 | tf_op jit(solution)/shard_map/ppermute | solution.py:453
  20.2 6.5 %collective-permute-start.3 = (f32[3,72,128]{2,1,0:T(8,128)S(1)}, f32[3,72,128]{2,1,0:T(8,128)S(1)}, u32[]{:S(2)}, u32[]{:S(2)}) collective-permute-start(f32[3,72,128]{2,1,0:T(8,128)S(1)} %get-tuple-element.51), channel_id=1, source_target_pairs={{0,8},{8,0},{16,24},{24,16},{1,9},{9,1},{17,25},{25,17},{2,10},{10... | collective-permute-start | bytes 331784 | tf_op jit(solution)/shard_map/ppermute | solution.py:452
  24.2 6.9 %collective-permute-start.8 = (f32[3,72,128]{2,1,0:T(8,128)S(1)}, f32[3,72,128]{2,1,0:T(8,128)S(1)}, u32[]{:S(2)}, u32[]{:S(2)}) collective-permute-start(f32[3,72,128]{2,1,0:T(8,128)S(1)} %get-tuple-element.62), channel_id=1, source_target_pairs={{8,16},{16,8},{24,0},{0,24},{9,17},{17,9},{25,1},{1,25},{10,18},{1... | collective-permute-start | bytes 331784 | tf_op jit(solution)/shard_map/ppermute | solution.py:453
  27.2 6.9 %collective-permute-start.4 = (f32[3,72,128]{2,1,0:T(8,128)S(1)}, f32[3,72,128]{2,1,0:T(8,128)S(1)}, u32[]{:S(2)}, u32[]{:S(2)}) collective-permute-start(f32[3,72,128]{2,1,0:T(8,128)S(1)} %get-tuple-element.54), channel_id=1, source_target_pairs={{0,8},{8,0},{16,24},{24,16},{1,9},{9,1},{17,25},{25,17},{2,10},{10... | collective-permute-start | bytes 331784 | tf_op jit(solution)/shard_map/ppermute | solution.py:452
  31.6 6.2 %collective-permute-start.9 = (f32[3,72,128]{2,1,0:T(8,128)S(1)}, f32[3,72,128]{2,1,0:T(8,128)S(1)}, u32[]{:S(2)}, u32[]{:S(2)}) collective-permute-start(f32[3,72,128]{2,1,0:T(8,128)S(1)} %get-tuple-element.63), channel_id=1, source_target_pairs={{8,16},{16,8},{24,0},{0,24},{9,17},{17,9},{25,1},{1,25},{10,18},{1... | collective-permute-start | bytes 331784 | tf_op jit(solution)/shard_map/ppermute | solution.py:453
  34.7 4.8 %collective-permute-start.6 = (f32[3,72,128]{2,1,0:T(8,128)S(1)}, f32[3,72,128]{2,1,0:T(8,128)S(1)}, u32[]{:S(2)}, u32[]{:S(2)}) collective-permute-start(f32[3,72,128]{2,1,0:T(8,128)S(1)} %get-tuple-element.58), channel_id=1, source_target_pairs={{0,8},{8,0},{16,24},{24,16},{1,9},{9,1},{17,25},{25,17},{2,10},{10... | collective-permute-start | bytes 331784 | tf_op jit(solution)/shard_map/ppermute | solution.py:452

commit v2 on v1

--- a/solution.py
+++ b/solution.py
@@ -150,9 +150,15 @@
     return turned[:rows], turned[rows:]
 
 
-def first_kernel(bins, spectrum, sea_ref, ice_ref, wind_ref, out_a, out_b, edge, sems):
+def first_kernel(bins, spectrum, sea_hbm, ice_hbm, wind_hbm, out_a, out_b, edge, sea_ref, ice_ref, wind_ref, sems):
     columns, rows = sea_ref.shape
     copies = []
+    masks = [
+        pltpu.make_async_copy(source, target, sems.at[2 + k])
+        for k, (source, target) in enumerate(((sea_hbm, sea_ref), (ice_hbm, ice_ref), (wind_hbm, wind_ref)))
+    ]
+    for copy in masks:
+        copy.start()
     for c in range(columns):
         for k, start in enumerate((0, rows - 8)):
             copy = pltpu.make_async_copy(
@@ -160,6 +166,8 @@
             )
             copy.start()
             copies.append(copy)
+    for copy in masks:
+        copy.wait()
     sea, gain = masks_kernel_part(sea_ref, ice_ref, wind_ref)
     shape = (8, LANES)
     lane = lane_index(shape)
@@ -189,13 +197,7 @@
                 out[pair, :, lanes_of(tile)] = jnp.where(keep, first, pltpu.roll(other, DEPTH, 0))
 
 
-def load_kernel(
-    bins, spectrum, sea_ref, ice_ref, wind_ref, speed_ref, angle_ref, coupling_ref,
-    edge_a, edge_b, inner, seas, gains, stay, go_x, go_y, wide, sems, landed,
-):
-    columns, rows = sea_ref.shape
-    copy = pltpu.make_async_copy(spectrum, landed, sems.at[0])
-    copy.start()
+def table_kernel(bins, rows, speed_ref, angle_ref, coupling_ref, stay, go_x, go_y, wide):
     tiles = lane_tiles(bins)
     padded = tiles * LANES
     used = bins % LANES
@@ -222,18 +224,23 @@
     )
     tail = jnp.concatenate([coupling_ref[:, body:], jnp.ones((bins, padded - bins), jnp.bfloat16)], axis=1)
     wide[:, body:] = jnp.concatenate([tail, jnp.zeros((padded - bins, LANES), jnp.bfloat16)], axis=0)
+
+
+def load_kernel(bins, spectrum, sea_ref, ice_ref, wind_ref, edge_a, edge_b, inner, seas, gains):
+    columns, rows = sea_ref.shape
+    tiles = lane_tiles(bins)
+    used = bins % LANES
     sea, gain = masks_kernel_part(sea_ref, ice_ref, wind_ref)
     for c in range(columns):
         s = jnp.broadcast_to(sea[:, c : c + 1], (rows, LANES))
         seas[c, :rows] = time_step * s
         gains[c, :rows] = s * jnp.broadcast_to(gain[:, c : c + 1], (rows, LANES))
     lane = lane_index((rows, LANES))
-    copy.wait()
 
     def put(target, c):
         s = seas[c, :rows] != 0.0
         for tile in range(tiles):
-            value = read_tile(landed, (c,), bins, tile)
+            value = read_tile(spectrum, (c,), bins, tile)
             keep = s
             if tile == tiles - 1:
                 keep = s & (lane < used)
@@ -291,8 +298,12 @@
     return adv * (gains - seas * share) + seas * product
 
 
-def last_edge_kernel(bins, second, *refs):
-    edge_step(bins, second, *refs[:10], None, refs[10])
+def last_edge_kernel(bins, second, halo, edge, inner, seas, gains, stay, go_x, go_y, wide, whole, out, adv_ref, column, sem):
+    edge_step(bins, second, halo, edge, inner, seas, gains, stay, go_x, go_y, wide, column, None, adv_ref)
+    mine = jnp.where(west_flag(second), 0, out.shape[0] - 1)
+    copy = pltpu.make_async_copy(column, out.at[mine], sem.at[0])
+    copy.start()
+    copy.wait()
 
 
 def edge_kernel(bins, second, *refs):
@@ -328,7 +339,7 @@
             pack[k] = value
 
 
-def inner_kernel(bins, last, edge_a, edge_b, inner, seas, gains, stay, go_x, go_y, wide, out, adv_ref, low_ref):
+def inner_kernel(bins, last, edge_a, edge_b, inner, seas, gains, stay, go_x, go_y, wide, out, adv_ref, low_ref, done=None, sems=None):
     tiles = lane_tiles(bins)
     count, rows = inner.shape[0], inner.shape[1]
     a_west = west_flag(False)
@@ -359,24 +370,14 @@
             here = lanes_of(t)
             value = combine(adv_ref[c, :, here], part[:, here], seas[c + 1], gains[c + 1], share)
             if last:
-                write_tile(out, (c,), bins, t, value)
+                write_tile(done, (c,), bins, t, value)
             else:
                 out[c, :, here] = value
-
-
-def finish_kernel(bins, edge_a, edge_b, inner, out, sems):
-    columns, rows = out.shape[0], out.shape[1]
-    a_west = west_flag(False)
-    west = jnp.where(a_west, 0, columns - 1)
-    copies = [
-        pltpu.make_async_copy(inner, out.at[pl.ds(1, columns - 2)], sems.at[0]),
-        pltpu.make_async_copy(edge_a, out.at[west], sems.at[1]),
-        pltpu.make_async_copy(edge_b, out.at[columns - 1 - west], sems.at[2]),
-    ]
-    for copy in copies:
-        copy.start()
-    for copy in copies:
-        copy.wait()
+        if last:
+            pltpu.make_async_copy(done.at[c], out.at[c + 1], sems.at[c]).start()
+    if last:
+        for c in range(count):
+            pltpu.make_async_copy(done.at[c], out.at[c + 1], sems.at[c]).wait()
 
 
 def angle_table(bins, freqs):
@@ -401,7 +402,7 @@
     lat_a, lat_b = swap_pairs(lat, 0, False), swap_pairs(lat, 1, False)
     vmem = pl.BlockSpec(memory_space=VMEM)
     smem = pl.BlockSpec(memory_space=SMEM)
-    anywhere = pl.BlockSpec(memory_space=pl.ANY)
+    hbm = pl.BlockSpec(memory_space=pltpu.HBM)
     edge_shape = VMEM((tall, padded), f32)
     inner_shape = VMEM((columns - 2, tall, padded), f32)
     mask_shape = VMEM((columns, tall, LANES), f32)
@@ -424,20 +425,23 @@
     send_a, send_b = call(
         functools.partial(first_kernel, bins), "first",
         (VMEM((columns // 2, 8, padded), f32),) * 2,
-        (spectrum, sea_mask, ice_flags, wind_forcing),
-        [anywhere, vmem, vmem, vmem],
-        [VMEM((2, columns, 8, bins), f32), pltpu.SemaphoreType.DMA((2,))],
-    )
+        [pltpu.with_memory_space_constraint(x, pltpu.HBM) for x in (spectrum, sea_mask, ice_flags, wind_forcing)],
+        [hbm] * 4,
+        [VMEM((2, columns, 8, bins), f32), VMEM((columns, rows), sea_mask.dtype), VMEM((columns, rows), ice_flags.dtype),
+         VMEM((columns, rows), f32), pltpu.SemaphoreType.DMA((5,))],
+    )
+    halo_b = lax.ppermute(send_b, "lat", lat_b)
     halo_a = lax.ppermute(send_a, "lat", lat_a)
-    halo_b = lax.ppermute(send_b, "lat", lat_b)
-    edge_a, edge_b, inner, seas, gains, stay, go_x, go_y, wide = call(
+    edge_a, edge_b, inner, seas, gains = call(
         functools.partial(load_kernel, bins), "load",
-        (edge_shape, edge_shape, inner_shape, mask_shape, mask_shape, table_shape, table_shape,
-         VMEM((8, padded), f32), VMEM((padded, padded), jnp.bfloat16)),
-        (spectrum, sea_mask, ice_flags, wind_forcing, group_speed, jnp.asarray(angle_table(bins, group_speed.shape[0])), coupling),
-        [anywhere, vmem, vmem, vmem, smem, vmem, vmem],
-        [pltpu.SemaphoreType.DMA((1,)), VMEM((columns, rows, bins), f32)],
-        flops=1 << 24,
+        (edge_shape, edge_shape, inner_shape, mask_shape, mask_shape),
+        (spectrum, sea_mask, ice_flags, wind_forcing), [vmem] * 4, flops=1 << 24,
+    )
+    stay, go_x, go_y, wide = call(
+        functools.partial(table_kernel, bins, rows), "tables",
+        (table_shape, table_shape, VMEM((8, padded), f32), VMEM((padded, padded), jnp.bfloat16)),
+        (group_speed, jnp.asarray(angle_table(bins, group_speed.shape[0])), coupling),
+        [smem, vmem, vmem], flops=1 << 24,
     )
     edge_a, edge_b, inner, seas, gains, pack_a, pack_b = call(
         functools.partial(join_kernel, bins), "join",
@@ -451,33 +455,31 @@
         last = step == STEPS - 1
         halo_a = lax.ppermute(pack_a, "lon", lon_a)
         halo_b = lax.ppermute(pack_b, "lon", lon_b)
+        whole = pltpu.HBM((columns, rows, bins), f32)
         new_inner = call(
-            functools.partial(inner_kernel, bins, last), "inner",
-            VMEM((columns - 2, rows, bins), f32) if last else inner_shape,
+            functools.partial(inner_kernel, bins, last), "inner", whole if last else inner_shape,
             (edge_a, edge_b, inner) + tables, [vmem] * 9,
-            [VMEM((columns - 2, tall, padded), f32), VMEM(((columns - 2) * tall, padded), jnp.bfloat16)],
-            flops=1 << 28,
+            [VMEM((columns - 2, tall, padded), f32), VMEM(((columns - 2) * tall, padded), jnp.bfloat16)]
+            + ([VMEM((columns - 2, rows, bins), f32), pltpu.SemaphoreType.DMA((columns - 2,))] if last else []),
+            flops=1 << 28, out_specs=hbm if last else vmem,
         )
+        if last:
+            for second, halo, edge in ((True, halo_b, edge_b), (False, halo_a, edge_a)):
+                new_inner = call(
+                    functools.partial(last_edge_kernel, bins, second), "edge", whole,
+                    (halo, edge, inner) + tables + (new_inner,), [vmem] * 9 + [hbm],
+                    [VMEM((tall, padded), f32), VMEM((rows, bins), f32), pltpu.SemaphoreType.DMA((1,))],
+                    aliases={9: 0}, flops=1 << 26, out_specs=hbm,
+                )
+            return new_inner
         fresh = []
         for second, halo, edge in ((False, halo_a, edge_a), (True, halo_b, edge_b)):
-            body = functools.partial(edge_kernel, bins, second)
-            if last:
-                body = functools.partial(last_edge_kernel, bins, second)
             fresh.append(call(
-                body, "edge", VMEM((rows, bins), f32) if last else (edge_shape, pack_shape),
+                functools.partial(edge_kernel, bins, second), "edge", (edge_shape, pack_shape),
                 (halo, edge, inner) + tables, [vmem] * 9, [VMEM((tall, padded), f32)], flops=1 << 26,
             ))
         inner = new_inner
-        if last:
-            edge_a, edge_b = fresh
-        else:
-            (edge_a, pack_a), (edge_b, pack_b) = fresh
-    return call(
-        functools.partial(finish_kernel, bins), "finish",
-        jax.ShapeDtypeStruct((columns, rows, bins), f32),
-        (edge_a, edge_b, inner), [vmem] * 3,
-        [pltpu.SemaphoreType.DMA((3,))], out_specs=anywhere,
-    )
+        (edge_a, pack_a), (edge_b, pack_b) = fresh
 
 
 def solution(mesh):

time: 41.3 us -> 38.3 us (0.927)
  local copies, waits for them, and re-layouts: 3.48 us -> 0.03 us
  Pallas kernels: 12.6 us -> 14 us
  waiting for transfers between devices: 9.26 us -> 8.45 us
  starting transfers between devices: 15.6 us -> 15.1 us
    unnamed x14, local copies, waits for them, and re-layouts: 3.48 us -> 0.03 us
    pallas_call x16, Pallas kernels: 12.6 us -> 14 us  [call(): pl.pallas_call(body, name=name, out_shape=outs, in_specs=specs, out_specs...]
    ppermute x4, waiting for transfers between devices: 1.24 us -> 0.01 us  [on_device(): halo_a = lax.ppermute(pack_a, 'lon', lon_a)]
    ppermute x1, waiting for transfers between devices: 2.08 us -> 2.94 us  [on_device(): halo_b = lax.ppermute(send_b, 'lat', lat_b)]
    ppermute x4, starting transfers between devices: 2.99 us -> 2.29 us  [on_device(): halo_a = lax.ppermute(pack_a, 'lon', lon_a)]
    ppermute x4, waiting for transfers between devices: 5.94 us -> 5.49 us  [on_device(): halo_b = lax.ppermute(pack_b, 'lon', lon_b)]
  transfers between devices with their start and end apart: 10 -> 10, of which waited for: 5 -> 4; matrix products, arithmetic and copies ran while one was open for 0% -> 0% of each run, Pallas kernels for 24% -> 31%
where the time goes in v2:
time: 38.3 us; the launch traced here: 37.8 us
  starting transfers between devices  15.1 us (39%)
  Pallas kernels  14 us (37%)
  waiting for transfers between devices  8.45 us (22%)
    pallas_call x16, Pallas kernels, call(): pl.pallas_call(body, name=name, out_shape=outs, in_specs=specs, out_specs...  14 us
    ppermute x4, starting transfers between devices, on_device(): halo_b = lax.ppermute(pack_b, 'lon', lon_b)  10.3 us
    ppermute x4, waiting for transfers between devices, on_device(): halo_b = lax.ppermute(pack_b, 'lon', lon_b)  5.49 us
    ppermute x1, waiting for transfers between devices, on_device(): halo_b = lax.ppermute(send_b, 'lat', lat_b)  2.94 us
    ppermute x1, starting transfers between devices, on_device(): halo_b = lax.ppermute(send_b, 'lat', lat_b)  2.45 us
    ppermute x4, starting transfers between devices, on_device(): halo_a = lax.ppermute(pack_a, 'lon', lon_a)  2.29 us
  transfers between devices with their start and end apart: 10, of which 4 were waited for; matrix products, arithmetic and copies ran while one was open for 0% of the time, Pallas kernels for 31%

profile of v2, /device:TPU:24, one launch (start us, length us, event | category | flops | bytes accessed | tf_op | source)
XLA Modules:
  0.0 37.8 jit_solution(16284837252437955209)
XLA Ops:
  0.0 0.0 copy-start.4
  0.0 0.0 copy-start
  0.0 1.2 %first.1 = (f32[4,8,768]{2,1,0:T(8,128)S(1)}, f32[4,8,768]{2,1,0:T(8,128)S(1)}) custom-call(f32[8,64,648]{2,1,0:T(8,128)} %spectrum.3, s32[8,64]{1,0:T(8,128)} %sea_ref.1, s32[8,64]{1,0:T(8,128)} %ice_ref.1, f32[8,64]{1,0:T(8,128)} %wind_ref.1), custom_call_target="tpu_custom_call" | custom-call | tf_op jit(solution)/shard_map/first/pallas_call | solution.py:413
  1.2 0.1 collective-permute-start
  1.3 2.4 %collective-permute-start.1 = (f32[4,8,768]{2,1,0:T(8,128)S(1)}, f32[4,8,768]{2,1,0:T(8,128)S(1)}, u32[]{:S(2)}, u32[]{:S(2)}) collective-permute-start(f32[4,8,768]{2,1,0:T(8,128)S(1)} %get-tuple-element.36), channel_id=1, source_target_pairs={{1,2},{2,1},{3,4},{4,3},{5,6},{6,5},{9,10},{10,9},{11,12},{12,11},... | collective-permute-start | bytes 294920 | tf_op jit(solution)/shard_map/ppermute | solution.py:433
  3.8 0.0 copy-done.5
  3.8 0.0 copy-done.4
  3.8 0.0 copy-done.3
  3.8 0.0 copy-done
  3.8 0.4 %load.1 = (f32[72,768]{1,0:T(8,128)S(1)}, f32[72,768]{1,0:T(8,128)S(1)}, f32[6,72,768]{2,1,0:T(8,128)S(1)}, f32[8,72,128]{2,1,0:T(8,128)S(1)}, f32[8,72,128]{2,1,0:T(8,128)S(1)}) custom-call(f32[8,64,648]{2,1,0:T(8,128)S(1)} %copy-done, s32[8,64]{1,0:T(8,128)S(1)} %copy-done.3, s32[8,64]{1,0:T(8,128)S(1)} %copy-done.4, f32[8,64]{1,0:T(8,128)S(1)} %copy-done.5), custom_call_target="tpu_custom_call" | custom-call | flops 16777216 | tf_op jit(solution)/shard_map/load/pallas_call | solution.py:413
  4.3 0.0 copy-start.1
  4.3 0.0 copy-start.2
  4.3 0.0 copy-start.6
  4.3 0.0 collective-permute-done.halo_a
  4.3 2.9 %collective-permute-done.1.halo_b = f32[4,8,768]{2,1,0:T(8,128)S(1)} collective-permute-done((f32[4,8,768]{2,1,0:T(8,128)S(1)}, f32[4,8,768]{2,1,0:T(8,128)S(1)}, u32[]{:S(2)}, u32[]{:S(2)}) %collective-permute-start.1) | collective-permute-done | bytes 98336 | tf_op jit(solution)/shard_map/ppermute | solution.py:433
  7.3 0.1 join.1
  7.4 2.5 %collective-permute-start.5 = (f32[3,72,128]{2,1,0:T(8,128)S(1)}, f32[3,72,128]{2,1,0:T(8,128)S(1)}, u32[]{:S(2)}, u32[]{:S(2)}) collective-permute-start(f32[3,72,128]{2,1,0:T(8,128)S(1)} %get-tuple-element.56), channel_id=1, source_target_pairs={{8,16},{16,8},{24,0},{0,24},{9,17},{17,9},{25,1},{1,25},{10,18},{1... | collective-permute-start | bytes 331784 | tf_op jit(solution)/shard_map/ppermute | solution.py:457
  9.9 0.5 %collective-permute-start.2 = (f32[3,72,128]{2,1,0:T(8,128)S(1)}, f32[3,72,128]{2,1,0:T(8,128)S(1)}, u32[]{:S(2)}, u32[]{:S(2)}) collective-permute-start(f32[3,72,128]{2,1,0:T(8,128)S(1)} %get-tuple-element.42), channel_id=1, source_target_pairs={{0,8},{8,0},{16,24},{24,16},{1,9},{9,1},{17,25},{25,17},{2,10},{10... | collective-permute-start | bytes 331784 | tf_op jit(solution)/shard_map/ppermute | solution.py:456
  10.4 0.0 copy-done.1
  10.4 0.0 copy-done.2
  10.4 0.0 copy-done.6
  10.4 0.8 %tables.1 = (f32[72,768]{1,0:T(8,128)S(1)}, f32[72,768]{1,0:T(8,128)S(1)}, f32[8,768]{1,0:T(8,128)S(1)}, bf16[768,768]{1,0:T(8,128)(2,1)S(1)}) custom-call(f32[18]{0:T(128)S(1)} %copy-done.6, f32[8,768]{1,0:T(8,128)S(1)} %copy-done.2, bf16[648,648]{1,0:T(8,128)(2,1)S(1)} %copy-done.1), custom_call_target="tpu_custom_call" | custom-call | flops 16777216 | tf_op jit(solution)/shard_map/tables/pallas_call | solution.py:413
  11.2 3.0 %collective-permute-done.5.refs_0_ = f32[3,72,128]{2,1,0:T(8,128)S(1)} collective-permute-done((f32[3,72,128]{2,1,0:T(8,128)S(1)}, f32[3,72,128]{2,1,0:T(8,128)S(1)}, u32[]{:S(2)}, u32[]{:S(2)}) %collective-permute-start.5) | collective-permute-done | bytes 110624 | tf_op jit(solution)/shard_map/ppermute | solution.py:457
  14.3 0.5 %edge.10 = (f32[72,768]{1,0:T(8,128)S(1)}, f32[3,72,128]{2,1,0:T(8,128)S(1)}) custom-call(f32[3,72,128]{2,1,0:T(8,128)S(1)} %collective-permute-done.5.refs_0_, f32[72,768]{1,0:T(8,128)S(1)} %get-tuple-element.53.edge_b.refs_1_, f32[6,72,768]{2,1,0:T(8,128)S(1)} %get-tuple-element.44.refs_2_.inner, f32[8,72,128]{2,1,0:T(8,128)S(1)} %get-tuple-element.45.refs_3_.seas, ...), custom_call_target="tpu_custom_call" | custom-call | flops 67108864 | tf_op jit(solution)/shard_map/edge/pallas_call | solution.py:413
  14.8 2.5 %collective-permute-start.7 = (f32[3,72,128]{2,1,0:T(8,128)S(1)}, f32[3,72,128]{2,1,0:T(8,128)S(1)}, u32[]{:S(2)}, u32[]{:S(2)}) collective-permute-start(f32[3,72,128]{2,1,0:T(8,128)S(1)} %get-tuple-element.60), channel_id=1, source_target_pairs={{8,16},{16,8},{24,0},{0,24},{9,17},{17,9},{25,1},{1,25},{10,18},{1... | collective-permute-start | bytes 331784 | tf_op jit(solution)/shard_map/ppermute | solution.py:457
  17.3 0.0 collective-permute-done.2.refs_0_
  17.3 0.5 %edge.8 = (f32[72,768]{1,0:T(8,128)S(1)}, f32[3,72,128]{2,1,0:T(8,128)S(1)}) custom-call(f32[3,72,128]{2,1,0:T(8,128)S(1)} %collective-permute-done.2.refs_0_, f32[72,768]{1,0:T(8,128)S(1)} %get-tuple-element.43.refs_1_.edge_a, f32[6,72,768]{2,1,0:T(8,128)S(1)} %get-tuple-element.44.refs_2_.inner, f32[8,72,128]{2,1,0:T(8,128)S(1)} %get-tuple-element.45.refs_3_.seas, ...), custom_call_target="tpu_custom_call" | custom-call | flops 67108864 | tf_op jit(solution)/shard_map/edge/pallas_call | solution.py:413
  17.8 0.8 %collective-permute-start.3 = (f32[3,72,128]{2,1,0:T(8,128)S(1)}, f32[3,72,128]{2,1,0:T(8,128)S(1)}, u32[]{:S(2)}, u32[]{:S(2)}) collective-permute-start(f32[3,72,128]{2,1,0:T(8,128)S(1)} %get-tuple-element.51), channel_id=1, source_target_pairs={{0,8},{8,0},{16,24},{24,16},{1,9},{9,1},{17,25},{25,17},{2,10},{10... | collective-permute-start | bytes 331784 | tf_op jit(solution)/shard_map/ppermute | solution.py:456
  18.7 1.3 %inner.4.refs_2_ = f32[6,72,768]{2,1,0:T(8,128)S(1)} custom-call(f32[72,768]{1,0:T(8,128)S(1)} %get-tuple-element.43.refs_1_.edge_a, f32[72,768]{1,0:T(8,128)S(1)} %get-tuple-element.53.edge_b.refs_1_, f32[6,72,768]{2,1,0:T(8,128)S(1)} %get-tuple-element.44.refs_2_.inner, f32[8,72,128]{2,1,0:T(8,128)S(1)} %get-tuple-element.45.refs_3_.seas, ...), custom_call_target="tpu_custom_call" | custom-call | flops 268435456 | tf_op jit(solution)/shard_map/inner/pallas_call | solution.py:413
  20.0 1.1 %collective-permute-done.7.refs_0_ = f32[3,72,128]{2,1,0:T(8,128)S(1)} collective-permute-done((f32[3,72,128]{2,1,0:T(8,128)S(1)}, f32[3,72,128]{2,1,0:T(8,128)S(1)}, u32[]{:S(2)}, u32[]{:S(2)}) %collective-permute-start.7) | collective-permute-done | bytes 110624 | tf_op jit(solution)/shard_map/ppermute | solution.py:457
  21.1 0.5 %edge.12 = (f32[72,768]{1,0:T(8,128)S(1)}, f32[3,72,128]{2,1,0:T(8,128)S(1)}) custom-call(f32[3,72,128]{2,1,0:T(8,128)S(1)} %collective-permute-done.7.refs_0_, f32[72,768]{1,0:T(8,128)S(1)} %get-tuple-element.57.edge_b.refs_1_, f32[6,72,768]{2,1,0:T(8,128)S(1)} %inner.4.refs_2_, f32[8,72,128]{2,1,0:T(8,128)S(1)} %get-tuple-element.45.refs_3_.seas, ...), custom_call_target="tpu_custom_call" | custom-call | flops 67108864 | tf_op jit(solution)/shard_map/edge/pallas_call | solution.py:413
  21.6 2.9 %collective-permute-start.8 = (f32[3,72,128]{2,1,0:T(8,128)S(1)}, f32[3,72,128]{2,1,0:T(8,128)S(1)}, u32[]{:S(2)}, u32[]{:S(2)}) collective-permute-start(f32[3,72,128]{2,1,0:T(8,128)S(1)} %get-tuple-element.62), channel_id=1, source_target_pairs={{8,16},{16,8},{24,0},{0,24},{9,17},{17,9},{25,1},{1,25},{10,18},{1... | collective-permute-start | bytes 331784 | tf_op jit(solution)/shard_map/ppermute | solution.py:457
  24.5 0.0 collective-permute-done.3.refs_0_
  24.5 0.5 %edge.9 = (f32[72,768]{1,0:T(8,128)S(1)}, f32[3,72,128]{2,1,0:T(8,128)S(1)}) custom-call(f32[3,72,128]{2,1,0:T(8,128)S(1)} %collective-permute-done.3.refs_0_, f32[72,768]{1,0:T(8,128)S(1)} %get-tuple-element.52.refs_1_.edge_a, f32[6,72,768]{2,1,0:T(8,128)S(1)} %inner.4.refs_2_, f32[8,72,128]{2,1,0:T(8,128)S(1)} %get-tuple-element.45.refs_3_.seas, ...), custom_call_target="tpu_custom_call" | custom-call | flops 67108864 | tf_op jit(solution)/shard_map/edge/pallas_call | solution.py:413
  25.1 0.2 collective-permute-start.4
  25.3 1.3 %inner.5.refs_2_ = f32[6,72,768]{2,1,0:T(8,128)S(1)} custom-call(f32[72,768]{1,0:T(8,128)S(1)} %get-tuple-element.52.refs_1_.edge_a, f32[72,768]{1,0:T(8,128)S(1)} %get-tuple-element.57.edge_b.refs_1_, f32[6,72,768]{2,1,0:T(8,128)S(1)} %inner.4.refs_2_, f32[8,72,128]{2,1,0:T(8,128)S(1)} %get-tuple-element.45.refs_3_.seas, ...), custom_call_target="tpu_custom_call" | custom-call | flops 268435456 | tf_op jit(solution)/shard_map/inner/pallas_call | solution.py:413
  26.6 1.3 %collective-permute-done.8.refs_0_ = f32[3,72,128]{2,1,0:T(8,128)S(1)} collective-permute-done((f32[3,72,128]{2,1,0:T(8,128)S(1)}, f32[3,72,128]{2,1,0:T(8,128)S(1)}, u32[]{:S(2)}, u32[]{:S(2)}) %collective-permute-start.8) | collective-permute-done | bytes 110624 | tf_op jit(solution)/shard_map/ppermute | solution.py:457
  27.9 0.5 %edge.13 = (f32[72,768]{1,0:T(8,128)S(1)}, f32[3,72,128]{2,1,0:T(8,128)S(1)}) custom-call(f32[3,72,128]{2,1,0:T(8,128)S(1)} %collective-permute-done.8.refs_0_, f32[72,768]{1,0:T(8,128)S(1)} %get-tuple-element.61.edge_b.refs_1_, f32[6,72,768]{2,1,0:T(8,128)S(1)} %inner.5.refs_2_, f32[8,72,128]{2,1,0:T(8,128)S(1)} %get-tuple-element.45.refs_3_.seas, ...), custom_call_target="tpu_custom_call" | custom-call | flops 67108864 | tf_op jit(solution)/shard_map/edge/pallas_call | solution.py:413
  28.4 2.4 %collective-permute-start.9 = (f32[3,72,128]{2,1,0:T(8,128)S(1)}, f32[3,72,128]{2,1,0:T(8,128)S(1)}, u32[]{:S(2)}, u32[]{:S(2)}) collective-permute-start(f32[3,72,128]{2,1,0:T(8,128)S(1)} %get-tuple-element.63), channel_id=1, source_target_pairs={{8,16},{16,8},{24,0},{0,24},{9,17},{17,9},{25,1},{1,25},{10,18},{1... | collective-permute-start | bytes 331784 | tf_op jit(solution)/shard_map/ppermute | solution.py:457
  30.8 0.0 collective-permute-done.4.refs_0_
  30.8 0.5 %edge.11 = (f32[72,768]{1,0:T(8,128)S(1)}, f32[3,72,128]{2,1,0:T(8,128)S(1)}) custom-call(f32[3,72,128]{2,1,0:T(8,128)S(1)} %collective-permute-done.4.refs_0_, f32[72,768]{1,0:T(8,128)S(1)} %get-tuple-element.55.refs_1_.edge_a, f32[6,72,768]{2,1,0:T(8,128)S(1)} %inner.5.refs_2_, f32[8,72,128]{2,1,0:T(8,128)S(1)} %get-tuple-element.45.refs_3_.seas, ...), custom_call_target="tpu_custom_call" | custom-call | flops 67108864 | tf_op jit(solution)/shard_map/edge/pallas_call | solution.py:413
  31.3 0.7 %collective-permute-start.6 = (f32[3,72,128]{2,1,0:T(8,128)S(1)}, f32[3,72,128]{2,1,0:T(8,128)S(1)}, u32[]{:S(2)}, u32[]{:S(2)}) collective-permute-start(f32[3,72,128]{2,1,0:T(8,128)S(1)} %get-tuple-element.58), channel_id=1, source_target_pairs={{0,8},{8,0},{16,24},{24,16},{1,9},{9,1},{17,25},{25,17},{2,10},{10... | collective-permute-start | bytes 331784 | tf_op jit(solution)/shard_map/ppermute | solution.py:456
  32.0 1.3 %inner.6 = f32[6,72,768]{2,1,0:T(8,128)S(1)} custom-call(f32[72,768]{1,0:T(8,128)S(1)} %get-tuple-element.55.refs_1_.edge_a, f32[72,768]{1,0:T(8,128)S(1)} %get-tuple-element.61.edge_b.refs_1_, f32[6,72,768]{2,1,0:T(8,128)S(1)} %inner.5.refs_2_, f32[8,72,128]{2,1,0:T(8,128)S(1)} %get-tuple-element.45.refs_3_.seas, ...), custom_call_target="tpu_custom_call" | custom-call | flops 268435456 | tf_op jit(solution)/shard_map/inner/pallas_call | solution.py:413
  33.4 2.2 %inner.7.whole = f32[8,64,648]{2,1,0:T(8,128)} custom-call(f32[72,768]{1,0:T(8,128)S(1)} %get-tuple-element.59.edge_a.edge, f32[72,768]{1,0:T(8,128)S(1)} %get-tuple-element.64.edge_b.edge, f32[6,72,768]{2,1,0:T(8,128)S(1)} %inner.6, f32[8,72,128]{2,1,0:T(8,128)S(1)} %get-tuple-element.45.refs_3_.seas, f32[8,72,128]{2,1,0:T(8,128)S(1)} %get-tuple-element.46.refs_4_.gains, ...), custom_call_target="tpu_custom_call" | custom-call | flops 268435456 | tf_op jit(solution)/shard_map/inner/pallas_call | solution.py:413
  35.5 0.0 collective-permute-done.9.halo
  35.6 1.1 %edge.14.whole = f32[8,64,648]{2,1,0:T(8,128)} custom-call(f32[3,72,128]{2,1,0:T(8,128)S(1)} %collective-permute-done.9.halo, f32[72,768]{1,0:T(8,128)S(1)} %get-tuple-element.64.edge_b.edge, f32[6,72,768]{2,1,0:T(8,128)S(1)} %inner.6, f32[8,72,128]{2,1,0:T(8,128)S(1)} %get-tuple-element.45.refs_3_.seas, ...), custom_call_target="tpu_custom_call", output_to_operand_aliasing={{}: (9, {})} | custom-call | flops 67108864 | tf_op jit(solution)/shard_map/edge/pallas_call | solution.py:413
  36.7 0.0 collective-permute-done.6.halo
  36.7 1.1 %edge.15 = f32[8,64,648]{2,1,0:T(8,128)} custom-call(f32[3,72,128]{2,1,0:T(8,128)S(1)} %collective-permute-done.6.halo, f32[72,768]{1,0:T(8,128)S(1)} %get-tuple-element.59.edge_a.edge, f32[6,72,768]{2,1,0:T(8,128)S(1)} %inner.6, f32[8,72,128]{2,1,0:T(8,128)S(1)} %get-tuple-element.45.refs_3_.seas, ...), custom_call_target="tpu_custom_call", output_to_operand_aliasing={{}: (9, {})} | custom-call | flops 67108864 | tf_op jit(solution)/shard_map/edge/pallas_call | solution.py:413
  (2 shorter events, 0.0 us)
Async XLA Ops:
  0.0 3.8 %copy-start.5 = (f32[8,64]{1,0:T(8,128)S(1)}, f32[8,64]{1,0:T(8,128)}, u32[]{:S(2)}) copy-start(f32[8,64]{1,0:T(8,128)} %wind_ref.1) | copy-start | bytes 6148
  0.0 3.8 %copy-start.4 = (s32[8,64]{1,0:T(8,128)S(1)}, s32[8,64]{1,0:T(8,128)}, u32[]{:S(2)}) copy-start(s32[8,64]{1,0:T(8,128)} %ice_ref.1) | copy-start | bytes 6148
  0.0 3.8 %copy-start.3 = (s32[8,64]{1,0:T(8,128)S(1)}, s32[8,64]{1,0:T(8,128)}, u32[]{:S(2)}) copy-start(s32[8,64]{1,0:T(8,128)} %sea_ref.1) | copy-start | bytes 6148
  0.0 3.8 %copy-start = (f32[8,64,648]{2,1,0:T(8,128)S(1)}, f32[8,64,648]{2,1,0:T(8,128)}, u32[]{:S(2)}) copy-start(f32[8,64,648]{2,1,0:T(8,128)} %spectrum.3) | copy-start | bytes 3981316
  1.2 3.1 %collective-permute-start = (f32[4,8,768]{2,1,0:T(8,128)S(1)}, f32[4,8,768]{2,1,0:T(8,128)S(1)}, u32[]{:S(2)}, u32[]{:S(2)}) collective-permute-start(f32[4,8,768]{2,1,0:T(8,128)S(1)} %get-tuple-element.35), channel_id=1, source_target_pairs={{0,1},{1,0},{2,3},{3,2},{4,5},{5,4},{6,7},{7,6},{8,9},{9,8},{10,11... | collective-permute-start | bytes 294920 | tf_op jit(solution)/shard_map/ppermute | solution.py:434
  1.3 5.9 %collective-permute-start.1 = (f32[4,8,768]{2,1,0:T(8,128)S(1)}, f32[4,8,768]{2,1,0:T(8,128)S(1)}, u32[]{:S(2)}, u32[]{:S(2)}) collective-permute-start(f32[4,8,768]{2,1,0:T(8,128)S(1)} %get-tuple-element.36), channel_id=1, source_target_pairs={{1,2},{2,1},{3,4},{4,3},{5,6},{6,5},{9,10},{10,9},{11,12},{12,11},... | collective-permute-start | bytes 294920 | tf_op jit(solution)/shard_map/ppermute | solution.py:433
  4.3 6.2 %copy-start.1 = (bf16[648,648]{1,0:T(8,128)(2,1)S(1)}, bf16[648,648]{1,0:T(8,128)(2,1)}, u32[]{:S(2)}) copy-start(bf16[648,648]{1,0:T(8,128)(2,1)} %coupling_ref.1) | copy-start | bytes 2519428
  4.3 6.2 %copy-start.2 = (f32[8,768]{1,0:T(8,128)S(1)}, f32[8,768]{1,0:T(8,128)}, u32[]{:S(2)}) copy-start(f32[8,768]{1,0:T(8,128)} %constant.2.clone.angle_ref) | copy-start | bytes 73732
  4.3 6.1 %copy-start.6 = (f32[18]{0:T(128)S(1)}, f32[18]{0:T(128)}, u32[]{:S(2)}) copy-start(f32[18]{0:T(128)} %speed_ref.1) | copy-start | bytes 220
  7.4 6.9 %collective-permute-start.5 = (f32[3,72,128]{2,1,0:T(8,128)S(1)}, f32[3,72,128]{2,1,0:T(8,128)S(1)}, u32[]{:S(2)}, u32[]{:S(2)}) collective-permute-start(f32[3,72,128]{2,1,0:T(8,128)S(1)} %get-tuple-element.56), channel_id=1, source_target_pairs={{8,16},{16,8},{24,0},{0,24},{9,17},{17,9},{25,1},{1,25},{10,18},{1... | collective-permute-start | bytes 331784 | tf_op jit(solution)/shard_map/ppermute | solution.py:457
  9.9 7.4 %collective-permute-start.2 = (f32[3,72,128]{2,1,0:T(8,128)S(1)}, f32[3,72,128]{2,1,0:T(8,128)S(1)}, u32[]{:S(2)}, u32[]{:S(2)}) collective-permute-start(f32[3,72,128]{2,1,0:T(8,128)S(1)} %get-tuple-element.42), channel_id=1, source_target_pairs={{0,8},{8,0},{16,24},{24,16},{1,9},{9,1},{17,25},{25,17},{2,10},{10... | collective-permute-start | bytes 331784 | tf_op jit(solution)/shard_map/ppermute | solution.py:456
  14.8 6.3 %collective-permute-start.7 = (f32[3,72,128]{2,1,0:T(8,128)S(1)}, f32[3,72,128]{2,1,0:T(8,128)S(1)}, u32[]{:S(2)}, u32[]{:S(2)}) collective-permute-start(f32[3,72,128]{2,1,0:T(8,128)S(1)} %get-tuple-element.60), channel_id=1, source_target_pairs={{8,16},{16,8},{24,0},{0,24},{9,17},{17,9},{25,1},{1,25},{10,18},{1... | collective-permute-start | bytes 331784 | tf_op jit(solution)/shard_map/ppermute | solution.py:457
  17.8 6.7 %collective-permute-start.3 = (f32[3,72,128]{2,1,0:T(8,128)S(1)}, f32[3,72,128]{2,1,0:T(8,128)S(1)}, u32[]{:S(2)}, u32[]{:S(2)}) collective-permute-start(f32[3,72,128]{2,1,0:T(8,128)S(1)} %get-tuple-element.51), channel_id=1, source_target_pairs={{0,8},{8,0},{16,24},{24,16},{1,9},{9,1},{17,25},{25,17},{2,10},{10... | collective-permute-start | bytes 331784 | tf_op jit(solution)/shard_map/ppermute | solution.py:456
  21.6 6.3 %collective-permute-start.8 = (f32[3,72,128]{2,1,0:T(8,128)S(1)}, f32[3,72,128]{2,1,0:T(8,128)S(1)}, u32[]{:S(2)}, u32[]{:S(2)}) collective-permute-start(f32[3,72,128]{2,1,0:T(8,128)S(1)} %get-tuple-element.62), channel_id=1, source_target_pairs={{8,16},{16,8},{24,0},{0,24},{9,17},{17,9},{25,1},{1,25},{10,18},{1... | collective-permute-start | bytes 331784 | tf_op jit(solution)/shard_map/ppermute | solution.py:457
  25.1 5.7 %collective-permute-start.4 = (f32[3,72,128]{2,1,0:T(8,128)S(1)}, f32[3,72,128]{2,1,0:T(8,128)S(1)}, u32[]{:S(2)}, u32[]{:S(2)}) collective-permute-start(f32[3,72,128]{2,1,0:T(8,128)S(1)} %get-tuple-element.54), channel_id=1, source_target_pairs={{0,8},{8,0},{16,24},{24,16},{1,9},{9,1},{17,25},{25,17},{2,10},{10... | collective-permute-start | bytes 331784 | tf_op jit(solution)/shard_map/ppermute | solution.py:456
  28.4 7.1 %collective-permute-start.9 = (f32[3,72,128]{2,1,0:T(8,128)S(1)}, f32[3,72,128]{2,1,0:T(8,128)S(1)}, u32[]{:S(2)}, u32[]{:S(2)}) collective-permute-start(f32[3,72,128]{2,1,0:T(8,128)S(1)} %get-tuple-element.63), channel_id=1, source_target_pairs={{8,16},{16,8},{24,0},{0,24},{9,17},{17,9},{25,1},{1,25},{10,18},{1... | collective-permute-start | bytes 331784 | tf_op jit(solution)/shard_map/ppermute | solution.py:457
  31.3 5.4 %collective-permute-start.6 = (f32[3,72,128]{2,1,0:T(8,128)S(1)}, f32[3,72,128]{2,1,0:T(8,128)S(1)}, u32[]{:S(2)}, u32[]{:S(2)}) collective-permute-start(f32[3,72,128]{2,1,0:T(8,128)S(1)} %get-tuple-element.58), channel_id=1, source_target_pairs={{0,8},{8,0},{16,24},{24,16},{1,9},{9,1},{17,25},{25,17},{2,10},{10... | collective-permute-start | bytes 331784 | tf_op jit(solution)/shard_map/ppermute | solution.py:456

commit v3 on v2

--- a/solution.py
+++ b/solution.py
@@ -90,32 +90,106 @@
     return stay * f + go_x * across + go_y * along
 
 
-def pack_half(tiles, west_edge, bins):
-    quarter = bins // 4
-    split = quarter - LANES
-    shape = tiles[0].shape
-    lane = lane_index(shape)
-    last = jnp.where(lane < split, tiles[1], jnp.where(lane >= LANES // 2, tiles[3], pltpu.roll(tiles[5], split, 1)))
-    return (
-        jnp.where(west_edge, tiles[2], tiles[0]),
-        jnp.where(west_edge, tiles[1], tiles[4]),
-        jnp.where(west_edge, tiles[3], last),
-    )
-
-
-def across_edge(halo, inner, west_edge, bins):
-    quarter = bins // 4
-    split = quarter - LANES
-    shape = inner[0].shape
-    pick = [eastward(bins, tile, shape) == west_edge for tile in (1, 3)]
-    return (
-        jnp.where(west_edge, halo[0], inner[0]),
-        jnp.where(pick[0], jnp.where(west_edge, halo[2], halo[1]), inner[1]),
-        jnp.where(west_edge, inner[2], halo[0]),
-        jnp.where(pick[1], halo[2], inner[3]),
-        jnp.where(west_edge, halo[1], inner[4]),
-        jnp.where(west_edge, pltpu.roll(halo[2], LANES - split, 1), inner[5]),
-    )
+def turn(value, shift):
+    shift = shift % LANES
+    return pltpu.roll(value, shift, 1) if shift else value
+
+
+def pack_plan(bins, west):
+    split = bins // 4 - LANES
+    high = bins - bins // 4 - 3 * LANES
+    width = 2 * split
+    return split, high, width, LANES - width, (split if west else high)
+
+
+def pack_count(rows, halo):
+    blocks = rows // 8
+    return 2 * blocks + blocks // 2 + 1 + (2 if halo else 0)
+
+
+def pack_half(tiles, west, bins, rows, halo, out):
+    split, high, width, kept, start = pack_plan(bins, west)
+    rest = width - kept
+    blocks = rows // 8
+    half = blocks // 2
+    lane = lane_index((8, LANES))
+
+    def parts(block):
+        t = [tile[8 * block : 8 * block + 8] for tile in tiles]
+        if west:
+            return t[2], jnp.where(lane < high, t[3], t[1]), t[1]
+        return t[0], t[4], jnp.where(lane < split, t[1], jnp.where(lane >= high, t[3], turn(t[5], split)))
+
+    left = jnp.zeros((8, LANES), jnp.float32)
+    held = {}
+    for block in range(blocks + (1 if halo else 0)):
+        full, other, part = parts(block)
+        if block < blocks:
+            out[block] = full
+            out[blocks + block] = other
+            if block < half:
+                held[block] = turn(part, -start)
+            else:
+                k = block - half
+                out[2 * blocks + k] = jnp.where(lane < width, held.pop(k), turn(part, width - start))
+                low = rest * k
+                left = jnp.where((lane >= low) & (lane < low + rest), turn(part, low - kept - start), left)
+        else:
+            left = jnp.where(lane >= half * rest, turn(part, half * rest - start), left)
+            out[2 * blocks + half + 1] = full
+            out[2 * blocks + half + 2] = other
+    out[2 * blocks + half] = left
+
+
+def across_edge(halo, inner, west, bins, rows, with_halo):
+    split, high, width, kept, start = pack_plan(bins, not west)
+    rest = width - kept
+    blocks = rows // 8
+    half = blocks // 2
+    lane = lane_index((8, LANES))
+    left = halo[2 * blocks + half]
+    found = [[] for _ in inner]
+    for block in range(blocks + 1):
+        near = [tile[8 * block : 8 * block + 8] for tile in inner]
+        if block == blocks and not with_halo:
+            new = near
+        else:
+            if block == blocks:
+                full, other = halo[2 * blocks + half + 1], halo[2 * blocks + half + 2]
+                part = turn(left, start - half * rest)
+            else:
+                full, other = halo[block], halo[blocks + block]
+                if block < half:
+                    part = turn(halo[2 * blocks + block], start)
+                else:
+                    k = block - half
+                    early = (lane >= high) | (lane < split) if west else lane < start + kept
+                    part = jnp.where(early, turn(halo[2 * blocks + k], start - width), turn(left, start + kept - rest * k))
+            if west:
+                new = [
+                    full, jnp.where(lane < split, part, near[1]), near[2],
+                    jnp.where(lane >= high, part, near[3]), other, turn(part, -split),
+                ]
+            else:
+                new = [
+                    near[0], jnp.where(lane < split, near[1], jnp.where(lane < high, part, other)), full,
+                    jnp.where(lane < high, other, near[3]), near[4], near[5],
+                ]
+        for k, value in enumerate(new):
+            found[k].append(value)
+    return [jnp.concatenate(values, axis=0) for values in found]
+
+
+def on_each_side(second, body):
+    west = west_flag(second)
+
+    @pl.when(west)
+    def _():
+        body(True)
+
+    @pl.when(jnp.logical_not(west))
+    def _():
+        body(False)
 
 
 def west_flag(second):
@@ -284,66 +358,82 @@
     for tile in range(tiles):
         for c in range(1, columns - 1):
             inner[c - 1, rows:, lanes_of(tile)] = values[c][tile]
-        for second, target in ((False, edge_a), (True, edge_b)):
-            target[rows:, lanes_of(tile)] = jnp.where(
-                west_flag(second), values[0][tile], values[columns - 1][tile]
-            )
     for second, target, pack in ((False, edge_a, pack_a), (True, edge_b, pack_b)):
-        packed = pack_half([target[:, lanes_of(t)] for t in range(tiles)], west_flag(second), bins)
-        for k, value in enumerate(packed):
-            pack[k] = value
+
+        def side(west, target=target, pack=pack):
+            for tile in range(tiles):
+                target[rows:, lanes_of(tile)] = values[0 if west else columns - 1][tile]
+            pack_half([target[:, lanes_of(t)] for t in range(tiles)], west, bins, rows, True, pack)
+
+        on_each_side(second, side)
 
 
 def combine(adv, product, seas, gains, share):
     return adv * (gains - seas * share) + seas * product
 
 
-def last_edge_kernel(bins, second, halo, edge, inner, seas, gains, stay, go_x, go_y, wide, whole, out, adv_ref, column, sem):
-    edge_step(bins, second, halo, edge, inner, seas, gains, stay, go_x, go_y, wide, column, None, adv_ref)
-    mine = jnp.where(west_flag(second), 0, out.shape[0] - 1)
-    copy = pltpu.make_async_copy(column, out.at[mine], sem.at[0])
-    copy.start()
-    copy.wait()
-
-
-def edge_kernel(bins, second, *refs):
-    edge_step(bins, second, *refs)
-
-
-def edge_step(bins, second, halo, edge, inner, seas, gains, stay, go_x, go_y, wide, out, pack, adv_ref):
-    last = pack is None
+def edge_kernel(bins, second, halo, edge, inner, seas, gains, stay, go_x, go_y, wide, after, out, pack, adv_ref):
+    rows = edge.shape[0] - 2 * DEPTH
+    halo_next = pack.shape[0] == pack_count(rows, True)
+
+    def side(west):
+        fresh = edge_step(bins, west, halo, edge, inner, seas, gains, stay, go_x, go_y, wide, adv_ref, False)
+        for t, value in enumerate(fresh):
+            out[:, lanes_of(t)] = value
+        pack_half(fresh, west, bins, rows, halo_next, pack)
+
+    on_each_side(second, side)
+
+
+def late_edge_kernel(bins, second, halo, edge, inner, seas, gains, stay, go_x, go_y, wide, after, out, adv_ref):
+    def side(west):
+        fresh = edge_step(bins, west, halo, edge, inner, seas, gains, stay, go_x, go_y, wide, adv_ref, True)
+        for t, value in enumerate(fresh):
+            write_tile(out, (), bins, t, value)
+
+    on_each_side(second, side)
+
+
+def last_edge_kernel(
+    bins, second, halo, edge, inner, seas, gains, stay, go_x, go_y, wide, done_inner, done_edge, out, adv_ref, column, sems
+):
+    columns = out.shape[0]
+    mine = jnp.where(west_flag(second), 0, columns - 1)
+    copies = [
+        pltpu.make_async_copy(done_inner, out.at[pl.ds(1, columns - 2)], sems.at[0]),
+        pltpu.make_async_copy(done_edge, out.at[columns - 1 - mine], sems.at[1]),
+    ]
+    for copy in copies:
+        copy.start()
+    late_edge_kernel(bins, second, halo, edge, inner, seas, gains, stay, go_x, go_y, wide, None, column, adv_ref)
+    copies.append(pltpu.make_async_copy(column, out.at[mine], sems.at[2]))
+    copies[2].start()
+    for copy in copies:
+        copy.wait()
+
+
+def edge_step(bins, west, halo, edge, inner, seas, gains, stay, go_x, go_y, wide, adv_ref, last):
     tiles = lane_tiles(bins)
     columns = inner.shape[0] + 2
-    west = west_flag(second)
-    near = jnp.where(west, 0, columns - 3)
-    mine = jnp.where(west, 0, columns - 1)
-    across = across_edge(
-        [halo[k] for k in range(3)], [inner[near, :, lanes_of(t)] for t in range(tiles)], west, bins
-    )
+    rows = edge.shape[0] - 2 * DEPTH
+    used = rows if last else edge.shape[0]
+    near, mine = (0, 0) if west else (columns - 3, columns - 1)
+    across = across_edge(halo, [inner[near, :, lanes_of(t)] for t in range(tiles)], west, bins, rows, not last)
     for t in range(tiles):
         here = lanes_of(t)
-        adv_ref[:, here] = advect(edge[:, here], across[t], stay[:, here], go_x[:, here], go_y[0:1, here], bins, t)
-    product = jnp.dot(adv_ref[...].astype(jnp.bfloat16), wide[...], preferred_element_type=jnp.float32)
-    share = jnp.broadcast_to(product[:, -1:], (product.shape[0], LANES)) * (dissipation / bins)
-    s, g = seas[mine], gains[mine]
-    fresh = []
-    for t in range(tiles):
-        here = lanes_of(t)
-        fresh.append(combine(adv_ref[:, here], product[:, here], s, g, share))
-        if last:
-            write_tile(out, (), bins, t, fresh[-1])
-        else:
-            out[:, here] = fresh[-1]
-    if not last:
-        for k, value in enumerate(pack_half(fresh, west, bins)):
-            pack[k] = value
-
-
-def inner_kernel(bins, last, edge_a, edge_b, inner, seas, gains, stay, go_x, go_y, wide, out, adv_ref, low_ref, done=None, sems=None):
-    tiles = lane_tiles(bins)
-    count, rows = inner.shape[0], inner.shape[1]
+        adv = advect(edge[:, here], across[t], stay[:, here], go_x[:, here], go_y[0:1, here], bins, t)
+        adv_ref[:used, here] = adv[:used]
+    product = jnp.dot(adv_ref[:used].astype(jnp.bfloat16), wide[...], preferred_element_type=jnp.float32)
+    share = jnp.broadcast_to(product[:, -1:], (used, LANES)) * (dissipation / bins)
+    s, g = seas[mine, :used], gains[mine, :used]
+    return [combine(adv_ref[:used, lanes_of(t)], product[:, lanes_of(t)], s, g, share) for t in range(tiles)]
+
+
+def inner_kernel(bins, edge_a, edge_b, inner, seas, gains, stay, go_x, go_y, wide, out, adv_ref, low_ref):
+    tiles = lane_tiles(bins)
+    count, tall = inner.shape[0], inner.shape[1]
+    rows = adv_ref.shape[1]
     a_west = west_flag(False)
-    shape = (rows, LANES)
     for t in range(tiles):
         here = lanes_of(t)
         found = kinds(bins, t, is_east(bins))
@@ -358,26 +448,21 @@
             elif east is None:
                 across = west
             else:
-                across = jnp.where(eastward(bins, t, shape), west, east)
-            adv = advect(inner[c, :, here], across, stay[:, here], go_x[:, here], go_y[0:1, here], bins, t)
+                across = jnp.where(eastward(bins, t, (tall, LANES)), west, east)
+            adv = advect(inner[c, :, here], across, stay[:, here], go_x[:, here], go_y[0:1, here], bins, t)[:rows]
             adv_ref[c, :, here] = adv
             low_ref[c * rows : (c + 1) * rows, here] = adv.astype(jnp.bfloat16)
     product = jnp.dot(low_ref[...], wide[...], preferred_element_type=jnp.float32)
     for c in range(count):
         part = product[c * rows : (c + 1) * rows]
-        share = jnp.broadcast_to(part[:, -1:], shape) * (dissipation / bins)
+        share = jnp.broadcast_to(part[:, -1:], (rows, LANES)) * (dissipation / bins)
         for t in range(tiles):
             here = lanes_of(t)
-            value = combine(adv_ref[c, :, here], part[:, here], seas[c + 1], gains[c + 1], share)
-            if last:
-                write_tile(done, (c,), bins, t, value)
+            value = combine(adv_ref[c, :, here], part[:, here], seas[c + 1, :rows], gains[c + 1, :rows], share)
+            if rows == tall:
+                out[c, :, here] = value
             else:
-                out[c, :, here] = value
-        if last:
-            pltpu.make_async_copy(done.at[c], out.at[c + 1], sems.at[c]).start()
-    if last:
-        for c in range(count):
-            pltpu.make_async_copy(done.at[c], out.at[c + 1], sems.at[c]).wait()
+                write_tile(out, (c,), bins, t, value)
 
 
 def angle_table(bins, freqs):
@@ -406,7 +491,7 @@
     edge_shape = VMEM((tall, padded), f32)
     inner_shape = VMEM((columns - 2, tall, padded), f32)
     mask_shape = VMEM((columns, tall, LANES), f32)
-    pack_shape = VMEM((3, tall, LANES), f32)
+    pack_shape = VMEM((pack_count(rows, True), 8, LANES), f32)
     table_shape = VMEM((tall, padded), f32)
 
     def call(body, name, outs, ins, specs, scratch=(), aliases=None, flops=0, out_specs=None):
@@ -455,28 +540,31 @@
         last = step == STEPS - 1
         halo_a = lax.ppermute(pack_a, "lon", lon_a)
         halo_b = lax.ppermute(pack_b, "lon", lon_b)
-        whole = pltpu.HBM((columns, rows, bins), f32)
+        used = rows if last else tall
         new_inner = call(
-            functools.partial(inner_kernel, bins, last), "inner", whole if last else inner_shape,
+            functools.partial(inner_kernel, bins), "inner", VMEM((columns - 2, rows, bins), f32) if last else inner_shape,
             (edge_a, edge_b, inner) + tables, [vmem] * 9,
-            [VMEM((columns - 2, tall, padded), f32), VMEM(((columns - 2) * tall, padded), jnp.bfloat16)]
-            + ([VMEM((columns - 2, rows, bins), f32), pltpu.SemaphoreType.DMA((columns - 2,))] if last else []),
-            flops=1 << 28, out_specs=hbm if last else vmem,
+            [VMEM((columns - 2, used, padded), f32), VMEM(((columns - 2) * used, padded), jnp.bfloat16)],
+            flops=1 << 28,
         )
         if last:
-            for second, halo, edge in ((True, halo_b, edge_b), (False, halo_a, edge_a)):
-                new_inner = call(
-                    functools.partial(last_edge_kernel, bins, second), "edge", whole,
-                    (halo, edge, inner) + tables + (new_inner,), [vmem] * 9 + [hbm],
-                    [VMEM((tall, padded), f32), VMEM((rows, bins), f32), pltpu.SemaphoreType.DMA((1,))],
-                    aliases={9: 0}, flops=1 << 26, out_specs=hbm,
-                )
-            return new_inner
+            column = VMEM((rows, bins), f32)
+            scratch = [VMEM((tall, padded), f32)]
+            done_b = call(
+                functools.partial(late_edge_kernel, bins, True), "late", column,
+                (halo_b, edge_b, inner) + tables + (new_inner,), [vmem] * 10, scratch, flops=1 << 26,
+            )
+            return call(
+                functools.partial(last_edge_kernel, bins, False), "last", pltpu.HBM((columns, rows, bins), f32),
+                (halo_a, edge_a, inner) + tables + (new_inner, done_b), [vmem] * 11,
+                scratch + [column, pltpu.SemaphoreType.DMA((3,))], flops=1 << 26, out_specs=hbm,
+            )
         fresh = []
+        pack_next = VMEM((pack_count(rows, step < STEPS - 2), 8, LANES), f32)
         for second, halo, edge in ((False, halo_a, edge_a), (True, halo_b, edge_b)):
             fresh.append(call(
-                functools.partial(edge_kernel, bins, second), "edge", (edge_shape, pack_shape),
-                (halo, edge, inner) + tables, [vmem] * 9, [VMEM((tall, padded), f32)], flops=1 << 26,
+                functools.partial(edge_kernel, bins, second), "edge", (edge_shape, pack_next),
+                (halo, edge, inner) + tables + (new_inner,), [vmem] * 10, [VMEM((tall, padded), f32)], flops=1 << 26,
             ))
         inner = new_inner
         (edge_a, pack_a), (edge_b, pack_b) = fresh

time: 38.3 us -> 36.7 us (0.958)
  Pallas kernels: 14 us -> 12.6 us
  waiting for transfers between devices: 8.45 us -> 9.58 us
  starting transfers between devices: 15.1 us -> 14.1 us
    pallas_call x16, Pallas kernels: 14 us -> 12.6 us  [call(): pl.pallas_call(body, name=name, out_shape=outs, in_specs=specs, out_specs...]
    ppermute x4, waiting for transfers between devices: 0.01 us -> 1.35 us  [on_device(): halo_a = lax.ppermute(pack_a, 'lon', lon_a)]
    ppermute x4, starting transfers between devices: 2.29 us -> 1.15 us  [on_device(): halo_a = lax.ppermute(pack_a, 'lon', lon_a)]
  transfers between devices with their start and end apart: 10 -> 10, of which waited for: 4 -> 6; matrix products, arithmetic and copies ran while one was open for 0% -> 0% of each run, Pallas kernels for 31% -> 27%
where the time goes in v3:
time: 36.7 us; the launch traced here: 36.5 us
  starting transfers between devices  14.1 us (38%)
  Pallas kernels  12.6 us (34%)
  waiting for transfers between devices  9.58 us (26%)
    pallas_call x16, Pallas kernels, call(): pl.pallas_call(body, name=name, out_shape=outs, in_specs=specs, out_specs...  12.6 us
    ppermute x4, starting transfers between devices, on_device(): halo_b = lax.ppermute(pack_b, 'lon', lon_b)  10.4 us
    ppermute x4, waiting for transfers between devices, on_device(): halo_b = lax.ppermute(pack_b, 'lon', lon_b)  5.29 us
    ppermute x1, waiting for transfers between devices, on_device(): halo_b = lax.ppermute(send_b, 'lat', lat_b)  2.94 us
    ppermute x1, starting transfers between devices, on_device(): halo_b = lax.ppermute(send_b, 'lat', lat_b)  2.45 us
    ppermute x4, waiting for transfers between devices, on_device(): halo_a = lax.ppermute(pack_a, 'lon', lon_a)  1.35 us
    ppermute x4, starting transfers between devices, on_device(): halo_a = lax.ppermute(pack_a, 'lon', lon_a)  1.15 us
  transfers between devices with their start and end apart: 10, of which 6 were waited for; matrix products, arithmetic and copies ran while one was open for 0% of the time, Pallas kernels for 27%

profile of v3, /device:TPU:24, one launch (start us, length us, event | category | flops | bytes accessed | tf_op | source)
XLA Modules:
  0.0 36.5 jit_solution(2794182882485977957)
XLA Ops:
  0.0 0.0 copy-start.5
  0.0 0.0 copy-start
  0.0 1.2 %first.1 = (f32[4,8,768]{2,1,0:T(8,128)S(1)}, f32[4,8,768]{2,1,0:T(8,128)S(1)}) custom-call(f32[8,64,648]{2,1,0:T(8,128)} %spectrum.3, s32[8,64]{1,0:T(8,128)} %sea_ref.1, s32[8,64]{1,0:T(8,128)} %ice_ref.1, f32[8,64]{1,0:T(8,128)} %wind_ref.1), custom_call_target="tpu_custom_call" | custom-call | tf_op jit(solution)/shard_map/first/pallas_call | solution.py:498
  1.2 0.1 collective-permute-start
  1.3 2.4 %collective-permute-start.1 = (f32[4,8,768]{2,1,0:T(8,128)S(1)}, f32[4,8,768]{2,1,0:T(8,128)S(1)}, u32[]{:S(2)}, u32[]{:S(2)}) collective-permute-start(f32[4,8,768]{2,1,0:T(8,128)S(1)} %get-tuple-element.36), channel_id=1, source_target_pairs={{1,2},{2,1},{3,4},{4,3},{5,6},{6,5},{9,10},{10,9},{11,12},{12,11},... | collective-permute-start | bytes 294920 | tf_op jit(solution)/shard_map/ppermute | solution.py:518
  3.8 0.0 copy-done.5
  3.8 0.0 copy-done.4
  3.8 0.0 copy-done.3
  3.8 0.0 copy-done
  3.8 0.4 %load.1 = (f32[72,768]{1,0:T(8,128)S(1)}, f32[72,768]{1,0:T(8,128)S(1)}, f32[6,72,768]{2,1,0:T(8,128)S(1)}, f32[8,72,128]{2,1,0:T(8,128)S(1)}, f32[8,72,128]{2,1,0:T(8,128)S(1)}) custom-call(f32[8,64,648]{2,1,0:T(8,128)S(1)} %copy-done, s32[8,64]{1,0:T(8,128)S(1)} %copy-done.3, s32[8,64]{1,0:T(8,128)S(1)} %copy-done.4, f32[8,64]{1,0:T(8,128)S(1)} %copy-done.5), custom_call_target="tpu_custom_call" | custom-call | flops 16777216 | tf_op jit(solution)/shard_map/load/pallas_call | solution.py:498
  4.3 0.0 copy-start.1
  4.3 0.0 copy-start.2
  4.3 0.0 copy-start.6
  4.3 0.0 collective-permute-done.halo_a
  4.3 2.9 %collective-permute-done.1.halo_b = f32[4,8,768]{2,1,0:T(8,128)S(1)} collective-permute-done((f32[4,8,768]{2,1,0:T(8,128)S(1)}, f32[4,8,768]{2,1,0:T(8,128)S(1)}, u32[]{:S(2)}, u32[]{:S(2)}) %collective-permute-start.1) | collective-permute-done | bytes 98336 | tf_op jit(solution)/shard_map/ppermute | solution.py:518
  7.3 0.3 join.1
  7.6 2.5 %collective-permute-start.4 = (f32[23,8,128]{2,1,0:T(8,128)S(1)}, f32[23,8,128]{2,1,0:T(8,128)S(1)}, u32[]{:S(2)}, u32[]{:S(2)}) collective-permute-start(f32[23,8,128]{2,1,0:T(8,128)S(1)} %get-tuple-element.54), channel_id=1, source_target_pairs={{8,16},{16,8},{24,0},{0,24},{9,17},{17,9},{25,1},{1,25},{10,18},{1... | collective-permute-start | bytes 282632 | tf_op jit(solution)/shard_map/ppermute | solution.py:542
  10.1 0.6 %collective-permute-start.2 = (f32[23,8,128]{2,1,0:T(8,128)S(1)}, f32[23,8,128]{2,1,0:T(8,128)S(1)}, u32[]{:S(2)}, u32[]{:S(2)}) collective-permute-start(f32[23,8,128]{2,1,0:T(8,128)S(1)} %get-tuple-element.42), channel_id=1, source_target_pairs={{0,8},{8,0},{16,24},{24,16},{1,9},{9,1},{17,25},{25,17},{2,10},{10... | collective-permute-start | bytes 282632 | tf_op jit(solution)/shard_map/ppermute | solution.py:541
  10.6 0.0 copy-done.1
  10.6 0.0 copy-done.2
  10.7 0.0 copy-done.6
  10.7 0.8 %tables.1 = (f32[72,768]{1,0:T(8,128)S(1)}, f32[72,768]{1,0:T(8,128)S(1)}, f32[8,768]{1,0:T(8,128)S(1)}, bf16[768,768]{1,0:T(8,128)(2,1)S(1)}) custom-call(f32[18]{0:T(128)S(1)} %copy-done.6, f32[8,768]{1,0:T(8,128)S(1)} %copy-done.2, bf16[648,648]{1,0:T(8,128)(2,1)S(1)} %copy-done.1), custom_call_target="tpu_custom_call" | custom-call | flops 16777216 | tf_op jit(solution)/shard_map/tables/pallas_call | solution.py:498
  11.5 1.3 %inner.4.after = f32[6,72,768]{2,1,0:T(8,128)S(1)} custom-call(f32[72,768]{1,0:T(8,128)S(1)} %get-tuple-element.43.edge_a.edge, f32[72,768]{1,0:T(8,128)S(1)} %get-tuple-element.51.edge_b.edge, f32[6,72,768]{2,1,0:T(8,128)S(1)} %get-tuple-element.44.inner, f32[8,72,128]{2,1,0:T(8,128)S(1)} %get-tuple-element.45.seas, ...), custom_call_target="tpu_custom_call" | custom-call | flops 268435456 | tf_op jit(solution)/shard_map/inner/pallas_call | solution.py:498
  12.7 1.4 %collective-permute-done.4.halo = f32[23,8,128]{2,1,0:T(8,128)S(1)} collective-permute-done((f32[23,8,128]{2,1,0:T(8,128)S(1)}, f32[23,8,128]{2,1,0:T(8,128)S(1)}, u32[]{:S(2)}, u32[]{:S(2)}) %collective-permute-start.4) | collective-permute-done | bytes 94240 | tf_op jit(solution)/shard_map/ppermute | solution.py:542
  14.1 0.5 %edge.7 = (f32[72,768]{1,0:T(8,128)S(1)}, f32[23,8,128]{2,1,0:T(8,128)S(1)}) custom-call(f32[23,8,128]{2,1,0:T(8,128)S(1)} %collective-permute-done.4.halo, f32[72,768]{1,0:T(8,128)S(1)} %get-tuple-element.51.edge_b.edge, f32[6,72,768]{2,1,0:T(8,128)S(1)} %get-tuple-element.44.inner, f32[8,72,128]{2,1,0:T(8,128)S(1)} %get-tuple-element.45.seas, ...), custom_call_target="tpu_custom_call" | custom-call | flops 67108864 | tf_op jit(solution)/shard_map/edge/pallas_call | solution.py:498
  14.7 2.5 %collective-permute-start.6 = (f32[23,8,128]{2,1,0:T(8,128)S(1)}, f32[23,8,128]{2,1,0:T(8,128)S(1)}, u32[]{:S(2)}, u32[]{:S(2)}) collective-permute-start(f32[23,8,128]{2,1,0:T(8,128)S(1)} %get-tuple-element.58), channel_id=1, source_target_pairs={{8,16},{16,8},{24,0},{0,24},{9,17},{17,9},{25,1},{1,25},{10,18},{1... | collective-permute-start | bytes 282632 | tf_op jit(solution)/shard_map/ppermute | solution.py:542
  17.2 0.0 collective-permute-done.2.halo
  17.2 0.6 %edge.6 = (f32[72,768]{1,0:T(8,128)S(1)}, f32[23,8,128]{2,1,0:T(8,128)S(1)}) custom-call(f32[23,8,128]{2,1,0:T(8,128)S(1)} %collective-permute-done.2.halo, f32[72,768]{1,0:T(8,128)S(1)} %get-tuple-element.43.edge_a.edge, f32[6,72,768]{2,1,0:T(8,128)S(1)} %get-tuple-element.44.inner, f32[8,72,128]{2,1,0:T(8,128)S(1)} %get-tuple-element.45.seas, ...), custom_call_target="tpu_custom_call" | custom-call | flops 67108864 | tf_op jit(solution)/shard_map/edge/pallas_call | solution.py:498
  17.8 0.4 %collective-permute-start.3 = (f32[23,8,128]{2,1,0:T(8,128)S(1)}, f32[23,8,128]{2,1,0:T(8,128)S(1)}, u32[]{:S(2)}, u32[]{:S(2)}) collective-permute-start(f32[23,8,128]{2,1,0:T(8,128)S(1)} %get-tuple-element.52), channel_id=1, source_target_pairs={{0,8},{8,0},{16,24},{24,16},{1,9},{9,1},{17,25},{25,17},{2,10},{10... | collective-permute-start | bytes 282632 | tf_op jit(solution)/shard_map/ppermute | solution.py:541
  18.2 1.2 %inner.5.after = f32[6,72,768]{2,1,0:T(8,128)S(1)} custom-call(f32[72,768]{1,0:T(8,128)S(1)} %get-tuple-element.53.edge_a.edge, f32[72,768]{1,0:T(8,128)S(1)} %get-tuple-element.55.edge_b.edge, f32[6,72,768]{2,1,0:T(8,128)S(1)} %inner.4.after, f32[8,72,128]{2,1,0:T(8,128)S(1)} %get-tuple-element.45.seas, f32[8,72,128]{2,1,0:T(8,128)S(1)} %get-tuple-element.46.gains, ...), custom_call_target="tpu_custom_call" | custom-call | flops 268435456 | tf_op jit(solution)/shard_map/inner/pallas_call | solution.py:498
  19.5 0.9 %collective-permute-done.6.halo = f32[23,8,128]{2,1,0:T(8,128)S(1)} collective-permute-done((f32[23,8,128]{2,1,0:T(8,128)S(1)}, f32[23,8,128]{2,1,0:T(8,128)S(1)}, u32[]{:S(2)}, u32[]{:S(2)}) %collective-permute-start.6) | collective-permute-done | bytes 94240 | tf_op jit(solution)/shard_map/ppermute | solution.py:542
  20.4 0.5 %edge.9 = (f32[72,768]{1,0:T(8,128)S(1)}, f32[23,8,128]{2,1,0:T(8,128)S(1)}) custom-call(f32[23,8,128]{2,1,0:T(8,128)S(1)} %collective-permute-done.6.halo, f32[72,768]{1,0:T(8,128)S(1)} %get-tuple-element.55.edge_b.edge, f32[6,72,768]{2,1,0:T(8,128)S(1)} %inner.4.after, f32[8,72,128]{2,1,0:T(8,128)S(1)} %get-tuple-element.45.seas, ...), custom_call_target="tpu_custom_call" | custom-call | flops 67108864 | tf_op jit(solution)/shard_map/edge/pallas_call | solution.py:498
  20.9 3.2 %collective-permute-start.8 = (f32[23,8,128]{2,1,0:T(8,128)S(1)}, f32[23,8,128]{2,1,0:T(8,128)S(1)}, u32[]{:S(2)}, u32[]{:S(2)}) collective-permute-start(f32[23,8,128]{2,1,0:T(8,128)S(1)} %get-tuple-element.62), channel_id=1, source_target_pairs={{8,16},{16,8},{24,0},{0,24},{9,17},{17,9},{25,1},{1,25},{10,18},{1... | collective-permute-start | bytes 282632 | tf_op jit(solution)/shard_map/ppermute | solution.py:542
  24.1 0.0 collective-permute-done.3.halo
  24.1 0.6 %edge.8 = (f32[72,768]{1,0:T(8,128)S(1)}, f32[23,8,128]{2,1,0:T(8,128)S(1)}) custom-call(f32[23,8,128]{2,1,0:T(8,128)S(1)} %collective-permute-done.3.halo, f32[72,768]{1,0:T(8,128)S(1)} %get-tuple-element.53.edge_a.edge, f32[6,72,768]{2,1,0:T(8,128)S(1)} %inner.4.after, f32[8,72,128]{2,1,0:T(8,128)S(1)} %get-tuple-element.45.seas, ...), custom_call_target="tpu_custom_call" | custom-call | flops 67108864 | tf_op jit(solution)/shard_map/edge/pallas_call | solution.py:498
  24.7 0.1 collective-permute-start.5
  24.8 1.2 %inner.6.after = f32[6,72,768]{2,1,0:T(8,128)S(1)} custom-call(f32[72,768]{1,0:T(8,128)S(1)} %get-tuple-element.57.edge_a.edge, f32[72,768]{1,0:T(8,128)S(1)} %get-tuple-element.59.edge_b.edge, f32[6,72,768]{2,1,0:T(8,128)S(1)} %inner.5.after, f32[8,72,128]{2,1,0:T(8,128)S(1)} %get-tuple-element.45.seas, f32[8,72,128]{2,1,0:T(8,128)S(1)} %get-tuple-element.46.gains, ...), custom_call_target="tpu_custom_call" | custom-call | flops 268435456 | tf_op jit(solution)/shard_map/inner/pallas_call | solution.py:498
  26.1 1.5 %collective-permute-done.8.halo = f32[23,8,128]{2,1,0:T(8,128)S(1)} collective-permute-done((f32[23,8,128]{2,1,0:T(8,128)S(1)}, f32[23,8,128]{2,1,0:T(8,128)S(1)}, u32[]{:S(2)}, u32[]{:S(2)}) %collective-permute-start.8) | collective-permute-done | bytes 94240 | tf_op jit(solution)/shard_map/ppermute | solution.py:542
  27.5 0.5 %edge.11 = (f32[72,768]{1,0:T(8,128)S(1)}, f32[21,8,128]{2,1,0:T(8,128)S(1)}) custom-call(f32[23,8,128]{2,1,0:T(8,128)S(1)} %collective-permute-done.8.halo, f32[72,768]{1,0:T(8,128)S(1)} %get-tuple-element.59.edge_b.edge, f32[6,72,768]{2,1,0:T(8,128)S(1)} %inner.5.after, f32[8,72,128]{2,1,0:T(8,128)S(1)} %get-tuple-element.45.seas, ...), custom_call_target="tpu_custom_call" | custom-call | flops 67108864 | tf_op jit(solution)/shard_map/edge/pallas_call | solution.py:498
  28.1 2.2 %collective-permute-start.9 = (f32[21,8,128]{2,1,0:T(8,128)S(1)}, f32[21,8,128]{2,1,0:T(8,128)S(1)}, u32[]{:S(2)}, u32[]{:S(2)}) collective-permute-start(f32[21,8,128]{2,1,0:T(8,128)S(1)} %get-tuple-element.64), channel_id=1, source_target_pairs={{8,16},{16,8},{24,0},{0,24},{9,17},{17,9},{25,1},{1,25},{10,18},{1... | collective-permute-start | bytes 258056 | tf_op jit(solution)/shard_map/ppermute | solution.py:542
  30.2 0.0 collective-permute-done.5.halo
  30.2 0.6 %edge.10 = (f32[72,768]{1,0:T(8,128)S(1)}, f32[21,8,128]{2,1,0:T(8,128)S(1)}) custom-call(f32[23,8,128]{2,1,0:T(8,128)S(1)} %collective-permute-done.5.halo, f32[72,768]{1,0:T(8,128)S(1)} %get-tuple-element.57.edge_a.edge, f32[6,72,768]{2,1,0:T(8,128)S(1)} %inner.5.after, f32[8,72,128]{2,1,0:T(8,128)S(1)} %get-tuple-element.45.seas, ...), custom_call_target="tpu_custom_call" | custom-call | flops 67108864 | tf_op jit(solution)/shard_map/edge/pallas_call | solution.py:498
  30.8 0.1 collective-permute-start.7
  30.9 1.1 %inner.7.after.done_inner = f32[6,64,648]{2,1,0:T(8,128)S(1)} custom-call(f32[72,768]{1,0:T(8,128)S(1)} %get-tuple-element.61.edge_a.edge, f32[72,768]{1,0:T(8,128)S(1)} %get-tuple-element.63.edge_b.edge, f32[6,72,768]{2,1,0:T(8,128)S(1)} %inner.6.after, f32[8,72,128]{2,1,0:T(8,128)S(1)} %get-tuple-element.45.seas, ...), custom_call_target="tpu_custom_call" | custom-call | flops 268435456 | tf_op jit(solution)/shard_map/inner/pallas_call | solution.py:498
  32.0 1.5 %collective-permute-done.9.halo = f32[21,8,128]{2,1,0:T(8,128)S(1)} collective-permute-done((f32[21,8,128]{2,1,0:T(8,128)S(1)}, f32[21,8,128]{2,1,0:T(8,128)S(1)}, u32[]{:S(2)}, u32[]{:S(2)}) %collective-permute-start.9) | collective-permute-done | bytes 86048 | tf_op jit(solution)/shard_map/ppermute | solution.py:542
  33.5 0.5 %late.1.done_edge = f32[64,648]{1,0:T(8,128)S(1)} custom-call(f32[21,8,128]{2,1,0:T(8,128)S(1)} %collective-permute-done.9.halo, f32[72,768]{1,0:T(8,128)S(1)} %get-tuple-element.63.edge_b.edge, f32[6,72,768]{2,1,0:T(8,128)S(1)} %inner.6.after, f32[8,72,128]{2,1,0:T(8,128)S(1)} %get-tuple-element.45.seas, f32[8,72,128]{2,1,0:T(8,128)S(1)} %get-tuple-element.46.gains, ...), custom_call_target="tpu_custom_call" | custom-call | flops 67108864 | tf_op jit(solution)/shard_map/late/pallas_call | solution.py:498
  34.0 1.3 %collective-permute-done.7.halo = f32[21,8,128]{2,1,0:T(8,128)S(1)} collective-permute-done((f32[21,8,128]{2,1,0:T(8,128)S(1)}, f32[21,8,128]{2,1,0:T(8,128)S(1)}, u32[]{:S(2)}, u32[]{:S(2)}) %collective-permute-start.7) | collective-permute-done | bytes 86048 | tf_op jit(solution)/shard_map/ppermute | solution.py:541
  35.4 1.2 %last.1 = f32[8,64,648]{2,1,0:T(8,128)} custom-call(f32[21,8,128]{2,1,0:T(8,128)S(1)} %collective-permute-done.7.halo, f32[72,768]{1,0:T(8,128)S(1)} %get-tuple-element.61.edge_a.edge, f32[6,72,768]{2,1,0:T(8,128)S(1)} %inner.6.after, f32[8,72,128]{2,1,0:T(8,128)S(1)} %get-tuple-element.45.seas, f32[8,72,128]{2,1,0:T(8,128)S(1)} %get-tuple-element.46.gains, ...), custom_call_target="tpu_custom_call" | custom-call | flops 67108864 | tf_op jit(solution)/shard_map/last/pallas_call | solution.py:498
  (2 shorter events, 0.0 us)
Async XLA Ops:
  0.0 3.8 %copy-start.5 = (f32[8,64]{1,0:T(8,128)S(1)}, f32[8,64]{1,0:T(8,128)}, u32[]{:S(2)}) copy-start(f32[8,64]{1,0:T(8,128)} %wind_ref.1) | copy-start | bytes 6148
  0.0 3.8 %copy-start.4 = (s32[8,64]{1,0:T(8,128)S(1)}, s32[8,64]{1,0:T(8,128)}, u32[]{:S(2)}) copy-start(s32[8,64]{1,0:T(8,128)} %ice_ref.1) | copy-start | bytes 6148
  0.0 3.8 %copy-start.3 = (s32[8,64]{1,0:T(8,128)S(1)}, s32[8,64]{1,0:T(8,128)}, u32[]{:S(2)}) copy-start(s32[8,64]{1,0:T(8,128)} %sea_ref.1) | copy-start | bytes 6148
  0.0 3.8 %copy-start = (f32[8,64,648]{2,1,0:T(8,128)S(1)}, f32[8,64,648]{2,1,0:T(8,128)}, u32[]{:S(2)}) copy-start(f32[8,64,648]{2,1,0:T(8,128)} %spectrum.3) | copy-start | bytes 3981316
  1.2 3.1 %collective-permute-start = (f32[4,8,768]{2,1,0:T(8,128)S(1)}, f32[4,8,768]{2,1,0:T(8,128)S(1)}, u32[]{:S(2)}, u32[]{:S(2)}) collective-permute-start(f32[4,8,768]{2,1,0:T(8,128)S(1)} %get-tuple-element.35), channel_id=1, source_target_pairs={{0,1},{1,0},{2,3},{3,2},{4,5},{5,4},{6,7},{7,6},{8,9},{9,8},{10,11... | collective-permute-start | bytes 294920 | tf_op jit(solution)/shard_map/ppermute | solution.py:519
  1.3 5.9 %collective-permute-start.1 = (f32[4,8,768]{2,1,0:T(8,128)S(1)}, f32[4,8,768]{2,1,0:T(8,128)S(1)}, u32[]{:S(2)}, u32[]{:S(2)}) collective-permute-start(f32[4,8,768]{2,1,0:T(8,128)S(1)} %get-tuple-element.36), channel_id=1, source_target_pairs={{1,2},{2,1},{3,4},{4,3},{5,6},{6,5},{9,10},{10,9},{11,12},{12,11},... | collective-permute-start | bytes 294920 | tf_op jit(solution)/shard_map/ppermute | solution.py:518
  4.3 6.4 %copy-start.1 = (bf16[648,648]{1,0:T(8,128)(2,1)S(1)}, bf16[648,648]{1,0:T(8,128)(2,1)}, u32[]{:S(2)}) copy-start(bf16[648,648]{1,0:T(8,128)(2,1)} %coupling_ref.1) | copy-start | bytes 2519428
  4.3 6.4 %copy-start.2 = (f32[8,768]{1,0:T(8,128)S(1)}, f32[8,768]{1,0:T(8,128)}, u32[]{:S(2)}) copy-start(f32[8,768]{1,0:T(8,128)} %constant.2.clone.angle_ref) | copy-start | bytes 73732
  4.3 6.4 %copy-start.6 = (f32[18]{0:T(128)S(1)}, f32[18]{0:T(128)}, u32[]{:S(2)}) copy-start(f32[18]{0:T(128)} %speed_ref.1) | copy-start | bytes 220
  7.6 6.5 %collective-permute-start.4 = (f32[23,8,128]{2,1,0:T(8,128)S(1)}, f32[23,8,128]{2,1,0:T(8,128)S(1)}, u32[]{:S(2)}, u32[]{:S(2)}) collective-permute-start(f32[23,8,128]{2,1,0:T(8,128)S(1)} %get-tuple-element.54), channel_id=1, source_target_pairs={{8,16},{16,8},{24,0},{0,24},{9,17},{17,9},{25,1},{1,25},{10,18},{1... | collective-permute-start | bytes 282632 | tf_op jit(solution)/shard_map/ppermute | solution.py:542
  10.1 7.1 %collective-permute-start.2 = (f32[23,8,128]{2,1,0:T(8,128)S(1)}, f32[23,8,128]{2,1,0:T(8,128)S(1)}, u32[]{:S(2)}, u32[]{:S(2)}) collective-permute-start(f32[23,8,128]{2,1,0:T(8,128)S(1)} %get-tuple-element.42), channel_id=1, source_target_pairs={{0,8},{8,0},{16,24},{24,16},{1,9},{9,1},{17,25},{25,17},{2,10},{10... | collective-permute-start | bytes 282632 | tf_op jit(solution)/shard_map/ppermute | solution.py:541
  14.7 5.7 %collective-permute-start.6 = (f32[23,8,128]{2,1,0:T(8,128)S(1)}, f32[23,8,128]{2,1,0:T(8,128)S(1)}, u32[]{:S(2)}, u32[]{:S(2)}) collective-permute-start(f32[23,8,128]{2,1,0:T(8,128)S(1)} %get-tuple-element.58), channel_id=1, source_target_pairs={{8,16},{16,8},{24,0},{0,24},{9,17},{17,9},{25,1},{1,25},{10,18},{1... | collective-permute-start | bytes 282632 | tf_op jit(solution)/shard_map/ppermute | solution.py:542
  17.8 6.3 %collective-permute-start.3 = (f32[23,8,128]{2,1,0:T(8,128)S(1)}, f32[23,8,128]{2,1,0:T(8,128)S(1)}, u32[]{:S(2)}, u32[]{:S(2)}) collective-permute-start(f32[23,8,128]{2,1,0:T(8,128)S(1)} %get-tuple-element.52), channel_id=1, source_target_pairs={{0,8},{8,0},{16,24},{24,16},{1,9},{9,1},{17,25},{25,17},{2,10},{10... | collective-permute-start | bytes 282632 | tf_op jit(solution)/shard_map/ppermute | solution.py:541
  20.9 6.6 %collective-permute-start.8 = (f32[23,8,128]{2,1,0:T(8,128)S(1)}, f32[23,8,128]{2,1,0:T(8,128)S(1)}, u32[]{:S(2)}, u32[]{:S(2)}) collective-permute-start(f32[23,8,128]{2,1,0:T(8,128)S(1)} %get-tuple-element.62), channel_id=1, source_target_pairs={{8,16},{16,8},{24,0},{0,24},{9,17},{17,9},{25,1},{1,25},{10,18},{1... | collective-permute-start | bytes 282632 | tf_op jit(solution)/shard_map/ppermute | solution.py:542
  24.7 5.5 %collective-permute-start.5 = (f32[23,8,128]{2,1,0:T(8,128)S(1)}, f32[23,8,128]{2,1,0:T(8,128)S(1)}, u32[]{:S(2)}, u32[]{:S(2)}) collective-permute-start(f32[23,8,128]{2,1,0:T(8,128)S(1)} %get-tuple-element.56), channel_id=1, source_target_pairs={{0,8},{8,0},{16,24},{24,16},{1,9},{9,1},{17,25},{25,17},{2,10},{10... | collective-permute-start | bytes 282632 | tf_op jit(solution)/shard_map/ppermute | solution.py:541
  28.1 5.4 %collective-permute-start.9 = (f32[21,8,128]{2,1,0:T(8,128)S(1)}, f32[21,8,128]{2,1,0:T(8,128)S(1)}, u32[]{:S(2)}, u32[]{:S(2)}) collective-permute-start(f32[21,8,128]{2,1,0:T(8,128)S(1)} %get-tuple-element.64), channel_id=1, source_target_pairs={{8,16},{16,8},{24,0},{0,24},{9,17},{17,9},{25,1},{1,25},{10,18},{1... | collective-permute-start | bytes 258056 | tf_op jit(solution)/shard_map/ppermute | solution.py:542
  30.8 4.6 %collective-permute-start.7 = (f32[21,8,128]{2,1,0:T(8,128)S(1)}, f32[21,8,128]{2,1,0:T(8,128)S(1)}, u32[]{:S(2)}, u32[]{:S(2)}) collective-permute-start(f32[21,8,128]{2,1,0:T(8,128)S(1)} %get-tuple-element.60), channel_id=1, source_target_pairs={{0,8},{8,0},{16,24},{24,16},{1,9},{9,1},{17,25},{25,17},{2,10},{10... | collective-permute-start | bytes 258056 | tf_op jit(solution)/shard_map/ppermute | solution.py:541

commit v4 on v3

--- a/solution.py
+++ b/solution.py
@@ -8,6 +8,7 @@
 from jax.experimental import pallas as pl
 from jax.experimental.pallas import tpu as pltpu
 from jax.sharding import PartitionSpec as P
+
 
 DIRS = 36
 STEPS = 4
@@ -107,23 +108,25 @@
     return 2 * blocks + blocks // 2 + 1 + (2 if halo else 0)
 
 
+def half_parts(t, west, bins):
+    split, high, _, _, _ = pack_plan(bins, west)
+    lane = lane_index(t[0].shape)
+    if west:
+        return t[2], jnp.where(lane < high, t[3], t[1]), t[1]
+    return t[0], t[4], jnp.where(lane < split, t[1], jnp.where(lane >= high, t[3], turn(t[5], split)))
+
+
 def pack_half(tiles, west, bins, rows, halo, out):
-    split, high, width, kept, start = pack_plan(bins, west)
+    _, _, width, kept, start = pack_plan(bins, west)
     rest = width - kept
     blocks = rows // 8
     half = blocks // 2
     lane = lane_index((8, LANES))
 
-    def parts(block):
-        t = [tile[8 * block : 8 * block + 8] for tile in tiles]
-        if west:
-            return t[2], jnp.where(lane < high, t[3], t[1]), t[1]
-        return t[0], t[4], jnp.where(lane < split, t[1], jnp.where(lane >= high, t[3], turn(t[5], split)))
-
     left = jnp.zeros((8, LANES), jnp.float32)
     held = {}
     for block in range(blocks + (1 if halo else 0)):
-        full, other, part = parts(block)
+        full, other, part = half_parts([tile[8 * block : 8 * block + 8] for tile in tiles], west, bins)
         if block < blocks:
             out[block] = full
             out[blocks + block] = other
@@ -141,7 +144,7 @@
     out[2 * blocks + half] = left
 
 
-def across_edge(halo, inner, west, bins, rows, with_halo):
+def across_edge(halo, inner, west, bins, rows, with_halo, corner=None):
     split, high, width, kept, start = pack_plan(bins, not west)
     rest = width - kept
     blocks = rows // 8
@@ -154,7 +157,9 @@
         if block == blocks and not with_halo:
             new = near
         else:
-            if block == blocks:
+            if block == blocks and corner is not None:
+                full, other, part = corner[0], corner[1], corner[2]
+            elif block == blocks:
                 full, other = halo[2 * blocks + half + 1], halo[2 * blocks + half + 2]
                 part = turn(left, start - half * rest)
             else:
@@ -218,7 +223,7 @@
 def masks_kernel_part(sea_ref, ice_ref, wind_ref):
     sea = sea_ref[...].astype(jnp.float32)
     gain = 1.0 + time_step * (wind_ref[...] * (1.0 - ice_ref[...].astype(jnp.float32)))
-    columns, rows = sea.shape
+    _, rows = sea.shape
     sea = jnp.concatenate([sea, gain], axis=1)
     turned = jnp.transpose(sea)
     return turned[:rows], turned[rows:]
@@ -300,7 +305,7 @@
     wide[:, body:] = jnp.concatenate([tail, jnp.zeros((padded - bins, LANES), jnp.bfloat16)], axis=0)
 
 
-def load_kernel(bins, spectrum, sea_ref, ice_ref, wind_ref, edge_a, edge_b, inner, seas, gains):
+def load_kernel(bins, spectrum, sea_ref, ice_ref, wind_ref, edge_a, edge_b, inner, seas, gains, pack_a, pack_b):
     columns, rows = sea_ref.shape
     tiles = lane_tiles(bins)
     used = bins % LANES
@@ -322,8 +327,13 @@
 
     for c in range(1, columns - 1):
         put(inner.at[c - 1], c)
-    for second, target in ((False, edge_a), (True, edge_b)):
-        put(target, jnp.where(west_flag(second), 0, columns - 1))
+    for second, target, pack in ((False, edge_a, pack_a), (True, edge_b, pack_b)):
+
+        def side(west, target=target, pack=pack):
+            put(target, 0 if west else columns - 1)
+            pack_half([target[:rows, lanes_of(t)] for t in range(tiles)], west, bins, rows, False, pack)
+
+        on_each_side(second, side)
 
 
 def join_kernel(
@@ -363,7 +373,8 @@
         def side(west, target=target, pack=pack):
             for tile in range(tiles):
                 target[rows:, lanes_of(tile)] = values[0 if west else columns - 1][tile]
-            pack_half([target[:, lanes_of(t)] for t in range(tiles)], west, bins, rows, True, pack)
+            for k, value in enumerate(half_parts(values[0 if west else columns - 1], west, bins)):
+                pack[k] = value
 
         on_each_side(second, side)
 
@@ -372,12 +383,18 @@
     return adv * (gains - seas * share) + seas * product
 
 
-def edge_kernel(bins, second, halo, edge, inner, seas, gains, stay, go_x, go_y, wide, after, out, pack, adv_ref):
+def first_edge_kernel(bins, second, corner, *refs):
+    edge_kernel(bins, second, *refs, corner=corner)
+
+
+def edge_kernel(
+    bins, second, halo, edge, inner, seas, gains, stay, go_x, go_y, wide, after, out, pack, adv_ref, corner=None
+):
     rows = edge.shape[0] - 2 * DEPTH
     halo_next = pack.shape[0] == pack_count(rows, True)
 
     def side(west):
-        fresh = edge_step(bins, west, halo, edge, inner, seas, gains, stay, go_x, go_y, wide, adv_ref, False)
+        fresh = edge_step(bins, west, halo, edge, inner, seas, gains, stay, go_x, go_y, wide, adv_ref, False, corner)
         for t, value in enumerate(fresh):
             out[:, lanes_of(t)] = value
         pack_half(fresh, west, bins, rows, halo_next, pack)
@@ -412,13 +429,13 @@
         copy.wait()
 
 
-def edge_step(bins, west, halo, edge, inner, seas, gains, stay, go_x, go_y, wide, adv_ref, last):
+def edge_step(bins, west, halo, edge, inner, seas, gains, stay, go_x, go_y, wide, adv_ref, last, corner=None):
     tiles = lane_tiles(bins)
     columns = inner.shape[0] + 2
     rows = edge.shape[0] - 2 * DEPTH
     used = rows if last else edge.shape[0]
     near, mine = (0, 0) if west else (columns - 3, columns - 1)
-    across = across_edge(halo, [inner[near, :, lanes_of(t)] for t in range(tiles)], west, bins, rows, not last)
+    across = across_edge(halo, [inner[near, :, lanes_of(t)] for t in range(tiles)], west, bins, rows, not last, corner)
     for t in range(tiles):
         here = lanes_of(t)
         adv = advect(edge[:, here], across[t], stay[:, here], go_x[:, here], go_y[0:1, here], bins, t)
@@ -476,7 +493,7 @@
     return table
 
 
-def on_device(spectrum, sea_mask, ice_flags, wind_forcing, group_speed, coupling):
+def steps(spectrum, sea_mask, ice_flags, wind_forcing, group_speed, coupling):
     columns, rows, bins = spectrum.shape
     tiles = lane_tiles(bins)
     padded = tiles * LANES
@@ -491,13 +508,11 @@
     edge_shape = VMEM((tall, padded), f32)
     inner_shape = VMEM((columns - 2, tall, padded), f32)
     mask_shape = VMEM((columns, tall, LANES), f32)
-    pack_shape = VMEM((pack_count(rows, True), 8, LANES), f32)
     table_shape = VMEM((tall, padded), f32)
 
-    def call(body, name, outs, ins, specs, scratch=(), aliases=None, flops=0, out_specs=None):
+    def call(body, outs, ins, specs, scratch=(), aliases=None, flops=0, out_specs=None):
         return pl.pallas_call(
             body,
-            name=name,
             out_shape=outs,
             in_specs=specs,
             out_specs=out_specs if out_specs is not None else jax.tree.map(lambda _: vmem, outs),
@@ -508,7 +523,7 @@
         )(*ins)
 
     send_a, send_b = call(
-        functools.partial(first_kernel, bins), "first",
+        functools.partial(first_kernel, bins),
         (VMEM((columns // 2, 8, padded), f32),) * 2,
         [pltpu.with_memory_space_constraint(x, pltpu.HBM) for x in (spectrum, sea_mask, ice_flags, wind_forcing)],
         [hbm] * 4,
@@ -517,20 +532,22 @@
     )
     halo_b = lax.ppermute(send_b, "lat", lat_b)
     halo_a = lax.ppermute(send_a, "lat", lat_a)
-    edge_a, edge_b, inner, seas, gains = call(
-        functools.partial(load_kernel, bins), "load",
-        (edge_shape, edge_shape, inner_shape, mask_shape, mask_shape),
+    pack_shape = VMEM((pack_count(rows, False), 8, LANES), f32)
+    corner_shape = VMEM((3, 8, LANES), f32)
+    edge_a, edge_b, inner, seas, gains, pack_a, pack_b = call(
+        functools.partial(load_kernel, bins),
+        (edge_shape, edge_shape, inner_shape, mask_shape, mask_shape, pack_shape, pack_shape),
         (spectrum, sea_mask, ice_flags, wind_forcing), [vmem] * 4, flops=1 << 24,
     )
     stay, go_x, go_y, wide = call(
-        functools.partial(table_kernel, bins, rows), "tables",
+        functools.partial(table_kernel, bins, rows),
         (table_shape, table_shape, VMEM((8, padded), f32), VMEM((padded, padded), jnp.bfloat16)),
         (group_speed, jnp.asarray(angle_table(bins, group_speed.shape[0])), coupling),
         [smem, vmem, vmem], flops=1 << 24,
     )
-    edge_a, edge_b, inner, seas, gains, pack_a, pack_b = call(
-        functools.partial(join_kernel, bins), "join",
-        (edge_shape, edge_shape, inner_shape, mask_shape, mask_shape, pack_shape, pack_shape),
+    edge_a, edge_b, inner, seas, gains, corner_a, corner_b = call(
+        functools.partial(join_kernel, bins),
+        (edge_shape, edge_shape, inner_shape, mask_shape, mask_shape, corner_shape, corner_shape),
         (halo_a, halo_b, edge_a, edge_b, inner, seas, gains),
         [vmem] * 7,
         aliases={2: 0, 3: 1, 4: 2, 5: 3, 6: 4},
@@ -538,11 +555,13 @@
     tables = (seas, gains, stay, go_x, go_y, wide)
     for step in range(STEPS):
         last = step == STEPS - 1
+        halo_b = lax.ppermute(pack_b, "lon", lon_b)
         halo_a = lax.ppermute(pack_a, "lon", lon_a)
-        halo_b = lax.ppermute(pack_b, "lon", lon_b)
+        if step == 0:
+            corners = (lax.ppermute(corner_a, "lon", lon_a), lax.ppermute(corner_b, "lon", lon_b))
         used = rows if last else tall
         new_inner = call(
-            functools.partial(inner_kernel, bins), "inner", VMEM((columns - 2, rows, bins), f32) if last else inner_shape,
+            functools.partial(inner_kernel, bins), VMEM((columns - 2, rows, bins), f32) if last else inner_shape,
             (edge_a, edge_b, inner) + tables, [vmem] * 9,
             [VMEM((columns - 2, used, padded), f32), VMEM(((columns - 2) * used, padded), jnp.bfloat16)],
             flops=1 << 28,
@@ -551,20 +570,23 @@
             column = VMEM((rows, bins), f32)
             scratch = [VMEM((tall, padded), f32)]
             done_b = call(
-                functools.partial(late_edge_kernel, bins, True), "late", column,
+                functools.partial(late_edge_kernel, bins, True), column,
                 (halo_b, edge_b, inner) + tables + (new_inner,), [vmem] * 10, scratch, flops=1 << 26,
             )
             return call(
-                functools.partial(last_edge_kernel, bins, False), "last", pltpu.HBM((columns, rows, bins), f32),
+                functools.partial(last_edge_kernel, bins, False), pltpu.HBM((columns, rows, bins), f32),
                 (halo_a, edge_a, inner) + tables + (new_inner, done_b), [vmem] * 11,
                 scratch + [column, pltpu.SemaphoreType.DMA((3,))], flops=1 << 26, out_specs=hbm,
             )
         fresh = []
         pack_next = VMEM((pack_count(rows, step < STEPS - 2), 8, LANES), f32)
         for second, halo, edge in ((False, halo_a, edge_a), (True, halo_b, edge_b)):
+            body, ins = edge_kernel, (halo, edge, inner) + tables + (new_inner,)
+            if step == 0:
+                body, ins = first_edge_kernel, (corners[second],) + ins
             fresh.append(call(
-                functools.partial(edge_kernel, bins, second), "edge", (edge_shape, pack_next),
-                (halo, edge, inner) + tables + (new_inner,), [vmem] * 10, [VMEM((tall, padded), f32)], flops=1 << 26,
+                functools.partial(body, bins, second), (edge_shape, pack_next),
+                ins, [vmem] * len(ins), [VMEM((tall, padded), f32)], flops=1 << 26,
             ))
         inner = new_inner
         (edge_a, pack_a), (edge_b, pack_b) = fresh
@@ -572,6 +594,4 @@
 
 def solution(mesh):
     placed = (P("lon", "lat", None), P("lon", "lat"), P("lon", "lat"), P("lon", "lat"), P(), P())
-    return jax.shard_map(
-        on_device, mesh=mesh, in_specs=placed, out_specs=P("lon", "lat", None), check_vma=False
-    )
+    return jax.shard_map(steps, mesh=mesh, in_specs=placed, out_specs=P("lon", "lat", None), check_vma=False)

time: 36.7 us -> 36.4 us (level); the launches traced: 36.5 us -> 35.7 us
  starting transfers between devices: 14.1 us -> 13.3 us
  waiting for transfers between devices: 9.58 us -> 9.05 us
  Pallas kernels: 12.6 us -> 13 us
    ppermute x10 -> x12, starting transfers between devices: 14.1 us -> 13.3 us  [the longest x4 5.11 us: steps(): halo_a = lax.ppermute(pack_a, 'lon', lon_a)]
    ppermute x10 -> x12, waiting for transfers between devices: 9.58 us -> 9.05 us  [the longest x4 6.1 us: steps(): halo_b = lax.ppermute(pack_b, 'lon', lon_b)]
    pallas_call x16, Pallas kernels: 12.6 us -> 13 us  [call(): pl.pallas_call(body, out_shape=outs, in_specs=specs, out_specs=out_specs...]
  transfers between devices with their start and end apart: 10 -> 12, of which waited for: 6 -> 5; matrix products, arithmetic and copies ran while one was open for 0% -> 0% of each run, Pallas kernels for 27% -> 30%
where the time goes in v4:
time: 36.4 us; the launch traced here: 35.7 us
  starting transfers between devices  13.3 us (37%)
  Pallas kernels  13 us (36%)
  waiting for transfers between devices  9.05 us (25%)
    pallas_call x16, Pallas kernels, call(): pl.pallas_call(body, out_shape=outs, in_specs=specs, out_specs=out_specs...  13 us
    ppermute x4, waiting for transfers between devices, steps(): halo_b = lax.ppermute(pack_b, 'lon', lon_b)  6.1 us
    ppermute x4, starting transfers between devices, steps(): halo_a = lax.ppermute(pack_a, 'lon', lon_a)  5.11 us
    ppermute x4, starting transfers between devices, steps(): halo_b = lax.ppermute(pack_b, 'lon', lon_b)  3.73 us
    ppermute x1, waiting for transfers between devices, steps(): lax.ppermute(corner_b, 'lon', lon_b)  2.76 us
    ppermute x1, starting transfers between devices, steps(): halo_b = lax.ppermute(send_b, 'lat', lat_b)  2.45 us
    ppermute x1, starting transfers between devices, steps(): lax.ppermute(corner_a, 'lon', lon_a)  1.49 us
  transfers between devices with their start and end apart: 12, of which 5 were waited for; matrix products, arithmetic and copies ran while one was open for 0% of the time, Pallas kernels for 30%

profile of v4, /device:TPU:24, one launch (start us, length us, event | category | flops | bytes accessed | tf_op | source)
XLA Modules:
  0.0 35.7 jit_solution(10640080702542046125)
XLA Ops:
  0.0 0.0 copy-start
  0.0 0.0 copy-start.2
  0.0 0.0 copy-start.1
  0.0 0.0 copy-start.6
  0.1 1.2 %shard_map.73 = (f32[4,8,768]{2,1,0:T(8,128)S(1)}, f32[4,8,768]{2,1,0:T(8,128)S(1)}) custom-call(f32[8,64,648]{2,1,0:T(8,128)} %spectrum.3, s32[8,64]{1,0:T(8,128)} %sea_ref.1, s32[8,64]{1,0:T(8,128)} %ice_ref.1, f32[8,64]{1,0:T(8,128)} %wind_ref.1), custom_call_target="tpu_custom_call" | custom-call | tf_op jit(solution)/shard_map/pallas_call | solution.py:514
  1.3 0.1 collective-permute-start
  1.4 2.4 %collective-permute-start.1 = (f32[4,8,768]{2,1,0:T(8,128)S(1)}, f32[4,8,768]{2,1,0:T(8,128)S(1)}, u32[]{:S(2)}, u32[]{:S(2)}) collective-permute-start(f32[4,8,768]{2,1,0:T(8,128)S(1)} %get-tuple-element.38), channel_id=1, source_target_pairs={{1,2},{2,1},{3,4},{4,3},{5,6},{6,5},{9,10},{10,9},{11,12},{12,11},... | collective-permute-start | bytes 294920 | tf_op jit(solution)/shard_map/ppermute | solution.py:533
  3.8 0.0 copy-done.5
  3.8 0.0 copy-done.4
  3.9 0.0 copy-done.3
  3.9 0.7 %shard_map.74 = (f32[72,768]{1,0:T(8,128)S(1)}, f32[72,768]{1,0:T(8,128)S(1)}, f32[6,72,768]{2,1,0:T(8,128)S(1)}, f32[8,72,128]{2,1,0:T(8,128)S(1)}, f32[8,72,12...) custom-call(f32[8,64,648]{2,1,0:T(8,128)S(1)} %copy-done, s32[8,64]{1,0:T(8,128)S(1)} %copy-done.3, ...), custom_call_target="tpu_custom_call" | custom-call | flops 16777216 | tf_op jit(solution)/shard_map/pallas_call | solution.py:514
  4.6 2.5 %collective-permute-start.6 = (f32[21,8,128]{2,1,0:T(8,128)S(1)}, f32[21,8,128]{2,1,0:T(8,128)S(1)}, u32[]{:S(2)}, u32[]{:S(2)}) collective-permute-start(f32[21,8,128]{2,1,0:T(8,128)S(1)} %get-tuple-element.58), channel_id=1, source_target_pairs={{8,16},{16,8},{24,0},{0,24},{9,17},{17,9},{25,1},{1,25},{10,18},{1... | collective-permute-start | bytes 258056 | tf_op jit(solution)/shard_map/ppermute | solution.py:558
  7.1 0.6 %collective-permute-start.3 = (f32[21,8,128]{2,1,0:T(8,128)S(1)}, f32[21,8,128]{2,1,0:T(8,128)S(1)}, u32[]{:S(2)}, u32[]{:S(2)}) collective-permute-start(f32[21,8,128]{2,1,0:T(8,128)S(1)} %get-tuple-element.45), channel_id=1, source_target_pairs={{0,8},{8,0},{16,24},{24,16},{1,9},{9,1},{17,25},{25,17},{2,10},{10... | collective-permute-start | bytes 258056 | tf_op jit(solution)/shard_map/ppermute | solution.py:559
  7.6 0.0 copy-done.1
  7.6 0.8 %shard_map.76 = (f32[72,768]{1,0:T(8,128)S(1)}, f32[72,768]{1,0:T(8,128)S(1)}, f32[8,768]{1,0:T(8,128)S(1)}, bf16[768,768]{1,0:T(8,128)(2,1)S(1)}) custom-call(f32[18]{0:T(128)S(1)} %copy-done.6, f32[8,768]{1,0:T(8,128)S(1)} %copy-done.2, bf16[648,648]{1,0:T(8,128)(2,1)S(1)} %copy-done.1), custom_call_target="tpu_custom_call" | custom-call | flops 16777216 | tf_op jit(solution)/shard_map/pallas_call | solution.py:514
  8.4 0.0 collective-permute-done.halo_a
  8.4 0.0 collective-permute-done.1.halo_b
  8.4 0.2 shard_map.75
  8.6 1.5 %collective-permute-start.2 = (f32[3,8,128]{2,1,0:T(8,128)S(1)}, f32[3,8,128]{2,1,0:T(8,128)S(1)}, u32[]{:S(2)}, u32[]{:S(2)}) collective-permute-start(f32[3,8,128]{2,1,0:T(8,128)S(1)} %get-tuple-element.44), channel_id=1, source_target_pairs={{0,8},{8,0},{16,24},{24,16},{1,9},{9,1},{17,25},{25,17},{2,10},{10... | collective-permute-start | bytes 36872 | tf_op jit(solution)/shard_map/ppermute | solution.py:561
  10.1 0.5 %collective-permute-start.5 = (f32[3,8,128]{2,1,0:T(8,128)S(1)}, f32[3,8,128]{2,1,0:T(8,128)S(1)}, u32[]{:S(2)}, u32[]{:S(2)}) collective-permute-start(f32[3,8,128]{2,1,0:T(8,128)S(1)} %get-tuple-element.57), channel_id=1, source_target_pairs={{8,16},{16,8},{24,0},{0,24},{9,17},{17,9},{25,1},{1,25},{10,18},{1... | collective-permute-start | bytes 36872 | tf_op jit(solution)/shard_map/ppermute | solution.py:561
  10.6 1.3 %shard_map.77.refs_9_.inner = f32[6,72,768]{2,1,0:T(8,128)S(1)} custom-call(f32[72,768]{1,0:T(8,128)S(1)} %get-tuple-element.46.edge_a.refs_1_, f32[72,768]{1,0:T(8,128)S(1)} %get-tuple-element.54.edge_b.refs_1_, f32[6,72,768]{2,1,0:T(8,128)S(1)} %get-tuple-element.47.inner.refs_2_, f32[8,72,128]{2,1,0:T(8,128)S(1)} %get-tuple-element.48.seas.refs_3_, ...), custom_call_target="tpu_custom_call" | custom-call | flops 268435456 | tf_op jit(solution)/shard_map/pallas_call | solution.py:514
  11.9 0.0 collective-permute-done.6.refs_0_
  12.0 2.8 %collective-permute-done.5.corner = f32[3,8,128]{2,1,0:T(8,128)S(1)} collective-permute-done((f32[3,8,128]{2,1,0:T(8,128)S(1)}, f32[3,8,128]{2,1,0:T(8,128)S(1)}, u32[]{:S(2)}, u32[]{:S(2)}) %collective-permute-start.5) | collective-permute-done | bytes 12320 | tf_op jit(solution)/shard_map/ppermute | solution.py:561
  14.7 0.5 %shard_map.79 = (f32[72,768]{1,0:T(8,128)S(1)}, f32[23,8,128]{2,1,0:T(8,128)S(1)}) custom-call(f32[3,8,128]{2,1,0:T(8,128)S(1)} %collective-permute-done.5.corner, f32[21,8,128]{2,1,0:T(8,128)S(1)} %collective-permute-done.6.refs_0_, f32[72,768]{1,0:T(8,128)S(1)} %get-tuple-element.54.edge_b.refs_1_, f32[6,72,768]{2,1,0:T(8,128)S(1)} %get-tuple-element.47.inner.refs_2_, ...), custom_call_target="tpu_custom_call" | custom-call | flops 67108864 | tf_op jit(solution)/shard_map/pallas_call | solution.py:514
  15.3 0.6 %collective-permute-start.8 = (f32[23,8,128]{2,1,0:T(8,128)S(1)}, f32[23,8,128]{2,1,0:T(8,128)S(1)}, u32[]{:S(2)}, u32[]{:S(2)}) collective-permute-start(f32[23,8,128]{2,1,0:T(8,128)S(1)} %get-tuple-element.62), channel_id=1, source_target_pairs={{8,16},{16,8},{24,0},{0,24},{9,17},{17,9},{25,1},{1,25},{10,18},{1... | collective-permute-start | bytes 282632 | tf_op jit(solution)/shard_map/ppermute | solution.py:558
  15.9 0.0 collective-permute-done.3.refs_0_
  15.9 0.0 collective-permute-done.2.corner
  15.9 0.6 %shard_map.78 = (f32[72,768]{1,0:T(8,128)S(1)}, f32[23,8,128]{2,1,0:T(8,128)S(1)}) custom-call(f32[3,8,128]{2,1,0:T(8,128)S(1)} %collective-permute-done.2.corner, f32[21,8,128]{2,1,0:T(8,128)S(1)} %collective-permute-done.3.refs_0_, f32[72,768]{1,0:T(8,128)S(1)} %get-tuple-element.46.edge_a.refs_1_, f32[6,72,768]{2,1,0:T(8,128)S(1)} %get-tuple-element.47.inner.refs_2_, ...), custom_call_target="tpu_custom_call" | custom-call | flops 67108864 | tf_op jit(solution)/shard_map/pallas_call | solution.py:514
  16.5 1.5 %collective-permute-start.4 = (f32[23,8,128]{2,1,0:T(8,128)S(1)}, f32[23,8,128]{2,1,0:T(8,128)S(1)}, u32[]{:S(2)}, u32[]{:S(2)}) collective-permute-start(f32[23,8,128]{2,1,0:T(8,128)S(1)} %get-tuple-element.55), channel_id=1, source_target_pairs={{0,8},{8,0},{16,24},{24,16},{1,9},{9,1},{17,25},{25,17},{2,10},{10... | collective-permute-start | bytes 282632 | tf_op jit(solution)/shard_map/ppermute | solution.py:559
  17.9 1.3 %shard_map.80.after.inner = f32[6,72,768]{2,1,0:T(8,128)S(1)} custom-call(f32[72,768]{1,0:T(8,128)S(1)} %get-tuple-element.56.edge_a.edge, f32[72,768]{1,0:T(8,128)S(1)} %get-tuple-element.59.edge_b.edge, f32[6,72,768]{2,1,0:T(8,128)S(1)} %shard_map.77.refs_9_.inner, f32[8,72,128]{2,1,0:T(8,128)S(1)} %get-tuple-element.48.seas.refs_3_, ...), custom_call_target="tpu_custom_call" | custom-call | flops 268435456 | tf_op jit(solution)/shard_map/pallas_call | solution.py:514
  19.2 1.9 %collective-permute-done.8.halo = f32[23,8,128]{2,1,0:T(8,128)S(1)} collective-permute-done((f32[23,8,128]{2,1,0:T(8,128)S(1)}, f32[23,8,128]{2,1,0:T(8,128)S(1)}, u32[]{:S(2)}, u32[]{:S(2)}) %collective-permute-start.8) | collective-permute-done | bytes 94240 | tf_op jit(solution)/shard_map/ppermute | solution.py:558
  21.1 0.5 %shard_map.82 = (f32[72,768]{1,0:T(8,128)S(1)}, f32[23,8,128]{2,1,0:T(8,128)S(1)}) custom-call(f32[23,8,128]{2,1,0:T(8,128)S(1)} %collective-permute-done.8.halo, f32[72,768]{1,0:T(8,128)S(1)} %get-tuple-element.59.edge_b.edge, f32[6,72,768]{2,1,0:T(8,128)S(1)} %shard_map.77.refs_9_.inner, f32[8,72,128]{2,1,0:T(8,128)S(1)} %get-tuple-element.48.seas.refs_3_, ...), custom_call_target="tpu_custom_call" | custom-call | flops 67108864 | tf_op jit(solution)/shard_map/pallas_call | solution.py:514
  21.6 0.3 collective-permute-start.10
  22.0 0.1 collective-permute-done.4.halo
  22.1 0.6 %shard_map.81 = (f32[72,768]{1,0:T(8,128)S(1)}, f32[23,8,128]{2,1,0:T(8,128)S(1)}) custom-call(f32[23,8,128]{2,1,0:T(8,128)S(1)} %collective-permute-done.4.halo, f32[72,768]{1,0:T(8,128)S(1)} %get-tuple-element.56.edge_a.edge, f32[6,72,768]{2,1,0:T(8,128)S(1)} %shard_map.77.refs_9_.inner, f32[8,72,128]{2,1,0:T(8,128)S(1)} %get-tuple-element.48.seas.refs_3_, ...), custom_call_target="tpu_custom_call" | custom-call | flops 67108864 | tf_op jit(solution)/shard_map/pallas_call | solution.py:514
  22.7 1.5 %collective-permute-start.7 = (f32[23,8,128]{2,1,0:T(8,128)S(1)}, f32[23,8,128]{2,1,0:T(8,128)S(1)}, u32[]{:S(2)}, u32[]{:S(2)}) collective-permute-start(f32[23,8,128]{2,1,0:T(8,128)S(1)} %get-tuple-element.60), channel_id=1, source_target_pairs={{0,8},{8,0},{16,24},{24,16},{1,9},{9,1},{17,25},{25,17},{2,10},{10... | collective-permute-start | bytes 282632 | tf_op jit(solution)/shard_map/ppermute | solution.py:559
  24.3 1.3 %shard_map.83.after.inner = f32[6,72,768]{2,1,0:T(8,128)S(1)} custom-call(f32[72,768]{1,0:T(8,128)S(1)} %get-tuple-element.61.edge_a.edge, f32[72,768]{1,0:T(8,128)S(1)} %get-tuple-element.63.edge_b.edge, f32[6,72,768]{2,1,0:T(8,128)S(1)} %shard_map.80.after.inner, f32[8,72,128]{2,1,0:T(8,128)S(1)} %get-tuple-element.48.seas.refs_3_, ...), custom_call_target="tpu_custom_call" | custom-call | flops 268435456 | tf_op jit(solution)/shard_map/pallas_call | solution.py:514
  25.6 2.4 %collective-permute-done.10.halo = f32[23,8,128]{2,1,0:T(8,128)S(1)} collective-permute-done((f32[23,8,128]{2,1,0:T(8,128)S(1)}, f32[23,8,128]{2,1,0:T(8,128)S(1)}, u32[]{:S(2)}, u32[]{:S(2)}) %collective-permute-start.10) | collective-permute-done | bytes 94240 | tf_op jit(solution)/shard_map/ppermute | solution.py:558
  28.0 0.5 %shard_map.85 = (f32[72,768]{1,0:T(8,128)S(1)}, f32[21,8,128]{2,1,0:T(8,128)S(1)}) custom-call(f32[23,8,128]{2,1,0:T(8,128)S(1)} %collective-permute-done.10.halo, f32[72,768]{1,0:T(8,128)S(1)} %get-tuple-element.63.edge_b.edge, f32[6,72,768]{2,1,0:T(8,128)S(1)} %shard_map.80.after.inner, f32[8,72,128]{2,1,0:T(8,128)S(1)} %get-tuple-element.48.seas.refs_3_, ...), custom_call_target="tpu_custom_call" | custom-call | flops 67108864 | tf_op jit(solution)/shard_map/pallas_call | solution.py:514
  28.5 0.3 collective-permute-start.11
  28.8 0.0 collective-permute-done.7.halo
  28.9 0.6 %shard_map.84 = (f32[72,768]{1,0:T(8,128)S(1)}, f32[21,8,128]{2,1,0:T(8,128)S(1)}) custom-call(f32[23,8,128]{2,1,0:T(8,128)S(1)} %collective-permute-done.7.halo, f32[72,768]{1,0:T(8,128)S(1)} %get-tuple-element.61.edge_a.edge, f32[6,72,768]{2,1,0:T(8,128)S(1)} %shard_map.80.after.inner, f32[8,72,128]{2,1,0:T(8,128)S(1)} %get-tuple-element.48.seas.refs_3_, ...), custom_call_target="tpu_custom_call" | custom-call | flops 67108864 | tf_op jit(solution)/shard_map/pallas_call | solution.py:514
  29.4 1.6 %collective-permute-start.9 = (f32[21,8,128]{2,1,0:T(8,128)S(1)}, f32[21,8,128]{2,1,0:T(8,128)S(1)}, u32[]{:S(2)}, u32[]{:S(2)}) collective-permute-start(f32[21,8,128]{2,1,0:T(8,128)S(1)} %get-tuple-element.64), channel_id=1, source_target_pairs={{0,8},{8,0},{16,24},{24,16},{1,9},{9,1},{17,25},{25,17},{2,10},{10... | collective-permute-start | bytes 258056 | tf_op jit(solution)/shard_map/ppermute | solution.py:559
  31.0 1.2 %shard_map.86.after.done_inner = f32[6,64,648]{2,1,0:T(8,128)S(1)} custom-call(f32[72,768]{1,0:T(8,128)S(1)} %get-tuple-element.65.edge_a.edge, f32[72,768]{1,0:T(8,128)S(1)} %get-tuple-element.67.edge_b.edge, f32[6,72,768]{2,1,0:T(8,128)S(1)} %shard_map.83.after.inner, f32[8,72,128]{2,1,0:T(8,128)S(1)} %get-tuple-element.48.seas.refs_3_, ...), custom_call_target="tpu_custom_call" | custom-call | flops 268435456 | tf_op jit(solution)/shard_map/pallas_call | solution.py:514
  32.2 1.8 %collective-permute-done.11.halo = f32[21,8,128]{2,1,0:T(8,128)S(1)} collective-permute-done((f32[21,8,128]{2,1,0:T(8,128)S(1)}, f32[21,8,128]{2,1,0:T(8,128)S(1)}, u32[]{:S(2)}, u32[]{:S(2)}) %collective-permute-start.11) | collective-permute-done | bytes 86048 | tf_op jit(solution)/shard_map/ppermute | solution.py:558
  34.0 0.5 %shard_map.87.done_edge = f32[64,648]{1,0:T(8,128)S(1)} custom-call(f32[21,8,128]{2,1,0:T(8,128)S(1)} %collective-permute-done.11.halo, f32[72,768]{1,0:T(8,128)S(1)} %get-tuple-element.67.edge_b.edge, f32[6,72,768]{2,1,0:T(8,128)S(1)} %shard_map.83.after.inner, f32[8,72,128]{2,1,0:T(8,128)S(1)} %get-tuple-element.48.seas.refs_3_, ...), custom_call_target="tpu_custom_call" | custom-call | flops 67108864 | tf_op jit(solution)/shard_map/pallas_call | solution.py:514
  34.5 0.0 collective-permute-done.9.halo
  34.5 1.2 %shard_map.88 = f32[8,64,648]{2,1,0:T(8,128)} custom-call(f32[21,8,128]{2,1,0:T(8,128)S(1)} %collective-permute-done.9.halo, f32[72,768]{1,0:T(8,128)S(1)} %get-tuple-element.65.edge_a.edge, f32[6,72,768]{2,1,0:T(8,128)S(1)} %shard_map.83.after.inner, f32[8,72,128]{2,1,0:T(8,128)S(1)} %get-tuple-element.48.seas.refs_3_, ...), custom_call_target="tpu_custom_call" | custom-call | flops 67108864 | tf_op jit(solution)/shard_map/pallas_call | solution.py:514
  (6 shorter events, 0.0 us)
Async XLA Ops:
  0.0 3.8 %copy-start.5 = (f32[8,64]{1,0:T(8,128)S(1)}, f32[8,64]{1,0:T(8,128)}, u32[]{:S(2)}) copy-start(f32[8,64]{1,0:T(8,128)} %wind_ref.1) | copy-start | bytes 6148
  0.0 3.8 %copy-start.4 = (s32[8,64]{1,0:T(8,128)S(1)}, s32[8,64]{1,0:T(8,128)}, u32[]{:S(2)}) copy-start(s32[8,64]{1,0:T(8,128)} %ice_ref.1) | copy-start | bytes 6148
  0.0 3.9 %copy-start.3 = (s32[8,64]{1,0:T(8,128)S(1)}, s32[8,64]{1,0:T(8,128)}, u32[]{:S(2)}) copy-start(s32[8,64]{1,0:T(8,128)} %sea_ref.1) | copy-start | bytes 6148
  0.0 3.9 %copy-start = (f32[8,64,648]{2,1,0:T(8,128)S(1)}, f32[8,64,648]{2,1,0:T(8,128)}, u32[]{:S(2)}) copy-start(f32[8,64,648]{2,1,0:T(8,128)} %spectrum.3) | copy-start | bytes 3981316
  0.0 7.6 %copy-start.2 = (f32[8,768]{1,0:T(8,128)S(1)}, f32[8,768]{1,0:T(8,128)}, u32[]{:S(2)}) copy-start(f32[8,768]{1,0:T(8,128)} %constant.2.clone.angle_ref) | copy-start | bytes 73732
  0.0 7.6 %copy-start.1 = (bf16[648,648]{1,0:T(8,128)(2,1)S(1)}, bf16[648,648]{1,0:T(8,128)(2,1)}, u32[]{:S(2)}) copy-start(bf16[648,648]{1,0:T(8,128)(2,1)} %coupling_ref.1) | copy-start | bytes 2519428
  0.0 7.6 %copy-start.6 = (f32[18]{0:T(128)S(1)}, f32[18]{0:T(128)}, u32[]{:S(2)}) copy-start(f32[18]{0:T(128)} %speed_ref.1) | copy-start | bytes 220
  1.3 7.1 %collective-permute-start = (f32[4,8,768]{2,1,0:T(8,128)S(1)}, f32[4,8,768]{2,1,0:T(8,128)S(1)}, u32[]{:S(2)}, u32[]{:S(2)}) collective-permute-start(f32[4,8,768]{2,1,0:T(8,128)S(1)} %get-tuple-element.37), channel_id=1, source_target_pairs={{0,1},{1,0},{2,3},{3,2},{4,5},{5,4},{6,7},{7,6},{8,9},{9,8},{10,11... | collective-permute-start | bytes 294920 | tf_op jit(solution)/shard_map/ppermute | solution.py:534
  1.4 7.1 %collective-permute-start.1 = (f32[4,8,768]{2,1,0:T(8,128)S(1)}, f32[4,8,768]{2,1,0:T(8,128)S(1)}, u32[]{:S(2)}, u32[]{:S(2)}) collective-permute-start(f32[4,8,768]{2,1,0:T(8,128)S(1)} %get-tuple-element.38), channel_id=1, source_target_pairs={{1,2},{2,1},{3,4},{4,3},{5,6},{6,5},{9,10},{10,9},{11,12},{12,11},... | collective-permute-start | bytes 294920 | tf_op jit(solution)/shard_map/ppermute | solution.py:533
  4.6 7.4 %collective-permute-start.6 = (f32[21,8,128]{2,1,0:T(8,128)S(1)}, f32[21,8,128]{2,1,0:T(8,128)S(1)}, u32[]{:S(2)}, u32[]{:S(2)}) collective-permute-start(f32[21,8,128]{2,1,0:T(8,128)S(1)} %get-tuple-element.58), channel_id=1, source_target_pairs={{8,16},{16,8},{24,0},{0,24},{9,17},{17,9},{25,1},{1,25},{10,18},{1... | collective-permute-start | bytes 258056 | tf_op jit(solution)/shard_map/ppermute | solution.py:558
  7.1 8.8 %collective-permute-start.3 = (f32[21,8,128]{2,1,0:T(8,128)S(1)}, f32[21,8,128]{2,1,0:T(8,128)S(1)}, u32[]{:S(2)}, u32[]{:S(2)}) collective-permute-start(f32[21,8,128]{2,1,0:T(8,128)S(1)} %get-tuple-element.45), channel_id=1, source_target_pairs={{0,8},{8,0},{16,24},{24,16},{1,9},{9,1},{17,25},{25,17},{2,10},{10... | collective-permute-start | bytes 258056 | tf_op jit(solution)/shard_map/ppermute | solution.py:559
  8.6 7.2 %collective-permute-start.2 = (f32[3,8,128]{2,1,0:T(8,128)S(1)}, f32[3,8,128]{2,1,0:T(8,128)S(1)}, u32[]{:S(2)}, u32[]{:S(2)}) collective-permute-start(f32[3,8,128]{2,1,0:T(8,128)S(1)} %get-tuple-element.44), channel_id=1, source_target_pairs={{0,8},{8,0},{16,24},{24,16},{1,9},{9,1},{17,25},{25,17},{2,10},{10... | collective-permute-start | bytes 36872 | tf_op jit(solution)/shard_map/ppermute | solution.py:561
  10.1 4.6 %collective-permute-start.5 = (f32[3,8,128]{2,1,0:T(8,128)S(1)}, f32[3,8,128]{2,1,0:T(8,128)S(1)}, u32[]{:S(2)}, u32[]{:S(2)}) collective-permute-start(f32[3,8,128]{2,1,0:T(8,128)S(1)} %get-tuple-element.57), channel_id=1, source_target_pairs={{8,16},{16,8},{24,0},{0,24},{9,17},{17,9},{25,1},{1,25},{10,18},{1... | collective-permute-start | bytes 36872 | tf_op jit(solution)/shard_map/ppermute | solution.py:561
  15.3 5.9 %collective-permute-start.8 = (f32[23,8,128]{2,1,0:T(8,128)S(1)}, f32[23,8,128]{2,1,0:T(8,128)S(1)}, u32[]{:S(2)}, u32[]{:S(2)}) collective-permute-start(f32[23,8,128]{2,1,0:T(8,128)S(1)} %get-tuple-element.62), channel_id=1, source_target_pairs={{8,16},{16,8},{24,0},{0,24},{9,17},{17,9},{25,1},{1,25},{10,18},{1... | collective-permute-start | bytes 282632 | tf_op jit(solution)/shard_map/ppermute | solution.py:558
  16.5 5.7 %collective-permute-start.4 = (f32[23,8,128]{2,1,0:T(8,128)S(1)}, f32[23,8,128]{2,1,0:T(8,128)S(1)}, u32[]{:S(2)}, u32[]{:S(2)}) collective-permute-start(f32[23,8,128]{2,1,0:T(8,128)S(1)} %get-tuple-element.55), channel_id=1, source_target_pairs={{0,8},{8,0},{16,24},{24,16},{1,9},{9,1},{17,25},{25,17},{2,10},{10... | collective-permute-start | bytes 282632 | tf_op jit(solution)/shard_map/ppermute | solution.py:559
  21.6 6.4 %collective-permute-start.10 = (f32[23,8,128]{2,1,0:T(8,128)S(1)}, f32[23,8,128]{2,1,0:T(8,128)S(1)}, u32[]{:S(2)}, u32[]{:S(2)}) collective-permute-start(f32[23,8,128]{2,1,0:T(8,128)S(1)} %get-tuple-element.66), channel_id=1, source_target_pairs={{8,16},{16,8},{24,0},{0,24},{9,17},{17,9},{25,1},{1,25},{10,18},{1... | collective-permute-start | bytes 282632 | tf_op jit(solution)/shard_map/ppermute | solution.py:558
  22.7 6.2 %collective-permute-start.7 = (f32[23,8,128]{2,1,0:T(8,128)S(1)}, f32[23,8,128]{2,1,0:T(8,128)S(1)}, u32[]{:S(2)}, u32[]{:S(2)}) collective-permute-start(f32[23,8,128]{2,1,0:T(8,128)S(1)} %get-tuple-element.60), channel_id=1, source_target_pairs={{0,8},{8,0},{16,24},{24,16},{1,9},{9,1},{17,25},{25,17},{2,10},{10... | collective-permute-start | bytes 282632 | tf_op jit(solution)/shard_map/ppermute | solution.py:559
  28.5 5.4 %collective-permute-start.11 = (f32[21,8,128]{2,1,0:T(8,128)S(1)}, f32[21,8,128]{2,1,0:T(8,128)S(1)}, u32[]{:S(2)}, u32[]{:S(2)}) collective-permute-start(f32[21,8,128]{2,1,0:T(8,128)S(1)} %get-tuple-element.68), channel_id=1, source_target_pairs={{8,16},{16,8},{24,0},{0,24},{9,17},{17,9},{25,1},{1,25},{10,18},{1... | collective-permute-start | bytes 258056 | tf_op jit(solution)/shard_map/ppermute | solution.py:558
  29.4 5.1 %collective-permute-start.9 = (f32[21,8,128]{2,1,0:T(8,128)S(1)}, f32[21,8,128]{2,1,0:T(8,128)S(1)}, u32[]{:S(2)}, u32[]{:S(2)}) collective-permute-start(f32[21,8,128]{2,1,0:T(8,128)S(1)} %get-tuple-element.64), channel_id=1, source_target_pairs={{0,8},{8,0},{16,24},{24,16},{1,9},{9,1},{17,25},{25,17},{2,10},{10... | collective-permute-start | bytes 258056 | tf_op jit(solution)/shard_map/ppermute | solution.py:559

commit v5 on v4

--- a/solution.py
+++ b/solution.py
@@ -142,6 +142,17 @@
             out[2 * blocks + half + 1] = full
             out[2 * blocks + half + 2] = other
     out[2 * blocks + half] = left
+
+
+def pack_corner(parts, before, west, bins, rows, out):
+    _, _, width, kept, start = pack_plan(bins, west)
+    rest = width - kept
+    half = rows // 16
+    spot = 5 * half
+    lane = lane_index((8, LANES))
+    out[spot] = jnp.where(lane >= half * rest, turn(parts[2], half * rest - start), before[spot])
+    out[spot + 1] = parts[0]
+    out[spot + 2] = parts[1]
 
 
 def across_edge(halo, inner, west, bins, rows, with_halo, corner=None):
@@ -337,8 +348,8 @@
 
 
 def join_kernel(
-    bins, halo_a, halo_b, edge_a_in, edge_b_in, inner_in, seas_in, gains_in,
-    edge_a, edge_b, inner, seas, gains, pack_a, pack_b,
+    bins, halo_a, halo_b, edge_a_in, edge_b_in, inner_in, seas_in, gains_in, pack_in,
+    edge_a, edge_b, inner, seas, gains, pack_a, corner_b,
 ):
     columns = seas.shape[0]
     rows = seas.shape[1] - 2 * DEPTH
@@ -368,13 +379,18 @@
     for tile in range(tiles):
         for c in range(1, columns - 1):
             inner[c - 1, rows:, lanes_of(tile)] = values[c][tile]
-    for second, target, pack in ((False, edge_a, pack_a), (True, edge_b, pack_b)):
-
-        def side(west, target=target, pack=pack):
+    for second, target in ((False, edge_a), (True, edge_b)):
+
+        def side(west, second=second, target=target):
+            mine = values[0 if west else columns - 1]
             for tile in range(tiles):
-                target[rows:, lanes_of(tile)] = values[0 if west else columns - 1][tile]
-            for k, value in enumerate(half_parts(values[0 if west else columns - 1], west, bins)):
-                pack[k] = value
+                target[rows:, lanes_of(tile)] = mine[tile]
+            parts = half_parts(mine, west, bins)
+            if second:
+                for k, value in enumerate(parts):
+                    corner_b[k] = value
+            else:
+                pack_corner(parts, pack_in, west, bins, rows, pack_a)
 
         on_each_side(second, side)
 
@@ -532,11 +548,12 @@
     )
     halo_b = lax.ppermute(send_b, "lat", lat_b)
     halo_a = lax.ppermute(send_a, "lat", lat_a)
-    pack_shape = VMEM((pack_count(rows, False), 8, LANES), f32)
+    pack_own = VMEM((pack_count(rows, False), 8, LANES), f32)
+    pack_shape = VMEM((pack_count(rows, True), 8, LANES), f32)
     corner_shape = VMEM((3, 8, LANES), f32)
     edge_a, edge_b, inner, seas, gains, pack_a, pack_b = call(
         functools.partial(load_kernel, bins),
-        (edge_shape, edge_shape, inner_shape, mask_shape, mask_shape, pack_shape, pack_shape),
+        (edge_shape, edge_shape, inner_shape, mask_shape, mask_shape, pack_shape, pack_own),
         (spectrum, sea_mask, ice_flags, wind_forcing), [vmem] * 4, flops=1 << 24,
     )
     stay, go_x, go_y, wide = call(
@@ -545,12 +562,12 @@
         (group_speed, jnp.asarray(angle_table(bins, group_speed.shape[0])), coupling),
         [smem, vmem, vmem], flops=1 << 24,
     )
-    edge_a, edge_b, inner, seas, gains, corner_a, corner_b = call(
+    edge_a, edge_b, inner, seas, gains, pack_a, corner_b = call(
         functools.partial(join_kernel, bins),
-        (edge_shape, edge_shape, inner_shape, mask_shape, mask_shape, corner_shape, corner_shape),
-        (halo_a, halo_b, edge_a, edge_b, inner, seas, gains),
-        [vmem] * 7,
-        aliases={2: 0, 3: 1, 4: 2, 5: 3, 6: 4},
+        (edge_shape, edge_shape, inner_shape, mask_shape, mask_shape, pack_shape, corner_shape),
+        (halo_a, halo_b, edge_a, edge_b, inner, seas, gains, pack_a),
+        [vmem] * 8,
+        aliases={2: 0, 3: 1, 4: 2, 5: 3, 6: 4, 7: 5},
     )
     tables = (seas, gains, stay, go_x, go_y, wide)
     for step in range(STEPS):
@@ -558,7 +575,7 @@
         halo_b = lax.ppermute(pack_b, "lon", lon_b)
         halo_a = lax.ppermute(pack_a, "lon", lon_a)
         if step == 0:
-            corners = (lax.ppermute(corner_a, "lon", lon_a), lax.ppermute(corner_b, "lon", lon_b))
+            corner = lax.ppermute(corner_b, "lon", lon_b)
         used = rows if last else tall
         new_inner = call(
             functools.partial(inner_kernel, bins), VMEM((columns - 2, rows, bins), f32) if last else inner_shape,
@@ -582,8 +599,8 @@
         pack_next = VMEM((pack_count(rows, step < STEPS - 2), 8, LANES), f32)
         for second, halo, edge in ((False, halo_a, edge_a), (True, halo_b, edge_b)):
             body, ins = edge_kernel, (halo, edge, inner) + tables + (new_inner,)
-            if step == 0:
-                body, ins = first_edge_kernel, (corners[second],) + ins
+            if step == 0 and second:
+                body, ins = first_edge_kernel, (corner,) + ins
             fresh.append(call(
                 functools.partial(body, bins, second), (edge_shape, pack_next),
                 ins, [vmem] * len(ins), [VMEM((tall, padded), f32)], flops=1 << 26,

time: 36.4 us -> 37.5 us (1.030); the launches traced: 35.7 us -> 37.3 us
  starting transfers between devices: 13.3 us -> 15.1 us
    ppermute x1, waiting for transfers between devices: 0.01 us -> 2.74 us  [steps(): halo_b = lax.ppermute(send_b, 'lat', lat_b)]
    ppermute x4, starting transfers between devices: 3.73 us -> 6.17 us  [steps(): halo_b = lax.ppermute(pack_b, 'lon', lon_b)]
    ppermute x4, waiting for transfers between devices: 6.1 us -> 3.92 us  [steps(): halo_b = lax.ppermute(pack_b, 'lon', lon_b)]
    ppermute x2 -> x1, waiting for transfers between devices: 2.77 us -> 1.63 us  [steps(): corner = lax.ppermute(corner_b, 'lon', lon_b)]
    ppermute x2 -> x1, starting transfers between devices: 1.98 us -> 1.45 us  [steps(): corner = lax.ppermute(corner_b, 'lon', lon_b)]
    ppermute x4, waiting for transfers between devices: 0.18 us -> 0.69 us  [steps(): halo_a = lax.ppermute(pack_a, 'lon', lon_a)]
  transfers between devices with their start and end apart: 12 -> 11, of which waited for: 5 -> 7; matrix products, arithmetic and copies ran while one was open for 0% -> 0% of each run, Pallas kernels for 30% -> 28%
where the time goes in v5:
time: 37.5 us; the launch traced here: 37.3 us
  starting transfers between devices  15.1 us (40%)
  Pallas kernels  13 us (35%)
  waiting for transfers between devices  8.99 us (24%)
    pallas_call x16, Pallas kernels, call(): pl.pallas_call(body, out_shape=outs, in_specs=specs, out_specs=out_specs...  13 us
    ppermute x4, starting transfers between devices, steps(): halo_b = lax.ppermute(pack_b, 'lon', lon_b)  6.17 us
    ppermute x4, starting transfers between devices, steps(): halo_a = lax.ppermute(pack_a, 'lon', lon_a)  4.96 us
    ppermute x4, waiting for transfers between devices, steps(): halo_b = lax.ppermute(pack_b, 'lon', lon_b)  3.92 us
    ppermute x1, waiting for transfers between devices, steps(): halo_b = lax.ppermute(send_b, 'lat', lat_b)  2.74 us
    ppermute x1, starting transfers between devices, steps(): halo_b = lax.ppermute(send_b, 'lat', lat_b)  2.45 us
    ppermute x1, waiting for transfers between devices, steps(): corner = lax.ppermute(corner_b, 'lon', lon_b)  1.63 us
    ppermute x1, starting transfers between devices, steps(): corner = lax.ppermute(corner_b, 'lon', lon_b)  1.45 us
  transfers between devices with their start and end apart: 11, of which 7 were waited for; matrix products, arithmetic and copies ran while one was open for 0% of the time, Pallas kernels for 28%

profile of v5, /device:TPU:24, one launch (start us, length us, event | category | flops | bytes accessed | tf_op | source)
XLA Modules:
  0.0 37.3 jit_solution(10405686979386174358)
XLA Ops:
  0.0 0.0 copy-start.5
  0.0 0.0 copy-start
  0.0 0.0 copy-start.4
  0.0 1.2 %shard_map.73 = (f32[4,8,768]{2,1,0:T(8,128)S(1)}, f32[4,8,768]{2,1,0:T(8,128)S(1)}) custom-call(f32[8,64,648]{2,1,0:T(8,128)} %spectrum.3, s32[8,64]{1,0:T(8,128)} %sea_ref.1, s32[8,64]{1,0:T(8,128)} %ice_ref.1, f32[8,64]{1,0:T(8,128)} %wind_ref.1), custom_call_target="tpu_custom_call" | custom-call | tf_op jit(solution)/shard_map/pallas_call | solution.py:530
  1.2 0.1 collective-permute-start
  1.3 2.4 %collective-permute-start.1 = (f32[4,8,768]{2,1,0:T(8,128)S(1)}, f32[4,8,768]{2,1,0:T(8,128)S(1)}, u32[]{:S(2)}, u32[]{:S(2)}) collective-permute-start(f32[4,8,768]{2,1,0:T(8,128)S(1)} %get-tuple-element.38), channel_id=1, source_target_pairs={{1,2},{2,1},{3,4},{4,3},{5,6},{6,5},{9,10},{10,9},{11,12},{12,11},... | collective-permute-start | bytes 294920 | tf_op jit(solution)/shard_map/ppermute | solution.py:549
  3.8 0.0 copy-done.5
  3.8 0.0 copy-done
  3.8 0.0 copy-done.3
  3.8 0.0 copy-done.4
  3.8 0.7 %shard_map.74 = (f32[72,768]{1,0:T(8,128)S(1)}, f32[72,768]{1,0:T(8,128)S(1)}, f32[6,72,768]{2,1,0:T(8,128)S(1)}, f32[8,72,128]{2,1,0:T(8,128)S(1)}, f32[8,72,12...) custom-call(f32[8,64,648]{2,1,0:T(8,128)S(1)} %copy-done, s32[8,64]{1,0:T(8,128)S(1)} %copy-done.3, ...), custom_call_target="tpu_custom_call" | custom-call | flops 16777216 | tf_op jit(solution)/shard_map/pallas_call | solution.py:530
  4.5 0.0 collective-permute-done.halo_a
  4.5 2.7 %collective-permute-done.1.halo_b = f32[4,8,768]{2,1,0:T(8,128)S(1)} collective-permute-done((f32[4,8,768]{2,1,0:T(8,128)S(1)}, f32[4,8,768]{2,1,0:T(8,128)S(1)}, u32[]{:S(2)}, u32[]{:S(2)}) %collective-permute-start.1) | collective-permute-done | bytes 98336 | tf_op jit(solution)/shard_map/ppermute | solution.py:549
  7.3 0.2 shard_map.75
  7.5 1.4 %collective-permute-start.2 = (f32[23,8,128]{2,1,0:T(8,128)S(1)}, f32[23,8,128]{2,1,0:T(8,128)S(1)}, u32[]{:S(2)}, u32[]{:S(2)}) collective-permute-start(f32[23,8,128]{2,1,0:T(8,128)S(1)} %get-tuple-element.45), channel_id=1, source_target_pairs={{0,8},{8,0},{16,24},{24,16},{1,9},{9,1},{17,25},{25,17},{2,10},{10... | collective-permute-start | bytes 282632 | tf_op jit(solution)/shard_map/ppermute | solution.py:576
  8.9 1.5 %collective-permute-start.5 = (f32[21,8,128]{2,1,0:T(8,128)S(1)}, f32[21,8,128]{2,1,0:T(8,128)S(1)}, u32[]{:S(2)}, u32[]{:S(2)}) collective-permute-start(f32[21,8,128]{2,1,0:T(8,128)S(1)} %get-tuple-element.58), channel_id=1, source_target_pairs={{8,16},{16,8},{24,0},{0,24},{9,17},{17,9},{25,1},{1,25},{10,18},{1... | collective-permute-start | bytes 258056 | tf_op jit(solution)/shard_map/ppermute | solution.py:575
  10.5 0.0 copy-done.1
  10.5 0.0 copy-done.2
  10.5 0.0 copy-done.6
  10.5 0.8 %shard_map.76 = (f32[72,768]{1,0:T(8,128)S(1)}, f32[72,768]{1,0:T(8,128)S(1)}, f32[8,768]{1,0:T(8,128)S(1)}, bf16[768,768]{1,0:T(8,128)(2,1)S(1)}) custom-call(f32[18]{0:T(128)S(1)} %copy-done.6, f32[8,768]{1,0:T(8,128)S(1)} %copy-done.2, bf16[648,648]{1,0:T(8,128)(2,1)S(1)} %copy-done.1), custom_call_target="tpu_custom_call" | custom-call | flops 16777216 | tf_op jit(solution)/shard_map/pallas_call | solution.py:530
  11.3 1.4 %collective-permute-start.4 = (f32[3,8,128]{2,1,0:T(8,128)S(1)}, f32[3,8,128]{2,1,0:T(8,128)S(1)}, u32[]{:S(2)}, u32[]{:S(2)}) collective-permute-start(f32[3,8,128]{2,1,0:T(8,128)S(1)} %get-tuple-element.57), channel_id=1, source_target_pairs={{8,16},{16,8},{24,0},{0,24},{9,17},{17,9},{25,1},{1,25},{10,18},{1... | collective-permute-start | bytes 36872 | tf_op jit(solution)/shard_map/ppermute | solution.py:578
  12.8 1.3 %shard_map.77.after.refs_9_.inner = f32[6,72,768]{2,1,0:T(8,128)S(1)} custom-call(f32[72,768]{1,0:T(8,128)S(1)} %get-tuple-element.46.edge_a.edge, f32[72,768]{1,0:T(8,128)S(1)} %get-tuple-element.54.edge_b.refs_1_, f32[6,72,768]{2,1,0:T(8,128)S(1)} %get-tuple-element.47.inner.refs_2_, f32[8,72,128]{2,1,0:T(8,128)S(1)} %get-tuple-element.48.seas.refs_3_, ...), custom_call_target="tpu_custom_call" | custom-call | flops 268435456 | tf_op jit(solution)/shard_map/pallas_call | solution.py:530
  14.1 0.3 collective-permute-done.5.refs_0_
  14.3 1.6 %collective-permute-done.4.corner = f32[3,8,128]{2,1,0:T(8,128)S(1)} collective-permute-done((f32[3,8,128]{2,1,0:T(8,128)S(1)}, f32[3,8,128]{2,1,0:T(8,128)S(1)}, u32[]{:S(2)}, u32[]{:S(2)}) %collective-permute-start.4) | collective-permute-done | bytes 12320 | tf_op jit(solution)/shard_map/ppermute | solution.py:578
  16.0 0.5 %shard_map.79 = (f32[72,768]{1,0:T(8,128)S(1)}, f32[23,8,128]{2,1,0:T(8,128)S(1)}) custom-call(f32[3,8,128]{2,1,0:T(8,128)S(1)} %collective-permute-done.4.corner, f32[21,8,128]{2,1,0:T(8,128)S(1)} %collective-permute-done.5.refs_0_, f32[72,768]{1,0:T(8,128)S(1)} %get-tuple-element.54.edge_b.refs_1_, f32[6,72,768]{2,1,0:T(8,128)S(1)} %get-tuple-element.47.inner.refs_2_, ...), custom_call_target="tpu_custom_call" | custom-call | flops 67108864 | tf_op jit(solution)/shard_map/pallas_call | solution.py:530
  16.5 1.6 %collective-permute-start.7 = (f32[23,8,128]{2,1,0:T(8,128)S(1)}, f32[23,8,128]{2,1,0:T(8,128)S(1)}, u32[]{:S(2)}, u32[]{:S(2)}) collective-permute-start(f32[23,8,128]{2,1,0:T(8,128)S(1)} %get-tuple-element.62), channel_id=1, source_target_pairs={{8,16},{16,8},{24,0},{0,24},{9,17},{17,9},{25,1},{1,25},{10,18},{1... | collective-permute-start | bytes 282632 | tf_op jit(solution)/shard_map/ppermute | solution.py:575
  18.1 0.0 collective-permute-done.2.halo
  18.1 0.6 %shard_map.78 = (f32[72,768]{1,0:T(8,128)S(1)}, f32[23,8,128]{2,1,0:T(8,128)S(1)}) custom-call(f32[23,8,128]{2,1,0:T(8,128)S(1)} %collective-permute-done.2.halo, f32[72,768]{1,0:T(8,128)S(1)} %get-tuple-element.46.edge_a.edge, f32[6,72,768]{2,1,0:T(8,128)S(1)} %get-tuple-element.47.inner.refs_2_, f32[8,72,128]{2,1,0:T(8,128)S(1)} %get-tuple-element.48.seas.refs_3_, ...), custom_call_target="tpu_custom_call" | custom-call | flops 67108864 | tf_op jit(solution)/shard_map/pallas_call | solution.py:530
  18.7 1.0 %collective-permute-start.3 = (f32[23,8,128]{2,1,0:T(8,128)S(1)}, f32[23,8,128]{2,1,0:T(8,128)S(1)}, u32[]{:S(2)}, u32[]{:S(2)}) collective-permute-start(f32[23,8,128]{2,1,0:T(8,128)S(1)} %get-tuple-element.55), channel_id=1, source_target_pairs={{0,8},{8,0},{16,24},{24,16},{1,9},{9,1},{17,25},{25,17},{2,10},{10... | collective-permute-start | bytes 282632 | tf_op jit(solution)/shard_map/ppermute | solution.py:576
  19.7 1.3 %shard_map.80.after.inner = f32[6,72,768]{2,1,0:T(8,128)S(1)} custom-call(f32[72,768]{1,0:T(8,128)S(1)} %get-tuple-element.56.edge_a.edge, f32[72,768]{1,0:T(8,128)S(1)} %get-tuple-element.59.edge_b.edge, f32[6,72,768]{2,1,0:T(8,128)S(1)} %shard_map.77.after.refs_9_.inner, f32[8,72,128]{2,1,0:T(8,128)S(1)} %get-tuple-element.48.seas.refs_3_, ...), custom_call_target="tpu_custom_call" | custom-call | flops 268435456 | tf_op jit(solution)/shard_map/pallas_call | solution.py:530
  21.0 1.9 %collective-permute-done.7.halo = f32[23,8,128]{2,1,0:T(8,128)S(1)} collective-permute-done((f32[23,8,128]{2,1,0:T(8,128)S(1)}, f32[23,8,128]{2,1,0:T(8,128)S(1)}, u32[]{:S(2)}, u32[]{:S(2)}) %collective-permute-start.7) | collective-permute-done | bytes 94240 | tf_op jit(solution)/shard_map/ppermute | solution.py:575
  22.9 0.5 %shard_map.82 = (f32[72,768]{1,0:T(8,128)S(1)}, f32[23,8,128]{2,1,0:T(8,128)S(1)}) custom-call(f32[23,8,128]{2,1,0:T(8,128)S(1)} %collective-permute-done.7.halo, f32[72,768]{1,0:T(8,128)S(1)} %get-tuple-element.59.edge_b.edge, f32[6,72,768]{2,1,0:T(8,128)S(1)} %shard_map.77.after.refs_9_.inner, f32[8,72,128]{2,1,0:T(8,128)S(1)} %get-tuple-element.48.seas.refs_3_, ...), custom_call_target="tpu_custom_call" | custom-call | flops 67108864 | tf_op jit(solution)/shard_map/pallas_call | solution.py:530
  23.4 1.5 %collective-permute-start.9 = (f32[23,8,128]{2,1,0:T(8,128)S(1)}, f32[23,8,128]{2,1,0:T(8,128)S(1)}, u32[]{:S(2)}, u32[]{:S(2)}) collective-permute-start(f32[23,8,128]{2,1,0:T(8,128)S(1)} %get-tuple-element.66), channel_id=1, source_target_pairs={{8,16},{16,8},{24,0},{0,24},{9,17},{17,9},{25,1},{1,25},{10,18},{1... | collective-permute-start | bytes 282632 | tf_op jit(solution)/shard_map/ppermute | solution.py:575
  24.9 0.0 collective-permute-done.3.halo
  24.9 0.6 %shard_map.81 = (f32[72,768]{1,0:T(8,128)S(1)}, f32[23,8,128]{2,1,0:T(8,128)S(1)}) custom-call(f32[23,8,128]{2,1,0:T(8,128)S(1)} %collective-permute-done.3.halo, f32[72,768]{1,0:T(8,128)S(1)} %get-tuple-element.56.edge_a.edge, f32[6,72,768]{2,1,0:T(8,128)S(1)} %shard_map.77.after.refs_9_.inner, f32[8,72,128]{2,1,0:T(8,128)S(1)} %get-tuple-element.48.seas.refs_3_, ...), custom_call_target="tpu_custom_call" | custom-call | flops 67108864 | tf_op jit(solution)/shard_map/pallas_call | solution.py:530
  25.5 1.3 %collective-permute-start.6 = (f32[23,8,128]{2,1,0:T(8,128)S(1)}, f32[23,8,128]{2,1,0:T(8,128)S(1)}, u32[]{:S(2)}, u32[]{:S(2)}) collective-permute-start(f32[23,8,128]{2,1,0:T(8,128)S(1)} %get-tuple-element.60), channel_id=1, source_target_pairs={{0,8},{8,0},{16,24},{24,16},{1,9},{9,1},{17,25},{25,17},{2,10},{10... | collective-permute-start | bytes 282632 | tf_op jit(solution)/shard_map/ppermute | solution.py:576
  26.8 1.3 %shard_map.83.after.inner = f32[6,72,768]{2,1,0:T(8,128)S(1)} custom-call(f32[72,768]{1,0:T(8,128)S(1)} %get-tuple-element.61.edge_a.edge, f32[72,768]{1,0:T(8,128)S(1)} %get-tuple-element.63.edge_b.edge, f32[6,72,768]{2,1,0:T(8,128)S(1)} %shard_map.80.after.inner, f32[8,72,128]{2,1,0:T(8,128)S(1)} %get-tuple-element.48.seas.refs_3_, ...), custom_call_target="tpu_custom_call" | custom-call | flops 268435456 | tf_op jit(solution)/shard_map/pallas_call | solution.py:530
  28.1 0.9 %collective-permute-done.9.halo = f32[23,8,128]{2,1,0:T(8,128)S(1)} collective-permute-done((f32[23,8,128]{2,1,0:T(8,128)S(1)}, f32[23,8,128]{2,1,0:T(8,128)S(1)}, u32[]{:S(2)}, u32[]{:S(2)}) %collective-permute-start.9) | collective-permute-done | bytes 94240 | tf_op jit(solution)/shard_map/ppermute | solution.py:575
  29.0 0.5 %shard_map.85 = (f32[72,768]{1,0:T(8,128)S(1)}, f32[21,8,128]{2,1,0:T(8,128)S(1)}) custom-call(f32[23,8,128]{2,1,0:T(8,128)S(1)} %collective-permute-done.9.halo, f32[72,768]{1,0:T(8,128)S(1)} %get-tuple-element.63.edge_b.edge, f32[6,72,768]{2,1,0:T(8,128)S(1)} %shard_map.80.after.inner, f32[8,72,128]{2,1,0:T(8,128)S(1)} %get-tuple-element.48.seas.refs_3_, ...), custom_call_target="tpu_custom_call" | custom-call | flops 67108864 | tf_op jit(solution)/shard_map/pallas_call | solution.py:530
  29.5 1.5 %collective-permute-start.10 = (f32[21,8,128]{2,1,0:T(8,128)S(1)}, f32[21,8,128]{2,1,0:T(8,128)S(1)}, u32[]{:S(2)}, u32[]{:S(2)}) collective-permute-start(f32[21,8,128]{2,1,0:T(8,128)S(1)} %get-tuple-element.68), channel_id=1, source_target_pairs={{8,16},{16,8},{24,0},{0,24},{9,17},{17,9},{25,1},{1,25},{10,18},{1... | collective-permute-start | bytes 258056 | tf_op jit(solution)/shard_map/ppermute | solution.py:575
  31.0 0.0 collective-permute-done.6.halo
  31.0 0.6 %shard_map.84 = (f32[72,768]{1,0:T(8,128)S(1)}, f32[21,8,128]{2,1,0:T(8,128)S(1)}) custom-call(f32[23,8,128]{2,1,0:T(8,128)S(1)} %collective-permute-done.6.halo, f32[72,768]{1,0:T(8,128)S(1)} %get-tuple-element.61.edge_a.edge, f32[6,72,768]{2,1,0:T(8,128)S(1)} %shard_map.80.after.inner, f32[8,72,128]{2,1,0:T(8,128)S(1)} %get-tuple-element.48.seas.refs_3_, ...), custom_call_target="tpu_custom_call" | custom-call | flops 67108864 | tf_op jit(solution)/shard_map/pallas_call | solution.py:530
  31.6 1.2 %collective-permute-start.8 = (f32[21,8,128]{2,1,0:T(8,128)S(1)}, f32[21,8,128]{2,1,0:T(8,128)S(1)}, u32[]{:S(2)}, u32[]{:S(2)}) collective-permute-start(f32[21,8,128]{2,1,0:T(8,128)S(1)} %get-tuple-element.64), channel_id=1, source_target_pairs={{0,8},{8,0},{16,24},{24,16},{1,9},{9,1},{17,25},{25,17},{2,10},{10... | collective-permute-start | bytes 258056 | tf_op jit(solution)/shard_map/ppermute | solution.py:576
  32.9 1.2 %shard_map.86.after.done_inner = f32[6,64,648]{2,1,0:T(8,128)S(1)} custom-call(f32[72,768]{1,0:T(8,128)S(1)} %get-tuple-element.65.edge_a.edge, f32[72,768]{1,0:T(8,128)S(1)} %get-tuple-element.67.edge_b.edge, f32[6,72,768]{2,1,0:T(8,128)S(1)} %shard_map.83.after.inner, f32[8,72,128]{2,1,0:T(8,128)S(1)} %get-tuple-element.48.seas.refs_3_, ...), custom_call_target="tpu_custom_call" | custom-call | flops 268435456 | tf_op jit(solution)/shard_map/pallas_call | solution.py:530
  34.1 0.9 %collective-permute-done.10.halo = f32[21,8,128]{2,1,0:T(8,128)S(1)} collective-permute-done((f32[21,8,128]{2,1,0:T(8,128)S(1)}, f32[21,8,128]{2,1,0:T(8,128)S(1)}, u32[]{:S(2)}, u32[]{:S(2)}) %collective-permute-start.10) | collective-permute-done | bytes 86048 | tf_op jit(solution)/shard_map/ppermute | solution.py:575
  35.0 0.5 %shard_map.87.done_edge = f32[64,648]{1,0:T(8,128)S(1)} custom-call(f32[21,8,128]{2,1,0:T(8,128)S(1)} %collective-permute-done.10.halo, f32[72,768]{1,0:T(8,128)S(1)} %get-tuple-element.67.edge_b.edge, f32[6,72,768]{2,1,0:T(8,128)S(1)} %shard_map.83.after.inner, f32[8,72,128]{2,1,0:T(8,128)S(1)} %get-tuple-element.48.seas.refs_3_, ...), custom_call_target="tpu_custom_call" | custom-call | flops 67108864 | tf_op jit(solution)/shard_map/pallas_call | solution.py:530
  35.5 0.7 %collective-permute-done.8.halo = f32[21,8,128]{2,1,0:T(8,128)S(1)} collective-permute-done((f32[21,8,128]{2,1,0:T(8,128)S(1)}, f32[21,8,128]{2,1,0:T(8,128)S(1)}, u32[]{:S(2)}, u32[]{:S(2)}) %collective-permute-start.8) | collective-permute-done | bytes 86048 | tf_op jit(solution)/shard_map/ppermute | solution.py:576
  36.2 1.2 %shard_map.88 = f32[8,64,648]{2,1,0:T(8,128)} custom-call(f32[21,8,128]{2,1,0:T(8,128)S(1)} %collective-permute-done.8.halo, f32[72,768]{1,0:T(8,128)S(1)} %get-tuple-element.65.edge_a.edge, f32[6,72,768]{2,1,0:T(8,128)S(1)} %shard_map.83.after.inner, f32[8,72,128]{2,1,0:T(8,128)S(1)} %get-tuple-element.48.seas.refs_3_, ...), custom_call_target="tpu_custom_call" | custom-call | flops 67108864 | tf_op jit(solution)/shard_map/pallas_call | solution.py:530
  (4 shorter events, 0.0 us)
Async XLA Ops:
  0.0 3.8 %copy-start.5 = (f32[8,64]{1,0:T(8,128)S(1)}, f32[8,64]{1,0:T(8,128)}, u32[]{:S(2)}) copy-start(f32[8,64]{1,0:T(8,128)} %wind_ref.1) | copy-start | bytes 6148
  0.0 3.8 %copy-start = (f32[8,64,648]{2,1,0:T(8,128)S(1)}, f32[8,64,648]{2,1,0:T(8,128)}, u32[]{:S(2)}) copy-start(f32[8,64,648]{2,1,0:T(8,128)} %spectrum.3) | copy-start | bytes 3981316
  0.0 3.8 %copy-start.3 = (s32[8,64]{1,0:T(8,128)S(1)}, s32[8,64]{1,0:T(8,128)}, u32[]{:S(2)}) copy-start(s32[8,64]{1,0:T(8,128)} %sea_ref.1) | copy-start | bytes 6148
  0.0 3.8 %copy-start.4 = (s32[8,64]{1,0:T(8,128)S(1)}, s32[8,64]{1,0:T(8,128)}, u32[]{:S(2)}) copy-start(s32[8,64]{1,0:T(8,128)} %ice_ref.1) | copy-start | bytes 6148
  1.2 3.3 %collective-permute-start = (f32[4,8,768]{2,1,0:T(8,128)S(1)}, f32[4,8,768]{2,1,0:T(8,128)S(1)}, u32[]{:S(2)}, u32[]{:S(2)}) collective-permute-start(f32[4,8,768]{2,1,0:T(8,128)S(1)} %get-tuple-element.37), channel_id=1, source_target_pairs={{0,1},{1,0},{2,3},{3,2},{4,5},{5,4},{6,7},{7,6},{8,9},{9,8},{10,11... | collective-permute-start | bytes 294920 | tf_op jit(solution)/shard_map/ppermute | solution.py:550
  1.3 5.9 %collective-permute-start.1 = (f32[4,8,768]{2,1,0:T(8,128)S(1)}, f32[4,8,768]{2,1,0:T(8,128)S(1)}, u32[]{:S(2)}, u32[]{:S(2)}) collective-permute-start(f32[4,8,768]{2,1,0:T(8,128)S(1)} %get-tuple-element.38), channel_id=1, source_target_pairs={{1,2},{2,1},{3,4},{4,3},{5,6},{6,5},{9,10},{10,9},{11,12},{12,11},... | collective-permute-start | bytes 294920 | tf_op jit(solution)/shard_map/ppermute | solution.py:549
  7.3 3.2 %copy-start.1 = (bf16[648,648]{1,0:T(8,128)(2,1)S(1)}, bf16[648,648]{1,0:T(8,128)(2,1)}, u32[]{:S(2)}) copy-start(bf16[648,648]{1,0:T(8,128)(2,1)} %coupling_ref.1) | copy-start | bytes 2519428
  7.3 3.2 %copy-start.2 = (f32[8,768]{1,0:T(8,128)S(1)}, f32[8,768]{1,0:T(8,128)}, u32[]{:S(2)}) copy-start(f32[8,768]{1,0:T(8,128)} %constant.2.clone.angle_ref) | copy-start | bytes 73732
  7.3 3.2 %copy-start.6 = (f32[18]{0:T(128)S(1)}, f32[18]{0:T(128)}, u32[]{:S(2)}) copy-start(f32[18]{0:T(128)} %speed_ref.1) | copy-start | bytes 220
  7.5 10.6 %collective-permute-start.2 = (f32[23,8,128]{2,1,0:T(8,128)S(1)}, f32[23,8,128]{2,1,0:T(8,128)S(1)}, u32[]{:S(2)}, u32[]{:S(2)}) collective-permute-start(f32[23,8,128]{2,1,0:T(8,128)S(1)} %get-tuple-element.45), channel_id=1, source_target_pairs={{0,8},{8,0},{16,24},{24,16},{1,9},{9,1},{17,25},{25,17},{2,10},{10... | collective-permute-start | bytes 282632 | tf_op jit(solution)/shard_map/ppermute | solution.py:576
  8.9 5.4 %collective-permute-start.5 = (f32[21,8,128]{2,1,0:T(8,128)S(1)}, f32[21,8,128]{2,1,0:T(8,128)S(1)}, u32[]{:S(2)}, u32[]{:S(2)}) collective-permute-start(f32[21,8,128]{2,1,0:T(8,128)S(1)} %get-tuple-element.58), channel_id=1, source_target_pairs={{8,16},{16,8},{24,0},{0,24},{9,17},{17,9},{25,1},{1,25},{10,18},{1... | collective-permute-start | bytes 258056 | tf_op jit(solution)/shard_map/ppermute | solution.py:575
  11.3 4.7 %collective-permute-start.4 = (f32[3,8,128]{2,1,0:T(8,128)S(1)}, f32[3,8,128]{2,1,0:T(8,128)S(1)}, u32[]{:S(2)}, u32[]{:S(2)}) collective-permute-start(f32[3,8,128]{2,1,0:T(8,128)S(1)} %get-tuple-element.57), channel_id=1, source_target_pairs={{8,16},{16,8},{24,0},{0,24},{9,17},{17,9},{25,1},{1,25},{10,18},{1... | collective-permute-start | bytes 36872 | tf_op jit(solution)/shard_map/ppermute | solution.py:578
  16.5 6.4 %collective-permute-start.7 = (f32[23,8,128]{2,1,0:T(8,128)S(1)}, f32[23,8,128]{2,1,0:T(8,128)S(1)}, u32[]{:S(2)}, u32[]{:S(2)}) collective-permute-start(f32[23,8,128]{2,1,0:T(8,128)S(1)} %get-tuple-element.62), channel_id=1, source_target_pairs={{8,16},{16,8},{24,0},{0,24},{9,17},{17,9},{25,1},{1,25},{10,18},{1... | collective-permute-start | bytes 282632 | tf_op jit(solution)/shard_map/ppermute | solution.py:575
  18.7 6.2 %collective-permute-start.3 = (f32[23,8,128]{2,1,0:T(8,128)S(1)}, f32[23,8,128]{2,1,0:T(8,128)S(1)}, u32[]{:S(2)}, u32[]{:S(2)}) collective-permute-start(f32[23,8,128]{2,1,0:T(8,128)S(1)} %get-tuple-element.55), channel_id=1, source_target_pairs={{0,8},{8,0},{16,24},{24,16},{1,9},{9,1},{17,25},{25,17},{2,10},{10... | collective-permute-start | bytes 282632 | tf_op jit(solution)/shard_map/ppermute | solution.py:576
  23.4 5.5 %collective-permute-start.9 = (f32[23,8,128]{2,1,0:T(8,128)S(1)}, f32[23,8,128]{2,1,0:T(8,128)S(1)}, u32[]{:S(2)}, u32[]{:S(2)}) collective-permute-start(f32[23,8,128]{2,1,0:T(8,128)S(1)} %get-tuple-element.66), channel_id=1, source_target_pairs={{8,16},{16,8},{24,0},{0,24},{9,17},{17,9},{25,1},{1,25},{10,18},{1... | collective-permute-start | bytes 282632 | tf_op jit(solution)/shard_map/ppermute | solution.py:575
  25.5 5.5 %collective-permute-start.6 = (f32[23,8,128]{2,1,0:T(8,128)S(1)}, f32[23,8,128]{2,1,0:T(8,128)S(1)}, u32[]{:S(2)}, u32[]{:S(2)}) collective-permute-start(f32[23,8,128]{2,1,0:T(8,128)S(1)} %get-tuple-element.60), channel_id=1, source_target_pairs={{0,8},{8,0},{16,24},{24,16},{1,9},{9,1},{17,25},{25,17},{2,10},{10... | collective-permute-start | bytes 282632 | tf_op jit(solution)/shard_map/ppermute | solution.py:576
  29.5 5.4 %collective-permute-start.10 = (f32[21,8,128]{2,1,0:T(8,128)S(1)}, f32[21,8,128]{2,1,0:T(8,128)S(1)}, u32[]{:S(2)}, u32[]{:S(2)}) collective-permute-start(f32[21,8,128]{2,1,0:T(8,128)S(1)} %get-tuple-element.68), channel_id=1, source_target_pairs={{8,16},{16,8},{24,0},{0,24},{9,17},{17,9},{25,1},{1,25},{10,18},{1... | collective-permute-start | bytes 258056 | tf_op jit(solution)/shard_map/ppermute | solution.py:575
  31.6 4.6 %collective-permute-start.8 = (f32[21,8,128]{2,1,0:T(8,128)S(1)}, f32[21,8,128]{2,1,0:T(8,128)S(1)}, u32[]{:S(2)}, u32[]{:S(2)}) collective-permute-start(f32[21,8,128]{2,1,0:T(8,128)S(1)} %get-tuple-element.64), channel_id=1, source_target_pairs={{0,8},{8,0},{16,24},{24,16},{1,9},{9,1},{17,25},{25,17},{2,10},{10... | collective-permute-start | bytes 258056 | tf_op jit(solution)/shard_map/ppermute | solution.py:576

commit v6 on v5

--- a/solution.py
+++ b/solution.py
@@ -348,7 +348,7 @@
 
 
 def join_kernel(
-    bins, halo_a, halo_b, edge_a_in, edge_b_in, inner_in, seas_in, gains_in, pack_in,
+    bins, halo_a, halo_b, edge_a_in, edge_b_in, inner_in, seas_in, gains_in, pack_in, after,
     edge_a, edge_b, inner, seas, gains, pack_a, corner_b,
 ):
     columns = seas.shape[0]
@@ -403,8 +403,12 @@
     edge_kernel(bins, second, *refs, corner=corner)
 
 
+def ordered_edge_kernel(bins, second, after, *refs):
+    edge_kernel(bins, second, *refs)
+
+
 def edge_kernel(
-    bins, second, halo, edge, inner, seas, gains, stay, go_x, go_y, wide, after, out, pack, adv_ref, corner=None
+    bins, second, halo, edge, inner, seas, gains, stay, go_x, go_y, wide, out, pack, adv_ref, corner=None
 ):
     rows = edge.shape[0] - 2 * DEPTH
     halo_next = pack.shape[0] == pack_count(rows, True)
@@ -418,7 +422,7 @@
     on_each_side(second, side)
 
 
-def late_edge_kernel(bins, second, halo, edge, inner, seas, gains, stay, go_x, go_y, wide, after, out, adv_ref):
+def late_edge_kernel(bins, second, halo, edge, inner, seas, gains, stay, go_x, go_y, wide, out, adv_ref):
     def side(west):
         fresh = edge_step(bins, west, halo, edge, inner, seas, gains, stay, go_x, go_y, wide, adv_ref, True)
         for t, value in enumerate(fresh):
@@ -438,7 +442,7 @@
     ]
     for copy in copies:
         copy.start()
-    late_edge_kernel(bins, second, halo, edge, inner, seas, gains, stay, go_x, go_y, wide, None, column, adv_ref)
+    late_edge_kernel(bins, second, halo, edge, inner, seas, gains, stay, go_x, go_y, wide, column, adv_ref)
     copies.append(pltpu.make_async_copy(column, out.at[mine], sems.at[2]))
     copies[2].start()
     for copy in copies:
@@ -565,8 +569,8 @@
     edge_a, edge_b, inner, seas, gains, pack_a, corner_b = call(
         functools.partial(join_kernel, bins),
         (edge_shape, edge_shape, inner_shape, mask_shape, mask_shape, pack_shape, corner_shape),
-        (halo_a, halo_b, edge_a, edge_b, inner, seas, gains, pack_a),
-        [vmem] * 8,
+        (halo_a, halo_b, edge_a, edge_b, inner, seas, gains, pack_a, go_y),
+        [vmem] * 9,
         aliases={2: 0, 3: 1, 4: 2, 5: 3, 6: 4, 7: 5},
     )
     tables = (seas, gains, stay, go_x, go_y, wide)
@@ -588,7 +592,7 @@
             scratch = [VMEM((tall, padded), f32)]
             done_b = call(
                 functools.partial(late_edge_kernel, bins, True), column,
-                (halo_b, edge_b, inner) + tables + (new_inner,), [vmem] * 10, scratch, flops=1 << 26,
+                (halo_b, edge_b, inner) + tables, [vmem] * 9, scratch, flops=1 << 26,
             )
             return call(
                 functools.partial(last_edge_kernel, bins, False), pltpu.HBM((columns, rows, bins), f32),
@@ -598,8 +602,10 @@
         fresh = []
         pack_next = VMEM((pack_count(rows, step < STEPS - 2), 8, LANES), f32)
         for second, halo, edge in ((False, halo_a, edge_a), (True, halo_b, edge_b)):
-            body, ins = edge_kernel, (halo, edge, inner) + tables + (new_inner,)
-            if step == 0 and second:
+            body, ins = edge_kernel, (halo, edge, inner) + tables
+            if not second:
+                body, ins = ordered_edge_kernel, (new_inner,) + ins
+            elif step == 0:
                 body, ins = first_edge_kernel, (corner,) + ins
             fresh.append(call(
                 functools.partial(body, bins, second), (edge_shape, pack_next),

time: 37.5 us -> 37.3 us (level)
  starting transfers between devices: 15.1 us -> 15.9 us
  waiting for transfers between devices: 8.99 us -> 8.28 us
    ppermute x1, waiting for transfers between devices: 2.74 us -> 1.91 us  [steps(): halo_b = lax.ppermute(send_b, 'lat', lat_b)]
    ppermute x1, waiting for transfers between devices: 1.63 us -> 0.83 us  [steps(): corner = lax.ppermute(corner_b, 'lon', lon_b)]
    ppermute x4, waiting for transfers between devices: 3.92 us -> 4.7 us  [steps(): halo_b = lax.ppermute(pack_b, 'lon', lon_b)]
    ppermute x4, starting transfers between devices: 4.96 us -> 5.51 us  [steps(): halo_a = lax.ppermute(pack_a, 'lon', lon_a)]
  transfers between devices with their start and end apart: 11 -> 11, of which waited for: 7 -> 7; matrix products, arithmetic and copies ran while one was open for 0% -> 0% of each run, Pallas kernels for 28% -> 27%
where the time goes in v6:
time: 37.3 us; the launch traced here: 37.2 us
  starting transfers between devices  15.9 us (43%)
  Pallas kernels  12.7 us (34%)
  waiting for transfers between devices  8.28 us (22%)
    pallas_call x16, Pallas kernels, call(): pl.pallas_call(body, out_shape=outs, in_specs=specs, out_specs=out_specs...  12.7 us
    ppermute x4, starting transfers between devices, steps(): halo_b = lax.ppermute(pack_b, 'lon', lon_b)  6.49 us
    ppermute x4, starting transfers between devices, steps(): halo_a = lax.ppermute(pack_a, 'lon', lon_a)  5.51 us
    ppermute x4, waiting for transfers between devices, steps(): halo_b = lax.ppermute(pack_b, 'lon', lon_b)  4.7 us
    ppermute x1, starting transfers between devices, steps(): halo_b = lax.ppermute(send_b, 'lat', lat_b)  2.45 us
    ppermute x1, waiting for transfers between devices, steps(): halo_b = lax.ppermute(send_b, 'lat', lat_b)  1.91 us
    ppermute x1, starting transfers between devices, steps(): corner = lax.ppermute(corner_b, 'lon', lon_b)  1.38 us
    ppermute x4, waiting for transfers between devices, steps(): halo_a = lax.ppermute(pack_a, 'lon', lon_a)  0.84 us
  transfers between devices with their start and end apart: 11, of which 7 were waited for; matrix products, arithmetic and copies ran while one was open for 0% of the time, Pallas kernels for 27%

profile of v6, /device:TPU:24, one launch (start us, length us, event | category | flops | bytes accessed | tf_op | source)
XLA Modules:
  0.0 37.2 jit_solution(3487277752715502167)
XLA Ops:
  0.0 0.0 copy-start
  0.0 0.0 copy-start.2
  0.0 0.0 copy-start.1
  0.0 0.0 copy-start.6
  0.1 1.2 %shard_map.73 = (f32[4,8,768]{2,1,0:T(8,128)S(1)}, f32[4,8,768]{2,1,0:T(8,128)S(1)}) custom-call(f32[8,64,648]{2,1,0:T(8,128)} %spectrum.3, s32[8,64]{1,0:T(8,128)} %sea_ref.1, s32[8,64]{1,0:T(8,128)} %ice_ref.1, f32[8,64]{1,0:T(8,128)} %wind_ref.1), custom_call_target="tpu_custom_call" | custom-call | tf_op jit(solution)/shard_map/pallas_call | solution.py:534
  1.3 0.1 collective-permute-start
  1.4 2.4 %collective-permute-start.1 = (f32[4,8,768]{2,1,0:T(8,128)S(1)}, f32[4,8,768]{2,1,0:T(8,128)S(1)}, u32[]{:S(2)}, u32[]{:S(2)}) collective-permute-start(f32[4,8,768]{2,1,0:T(8,128)S(1)} %get-tuple-element.38), channel_id=1, source_target_pairs={{1,2},{2,1},{3,4},{4,3},{5,6},{6,5},{9,10},{10,9},{11,12},{12,11},... | collective-permute-start | bytes 294920 | tf_op jit(solution)/shard_map/ppermute | solution.py:553
  3.8 0.0 copy-done.5
  3.8 0.0 copy-done.4
  3.9 0.0 copy-done.3
  3.9 0.0 copy-done
  3.9 0.7 %shard_map.74 = (f32[72,768]{1,0:T(8,128)S(1)}, f32[72,768]{1,0:T(8,128)S(1)}, f32[6,72,768]{2,1,0:T(8,128)S(1)}, f32[8,72,128]{2,1,0:T(8,128)S(1)}, f32[8,72,12...) custom-call(f32[8,64,648]{2,1,0:T(8,128)S(1)} %copy-done, s32[8,64]{1,0:T(8,128)S(1)} %copy-done.3, ...), custom_call_target="tpu_custom_call" | custom-call | flops 16777216 | tf_op jit(solution)/shard_map/pallas_call | solution.py:534
  4.6 0.0 copy-done.2
  4.6 0.0 copy-done.1
  4.6 0.8 %shard_map.75 = (f32[72,768]{1,0:T(8,128)S(1)}, f32[72,768]{1,0:T(8,128)S(1)}, f32[8,768]{1,0:T(8,128)S(1)}, bf16[768,768]{1,0:T(8,128)(2,1)S(1)}) custom-call(f32[18]{0:T(128)S(1)} %copy-done.6, f32[8,768]{1,0:T(8,128)S(1)} %copy-done.2, bf16[648,648]{1,0:T(8,128)(2,1)S(1)} %copy-done.1), custom_call_target="tpu_custom_call" | custom-call | flops 16777216 | tf_op jit(solution)/shard_map/pallas_call | solution.py:534
  5.4 0.0 collective-permute-done.halo_a
  5.4 1.9 %collective-permute-done.1.halo_b = f32[4,8,768]{2,1,0:T(8,128)S(1)} collective-permute-done((f32[4,8,768]{2,1,0:T(8,128)S(1)}, f32[4,8,768]{2,1,0:T(8,128)S(1)}, u32[]{:S(2)}, u32[]{:S(2)}) %collective-permute-start.1) | collective-permute-done | bytes 98336 | tf_op jit(solution)/shard_map/ppermute | solution.py:553
  7.3 0.2 shard_map.76
  7.6 1.4 %collective-permute-start.2 = (f32[23,8,128]{2,1,0:T(8,128)S(1)}, f32[23,8,128]{2,1,0:T(8,128)S(1)}, u32[]{:S(2)}, u32[]{:S(2)}) collective-permute-start(f32[23,8,128]{2,1,0:T(8,128)S(1)} %get-tuple-element.54), channel_id=1, source_target_pairs={{0,8},{8,0},{16,24},{24,16},{1,9},{9,1},{17,25},{25,17},{2,10},{10... | collective-permute-start | bytes 282632 | tf_op jit(solution)/shard_map/ppermute | solution.py:580
  9.0 1.5 %collective-permute-start.4 = (f32[21,8,128]{2,1,0:T(8,128)S(1)}, f32[21,8,128]{2,1,0:T(8,128)S(1)}, u32[]{:S(2)}, u32[]{:S(2)}) collective-permute-start(f32[21,8,128]{2,1,0:T(8,128)S(1)} %get-tuple-element.57), channel_id=1, source_target_pairs={{8,16},{16,8},{24,0},{0,24},{9,17},{17,9},{25,1},{1,25},{10,18},{1... | collective-permute-start | bytes 258056 | tf_op jit(solution)/shard_map/ppermute | solution.py:579
  10.5 1.4 %collective-permute-start.3 = (f32[3,8,128]{2,1,0:T(8,128)S(1)}, f32[3,8,128]{2,1,0:T(8,128)S(1)}, u32[]{:S(2)}, u32[]{:S(2)}) collective-permute-start(f32[3,8,128]{2,1,0:T(8,128)S(1)} %get-tuple-element.56), channel_id=1, source_target_pairs={{8,16},{16,8},{24,0},{0,24},{9,17},{17,9},{25,1},{1,25},{10,18},{1... | collective-permute-start | bytes 36872 | tf_op jit(solution)/shard_map/ppermute | solution.py:582
  11.9 1.2 %shard_map.77.after.inner.refs_2_ = f32[6,72,768]{2,1,0:T(8,128)S(1)} custom-call(f32[72,768]{1,0:T(8,128)S(1)} %get-tuple-element.46.edge_a.refs_1_, f32[72,768]{1,0:T(8,128)S(1)} %get-tuple-element.47.edge_b.refs_1_, f32[6,72,768]{2,1,0:T(8,128)S(1)} %get-tuple-element.48.inner.refs_2_, f32[8,72,128]{2,1,0:T(8,128)S(1)} %get-tuple-element.49.seas.refs_3_, ...), custom_call_target="tpu_custom_call" | custom-call | flops 268435456 | tf_op jit(solution)/shard_map/pallas_call | solution.py:534
  13.2 1.3 %collective-permute-done.4.refs_0_ = f32[21,8,128]{2,1,0:T(8,128)S(1)} collective-permute-done((f32[21,8,128]{2,1,0:T(8,128)S(1)}, f32[21,8,128]{2,1,0:T(8,128)S(1)}, u32[]{:S(2)}, u32[]{:S(2)}) %collective-permute-start.4) | collective-permute-done | bytes 86048 | tf_op jit(solution)/shard_map/ppermute | solution.py:579
  14.4 0.8 %collective-permute-done.3.corner = f32[3,8,128]{2,1,0:T(8,128)S(1)} collective-permute-done((f32[3,8,128]{2,1,0:T(8,128)S(1)}, f32[3,8,128]{2,1,0:T(8,128)S(1)}, u32[]{:S(2)}, u32[]{:S(2)}) %collective-permute-start.3) | collective-permute-done | bytes 12320 | tf_op jit(solution)/shard_map/ppermute | solution.py:582
  15.3 0.5 %shard_map.79 = (f32[72,768]{1,0:T(8,128)S(1)}, f32[23,8,128]{2,1,0:T(8,128)S(1)}) custom-call(f32[3,8,128]{2,1,0:T(8,128)S(1)} %collective-permute-done.3.corner, f32[21,8,128]{2,1,0:T(8,128)S(1)} %collective-permute-done.4.refs_0_, f32[72,768]{1,0:T(8,128)S(1)} %get-tuple-element.47.edge_b.refs_1_, f32[6,72,768]{2,1,0:T(8,128)S(1)} %get-tuple-element.48.inner.refs_2_, ...), custom_call_target="tpu_custom_call" | custom-call | flops 67108864 | tf_op jit(solution)/shard_map/pallas_call | solution.py:534
  15.8 1.5 %collective-permute-start.6 = (f32[23,8,128]{2,1,0:T(8,128)S(1)}, f32[23,8,128]{2,1,0:T(8,128)S(1)}, u32[]{:S(2)}, u32[]{:S(2)}) collective-permute-start(f32[23,8,128]{2,1,0:T(8,128)S(1)} %get-tuple-element.61), channel_id=1, source_target_pairs={{8,16},{16,8},{24,0},{0,24},{9,17},{17,9},{25,1},{1,25},{10,18},{1... | collective-permute-start | bytes 282632 | tf_op jit(solution)/shard_map/ppermute | solution.py:579
  17.3 0.0 collective-permute-done.2.refs_0_
  17.3 0.6 %shard_map.78 = (f32[72,768]{1,0:T(8,128)S(1)}, f32[23,8,128]{2,1,0:T(8,128)S(1)}) custom-call(f32[6,72,768]{2,1,0:T(8,128)S(1)} %shard_map.77.after.inner.refs_2_, f32[23,8,128]{2,1,0:T(8,128)S(1)} %collective-permute-done.2.refs_0_, f32[72,768]{1,0:T(8,128)S(1)} %get-tuple-element.46.edge_a.refs_1_, f32[6,72,768]{2,1,0:T(8,128)S(1)} %get-tuple-element.48.inner.refs_2_, ...), custom_call_target="tpu_custom_call" | custom-call | flops 67108864 | tf_op jit(solution)/shard_map/pallas_call | solution.py:534
  17.9 1.4 %collective-permute-start.5 = (f32[23,8,128]{2,1,0:T(8,128)S(1)}, f32[23,8,128]{2,1,0:T(8,128)S(1)}, u32[]{:S(2)}, u32[]{:S(2)}) collective-permute-start(f32[23,8,128]{2,1,0:T(8,128)S(1)} %get-tuple-element.59), channel_id=1, source_target_pairs={{0,8},{8,0},{16,24},{24,16},{1,9},{9,1},{17,25},{25,17},{2,10},{10... | collective-permute-start | bytes 282632 | tf_op jit(solution)/shard_map/ppermute | solution.py:580
  19.2 1.2 %shard_map.80.after.inner.refs_2_ = f32[6,72,768]{2,1,0:T(8,128)S(1)} custom-call(f32[72,768]{1,0:T(8,128)S(1)} %get-tuple-element.55.edge_a.refs_1_, f32[72,768]{1,0:T(8,128)S(1)} %get-tuple-element.58.edge_b.edge, f32[6,72,768]{2,1,0:T(8,128)S(1)} %shard_map.77.after.inner.refs_2_, f32[8,72,128]{2,1,0:T(8,128)S(1)} %get-tuple-element.49.seas.refs_3_, ...), custom_call_target="tpu_custom_call" | custom-call | flops 268435456 | tf_op jit(solution)/shard_map/pallas_call | solution.py:534
  20.5 1.2 %collective-permute-done.6.halo = f32[23,8,128]{2,1,0:T(8,128)S(1)} collective-permute-done((f32[23,8,128]{2,1,0:T(8,128)S(1)}, f32[23,8,128]{2,1,0:T(8,128)S(1)}, u32[]{:S(2)}, u32[]{:S(2)}) %collective-permute-start.6) | collective-permute-done | bytes 94240 | tf_op jit(solution)/shard_map/ppermute | solution.py:579
  21.7 0.5 %shard_map.82 = (f32[72,768]{1,0:T(8,128)S(1)}, f32[23,8,128]{2,1,0:T(8,128)S(1)}) custom-call(f32[23,8,128]{2,1,0:T(8,128)S(1)} %collective-permute-done.6.halo, f32[72,768]{1,0:T(8,128)S(1)} %get-tuple-element.58.edge_b.edge, f32[6,72,768]{2,1,0:T(8,128)S(1)} %shard_map.77.after.inner.refs_2_, f32[8,72,128]{2,1,0:T(8,128)S(1)} %get-tuple-element.49.seas.refs_3_, ...), custom_call_target="tpu_custom_call" | custom-call | flops 67108864 | tf_op jit(solution)/shard_map/pallas_call | solution.py:534
  22.2 1.8 %collective-permute-start.9 = (f32[23,8,128]{2,1,0:T(8,128)S(1)}, f32[23,8,128]{2,1,0:T(8,128)S(1)}, u32[]{:S(2)}, u32[]{:S(2)}) collective-permute-start(f32[23,8,128]{2,1,0:T(8,128)S(1)} %get-tuple-element.66), channel_id=1, source_target_pairs={{8,16},{16,8},{24,0},{0,24},{9,17},{17,9},{25,1},{1,25},{10,18},{1... | collective-permute-start | bytes 282632 | tf_op jit(solution)/shard_map/ppermute | solution.py:579
  24.0 0.0 collective-permute-done.5.refs_0_
  24.0 0.6 %shard_map.81 = (f32[72,768]{1,0:T(8,128)S(1)}, f32[23,8,128]{2,1,0:T(8,128)S(1)}) custom-call(f32[6,72,768]{2,1,0:T(8,128)S(1)} %shard_map.80.after.inner.refs_2_, f32[23,8,128]{2,1,0:T(8,128)S(1)} %collective-permute-done.5.refs_0_, f32[72,768]{1,0:T(8,128)S(1)} %get-tuple-element.55.edge_a.refs_1_, f32[6,72,768]{2,1,0:T(8,128)S(1)} %shard_map.77.after.inner.refs_2_, ...), custom_call_target="tpu_custom_call" | custom-call | flops 67108864 | tf_op jit(solution)/shard_map/pallas_call | solution.py:534
  24.6 1.7 %collective-permute-start.7 = (f32[23,8,128]{2,1,0:T(8,128)S(1)}, f32[23,8,128]{2,1,0:T(8,128)S(1)}, u32[]{:S(2)}, u32[]{:S(2)}) collective-permute-start(f32[23,8,128]{2,1,0:T(8,128)S(1)} %get-tuple-element.63), channel_id=1, source_target_pairs={{0,8},{8,0},{16,24},{24,16},{1,9},{9,1},{17,25},{25,17},{2,10},{10... | collective-permute-start | bytes 282632 | tf_op jit(solution)/shard_map/ppermute | solution.py:580
  26.3 1.2 %shard_map.83.after.inner = f32[6,72,768]{2,1,0:T(8,128)S(1)} custom-call(f32[72,768]{1,0:T(8,128)S(1)} %get-tuple-element.60.edge_a.refs_1_, f32[72,768]{1,0:T(8,128)S(1)} %get-tuple-element.62.edge_b.edge, f32[6,72,768]{2,1,0:T(8,128)S(1)} %shard_map.80.after.inner.refs_2_, f32[8,72,128]{2,1,0:T(8,128)S(1)} %get-tuple-element.49.seas.refs_3_, ...), custom_call_target="tpu_custom_call" | custom-call | flops 268435456 | tf_op jit(solution)/shard_map/pallas_call | solution.py:534
  27.6 1.1 %collective-permute-done.9.halo = f32[23,8,128]{2,1,0:T(8,128)S(1)} collective-permute-done((f32[23,8,128]{2,1,0:T(8,128)S(1)}, f32[23,8,128]{2,1,0:T(8,128)S(1)}, u32[]{:S(2)}, u32[]{:S(2)}) %collective-permute-start.9) | collective-permute-done | bytes 94240 | tf_op jit(solution)/shard_map/ppermute | solution.py:579
  28.7 0.5 %shard_map.85 = (f32[72,768]{1,0:T(8,128)S(1)}, f32[21,8,128]{2,1,0:T(8,128)S(1)}) custom-call(f32[23,8,128]{2,1,0:T(8,128)S(1)} %collective-permute-done.9.halo, f32[72,768]{1,0:T(8,128)S(1)} %get-tuple-element.62.edge_b.edge, f32[6,72,768]{2,1,0:T(8,128)S(1)} %shard_map.80.after.inner.refs_2_, f32[8,72,128]{2,1,0:T(8,128)S(1)} %get-tuple-element.49.seas.refs_3_, ...), custom_call_target="tpu_custom_call" | custom-call | flops 67108864 | tf_op jit(solution)/shard_map/pallas_call | solution.py:534
  29.2 1.7 %collective-permute-start.10 = (f32[21,8,128]{2,1,0:T(8,128)S(1)}, f32[21,8,128]{2,1,0:T(8,128)S(1)}, u32[]{:S(2)}, u32[]{:S(2)}) collective-permute-start(f32[21,8,128]{2,1,0:T(8,128)S(1)} %get-tuple-element.68), channel_id=1, source_target_pairs={{8,16},{16,8},{24,0},{0,24},{9,17},{17,9},{25,1},{1,25},{10,18},{1... | collective-permute-start | bytes 258056 | tf_op jit(solution)/shard_map/ppermute | solution.py:579
  30.9 0.0 collective-permute-done.7.refs_0_
  30.9 0.6 %shard_map.84 = (f32[72,768]{1,0:T(8,128)S(1)}, f32[21,8,128]{2,1,0:T(8,128)S(1)}) custom-call(f32[6,72,768]{2,1,0:T(8,128)S(1)} %shard_map.83.after.inner, f32[23,8,128]{2,1,0:T(8,128)S(1)} %collective-permute-done.7.refs_0_, f32[72,768]{1,0:T(8,128)S(1)} %get-tuple-element.60.edge_a.refs_1_, f32[6,72,768]{2,1,0:T(8,128)S(1)} %shard_map.80.after.inner.refs_2_, ...), custom_call_target="tpu_custom_call" | custom-call | flops 67108864 | tf_op jit(solution)/shard_map/pallas_call | solution.py:534
  31.4 0.9 %collective-permute-start.8 = (f32[21,8,128]{2,1,0:T(8,128)S(1)}, f32[21,8,128]{2,1,0:T(8,128)S(1)}, u32[]{:S(2)}, u32[]{:S(2)}) collective-permute-start(f32[21,8,128]{2,1,0:T(8,128)S(1)} %get-tuple-element.64), channel_id=1, source_target_pairs={{0,8},{8,0},{16,24},{24,16},{1,9},{9,1},{17,25},{25,17},{2,10},{10... | collective-permute-start | bytes 258056 | tf_op jit(solution)/shard_map/ppermute | solution.py:580
  32.4 1.1 %shard_map.86.done_inner = f32[6,64,648]{2,1,0:T(8,128)S(1)} custom-call(f32[72,768]{1,0:T(8,128)S(1)} %get-tuple-element.65.edge_a.edge, f32[72,768]{1,0:T(8,128)S(1)} %get-tuple-element.67.edge_b.edge, f32[6,72,768]{2,1,0:T(8,128)S(1)} %shard_map.83.after.inner, f32[8,72,128]{2,1,0:T(8,128)S(1)} %get-tuple-element.49.seas.refs_3_, ...), custom_call_target="tpu_custom_call" | custom-call | flops 268435456 | tf_op jit(solution)/shard_map/pallas_call | solution.py:534
  33.5 1.1 %collective-permute-done.10.halo = f32[21,8,128]{2,1,0:T(8,128)S(1)} collective-permute-done((f32[21,8,128]{2,1,0:T(8,128)S(1)}, f32[21,8,128]{2,1,0:T(8,128)S(1)}, u32[]{:S(2)}, u32[]{:S(2)}) %collective-permute-start.10) | collective-permute-done | bytes 86048 | tf_op jit(solution)/shard_map/ppermute | solution.py:579
  34.7 0.5 %shard_map.87.done_edge = f32[64,648]{1,0:T(8,128)S(1)} custom-call(f32[21,8,128]{2,1,0:T(8,128)S(1)} %collective-permute-done.10.halo, f32[72,768]{1,0:T(8,128)S(1)} %get-tuple-element.67.edge_b.edge, f32[6,72,768]{2,1,0:T(8,128)S(1)} %shard_map.83.after.inner, f32[8,72,128]{2,1,0:T(8,128)S(1)} %get-tuple-element.49.seas.refs_3_, ...), custom_call_target="tpu_custom_call" | custom-call | flops 67108864 | tf_op jit(solution)/shard_map/pallas_call | solution.py:534
  35.2 0.8 %collective-permute-done.8.halo = f32[21,8,128]{2,1,0:T(8,128)S(1)} collective-permute-done((f32[21,8,128]{2,1,0:T(8,128)S(1)}, f32[21,8,128]{2,1,0:T(8,128)S(1)}, u32[]{:S(2)}, u32[]{:S(2)}) %collective-permute-start.8) | collective-permute-done | bytes 86048 | tf_op jit(solution)/shard_map/ppermute | solution.py:580
  36.0 1.2 %shard_map.88 = f32[8,64,648]{2,1,0:T(8,128)} custom-call(f32[21,8,128]{2,1,0:T(8,128)S(1)} %collective-permute-done.8.halo, f32[72,768]{1,0:T(8,128)S(1)} %get-tuple-element.65.edge_a.edge, f32[6,72,768]{2,1,0:T(8,128)S(1)} %shard_map.83.after.inner, f32[8,72,128]{2,1,0:T(8,128)S(1)} %get-tuple-element.49.seas.refs_3_, ...), custom_call_target="tpu_custom_call" | custom-call | flops 67108864 | tf_op jit(solution)/shard_map/pallas_call | solution.py:534
  (4 shorter events, 0.0 us)
Async XLA Ops:
  0.0 3.8 %copy-start.5 = (f32[8,64]{1,0:T(8,128)S(1)}, f32[8,64]{1,0:T(8,128)}, u32[]{:S(2)}) copy-start(f32[8,64]{1,0:T(8,128)} %wind_ref.1) | copy-start | bytes 6148
  0.0 3.8 %copy-start.4 = (s32[8,64]{1,0:T(8,128)S(1)}, s32[8,64]{1,0:T(8,128)}, u32[]{:S(2)}) copy-start(s32[8,64]{1,0:T(8,128)} %ice_ref.1) | copy-start | bytes 6148
  0.0 3.9 %copy-start.3 = (s32[8,64]{1,0:T(8,128)S(1)}, s32[8,64]{1,0:T(8,128)}, u32[]{:S(2)}) copy-start(s32[8,64]{1,0:T(8,128)} %sea_ref.1) | copy-start | bytes 6148
  0.0 3.9 %copy-start = (f32[8,64,648]{2,1,0:T(8,128)S(1)}, f32[8,64,648]{2,1,0:T(8,128)}, u32[]{:S(2)}) copy-start(f32[8,64,648]{2,1,0:T(8,128)} %spectrum.3) | copy-start | bytes 3981316
  0.0 4.5 %copy-start.2 = (f32[8,768]{1,0:T(8,128)S(1)}, f32[8,768]{1,0:T(8,128)}, u32[]{:S(2)}) copy-start(f32[8,768]{1,0:T(8,128)} %constant.2.clone.angle_ref) | copy-start | bytes 73732
  0.0 4.5 %copy-start.1 = (bf16[648,648]{1,0:T(8,128)(2,1)S(1)}, bf16[648,648]{1,0:T(8,128)(2,1)}, u32[]{:S(2)}) copy-start(bf16[648,648]{1,0:T(8,128)(2,1)} %coupling_ref.1) | copy-start | bytes 2519428
  0.0 4.5 %copy-start.6 = (f32[18]{0:T(128)S(1)}, f32[18]{0:T(128)}, u32[]{:S(2)}) copy-start(f32[18]{0:T(128)} %speed_ref.1) | copy-start | bytes 220
  1.3 4.1 %collective-permute-start = (f32[4,8,768]{2,1,0:T(8,128)S(1)}, f32[4,8,768]{2,1,0:T(8,128)S(1)}, u32[]{:S(2)}, u32[]{:S(2)}) collective-permute-start(f32[4,8,768]{2,1,0:T(8,128)S(1)} %get-tuple-element.37), channel_id=1, source_target_pairs={{0,1},{1,0},{2,3},{3,2},{4,5},{5,4},{6,7},{7,6},{8,9},{9,8},{10,11... | collective-permute-start | bytes 294920 | tf_op jit(solution)/shard_map/ppermute | solution.py:554
  1.4 5.9 %collective-permute-start.1 = (f32[4,8,768]{2,1,0:T(8,128)S(1)}, f32[4,8,768]{2,1,0:T(8,128)S(1)}, u32[]{:S(2)}, u32[]{:S(2)}) collective-permute-start(f32[4,8,768]{2,1,0:T(8,128)S(1)} %get-tuple-element.38), channel_id=1, source_target_pairs={{1,2},{2,1},{3,4},{4,3},{5,6},{6,5},{9,10},{10,9},{11,12},{12,11},... | collective-permute-start | bytes 294920 | tf_op jit(solution)/shard_map/ppermute | solution.py:553
  7.6 9.7 %collective-permute-start.2 = (f32[23,8,128]{2,1,0:T(8,128)S(1)}, f32[23,8,128]{2,1,0:T(8,128)S(1)}, u32[]{:S(2)}, u32[]{:S(2)}) collective-permute-start(f32[23,8,128]{2,1,0:T(8,128)S(1)} %get-tuple-element.54), channel_id=1, source_target_pairs={{0,8},{8,0},{16,24},{24,16},{1,9},{9,1},{17,25},{25,17},{2,10},{10... | collective-permute-start | bytes 282632 | tf_op jit(solution)/shard_map/ppermute | solution.py:580
  9.0 5.4 %collective-permute-start.4 = (f32[21,8,128]{2,1,0:T(8,128)S(1)}, f32[21,8,128]{2,1,0:T(8,128)S(1)}, u32[]{:S(2)}, u32[]{:S(2)}) collective-permute-start(f32[21,8,128]{2,1,0:T(8,128)S(1)} %get-tuple-element.57), channel_id=1, source_target_pairs={{8,16},{16,8},{24,0},{0,24},{9,17},{17,9},{25,1},{1,25},{10,18},{1... | collective-permute-start | bytes 258056 | tf_op jit(solution)/shard_map/ppermute | solution.py:579
  10.5 4.7 %collective-permute-start.3 = (f32[3,8,128]{2,1,0:T(8,128)S(1)}, f32[3,8,128]{2,1,0:T(8,128)S(1)}, u32[]{:S(2)}, u32[]{:S(2)}) collective-permute-start(f32[3,8,128]{2,1,0:T(8,128)S(1)} %get-tuple-element.56), channel_id=1, source_target_pairs={{8,16},{16,8},{24,0},{0,24},{9,17},{17,9},{25,1},{1,25},{10,18},{1... | collective-permute-start | bytes 36872 | tf_op jit(solution)/shard_map/ppermute | solution.py:582
  15.8 5.9 %collective-permute-start.6 = (f32[23,8,128]{2,1,0:T(8,128)S(1)}, f32[23,8,128]{2,1,0:T(8,128)S(1)}, u32[]{:S(2)}, u32[]{:S(2)}) collective-permute-start(f32[23,8,128]{2,1,0:T(8,128)S(1)} %get-tuple-element.61), channel_id=1, source_target_pairs={{8,16},{16,8},{24,0},{0,24},{9,17},{17,9},{25,1},{1,25},{10,18},{1... | collective-permute-start | bytes 282632 | tf_op jit(solution)/shard_map/ppermute | solution.py:579
  17.9 6.1 %collective-permute-start.5 = (f32[23,8,128]{2,1,0:T(8,128)S(1)}, f32[23,8,128]{2,1,0:T(8,128)S(1)}, u32[]{:S(2)}, u32[]{:S(2)}) collective-permute-start(f32[23,8,128]{2,1,0:T(8,128)S(1)} %get-tuple-element.59), channel_id=1, source_target_pairs={{0,8},{8,0},{16,24},{24,16},{1,9},{9,1},{17,25},{25,17},{2,10},{10... | collective-permute-start | bytes 282632 | tf_op jit(solution)/shard_map/ppermute | solution.py:580
  22.2 6.5 %collective-permute-start.9 = (f32[23,8,128]{2,1,0:T(8,128)S(1)}, f32[23,8,128]{2,1,0:T(8,128)S(1)}, u32[]{:S(2)}, u32[]{:S(2)}) collective-permute-start(f32[23,8,128]{2,1,0:T(8,128)S(1)} %get-tuple-element.66), channel_id=1, source_target_pairs={{8,16},{16,8},{24,0},{0,24},{9,17},{17,9},{25,1},{1,25},{10,18},{1... | collective-permute-start | bytes 282632 | tf_op jit(solution)/shard_map/ppermute | solution.py:579
  24.6 6.3 %collective-permute-start.7 = (f32[23,8,128]{2,1,0:T(8,128)S(1)}, f32[23,8,128]{2,1,0:T(8,128)S(1)}, u32[]{:S(2)}, u32[]{:S(2)}) collective-permute-start(f32[23,8,128]{2,1,0:T(8,128)S(1)} %get-tuple-element.63), channel_id=1, source_target_pairs={{0,8},{8,0},{16,24},{24,16},{1,9},{9,1},{17,25},{25,17},{2,10},{10... | collective-permute-start | bytes 282632 | tf_op jit(solution)/shard_map/ppermute | solution.py:580
  29.2 5.4 %collective-permute-start.10 = (f32[21,8,128]{2,1,0:T(8,128)S(1)}, f32[21,8,128]{2,1,0:T(8,128)S(1)}, u32[]{:S(2)}, u32[]{:S(2)}) collective-permute-start(f32[21,8,128]{2,1,0:T(8,128)S(1)} %get-tuple-element.68), channel_id=1, source_target_pairs={{8,16},{16,8},{24,0},{0,24},{9,17},{17,9},{25,1},{1,25},{10,18},{1... | collective-permute-start | bytes 258056 | tf_op jit(solution)/shard_map/ppermute | solution.py:579
  31.4 4.6 %collective-permute-start.8 = (f32[21,8,128]{2,1,0:T(8,128)S(1)}, f32[21,8,128]{2,1,0:T(8,128)S(1)}, u32[]{:S(2)}, u32[]{:S(2)}) collective-permute-start(f32[21,8,128]{2,1,0:T(8,128)S(1)} %get-tuple-element.64), channel_id=1, source_target_pairs={{0,8},{8,0},{16,24},{24,16},{1,9},{9,1},{17,25},{25,17},{2,10},{10... | collective-permute-start | bytes 258056 | tf_op jit(solution)/shard_map/ppermute | solution.py:580

commit v7 on v6

--- a/solution.py
+++ b/solution.py
@@ -266,8 +266,10 @@
     for copy in copies:
         copy.wait()
     tiles = lane_tiles(bins)
+    space = LANES // (columns // 2)
     for second, out in ((False, out_a), (True, out_b)):
         to_south = south_flag(second)
+        ends = jnp.zeros(shape, jnp.float32)
         for pair in range(columns // 2):
             for tile in range(tiles):
                 halves = []
@@ -284,7 +286,13 @@
                     halves.append(value)
                 first, other = halves
                 keep = (row < DEPTH) == to_south
-                out[pair, :, lanes_of(tile)] = jnp.where(keep, first, pltpu.roll(other, DEPTH, 0))
+                value = jnp.where(keep, first, pltpu.roll(other, DEPTH, 0))
+                if tile < tiles - 1:
+                    out[pair * (tiles - 1) + tile] = value
+                else:
+                    here = (lane >= pair * space) & (lane < (pair + 1) * space)
+                    ends = jnp.where(here, turn(value, pair * space), ends)
+        out[columns // 2 * (tiles - 1)] = ends
 
 
 def table_kernel(bins, rows, speed_ref, angle_ref, coupling_ref, stay, go_x, go_y, wide):
@@ -348,7 +356,7 @@
 
 
 def join_kernel(
-    bins, halo_a, halo_b, edge_a_in, edge_b_in, inner_in, seas_in, gains_in, pack_in, after,
+    bins, halo_a, halo_b, edge_a_in, edge_b_in, inner_in, seas_in, gains_in, pack_in,
     edge_a, edge_b, inner, seas, gains, pack_a, corner_b,
 ):
     columns = seas.shape[0]
@@ -364,7 +372,11 @@
     for c in range(columns):
         tile_values = []
         for tile in range(tiles):
-            from_a, from_b = halo_a[c // 2, :, lanes_of(tile)], halo_b[c // 2, :, lanes_of(tile)]
+            spot = columns // 2 * (tiles - 1) if tile == tiles - 1 else c // 2 * (tiles - 1) + tile
+            from_a, from_b = halo_a[spot], halo_b[spot]
+            if tile == tiles - 1:
+                back = -(c // 2) * (LANES // (columns // 2))
+                from_a, from_b = turn(from_a, back), turn(from_b, back)
             low, high = jnp.where(a_south, from_a, from_b), jnp.where(a_south, from_b, from_a)
             if c % 2:
                 low, high = pltpu.roll(low, DEPTH, 0), pltpu.roll(high, DEPTH, 0)
@@ -420,6 +432,10 @@
         pack_half(fresh, west, bins, rows, halo_next, pack)
 
     on_each_side(second, side)
+
+
+def ordered_late_kernel(bins, second, after, *refs):
+    late_edge_kernel(bins, second, *refs)
 
 
 def late_edge_kernel(bins, second, halo, edge, inner, seas, gains, stay, go_x, go_y, wide, out, adv_ref):
@@ -544,7 +560,7 @@
 
     send_a, send_b = call(
         functools.partial(first_kernel, bins),
-        (VMEM((columns // 2, 8, padded), f32),) * 2,
+        (VMEM((columns // 2 * (tiles - 1) + 1, 8, LANES), f32),) * 2,
         [pltpu.with_memory_space_constraint(x, pltpu.HBM) for x in (spectrum, sea_mask, ice_flags, wind_forcing)],
         [hbm] * 4,
         [VMEM((2, columns, 8, bins), f32), VMEM((columns, rows), sea_mask.dtype), VMEM((columns, rows), ice_flags.dtype),
@@ -569,8 +585,8 @@
     edge_a, edge_b, inner, seas, gains, pack_a, corner_b = call(
         functools.partial(join_kernel, bins),
         (edge_shape, edge_shape, inner_shape, mask_shape, mask_shape, pack_shape, corner_shape),
-        (halo_a, halo_b, edge_a, edge_b, inner, seas, gains, pack_a, go_y),
-        [vmem] * 9,
+        (halo_a, halo_b, edge_a, edge_b, inner, seas, gains, pack_a),
+        [vmem] * 8,
         aliases={2: 0, 3: 1, 4: 2, 5: 3, 6: 4, 7: 5},
     )
     tables = (seas, gains, stay, go_x, go_y, wide)
@@ -591,8 +607,8 @@
             column = VMEM((rows, bins), f32)
             scratch = [VMEM((tall, padded), f32)]
             done_b = call(
-                functools.partial(late_edge_kernel, bins, True), column,
-                (halo_b, edge_b, inner) + tables, [vmem] * 9, scratch, flops=1 << 26,
+                functools.partial(ordered_late_kernel, bins, True), column,
+                (new_inner, halo_b, edge_b, inner) + tables, [vmem] * 10, scratch, flops=1 << 26,
             )
             return call(
                 functools.partial(last_edge_kernel, bins, False), pltpu.HBM((columns, rows, bins), f32),
@@ -603,9 +619,9 @@
         pack_next = VMEM((pack_count(rows, step < STEPS - 2), 8, LANES), f32)
         for second, halo, edge in ((False, halo_a, edge_a), (True, halo_b, edge_b)):
             body, ins = edge_kernel, (halo, edge, inner) + tables
-            if not second:
+            if step > 0:
                 body, ins = ordered_edge_kernel, (new_inner,) + ins
-            elif step == 0:
+            elif second:
                 body, ins = first_edge_kernel, (corner,) + ins
             fresh.append(call(
                 functools.partial(body, bins, second), (edge_shape, pack_next),

time: 37.3 us -> 37.1 us (level)
  waiting for transfers between devices: 8.28 us -> 6.97 us
  starting transfers between devices: 15.9 us -> 16.9 us
    ppermute x4, waiting for transfers between devices: 4.7 us -> 3.11 us  [steps(): halo_b = lax.ppermute(pack_b, 'lon', lon_b)]
    ppermute x1, waiting for transfers between devices: 1.91 us -> 2.57 us  [steps(): halo_b = lax.ppermute(send_b, 'lat', lat_b)]
    ppermute x1, waiting for transfers between devices: 0.83 us -> 0.26 us  [steps(): corner = lax.ppermute(corner_b, 'lon', lon_b)]
    ppermute x4, starting transfers between devices: 6.49 us -> 7.01 us  [steps(): halo_b = lax.ppermute(pack_b, 'lon', lon_b)]
    ppermute x4, starting transfers between devices: 5.51 us -> 5.98 us  [steps(): halo_a = lax.ppermute(pack_a, 'lon', lon_a)]
  transfers between devices with their start and end apart: 11 -> 11, of which waited for: 7 -> 6; matrix products, arithmetic and copies ran while one was open for 0% -> 0% of each run, Pallas kernels for 27% -> 27%
where the time goes in v7:
time: 37.1 us; the launch traced here: 36.9 us
  starting transfers between devices  16.9 us (46%)
  Pallas kernels  12.8 us (35%)
  waiting for transfers between devices  6.97 us (19%)
    pallas_call x16, Pallas kernels, call(): pl.pallas_call(body, out_shape=outs, in_specs=specs, out_specs=out_specs...  12.8 us
    ppermute x4, starting transfers between devices, steps(): halo_b = lax.ppermute(pack_b, 'lon', lon_b)  7.01 us
    ppermute x4, starting transfers between devices, steps(): halo_a = lax.ppermute(pack_a, 'lon', lon_a)  5.98 us
    ppermute x4, waiting for transfers between devices, steps(): halo_b = lax.ppermute(pack_b, 'lon', lon_b)  3.11 us
    ppermute x1, waiting for transfers between devices, steps(): halo_b = lax.ppermute(send_b, 'lat', lat_b)  2.57 us
    ppermute x1, starting transfers between devices, steps(): halo_b = lax.ppermute(send_b, 'lat', lat_b)  2.45 us
    ppermute x1, starting transfers between devices, steps(): corner = lax.ppermute(corner_b, 'lon', lon_b)  1.38 us
    ppermute x4, waiting for transfers between devices, steps(): halo_a = lax.ppermute(pack_a, 'lon', lon_a)  1.02 us
  transfers between devices with their start and end apart: 11, of which 6 were waited for; matrix products, arithmetic and copies ran while one was open for 0% of the time, Pallas kernels for 27%

profile of v7, /device:TPU:24, one launch (start us, length us, event | category | flops | bytes accessed | tf_op | source)
XLA Modules:
  0.0 36.9 jit_solution(18169982561286350718)
XLA Ops:
  0.0 0.0 copy-start.4
  0.0 1.3 %shard_map.73 = (f32[21,8,128]{2,1,0:T(8,128)S(1)}, f32[21,8,128]{2,1,0:T(8,128)S(1)}) custom-call(f32[8,64,648]{2,1,0:T(8,128)} %spectrum.3, s32[8,64]{1,0:T(8,128)} %sea_ref.1, s32[8,64]{1,0:T(8,128)} %ice_ref.1, f32[8,64]{1,0:T(8,128)} %wind_ref.1), custom_call_target="tpu_custom_call" | custom-call | tf_op jit(solution)/shard_map/pallas_call | solution.py:550
  1.3 0.1 collective-permute-start
  1.4 2.4 %collective-permute-start.1 = (f32[21,8,128]{2,1,0:T(8,128)S(1)}, f32[21,8,128]{2,1,0:T(8,128)S(1)}, u32[]{:S(2)}, u32[]{:S(2)}) collective-permute-start(f32[21,8,128]{2,1,0:T(8,128)S(1)} %get-tuple-element.38), channel_id=1, source_target_pairs={{1,2},{2,1},{3,4},{4,3},{5,6},{6,5},{9,10},{10,9},{11,12},{12,11},... | collective-permute-start | bytes 258056 | tf_op jit(solution)/shard_map/ppermute | solution.py:569
  3.8 0.0 copy-done.5
  3.8 0.0 copy-done
  3.8 0.0 copy-done.3
  3.9 0.0 copy-done.4
  3.9 0.7 %shard_map.74 = (f32[72,768]{1,0:T(8,128)S(1)}, f32[72,768]{1,0:T(8,128)S(1)}, f32[6,72,768]{2,1,0:T(8,128)S(1)}, f32[8,72,128]{2,1,0:T(8,128)S(1)}, f32[8,72,12...) custom-call(f32[8,64,648]{2,1,0:T(8,128)S(1)} %copy-done, s32[8,64]{1,0:T(8,128)S(1)} %copy-done.3, ...), custom_call_target="tpu_custom_call" | custom-call | flops 16777216 | tf_op jit(solution)/shard_map/pallas_call | solution.py:550
  4.6 0.0 copy-start.1
  4.6 0.0 copy-start.2
  4.6 0.0 copy-start.6
  4.6 0.0 collective-permute-done.halo_a
  4.6 2.6 %collective-permute-done.1.halo_b = f32[21,8,128]{2,1,0:T(8,128)S(1)} collective-permute-done((f32[21,8,128]{2,1,0:T(8,128)S(1)}, f32[21,8,128]{2,1,0:T(8,128)S(1)}, u32[]{:S(2)}, u32[]{:S(2)}) %collective-permute-start.1) | collective-permute-done | bytes 86048 | tf_op jit(solution)/shard_map/ppermute | solution.py:569
  7.2 0.3 shard_map.75
  7.5 1.4 %collective-permute-start.2 = (f32[23,8,128]{2,1,0:T(8,128)S(1)}, f32[23,8,128]{2,1,0:T(8,128)S(1)}, u32[]{:S(2)}, u32[]{:S(2)}) collective-permute-start(f32[23,8,128]{2,1,0:T(8,128)S(1)} %get-tuple-element.45), channel_id=1, source_target_pairs={{0,8},{8,0},{16,24},{24,16},{1,9},{9,1},{17,25},{25,17},{2,10},{10... | collective-permute-start | bytes 282632 | tf_op jit(solution)/shard_map/ppermute | solution.py:596
  8.9 1.5 %collective-permute-start.4 = (f32[21,8,128]{2,1,0:T(8,128)S(1)}, f32[21,8,128]{2,1,0:T(8,128)S(1)}, u32[]{:S(2)}, u32[]{:S(2)}) collective-permute-start(f32[21,8,128]{2,1,0:T(8,128)S(1)} %get-tuple-element.56), channel_id=1, source_target_pairs={{8,16},{16,8},{24,0},{0,24},{9,17},{17,9},{25,1},{1,25},{10,18},{1... | collective-permute-start | bytes 258056 | tf_op jit(solution)/shard_map/ppermute | solution.py:595
  10.5 1.4 %collective-permute-start.3 = (f32[3,8,128]{2,1,0:T(8,128)S(1)}, f32[3,8,128]{2,1,0:T(8,128)S(1)}, u32[]{:S(2)}, u32[]{:S(2)}) collective-permute-start(f32[3,8,128]{2,1,0:T(8,128)S(1)} %get-tuple-element.55), channel_id=1, source_target_pairs={{8,16},{16,8},{24,0},{0,24},{9,17},{17,9},{25,1},{1,25},{10,18},{1... | collective-permute-start | bytes 36872 | tf_op jit(solution)/shard_map/ppermute | solution.py:598
  11.8 0.0 copy-done.1
  11.8 0.0 copy-done.2
  11.8 0.8 %shard_map.76 = (f32[72,768]{1,0:T(8,128)S(1)}, f32[72,768]{1,0:T(8,128)S(1)}, f32[8,768]{1,0:T(8,128)S(1)}, bf16[768,768]{1,0:T(8,128)(2,1)S(1)}) custom-call(f32[18]{0:T(128)S(1)} %copy-done.6, f32[8,768]{1,0:T(8,128)S(1)} %copy-done.2, bf16[648,648]{1,0:T(8,128)(2,1)S(1)} %copy-done.1), custom_call_target="tpu_custom_call" | custom-call | flops 16777216 | tf_op jit(solution)/shard_map/pallas_call | solution.py:550
  12.6 2.4 %collective-permute-done.4.refs_0_ = f32[21,8,128]{2,1,0:T(8,128)S(1)} collective-permute-done((f32[21,8,128]{2,1,0:T(8,128)S(1)}, f32[21,8,128]{2,1,0:T(8,128)S(1)}, u32[]{:S(2)}, u32[]{:S(2)}) %collective-permute-start.4) | collective-permute-done | bytes 86048 | tf_op jit(solution)/shard_map/ppermute | solution.py:595
  15.0 0.3 collective-permute-done.3.corner
  15.3 0.5 %shard_map.78 = (f32[72,768]{1,0:T(8,128)S(1)}, f32[23,8,128]{2,1,0:T(8,128)S(1)}) custom-call(f32[3,8,128]{2,1,0:T(8,128)S(1)} %collective-permute-done.3.corner, f32[21,8,128]{2,1,0:T(8,128)S(1)} %collective-permute-done.4.refs_0_, f32[72,768]{1,0:T(8,128)S(1)} %get-tuple-element.57.refs_1_.edge_b, f32[6,72,768]{2,1,0:T(8,128)S(1)} %get-tuple-element.47.inner.refs_2_, ...), custom_call_target="tpu_custom_call" | custom-call | flops 67108864 | tf_op jit(solution)/shard_map/pallas_call | solution.py:550
  15.8 1.8 %collective-permute-start.6 = (f32[23,8,128]{2,1,0:T(8,128)S(1)}, f32[23,8,128]{2,1,0:T(8,128)S(1)}, u32[]{:S(2)}, u32[]{:S(2)}) collective-permute-start(f32[23,8,128]{2,1,0:T(8,128)S(1)} %get-tuple-element.61), channel_id=1, source_target_pairs={{8,16},{16,8},{24,0},{0,24},{9,17},{17,9},{25,1},{1,25},{10,18},{1... | collective-permute-start | bytes 282632 | tf_op jit(solution)/shard_map/ppermute | solution.py:595
  17.6 0.0 collective-permute-done.2.halo
  17.6 0.5 %shard_map.77 = (f32[72,768]{1,0:T(8,128)S(1)}, f32[23,8,128]{2,1,0:T(8,128)S(1)}) custom-call(f32[23,8,128]{2,1,0:T(8,128)S(1)} %collective-permute-done.2.halo, f32[72,768]{1,0:T(8,128)S(1)} %get-tuple-element.46.edge.edge_a, f32[6,72,768]{2,1,0:T(8,128)S(1)} %get-tuple-element.47.inner.refs_2_, f32[8,72,128]{2,1,0:T(8,128)S(1)} %get-tuple-element.48.seas.refs_3_, ...), custom_call_target="tpu_custom_call" | custom-call | flops 67108864 | tf_op jit(solution)/shard_map/pallas_call | solution.py:550
  18.2 1.5 %collective-permute-start.5 = (f32[23,8,128]{2,1,0:T(8,128)S(1)}, f32[23,8,128]{2,1,0:T(8,128)S(1)}, u32[]{:S(2)}, u32[]{:S(2)}) collective-permute-start(f32[23,8,128]{2,1,0:T(8,128)S(1)} %get-tuple-element.59), channel_id=1, source_target_pairs={{0,8},{8,0},{16,24},{24,16},{1,9},{9,1},{17,25},{25,17},{2,10},{10... | collective-permute-start | bytes 282632 | tf_op jit(solution)/shard_map/ppermute | solution.py:596
  19.7 1.2 %shard_map.79.inner.refs_2_ = f32[6,72,768]{2,1,0:T(8,128)S(1)} custom-call(f32[72,768]{1,0:T(8,128)S(1)} %get-tuple-element.46.edge.edge_a, f32[72,768]{1,0:T(8,128)S(1)} %get-tuple-element.57.refs_1_.edge_b, f32[6,72,768]{2,1,0:T(8,128)S(1)} %get-tuple-element.47.inner.refs_2_, f32[8,72,128]{2,1,0:T(8,128)S(1)} %get-tuple-element.48.seas.refs_3_, ...), custom_call_target="tpu_custom_call" | custom-call | flops 268435456 | tf_op jit(solution)/shard_map/pallas_call | solution.py:550
  20.9 1.2 %shard_map.80.after.inner.refs_2_ = f32[6,72,768]{2,1,0:T(8,128)S(1)} custom-call(f32[72,768]{1,0:T(8,128)S(1)} %get-tuple-element.54.edge_a.refs_1_, f32[72,768]{1,0:T(8,128)S(1)} %get-tuple-element.58.edge_b.refs_1_, f32[6,72,768]{2,1,0:T(8,128)S(1)} %shard_map.79.inner.refs_2_, f32[8,72,128]{2,1,0:T(8,128)S(1)} %get-tuple-element.48.seas.refs_3_, ...), custom_call_target="tpu_custom_call" | custom-call | flops 268435456 | tf_op jit(solution)/shard_map/pallas_call | solution.py:550
  22.2 0.0 collective-permute-done.6.refs_0_
  22.2 0.5 %shard_map.82 = (f32[72,768]{1,0:T(8,128)S(1)}, f32[23,8,128]{2,1,0:T(8,128)S(1)}) custom-call(f32[6,72,768]{2,1,0:T(8,128)S(1)} %shard_map.80.after.inner.refs_2_, f32[23,8,128]{2,1,0:T(8,128)S(1)} %collective-permute-done.6.refs_0_, f32[72,768]{1,0:T(8,128)S(1)} %get-tuple-element.58.edge_b.refs_1_, f32[6,72,768]{2,1,0:T(8,128)S(1)} %shard_map.79.inner.refs_2_, ...), custom_call_target="tpu_custom_call" | custom-call | flops 67108864 | tf_op jit(solution)/shard_map/pallas_call | solution.py:550
  22.7 1.8 %collective-permute-start.9 = (f32[23,8,128]{2,1,0:T(8,128)S(1)}, f32[23,8,128]{2,1,0:T(8,128)S(1)}, u32[]{:S(2)}, u32[]{:S(2)}) collective-permute-start(f32[23,8,128]{2,1,0:T(8,128)S(1)} %get-tuple-element.66), channel_id=1, source_target_pairs={{8,16},{16,8},{24,0},{0,24},{9,17},{17,9},{25,1},{1,25},{10,18},{1... | collective-permute-start | bytes 282632 | tf_op jit(solution)/shard_map/ppermute | solution.py:595
  24.5 0.0 collective-permute-done.5.refs_0_
  24.5 0.5 %shard_map.81 = (f32[72,768]{1,0:T(8,128)S(1)}, f32[23,8,128]{2,1,0:T(8,128)S(1)}) custom-call(f32[6,72,768]{2,1,0:T(8,128)S(1)} %shard_map.80.after.inner.refs_2_, f32[23,8,128]{2,1,0:T(8,128)S(1)} %collective-permute-done.5.refs_0_, f32[72,768]{1,0:T(8,128)S(1)} %get-tuple-element.54.edge_a.refs_1_, f32[6,72,768]{2,1,0:T(8,128)S(1)} %shard_map.79.inner.refs_2_, ...), custom_call_target="tpu_custom_call" | custom-call | flops 67108864 | tf_op jit(solution)/shard_map/pallas_call | solution.py:550
  25.1 1.5 %collective-permute-start.7 = (f32[23,8,128]{2,1,0:T(8,128)S(1)}, f32[23,8,128]{2,1,0:T(8,128)S(1)}, u32[]{:S(2)}, u32[]{:S(2)}) collective-permute-start(f32[23,8,128]{2,1,0:T(8,128)S(1)} %get-tuple-element.63), channel_id=1, source_target_pairs={{0,8},{8,0},{16,24},{24,16},{1,9},{9,1},{17,25},{25,17},{2,10},{10... | collective-permute-start | bytes 282632 | tf_op jit(solution)/shard_map/ppermute | solution.py:596
  26.7 1.2 %shard_map.83.after.inner.refs_2_ = f32[6,72,768]{2,1,0:T(8,128)S(1)} custom-call(f32[72,768]{1,0:T(8,128)S(1)} %get-tuple-element.60.edge_a.refs_1_, f32[72,768]{1,0:T(8,128)S(1)} %get-tuple-element.62.edge_b.refs_1_, f32[6,72,768]{2,1,0:T(8,128)S(1)} %shard_map.80.after.inner.refs_2_, f32[8,72,128]{2,1,0:T(8,128)S(1)} %get-tuple-element.48.seas.refs_3_, ...), custom_call_target="tpu_custom_call" | custom-call | flops 268435456 | tf_op jit(solution)/shard_map/pallas_call | solution.py:550
  27.9 0.4 collective-permute-done.9.refs_0_
  28.3 0.5 %shard_map.85 = (f32[72,768]{1,0:T(8,128)S(1)}, f32[21,8,128]{2,1,0:T(8,128)S(1)}) custom-call(f32[6,72,768]{2,1,0:T(8,128)S(1)} %shard_map.83.after.inner.refs_2_, f32[23,8,128]{2,1,0:T(8,128)S(1)} %collective-permute-done.9.refs_0_, f32[72,768]{1,0:T(8,128)S(1)} %get-tuple-element.62.edge_b.refs_1_, f32[6,72,768]{2,1,0:T(8,128)S(1)} %shard_map.80.after.inner.refs_2_, ...), custom_call_target="tpu_custom_call" | custom-call | flops 67108864 | tf_op jit(solution)/shard_map/pallas_call | solution.py:550
  28.8 1.8 %collective-permute-start.10 = (f32[21,8,128]{2,1,0:T(8,128)S(1)}, f32[21,8,128]{2,1,0:T(8,128)S(1)}, u32[]{:S(2)}, u32[]{:S(2)}) collective-permute-start(f32[21,8,128]{2,1,0:T(8,128)S(1)} %get-tuple-element.68), channel_id=1, source_target_pairs={{8,16},{16,8},{24,0},{0,24},{9,17},{17,9},{25,1},{1,25},{10,18},{1... | collective-permute-start | bytes 258056 | tf_op jit(solution)/shard_map/ppermute | solution.py:595
  30.6 0.0 collective-permute-done.7.refs_0_
  30.6 0.6 %shard_map.84 = (f32[72,768]{1,0:T(8,128)S(1)}, f32[21,8,128]{2,1,0:T(8,128)S(1)}) custom-call(f32[6,72,768]{2,1,0:T(8,128)S(1)} %shard_map.83.after.inner.refs_2_, f32[23,8,128]{2,1,0:T(8,128)S(1)} %collective-permute-done.7.refs_0_, f32[72,768]{1,0:T(8,128)S(1)} %get-tuple-element.60.edge_a.refs_1_, f32[6,72,768]{2,1,0:T(8,128)S(1)} %shard_map.80.after.inner.refs_2_, ...), custom_call_target="tpu_custom_call" | custom-call | flops 67108864 | tf_op jit(solution)/shard_map/pallas_call | solution.py:550
  31.2 1.5 %collective-permute-start.8 = (f32[21,8,128]{2,1,0:T(8,128)S(1)}, f32[21,8,128]{2,1,0:T(8,128)S(1)}, u32[]{:S(2)}, u32[]{:S(2)}) collective-permute-start(f32[21,8,128]{2,1,0:T(8,128)S(1)} %get-tuple-element.64), channel_id=1, source_target_pairs={{0,8},{8,0},{16,24},{24,16},{1,9},{9,1},{17,25},{25,17},{2,10},{10... | collective-permute-start | bytes 258056 | tf_op jit(solution)/shard_map/ppermute | solution.py:596
  32.7 1.1 %shard_map.86.after.done_inner = f32[6,64,648]{2,1,0:T(8,128)S(1)} custom-call(f32[72,768]{1,0:T(8,128)S(1)} %get-tuple-element.65.edge_a.edge, f32[72,768]{1,0:T(8,128)S(1)} %get-tuple-element.67.edge_b.refs_1_, f32[6,72,768]{2,1,0:T(8,128)S(1)} %shard_map.83.after.inner.refs_2_, f32[8,72,128]{2,1,0:T(8,128)S(1)} %get-tuple-element.48.seas.refs_3_, ...), custom_call_target="tpu_custom_call" | custom-call | flops 268435456 | tf_op jit(solution)/shard_map/pallas_call | solution.py:550
  33.9 0.4 %collective-permute-done.10.refs_0_ = f32[21,8,128]{2,1,0:T(8,128)S(1)} collective-permute-done((f32[21,8,128]{2,1,0:T(8,128)S(1)}, f32[21,8,128]{2,1,0:T(8,128)S(1)}, u32[]{:S(2)}, u32[]{:S(2)}) %collective-permute-start.10) | collective-permute-done | bytes 86048 | tf_op jit(solution)/shard_map/ppermute | solution.py:595
  34.2 0.5 %shard_map.87.done_edge = f32[64,648]{1,0:T(8,128)S(1)} custom-call(f32[6,64,648]{2,1,0:T(8,128)S(1)} %shard_map.86.after.done_inner, f32[21,8,128]{2,1,0:T(8,128)S(1)} %collective-permute-done.10.refs_0_, f32[72,768]{1,0:T(8,128)S(1)} %get-tuple-element.67.edge_b.refs_1_, f32[6,72,768]{2,1,0:T(8,128)S(1)} %shard_map.83.after.inner.refs_2_, ...), custom_call_target="tpu_custom_call" | custom-call | flops 67108864 | tf_op jit(solution)/shard_map/pallas_call | solution.py:550
  34.8 1.0 %collective-permute-done.8.halo = f32[21,8,128]{2,1,0:T(8,128)S(1)} collective-permute-done((f32[21,8,128]{2,1,0:T(8,128)S(1)}, f32[21,8,128]{2,1,0:T(8,128)S(1)}, u32[]{:S(2)}, u32[]{:S(2)}) %collective-permute-start.8) | collective-permute-done | bytes 86048 | tf_op jit(solution)/shard_map/ppermute | solution.py:596
  35.8 1.2 %shard_map.88 = f32[8,64,648]{2,1,0:T(8,128)} custom-call(f32[21,8,128]{2,1,0:T(8,128)S(1)} %collective-permute-done.8.halo, f32[72,768]{1,0:T(8,128)S(1)} %get-tuple-element.65.edge_a.edge, f32[6,72,768]{2,1,0:T(8,128)S(1)} %shard_map.83.after.inner.refs_2_, f32[8,72,128]{2,1,0:T(8,128)S(1)} %get-tuple-element.48.seas.refs_3_, ...), custom_call_target="tpu_custom_call" | custom-call | flops 67108864 | tf_op jit(solution)/shard_map/pallas_call | solution.py:550
  (4 shorter events, 0.0 us)
Async XLA Ops:
  0.0 3.8 %copy-start.5 = (f32[8,64]{1,0:T(8,128)S(1)}, f32[8,64]{1,0:T(8,128)}, u32[]{:S(2)}) copy-start(f32[8,64]{1,0:T(8,128)} %wind_ref.1) | copy-start | bytes 6148
  0.0 3.8 %copy-start = (f32[8,64,648]{2,1,0:T(8,128)S(1)}, f32[8,64,648]{2,1,0:T(8,128)}, u32[]{:S(2)}) copy-start(f32[8,64,648]{2,1,0:T(8,128)} %spectrum.3) | copy-start | bytes 3981316
  0.0 3.8 %copy-start.3 = (s32[8,64]{1,0:T(8,128)S(1)}, s32[8,64]{1,0:T(8,128)}, u32[]{:S(2)}) copy-start(s32[8,64]{1,0:T(8,128)} %sea_ref.1) | copy-start | bytes 6148
  0.0 3.8 %copy-start.4 = (s32[8,64]{1,0:T(8,128)S(1)}, s32[8,64]{1,0:T(8,128)}, u32[]{:S(2)}) copy-start(s32[8,64]{1,0:T(8,128)} %ice_ref.1) | copy-start | bytes 6148
  1.3 3.3 %collective-permute-start = (f32[21,8,128]{2,1,0:T(8,128)S(1)}, f32[21,8,128]{2,1,0:T(8,128)S(1)}, u32[]{:S(2)}, u32[]{:S(2)}) collective-permute-start(f32[21,8,128]{2,1,0:T(8,128)S(1)} %get-tuple-element.37), channel_id=1, source_target_pairs={{0,1},{1,0},{2,3},{3,2},{4,5},{5,4},{6,7},{7,6},{8,9},{9,8},{10,11... | collective-permute-start | bytes 258056 | tf_op jit(solution)/shard_map/ppermute | solution.py:570
  1.4 5.8 %collective-permute-start.1 = (f32[21,8,128]{2,1,0:T(8,128)S(1)}, f32[21,8,128]{2,1,0:T(8,128)S(1)}, u32[]{:S(2)}, u32[]{:S(2)}) collective-permute-start(f32[21,8,128]{2,1,0:T(8,128)S(1)} %get-tuple-element.38), channel_id=1, source_target_pairs={{1,2},{2,1},{3,4},{4,3},{5,6},{6,5},{9,10},{10,9},{11,12},{12,11},... | collective-permute-start | bytes 258056 | tf_op jit(solution)/shard_map/ppermute | solution.py:569
  4.6 7.3 %copy-start.1 = (bf16[648,648]{1,0:T(8,128)(2,1)S(1)}, bf16[648,648]{1,0:T(8,128)(2,1)}, u32[]{:S(2)}) copy-start(bf16[648,648]{1,0:T(8,128)(2,1)} %coupling_ref.1) | copy-start | bytes 2519428
  4.6 7.3 %copy-start.2 = (f32[8,768]{1,0:T(8,128)S(1)}, f32[8,768]{1,0:T(8,128)}, u32[]{:S(2)}) copy-start(f32[8,768]{1,0:T(8,128)} %constant.2.clone.angle_ref) | copy-start | bytes 73732
  4.6 7.3 %copy-start.6 = (f32[18]{0:T(128)S(1)}, f32[18]{0:T(128)}, u32[]{:S(2)}) copy-start(f32[18]{0:T(128)} %speed_ref.1) | copy-start | bytes 220
  7.5 10.1 %collective-permute-start.2 = (f32[23,8,128]{2,1,0:T(8,128)S(1)}, f32[23,8,128]{2,1,0:T(8,128)S(1)}, u32[]{:S(2)}, u32[]{:S(2)}) collective-permute-start(f32[23,8,128]{2,1,0:T(8,128)S(1)} %get-tuple-element.45), channel_id=1, source_target_pairs={{0,8},{8,0},{16,24},{24,16},{1,9},{9,1},{17,25},{25,17},{2,10},{10... | collective-permute-start | bytes 282632 | tf_op jit(solution)/shard_map/ppermute | solution.py:596
  8.9 6.1 %collective-permute-start.4 = (f32[21,8,128]{2,1,0:T(8,128)S(1)}, f32[21,8,128]{2,1,0:T(8,128)S(1)}, u32[]{:S(2)}, u32[]{:S(2)}) collective-permute-start(f32[21,8,128]{2,1,0:T(8,128)S(1)} %get-tuple-element.56), channel_id=1, source_target_pairs={{8,16},{16,8},{24,0},{0,24},{9,17},{17,9},{25,1},{1,25},{10,18},{1... | collective-permute-start | bytes 258056 | tf_op jit(solution)/shard_map/ppermute | solution.py:595
  10.5 4.8 %collective-permute-start.3 = (f32[3,8,128]{2,1,0:T(8,128)S(1)}, f32[3,8,128]{2,1,0:T(8,128)S(1)}, u32[]{:S(2)}, u32[]{:S(2)}) collective-permute-start(f32[3,8,128]{2,1,0:T(8,128)S(1)} %get-tuple-element.55), channel_id=1, source_target_pairs={{8,16},{16,8},{24,0},{0,24},{9,17},{17,9},{25,1},{1,25},{10,18},{1... | collective-permute-start | bytes 36872 | tf_op jit(solution)/shard_map/ppermute | solution.py:598
  15.8 6.3 %collective-permute-start.6 = (f32[23,8,128]{2,1,0:T(8,128)S(1)}, f32[23,8,128]{2,1,0:T(8,128)S(1)}, u32[]{:S(2)}, u32[]{:S(2)}) collective-permute-start(f32[23,8,128]{2,1,0:T(8,128)S(1)} %get-tuple-element.61), channel_id=1, source_target_pairs={{8,16},{16,8},{24,0},{0,24},{9,17},{17,9},{25,1},{1,25},{10,18},{1... | collective-permute-start | bytes 282632 | tf_op jit(solution)/shard_map/ppermute | solution.py:595
  18.2 6.4 %collective-permute-start.5 = (f32[23,8,128]{2,1,0:T(8,128)S(1)}, f32[23,8,128]{2,1,0:T(8,128)S(1)}, u32[]{:S(2)}, u32[]{:S(2)}) collective-permute-start(f32[23,8,128]{2,1,0:T(8,128)S(1)} %get-tuple-element.59), channel_id=1, source_target_pairs={{0,8},{8,0},{16,24},{24,16},{1,9},{9,1},{17,25},{25,17},{2,10},{10... | collective-permute-start | bytes 282632 | tf_op jit(solution)/shard_map/ppermute | solution.py:596
  22.7 5.5 %collective-permute-start.9 = (f32[23,8,128]{2,1,0:T(8,128)S(1)}, f32[23,8,128]{2,1,0:T(8,128)S(1)}, u32[]{:S(2)}, u32[]{:S(2)}) collective-permute-start(f32[23,8,128]{2,1,0:T(8,128)S(1)} %get-tuple-element.66), channel_id=1, source_target_pairs={{8,16},{16,8},{24,0},{0,24},{9,17},{17,9},{25,1},{1,25},{10,18},{1... | collective-permute-start | bytes 282632 | tf_op jit(solution)/shard_map/ppermute | solution.py:595
  25.1 5.5 %collective-permute-start.7 = (f32[23,8,128]{2,1,0:T(8,128)S(1)}, f32[23,8,128]{2,1,0:T(8,128)S(1)}, u32[]{:S(2)}, u32[]{:S(2)}) collective-permute-start(f32[23,8,128]{2,1,0:T(8,128)S(1)} %get-tuple-element.63), channel_id=1, source_target_pairs={{0,8},{8,0},{16,24},{24,16},{1,9},{9,1},{17,25},{25,17},{2,10},{10... | collective-permute-start | bytes 282632 | tf_op jit(solution)/shard_map/ppermute | solution.py:596
  28.8 5.4 %collective-permute-start.10 = (f32[21,8,128]{2,1,0:T(8,128)S(1)}, f32[21,8,128]{2,1,0:T(8,128)S(1)}, u32[]{:S(2)}, u32[]{:S(2)}) collective-permute-start(f32[21,8,128]{2,1,0:T(8,128)S(1)} %get-tuple-element.68), channel_id=1, source_target_pairs={{8,16},{16,8},{24,0},{0,24},{9,17},{17,9},{25,1},{1,25},{10,18},{1... | collective-permute-start | bytes 258056 | tf_op jit(solution)/shard_map/ppermute | solution.py:595
  31.2 4.6 %collective-permute-start.8 = (f32[21,8,128]{2,1,0:T(8,128)S(1)}, f32[21,8,128]{2,1,0:T(8,128)S(1)}, u32[]{:S(2)}, u32[]{:S(2)}) collective-permute-start(f32[21,8,128]{2,1,0:T(8,128)S(1)} %get-tuple-element.64), channel_id=1, source_target_pairs={{0,8},{8,0},{16,24},{24,16},{1,9},{9,1},{17,25},{25,17},{2,10},{10... | collective-permute-start | bytes 258056 | tf_op jit(solution)/shard_map/ppermute | solution.py:596

commit v8 on v7

--- a/solution.py
+++ b/solution.py
@@ -407,11 +407,7 @@
         on_each_side(second, side)
 
 
-def combine(adv, product, seas, gains, share):
-    return adv * (gains - seas * share) + seas * product
-
-
-def first_edge_kernel(bins, second, corner, *refs):
+def ordered_first_kernel(bins, second, after, corner, *refs):
     edge_kernel(bins, second, *refs, corner=corner)
 
 
@@ -476,46 +472,70 @@
         here = lanes_of(t)
         adv = advect(edge[:, here], across[t], stay[:, here], go_x[:, here], go_y[0:1, here], bins, t)
         adv_ref[:used, here] = adv[:used]
-    product = jnp.dot(adv_ref[:used].astype(jnp.bfloat16), wide[...], preferred_element_type=jnp.float32)
-    share = jnp.broadcast_to(product[:, -1:], (used, LANES)) * (dissipation / bins)
+    low = adv_ref[:used].astype(jnp.bfloat16)
     s, g = seas[mine, :used], gains[mine, :used]
-    return [combine(adv_ref[:used, lanes_of(t)], product[:, lanes_of(t)], s, g, share) for t in range(tiles)]
-
-
-def inner_kernel(bins, edge_a, edge_b, inner, seas, gains, stay, go_x, go_y, wide, out, adv_ref, low_ref):
+    fresh = [None] * tiles
+    keep = None
+    for block in lane_blocks(tiles):
+        product = jnp.dot(low, wide[:, block[0] * LANES : (block[-1] + 1) * LANES], preferred_element_type=jnp.float32)
+        if keep is None:
+            share = jnp.broadcast_to(product[:, -1:], (used, LANES)) * (dissipation / bins)
+            keep = g - s * share
+        for k, t in enumerate(block):
+            fresh[t] = adv_ref[:used, lanes_of(t)] * keep + s * product[:, lanes_of(k)]
+    return fresh
+
+
+def lane_blocks(tiles):
+    return [(t - 1, t) for t in range(tiles - 1, 0, -2)]
+
+
+def inner_kernel(bins, edge_a, edge_b, inner, seas, gains, stay, go_x, go_y, wide, out, adv_ref, low_ref, keep_ref):
     tiles = lane_tiles(bins)
     count, tall = inner.shape[0], inner.shape[1]
-    rows = adv_ref.shape[1]
+    rows = adv_ref.shape[0] // count
     a_west = west_flag(False)
-    for t in range(tiles):
-        here = lanes_of(t)
-        found = kinds(bins, t, is_east(bins))
-        for c in range(count):
-            west = east = None
-            if True in found:
-                west = inner[c - 1, :, here] if c else jnp.where(a_west, edge_a[:, here], edge_b[:, here])
-            if False in found:
-                east = inner[c + 1, :, here] if c < count - 1 else jnp.where(a_west, edge_b[:, here], edge_a[:, here])
-            if west is None:
-                across = east
-            elif east is None:
-                across = west
-            else:
-                across = jnp.where(eastward(bins, t, (tall, LANES)), west, east)
-            adv = advect(inner[c, :, here], across, stay[:, here], go_x[:, here], go_y[0:1, here], bins, t)[:rows]
-            adv_ref[c, :, here] = adv
-            low_ref[c * rows : (c + 1) * rows, here] = adv.astype(jnp.bfloat16)
-    product = jnp.dot(low_ref[...], wide[...], preferred_element_type=jnp.float32)
-    for c in range(count):
-        part = product[c * rows : (c + 1) * rows]
-        share = jnp.broadcast_to(part[:, -1:], (rows, LANES)) * (dissipation / bins)
+    parts = 2
+    if count % parts:
+        parts = 1
+    for part in range(parts):
+        group = range(part * count // parts, (part + 1) * count // parts)
+        whole = slice(group[0] * rows, (group[-1] + 1) * rows)
         for t in range(tiles):
             here = lanes_of(t)
-            value = combine(adv_ref[c, :, here], part[:, here], seas[c + 1, :rows], gains[c + 1, :rows], share)
-            if rows == tall:
-                out[c, :, here] = value
-            else:
-                write_tile(out, (c,), bins, t, value)
+            found = kinds(bins, t, is_east(bins))
+            for c in group:
+                west = east = None
+                if True in found:
+                    west = inner[c - 1, :, here] if c else jnp.where(a_west, edge_a[:, here], edge_b[:, here])
+                if False in found:
+                    east = inner[c + 1, :, here] if c < count - 1 else jnp.where(a_west, edge_b[:, here], edge_a[:, here])
+                if west is None:
+                    across = east
+                elif east is None:
+                    across = west
+                else:
+                    across = jnp.where(eastward(bins, t, (tall, LANES)), west, east)
+                adv = advect(inner[c, :, here], across, stay[:, here], go_x[:, here], go_y[0:1, here], bins, t)[:rows]
+                adv_ref[c * rows : (c + 1) * rows, here] = adv
+        low_ref[whole] = adv_ref[whole].astype(jnp.bfloat16)
+        for block in lane_blocks(tiles):
+            product = jnp.dot(
+                low_ref[whole], wide[:, block[0] * LANES : (block[-1] + 1) * LANES], preferred_element_type=jnp.float32
+            )
+            for c in group:
+                span = slice(c * rows, (c + 1) * rows)
+                mine = slice((c - group[0]) * rows, (c - group[0] + 1) * rows)
+                s = seas[c + 1, :rows]
+                if block[-1] == tiles - 1:
+                    share = jnp.broadcast_to(product[mine, -1:], (rows, LANES)) * (dissipation / bins)
+                    keep_ref[span] = gains[c + 1, :rows] - s * share
+                for k, t in enumerate(block):
+                    value = adv_ref[span, lanes_of(t)] * keep_ref[span] + s * product[mine, lanes_of(k)]
+                    if rows == tall:
+                        out[c, :, lanes_of(t)] = value
+                    else:
+                        write_tile(out, (c,), bins, t, value)
 
 
 def angle_table(bins, freqs):
@@ -600,7 +620,8 @@
         new_inner = call(
             functools.partial(inner_kernel, bins), VMEM((columns - 2, rows, bins), f32) if last else inner_shape,
             (edge_a, edge_b, inner) + tables, [vmem] * 9,
-            [VMEM((columns - 2, used, padded), f32), VMEM(((columns - 2) * used, padded), jnp.bfloat16)],
+            [VMEM(((columns - 2) * used, padded), f32), VMEM(((columns - 2) * used, padded), jnp.bfloat16),
+             VMEM(((columns - 2) * used, LANES), f32)],
             flops=1 << 28,
         )
         if last:
@@ -622,7 +643,7 @@
             if step > 0:
                 body, ins = ordered_edge_kernel, (new_inner,) + ins
             elif second:
-                body, ins = first_edge_kernel, (corner,) + ins
+                body, ins = ordered_first_kernel, (new_inner, corner) + ins
             fresh.append(call(
                 functools.partial(body, bins, second), (edge_shape, pack_next),
                 ins, [vmem] * len(ins), [VMEM((tall, padded), f32)], flops=1 << 26,

time: 37.1 us -> 36.9 us (level)
  waiting for transfers between devices: 6.97 us -> 10.3 us
  starting transfers between devices: 16.9 us -> 14.9 us
  Pallas kernels: 12.8 us -> 11.3 us
    ppermute x4, waiting for transfers between devices: 3.11 us -> 5.78 us  [steps(): halo_b = lax.ppermute(pack_b, 'lon', lon_b)]
    ppermute x4, starting transfers between devices: 7.01 us -> 5.42 us  [steps(): halo_b = lax.ppermute(pack_b, 'lon', lon_b)]
    pallas_call x16, Pallas kernels: 12.8 us -> 11.3 us  [call(): pl.pallas_call(body, out_shape=outs, in_specs=specs, out_specs=out_specs...]
    ppermute x1, waiting for transfers between devices: 0.26 us -> 1.63 us  [steps(): corner = lax.ppermute(corner_b, 'lon', lon_b)]
    ppermute x4, waiting for transfers between devices: 1.02 us -> 0.33 us  [steps(): halo_a = lax.ppermute(pack_a, 'lon', lon_a)]
    ppermute x4, starting transfers between devices: 5.98 us -> 5.51 us  [steps(): halo_a = lax.ppermute(pack_a, 'lon', lon_a)]
  transfers between devices with their start and end apart: 11 -> 11, of which waited for: 6 -> 7; matrix products, arithmetic and copies ran while one was open for 0% -> 0% of each run, Pallas kernels for 27% -> 23%
where the time goes in v8:
time: 36.9 us; the launch traced here: 36.8 us
  starting transfers between devices  14.9 us (40%)
  Pallas kernels  11.3 us (31%)
  waiting for transfers between devices  10.3 us (28%)
    pallas_call x16, Pallas kernels, call(): pl.pallas_call(body, out_shape=outs, in_specs=specs, out_specs=out_specs...  11.3 us
    ppermute x4, waiting for transfers between devices, steps(): halo_b = lax.ppermute(pack_b, 'lon', lon_b)  5.78 us
    ppermute x4, starting transfers between devices, steps(): halo_a = lax.ppermute(pack_a, 'lon', lon_a)  5.51 us
    ppermute x4, starting transfers between devices, steps(): halo_b = lax.ppermute(pack_b, 'lon', lon_b)  5.42 us
    ppermute x1, waiting for transfers between devices, steps(): halo_b = lax.ppermute(send_b, 'lat', lat_b)  2.57 us
    ppermute x1, starting transfers between devices, steps(): halo_b = lax.ppermute(send_b, 'lat', lat_b)  2.45 us
    ppermute x1, waiting for transfers between devices, steps(): corner = lax.ppermute(corner_b, 'lon', lon_b)  1.63 us
    ppermute x1, starting transfers between devices, steps(): corner = lax.ppermute(corner_b, 'lon', lon_b)  1.44 us
  transfers between devices with their start and end apart: 11, of which 7 were waited for; matrix products, arithmetic and copies ran while one was open for 0% of the time, Pallas kernels for 23%

profile of v8, /device:TPU:24, one launch (start us, length us, event | category | flops | bytes accessed | tf_op | source)
XLA Modules:
  0.0 36.8 jit_solution(5731208232397982603)
XLA Ops:
  0.0 0.0 copy-start.4
  0.0 1.3 %shard_map.73 = (f32[21,8,128]{2,1,0:T(8,128)S(1)}, f32[21,8,128]{2,1,0:T(8,128)S(1)}) custom-call(f32[8,64,648]{2,1,0:T(8,128)} %spectrum.3, s32[8,64]{1,0:T(8,128)} %sea_ref.1, s32[8,64]{1,0:T(8,128)} %ice_ref.1, f32[8,64]{1,0:T(8,128)} %wind_ref.1), custom_call_target="tpu_custom_call" | custom-call | tf_op jit(solution)/shard_map/pallas_call | solution.py:570
  1.3 0.1 collective-permute-start
  1.4 2.4 %collective-permute-start.1 = (f32[21,8,128]{2,1,0:T(8,128)S(1)}, f32[21,8,128]{2,1,0:T(8,128)S(1)}, u32[]{:S(2)}, u32[]{:S(2)}) collective-permute-start(f32[21,8,128]{2,1,0:T(8,128)S(1)} %get-tuple-element.38), channel_id=1, source_target_pairs={{1,2},{2,1},{3,4},{4,3},{5,6},{6,5},{9,10},{10,9},{11,12},{12,11},... | collective-permute-start | bytes 258056 | tf_op jit(solution)/shard_map/ppermute | solution.py:589
  3.8 0.0 copy-done.5
  3.8 0.0 copy-done
  3.8 0.0 copy-done.3
  3.9 0.0 copy-done.4
  3.9 0.7 %shard_map.74 = (f32[72,768]{1,0:T(8,128)S(1)}, f32[72,768]{1,0:T(8,128)S(1)}, f32[6,72,768]{2,1,0:T(8,128)S(1)}, f32[8,72,128]{2,1,0:T(8,128)S(1)}, f32[8,72,12...) custom-call(f32[8,64,648]{2,1,0:T(8,128)S(1)} %copy-done, s32[8,64]{1,0:T(8,128)S(1)} %copy-done.3, ...), custom_call_target="tpu_custom_call" | custom-call | flops 16777216 | tf_op jit(solution)/shard_map/pallas_call | solution.py:570
  4.6 0.0 copy-start.1
  4.6 0.0 copy-start.2
  4.6 0.0 copy-start.6
  4.6 0.0 collective-permute-done.halo_a
  4.6 2.6 %collective-permute-done.1.halo_b = f32[21,8,128]{2,1,0:T(8,128)S(1)} collective-permute-done((f32[21,8,128]{2,1,0:T(8,128)S(1)}, f32[21,8,128]{2,1,0:T(8,128)S(1)}, u32[]{:S(2)}, u32[]{:S(2)}) %collective-permute-start.1) | collective-permute-done | bytes 86048 | tf_op jit(solution)/shard_map/ppermute | solution.py:589
  7.2 0.3 shard_map.75
  7.5 1.4 %collective-permute-start.2 = (f32[23,8,128]{2,1,0:T(8,128)S(1)}, f32[23,8,128]{2,1,0:T(8,128)S(1)}, u32[]{:S(2)}, u32[]{:S(2)}) collective-permute-start(f32[23,8,128]{2,1,0:T(8,128)S(1)} %get-tuple-element.45), channel_id=1, source_target_pairs={{0,8},{8,0},{16,24},{24,16},{1,9},{9,1},{17,25},{25,17},{2,10},{10... | collective-permute-start | bytes 282632 | tf_op jit(solution)/shard_map/ppermute | solution.py:616
  8.9 1.5 %collective-permute-start.4 = (f32[21,8,128]{2,1,0:T(8,128)S(1)}, f32[21,8,128]{2,1,0:T(8,128)S(1)}, u32[]{:S(2)}, u32[]{:S(2)}) collective-permute-start(f32[21,8,128]{2,1,0:T(8,128)S(1)} %get-tuple-element.57), channel_id=1, source_target_pairs={{8,16},{16,8},{24,0},{0,24},{9,17},{17,9},{25,1},{1,25},{10,18},{1... | collective-permute-start | bytes 258056 | tf_op jit(solution)/shard_map/ppermute | solution.py:615
  10.5 0.0 copy-done.1
  10.5 0.0 copy-done.6
  10.5 0.8 %shard_map.76 = (f32[72,768]{1,0:T(8,128)S(1)}, f32[72,768]{1,0:T(8,128)S(1)}, f32[8,768]{1,0:T(8,128)S(1)}, bf16[768,768]{1,0:T(8,128)(2,1)S(1)}) custom-call(f32[18]{0:T(128)S(1)} %copy-done.6, f32[8,768]{1,0:T(8,128)S(1)} %copy-done.2, bf16[648,648]{1,0:T(8,128)(2,1)S(1)} %copy-done.1), custom_call_target="tpu_custom_call" | custom-call | flops 16777216 | tf_op jit(solution)/shard_map/pallas_call | solution.py:570
  11.3 1.4 %collective-permute-start.3 = (f32[3,8,128]{2,1,0:T(8,128)S(1)}, f32[3,8,128]{2,1,0:T(8,128)S(1)}, u32[]{:S(2)}, u32[]{:S(2)}) collective-permute-start(f32[3,8,128]{2,1,0:T(8,128)S(1)} %get-tuple-element.56), channel_id=1, source_target_pairs={{8,16},{16,8},{24,0},{0,24},{9,17},{17,9},{25,1},{1,25},{10,18},{1... | collective-permute-start | bytes 36872 | tf_op jit(solution)/shard_map/ppermute | solution.py:618
  12.7 1.0 %shard_map.78.after.inner.refs_2_ = f32[6,72,768]{2,1,0:T(8,128)S(1)} custom-call(f32[72,768]{1,0:T(8,128)S(1)} %get-tuple-element.46.edge.edge_a, f32[72,768]{1,0:T(8,128)S(1)} %get-tuple-element.55.edge_b.refs_1_, f32[6,72,768]{2,1,0:T(8,128)S(1)} %get-tuple-element.47.inner.refs_2_, f32[8,72,128]{2,1,0:T(8,128)S(1)} %get-tuple-element.48.seas.refs_3_, ...), custom_call_target="tpu_custom_call" | custom-call | flops 268435456 | tf_op jit(solution)/shard_map/pallas_call | solution.py:570
  13.7 0.6 %collective-permute-done.4.refs_0_ = f32[21,8,128]{2,1,0:T(8,128)S(1)} collective-permute-done((f32[21,8,128]{2,1,0:T(8,128)S(1)}, f32[21,8,128]{2,1,0:T(8,128)S(1)}, u32[]{:S(2)}, u32[]{:S(2)}) %collective-permute-start.4) | collective-permute-done | bytes 86048 | tf_op jit(solution)/shard_map/ppermute | solution.py:615
  14.3 1.6 %collective-permute-done.3.corner = f32[3,8,128]{2,1,0:T(8,128)S(1)} collective-permute-done((f32[3,8,128]{2,1,0:T(8,128)S(1)}, f32[3,8,128]{2,1,0:T(8,128)S(1)}, u32[]{:S(2)}, u32[]{:S(2)}) %collective-permute-start.3) | collective-permute-done | bytes 12320 | tf_op jit(solution)/shard_map/ppermute | solution.py:618
  15.9 0.5 %shard_map.79 = (f32[72,768]{1,0:T(8,128)S(1)}, f32[23,8,128]{2,1,0:T(8,128)S(1)}) custom-call(f32[6,72,768]{2,1,0:T(8,128)S(1)} %shard_map.78.after.inner.refs_2_, f32[3,8,128]{2,1,0:T(8,128)S(1)} %collective-permute-done.3.corner, f32[21,8,128]{2,1,0:T(8,128)S(1)} %collective-permute-done.4.refs_0_, f32[72,768]{1,0:T(8,128)S(1)} %get-tuple-element.55.edge_b.refs_1_, ...), custom_call_target="tpu_custom_call" | custom-call | flops 67108864 | tf_op jit(solution)/shard_map/pallas_call | solution.py:570
  16.4 1.6 %collective-permute-start.6 = (f32[23,8,128]{2,1,0:T(8,128)S(1)}, f32[23,8,128]{2,1,0:T(8,128)S(1)}, u32[]{:S(2)}, u32[]{:S(2)}) collective-permute-start(f32[23,8,128]{2,1,0:T(8,128)S(1)} %get-tuple-element.61), channel_id=1, source_target_pairs={{8,16},{16,8},{24,0},{0,24},{9,17},{17,9},{25,1},{1,25},{10,18},{1... | collective-permute-start | bytes 282632 | tf_op jit(solution)/shard_map/ppermute | solution.py:615
  18.0 0.0 collective-permute-done.2.halo
  18.0 0.5 %shard_map.77 = (f32[72,768]{1,0:T(8,128)S(1)}, f32[23,8,128]{2,1,0:T(8,128)S(1)}) custom-call(f32[23,8,128]{2,1,0:T(8,128)S(1)} %collective-permute-done.2.halo, f32[72,768]{1,0:T(8,128)S(1)} %get-tuple-element.46.edge.edge_a, f32[6,72,768]{2,1,0:T(8,128)S(1)} %get-tuple-element.47.inner.refs_2_, f32[8,72,128]{2,1,0:T(8,128)S(1)} %get-tuple-element.48.seas.refs_3_, ...), custom_call_target="tpu_custom_call" | custom-call | flops 67108864 | tf_op jit(solution)/shard_map/pallas_call | solution.py:570
  18.5 1.1 %collective-permute-start.5 = (f32[23,8,128]{2,1,0:T(8,128)S(1)}, f32[23,8,128]{2,1,0:T(8,128)S(1)}, u32[]{:S(2)}, u32[]{:S(2)}) collective-permute-start(f32[23,8,128]{2,1,0:T(8,128)S(1)} %get-tuple-element.59), channel_id=1, source_target_pairs={{0,8},{8,0},{16,24},{24,16},{1,9},{9,1},{17,25},{25,17},{2,10},{10... | collective-permute-start | bytes 282632 | tf_op jit(solution)/shard_map/ppermute | solution.py:616
  19.5 1.0 %shard_map.80.after.inner.refs_2_ = f32[6,72,768]{2,1,0:T(8,128)S(1)} custom-call(f32[72,768]{1,0:T(8,128)S(1)} %get-tuple-element.54.edge_a.refs_1_, f32[72,768]{1,0:T(8,128)S(1)} %get-tuple-element.58.edge_b.refs_1_, f32[6,72,768]{2,1,0:T(8,128)S(1)} %shard_map.78.after.inner.refs_2_, f32[8,72,128]{2,1,0:T(8,128)S(1)} %get-tuple-element.48.seas.refs_3_, ...), custom_call_target="tpu_custom_call" | custom-call | flops 268435456 | tf_op jit(solution)/shard_map/pallas_call | solution.py:570
  20.5 2.4 %collective-permute-done.6.refs_0_ = f32[23,8,128]{2,1,0:T(8,128)S(1)} collective-permute-done((f32[23,8,128]{2,1,0:T(8,128)S(1)}, f32[23,8,128]{2,1,0:T(8,128)S(1)}, u32[]{:S(2)}, u32[]{:S(2)}) %collective-permute-start.6) | collective-permute-done | bytes 94240 | tf_op jit(solution)/shard_map/ppermute | solution.py:615
  22.9 0.5 %shard_map.82 = (f32[72,768]{1,0:T(8,128)S(1)}, f32[23,8,128]{2,1,0:T(8,128)S(1)}) custom-call(f32[6,72,768]{2,1,0:T(8,128)S(1)} %shard_map.80.after.inner.refs_2_, f32[23,8,128]{2,1,0:T(8,128)S(1)} %collective-permute-done.6.refs_0_, f32[72,768]{1,0:T(8,128)S(1)} %get-tuple-element.58.edge_b.refs_1_, f32[6,72,768]{2,1,0:T(8,128)S(1)} %shard_map.78.after.inner.refs_2_, ...), custom_call_target="tpu_custom_call" | custom-call | flops 67108864 | tf_op jit(solution)/shard_map/pallas_call | solution.py:570
  23.4 1.2 %collective-permute-start.9 = (f32[23,8,128]{2,1,0:T(8,128)S(1)}, f32[23,8,128]{2,1,0:T(8,128)S(1)}, u32[]{:S(2)}, u32[]{:S(2)}) collective-permute-start(f32[23,8,128]{2,1,0:T(8,128)S(1)} %get-tuple-element.66), channel_id=1, source_target_pairs={{8,16},{16,8},{24,0},{0,24},{9,17},{17,9},{25,1},{1,25},{10,18},{1... | collective-permute-start | bytes 282632 | tf_op jit(solution)/shard_map/ppermute | solution.py:615
  24.6 0.0 collective-permute-done.5.refs_0_
  24.6 0.5 %shard_map.81 = (f32[72,768]{1,0:T(8,128)S(1)}, f32[23,8,128]{2,1,0:T(8,128)S(1)}) custom-call(f32[6,72,768]{2,1,0:T(8,128)S(1)} %shard_map.80.after.inner.refs_2_, f32[23,8,128]{2,1,0:T(8,128)S(1)} %collective-permute-done.5.refs_0_, f32[72,768]{1,0:T(8,128)S(1)} %get-tuple-element.54.edge_a.refs_1_, f32[6,72,768]{2,1,0:T(8,128)S(1)} %shard_map.78.after.inner.refs_2_, ...), custom_call_target="tpu_custom_call" | custom-call | flops 67108864 | tf_op jit(solution)/shard_map/pallas_call | solution.py:570
  25.1 1.5 %collective-permute-start.7 = (f32[23,8,128]{2,1,0:T(8,128)S(1)}, f32[23,8,128]{2,1,0:T(8,128)S(1)}, u32[]{:S(2)}, u32[]{:S(2)}) collective-permute-start(f32[23,8,128]{2,1,0:T(8,128)S(1)} %get-tuple-element.63), channel_id=1, source_target_pairs={{0,8},{8,0},{16,24},{24,16},{1,9},{9,1},{17,25},{25,17},{2,10},{10... | collective-permute-start | bytes 282632 | tf_op jit(solution)/shard_map/ppermute | solution.py:616
  26.6 1.0 %shard_map.83.after.inner.refs_2_ = f32[6,72,768]{2,1,0:T(8,128)S(1)} custom-call(f32[72,768]{1,0:T(8,128)S(1)} %get-tuple-element.60.edge_a.refs_1_, f32[72,768]{1,0:T(8,128)S(1)} %get-tuple-element.62.edge_b.refs_1_, f32[6,72,768]{2,1,0:T(8,128)S(1)} %shard_map.80.after.inner.refs_2_, f32[8,72,128]{2,1,0:T(8,128)S(1)} %get-tuple-element.48.seas.refs_3_, ...), custom_call_target="tpu_custom_call" | custom-call | flops 268435456 | tf_op jit(solution)/shard_map/pallas_call | solution.py:570
  27.6 1.4 %collective-permute-done.9.refs_0_ = f32[23,8,128]{2,1,0:T(8,128)S(1)} collective-permute-done((f32[23,8,128]{2,1,0:T(8,128)S(1)}, f32[23,8,128]{2,1,0:T(8,128)S(1)}, u32[]{:S(2)}, u32[]{:S(2)}) %collective-permute-start.9) | collective-permute-done | bytes 94240 | tf_op jit(solution)/shard_map/ppermute | solution.py:615
  29.0 0.5 %shard_map.85 = (f32[72,768]{1,0:T(8,128)S(1)}, f32[21,8,128]{2,1,0:T(8,128)S(1)}) custom-call(f32[6,72,768]{2,1,0:T(8,128)S(1)} %shard_map.83.after.inner.refs_2_, f32[23,8,128]{2,1,0:T(8,128)S(1)} %collective-permute-done.9.refs_0_, f32[72,768]{1,0:T(8,128)S(1)} %get-tuple-element.62.edge_b.refs_1_, f32[6,72,768]{2,1,0:T(8,128)S(1)} %shard_map.80.after.inner.refs_2_, ...), custom_call_target="tpu_custom_call" | custom-call | flops 67108864 | tf_op jit(solution)/shard_map/pallas_call | solution.py:570
  29.4 1.2 %collective-permute-start.10 = (f32[21,8,128]{2,1,0:T(8,128)S(1)}, f32[21,8,128]{2,1,0:T(8,128)S(1)}, u32[]{:S(2)}, u32[]{:S(2)}) collective-permute-start(f32[21,8,128]{2,1,0:T(8,128)S(1)} %get-tuple-element.68), channel_id=1, source_target_pairs={{8,16},{16,8},{24,0},{0,24},{9,17},{17,9},{25,1},{1,25},{10,18},{1... | collective-permute-start | bytes 258056 | tf_op jit(solution)/shard_map/ppermute | solution.py:615
  30.6 0.0 collective-permute-done.7.refs_0_
  30.6 0.5 %shard_map.84 = (f32[72,768]{1,0:T(8,128)S(1)}, f32[21,8,128]{2,1,0:T(8,128)S(1)}) custom-call(f32[6,72,768]{2,1,0:T(8,128)S(1)} %shard_map.83.after.inner.refs_2_, f32[23,8,128]{2,1,0:T(8,128)S(1)} %collective-permute-done.7.refs_0_, f32[72,768]{1,0:T(8,128)S(1)} %get-tuple-element.60.edge_a.refs_1_, f32[6,72,768]{2,1,0:T(8,128)S(1)} %shard_map.80.after.inner.refs_2_, ...), custom_call_target="tpu_custom_call" | custom-call | flops 67108864 | tf_op jit(solution)/shard_map/pallas_call | solution.py:570
  31.1 1.5 %collective-permute-start.8 = (f32[21,8,128]{2,1,0:T(8,128)S(1)}, f32[21,8,128]{2,1,0:T(8,128)S(1)}, u32[]{:S(2)}, u32[]{:S(2)}) collective-permute-start(f32[21,8,128]{2,1,0:T(8,128)S(1)} %get-tuple-element.64), channel_id=1, source_target_pairs={{0,8},{8,0},{16,24},{24,16},{1,9},{9,1},{17,25},{25,17},{2,10},{10... | collective-permute-start | bytes 258056 | tf_op jit(solution)/shard_map/ppermute | solution.py:616
  32.6 0.9 %shard_map.86.after.done_inner = f32[6,64,648]{2,1,0:T(8,128)S(1)} custom-call(f32[72,768]{1,0:T(8,128)S(1)} %get-tuple-element.65.edge_a.edge, f32[72,768]{1,0:T(8,128)S(1)} %get-tuple-element.67.edge_b.refs_1_, f32[6,72,768]{2,1,0:T(8,128)S(1)} %shard_map.83.after.inner.refs_2_, f32[8,72,128]{2,1,0:T(8,128)S(1)} %get-tuple-element.48.seas.refs_3_, ...), custom_call_target="tpu_custom_call" | custom-call | flops 268435456 | tf_op jit(solution)/shard_map/pallas_call | solution.py:570
  33.5 1.4 %collective-permute-done.10.refs_0_ = f32[21,8,128]{2,1,0:T(8,128)S(1)} collective-permute-done((f32[21,8,128]{2,1,0:T(8,128)S(1)}, f32[21,8,128]{2,1,0:T(8,128)S(1)}, u32[]{:S(2)}, u32[]{:S(2)}) %collective-permute-start.10) | collective-permute-done | bytes 86048 | tf_op jit(solution)/shard_map/ppermute | solution.py:615
  34.9 0.4 %shard_map.87.done_edge = f32[64,648]{1,0:T(8,128)S(1)} custom-call(f32[6,64,648]{2,1,0:T(8,128)S(1)} %shard_map.86.after.done_inner, f32[21,8,128]{2,1,0:T(8,128)S(1)} %collective-permute-done.10.refs_0_, f32[72,768]{1,0:T(8,128)S(1)} %get-tuple-element.67.edge_b.refs_1_, f32[6,72,768]{2,1,0:T(8,128)S(1)} %shard_map.83.after.inner.refs_2_, ...), custom_call_target="tpu_custom_call" | custom-call | flops 67108864 | tf_op jit(solution)/shard_map/pallas_call | solution.py:570
  35.3 0.3 collective-permute-done.8.halo
  35.6 1.2 %shard_map.88 = f32[8,64,648]{2,1,0:T(8,128)} custom-call(f32[21,8,128]{2,1,0:T(8,128)S(1)} %collective-permute-done.8.halo, f32[72,768]{1,0:T(8,128)S(1)} %get-tuple-element.65.edge_a.edge, f32[6,72,768]{2,1,0:T(8,128)S(1)} %shard_map.83.after.inner.refs_2_, f32[8,72,128]{2,1,0:T(8,128)S(1)} %get-tuple-element.48.seas.refs_3_, ...), custom_call_target="tpu_custom_call" | custom-call | flops 67108864 | tf_op jit(solution)/shard_map/pallas_call | solution.py:570
  (4 shorter events, 0.0 us)
Async XLA Ops:
  0.0 3.8 %copy-start.5 = (f32[8,64]{1,0:T(8,128)S(1)}, f32[8,64]{1,0:T(8,128)}, u32[]{:S(2)}) copy-start(f32[8,64]{1,0:T(8,128)} %wind_ref.1) | copy-start | bytes 6148
  0.0 3.8 %copy-start = (f32[8,64,648]{2,1,0:T(8,128)S(1)}, f32[8,64,648]{2,1,0:T(8,128)}, u32[]{:S(2)}) copy-start(f32[8,64,648]{2,1,0:T(8,128)} %spectrum.3) | copy-start | bytes 3981316
  0.0 3.8 %copy-start.3 = (s32[8,64]{1,0:T(8,128)S(1)}, s32[8,64]{1,0:T(8,128)}, u32[]{:S(2)}) copy-start(s32[8,64]{1,0:T(8,128)} %sea_ref.1) | copy-start | bytes 6148
  0.0 3.8 %copy-start.4 = (s32[8,64]{1,0:T(8,128)S(1)}, s32[8,64]{1,0:T(8,128)}, u32[]{:S(2)}) copy-start(s32[8,64]{1,0:T(8,128)} %ice_ref.1) | copy-start | bytes 6148
  1.3 3.3 %collective-permute-start = (f32[21,8,128]{2,1,0:T(8,128)S(1)}, f32[21,8,128]{2,1,0:T(8,128)S(1)}, u32[]{:S(2)}, u32[]{:S(2)}) collective-permute-start(f32[21,8,128]{2,1,0:T(8,128)S(1)} %get-tuple-element.37), channel_id=1, source_target_pairs={{0,1},{1,0},{2,3},{3,2},{4,5},{5,4},{6,7},{7,6},{8,9},{9,8},{10,11... | collective-permute-start | bytes 258056 | tf_op jit(solution)/shard_map/ppermute | solution.py:590
  1.4 5.8 %collective-permute-start.1 = (f32[21,8,128]{2,1,0:T(8,128)S(1)}, f32[21,8,128]{2,1,0:T(8,128)S(1)}, u32[]{:S(2)}, u32[]{:S(2)}) collective-permute-start(f32[21,8,128]{2,1,0:T(8,128)S(1)} %get-tuple-element.38), channel_id=1, source_target_pairs={{1,2},{2,1},{3,4},{4,3},{5,6},{6,5},{9,10},{10,9},{11,12},{12,11},... | collective-permute-start | bytes 258056 | tf_op jit(solution)/shard_map/ppermute | solution.py:589
  4.6 5.9 %copy-start.1 = (bf16[648,648]{1,0:T(8,128)(2,1)S(1)}, bf16[648,648]{1,0:T(8,128)(2,1)}, u32[]{:S(2)}) copy-start(bf16[648,648]{1,0:T(8,128)(2,1)} %coupling_ref.1) | copy-start | bytes 2519428
  4.6 5.9 %copy-start.2 = (f32[8,768]{1,0:T(8,128)S(1)}, f32[8,768]{1,0:T(8,128)}, u32[]{:S(2)}) copy-start(f32[8,768]{1,0:T(8,128)} %constant.2.clone.angle_ref) | copy-start | bytes 73732
  4.6 5.9 %copy-start.6 = (f32[18]{0:T(128)S(1)}, f32[18]{0:T(128)}, u32[]{:S(2)}) copy-start(f32[18]{0:T(128)} %speed_ref.1) | copy-start | bytes 220
  7.5 10.5 %collective-permute-start.2 = (f32[23,8,128]{2,1,0:T(8,128)S(1)}, f32[23,8,128]{2,1,0:T(8,128)S(1)}, u32[]{:S(2)}, u32[]{:S(2)}) collective-permute-start(f32[23,8,128]{2,1,0:T(8,128)S(1)} %get-tuple-element.45), channel_id=1, source_target_pairs={{0,8},{8,0},{16,24},{24,16},{1,9},{9,1},{17,25},{25,17},{2,10},{10... | collective-permute-start | bytes 282632 | tf_op jit(solution)/shard_map/ppermute | solution.py:616
  8.9 5.4 %collective-permute-start.4 = (f32[21,8,128]{2,1,0:T(8,128)S(1)}, f32[21,8,128]{2,1,0:T(8,128)S(1)}, u32[]{:S(2)}, u32[]{:S(2)}) collective-permute-start(f32[21,8,128]{2,1,0:T(8,128)S(1)} %get-tuple-element.57), channel_id=1, source_target_pairs={{8,16},{16,8},{24,0},{0,24},{9,17},{17,9},{25,1},{1,25},{10,18},{1... | collective-permute-start | bytes 258056 | tf_op jit(solution)/shard_map/ppermute | solution.py:615
  11.3 4.7 %collective-permute-start.3 = (f32[3,8,128]{2,1,0:T(8,128)S(1)}, f32[3,8,128]{2,1,0:T(8,128)S(1)}, u32[]{:S(2)}, u32[]{:S(2)}) collective-permute-start(f32[3,8,128]{2,1,0:T(8,128)S(1)} %get-tuple-element.56), channel_id=1, source_target_pairs={{8,16},{16,8},{24,0},{0,24},{9,17},{17,9},{25,1},{1,25},{10,18},{1... | collective-permute-start | bytes 36872 | tf_op jit(solution)/shard_map/ppermute | solution.py:618
  16.4 6.5 %collective-permute-start.6 = (f32[23,8,128]{2,1,0:T(8,128)S(1)}, f32[23,8,128]{2,1,0:T(8,128)S(1)}, u32[]{:S(2)}, u32[]{:S(2)}) collective-permute-start(f32[23,8,128]{2,1,0:T(8,128)S(1)} %get-tuple-element.61), channel_id=1, source_target_pairs={{8,16},{16,8},{24,0},{0,24},{9,17},{17,9},{25,1},{1,25},{10,18},{1... | collective-permute-start | bytes 282632 | tf_op jit(solution)/shard_map/ppermute | solution.py:615
  18.5 6.1 %collective-permute-start.5 = (f32[23,8,128]{2,1,0:T(8,128)S(1)}, f32[23,8,128]{2,1,0:T(8,128)S(1)}, u32[]{:S(2)}, u32[]{:S(2)}) collective-permute-start(f32[23,8,128]{2,1,0:T(8,128)S(1)} %get-tuple-element.59), channel_id=1, source_target_pairs={{0,8},{8,0},{16,24},{24,16},{1,9},{9,1},{17,25},{25,17},{2,10},{10... | collective-permute-start | bytes 282632 | tf_op jit(solution)/shard_map/ppermute | solution.py:616
  23.4 5.5 %collective-permute-start.9 = (f32[23,8,128]{2,1,0:T(8,128)S(1)}, f32[23,8,128]{2,1,0:T(8,128)S(1)}, u32[]{:S(2)}, u32[]{:S(2)}) collective-permute-start(f32[23,8,128]{2,1,0:T(8,128)S(1)} %get-tuple-element.66), channel_id=1, source_target_pairs={{8,16},{16,8},{24,0},{0,24},{9,17},{17,9},{25,1},{1,25},{10,18},{1... | collective-permute-start | bytes 282632 | tf_op jit(solution)/shard_map/ppermute | solution.py:615
  25.1 5.5 %collective-permute-start.7 = (f32[23,8,128]{2,1,0:T(8,128)S(1)}, f32[23,8,128]{2,1,0:T(8,128)S(1)}, u32[]{:S(2)}, u32[]{:S(2)}) collective-permute-start(f32[23,8,128]{2,1,0:T(8,128)S(1)} %get-tuple-element.63), channel_id=1, source_target_pairs={{0,8},{8,0},{16,24},{24,16},{1,9},{9,1},{17,25},{25,17},{2,10},{10... | collective-permute-start | bytes 282632 | tf_op jit(solution)/shard_map/ppermute | solution.py:616
  29.4 5.5 %collective-permute-start.10 = (f32[21,8,128]{2,1,0:T(8,128)S(1)}, f32[21,8,128]{2,1,0:T(8,128)S(1)}, u32[]{:S(2)}, u32[]{:S(2)}) collective-permute-start(f32[21,8,128]{2,1,0:T(8,128)S(1)} %get-tuple-element.68), channel_id=1, source_target_pairs={{8,16},{16,8},{24,0},{0,24},{9,17},{17,9},{25,1},{1,25},{10,18},{1... | collective-permute-start | bytes 258056 | tf_op jit(solution)/shard_map/ppermute | solution.py:615
  31.1 4.6 %collective-permute-start.8 = (f32[21,8,128]{2,1,0:T(8,128)S(1)}, f32[21,8,128]{2,1,0:T(8,128)S(1)}, u32[]{:S(2)}, u32[]{:S(2)}) collective-permute-start(f32[21,8,128]{2,1,0:T(8,128)S(1)} %get-tuple-element.64), channel_id=1, source_target_pairs={{0,8},{8,0},{16,24},{24,16},{1,9},{9,1},{17,25},{25,17},{2,10},{10... | collective-permute-start | bytes 258056 | tf_op jit(solution)/shard_map/ppermute | solution.py:616

commit v9 on v8

--- a/solution.py
+++ b/solution.py
@@ -155,7 +155,7 @@
     out[spot + 2] = parts[1]
 
 
-def across_edge(halo, inner, west, bins, rows, with_halo, corner=None):
+def across_edge(halo, inner, west, bins, rows, with_halo):
     split, high, width, kept, start = pack_plan(bins, not west)
     rest = width - kept
     blocks = rows // 8
@@ -168,9 +168,7 @@
         if block == blocks and not with_halo:
             new = near
         else:
-            if block == blocks and corner is not None:
-                full, other, part = corner[0], corner[1], corner[2]
-            elif block == blocks:
+            if block == blocks:
                 full, other = halo[2 * blocks + half + 1], halo[2 * blocks + half + 2]
                 part = turn(left, start - half * rest)
             else:
@@ -240,7 +238,17 @@
     return turned[:rows], turned[rows:]
 
 
-def first_kernel(bins, spectrum, sea_hbm, ice_hbm, wind_hbm, out_a, out_b, edge, sea_ref, ice_ref, wind_ref, sems):
+def column_pairs(columns):
+    return [(0, columns - 1)] + [(c, c + 1) for c in range(1, columns - 1, 2)]
+
+
+def halo_tiles(pairs, tiles):
+    return pairs * (tiles - 1) + 1
+
+
+def first_kernel(
+    bins, spectrum, sea_hbm, ice_hbm, wind_hbm, out_a, out_b, out_c, edge, sea_ref, ice_ref, wind_ref, sems
+):
     columns, rows = sea_ref.shape
     copies = []
     masks = [
@@ -266,14 +274,15 @@
     for copy in copies:
         copy.wait()
     tiles = lane_tiles(bins)
-    space = LANES // (columns // 2)
-    for second, out in ((False, out_a), (True, out_b)):
+    pairs = column_pairs(columns)
+    for second, group, out in ((False, pairs, out_a), (True, pairs[:1], out_b), (True, pairs[1:], out_c)):
         to_south = south_flag(second)
+        space = LANES // len(group)
         ends = jnp.zeros(shape, jnp.float32)
-        for pair in range(columns // 2):
+        for index, pair in enumerate(group):
             for tile in range(tiles):
                 halves = []
-                for c in (2 * pair, 2 * pair + 1):
+                for c in pair:
                     low, high = read_tile(edge, (0, c), bins, tile), read_tile(edge, (1, c), bins, tile)
                     here = jnp.where(to_south, low, high)
                     s = jnp.where(to_south, sea[0:8, c : c + 1], sea[rows - 8 : rows, c : c + 1])
@@ -288,11 +297,11 @@
                 keep = (row < DEPTH) == to_south
                 value = jnp.where(keep, first, pltpu.roll(other, DEPTH, 0))
                 if tile < tiles - 1:
-                    out[pair * (tiles - 1) + tile] = value
+                    out[index * (tiles - 1) + tile] = value
                 else:
-                    here = (lane >= pair * space) & (lane < (pair + 1) * space)
-                    ends = jnp.where(here, turn(value, pair * space), ends)
-        out[columns // 2 * (tiles - 1)] = ends
+                    here = (lane >= index * space) & (lane < (index + 1) * space)
+                    ends = jnp.where(here, turn(value, index * space), ends)
+        out[len(group) * (tiles - 1)] = ends
 
 
 def table_kernel(bins, rows, speed_ref, angle_ref, coupling_ref, stay, go_x, go_y, wide):
@@ -355,60 +364,66 @@
         on_each_side(second, side)
 
 
-def join_kernel(
-    bins, halo_a, halo_b, edge_a_in, edge_b_in, inner_in, seas_in, gains_in, pack_in,
-    edge_a, edge_b, inner, seas, gains, pack_a, corner_b,
+def halo_rows(bins, from_a, from_b, slot, seas, gains, column):
+    tiles = lane_tiles(bins)
+    rows = seas.shape[1] - 2 * DEPTH
+    used = bins % LANES
+    shape = (8, LANES)
+    top = row_index(shape) < DEPTH
+    a_south = south_flag(False)
+    values = []
+    for tile in range(tiles):
+        here = []
+        for ref, pairs, index in (from_a, from_b):
+            if tile < tiles - 1:
+                here.append(ref[index * (tiles - 1) + tile])
+            else:
+                here.append(turn(ref[pairs * (tiles - 1)], -index * (LANES // pairs)))
+        low, high = jnp.where(a_south, here[0], here[1]), jnp.where(a_south, here[1], here[0])
+        if slot:
+            low, high = pltpu.roll(low, DEPTH, 0), pltpu.roll(high, DEPTH, 0)
+        values.append(jnp.where(top, high, low))
+    last = values[-1]
+    s = jnp.broadcast_to(last[:, used : used + 1], shape)
+    g = jnp.broadcast_to(last[:, used + 1 : used + 2], shape)
+    seas[column, rows:] = time_step * s
+    gains[column, rows:] = s * g
+    values[-1] = jnp.where(lane_index(shape) < used, last, 0.0)
+    return values
+
+
+def join_edges_kernel(
+    bins, halo_a, halo_b, edge_a_in, edge_b_in, seas_in, gains_in, pack_a_in, pack_b_in,
+    edge_a, edge_b, seas, gains, pack_a, pack_b,
 ):
     columns = seas.shape[0]
     rows = seas.shape[1] - 2 * DEPTH
-    tiles = lane_tiles(bins)
-    used = bins % LANES
-    shape = (8, LANES)
-    row = row_index(shape)
-    lane = lane_index(shape)
-    a_south = south_flag(False)
-    top = row < DEPTH
-    values = []
-    for c in range(columns):
-        tile_values = []
-        for tile in range(tiles):
-            spot = columns // 2 * (tiles - 1) if tile == tiles - 1 else c // 2 * (tiles - 1) + tile
-            from_a, from_b = halo_a[spot], halo_b[spot]
-            if tile == tiles - 1:
-                back = -(c // 2) * (LANES // (columns // 2))
-                from_a, from_b = turn(from_a, back), turn(from_b, back)
-            low, high = jnp.where(a_south, from_a, from_b), jnp.where(a_south, from_b, from_a)
-            if c % 2:
-                low, high = pltpu.roll(low, DEPTH, 0), pltpu.roll(high, DEPTH, 0)
-            tile_values.append(jnp.where(top, high, low))
-        last = tile_values[-1]
-        s = jnp.broadcast_to(last[:, used : used + 1], shape)
-        g = jnp.broadcast_to(last[:, used + 1 : used + 2], shape)
-        seas[c, rows:] = time_step * s
-        gains[c, rows:] = s * g
-        tile_values[-1] = jnp.where(lane < used, last, 0.0)
-        values.append(tile_values)
-    for tile in range(tiles):
-        for c in range(1, columns - 1):
-            inner[c - 1, rows:, lanes_of(tile)] = values[c][tile]
-    for second, target in ((False, edge_a), (True, edge_b)):
-
-        def side(west, second=second, target=target):
-            mine = values[0 if west else columns - 1]
-            for tile in range(tiles):
-                target[rows:, lanes_of(tile)] = mine[tile]
-            parts = half_parts(mine, west, bins)
-            if second:
-                for k, value in enumerate(parts):
-                    corner_b[k] = value
-            else:
-                pack_corner(parts, pack_in, west, bins, rows, pack_a)
+    count = columns // 2
+    values = [
+        halo_rows(bins, (halo_a, count, 0), (halo_b, 1, 0), slot, seas, gains, c)
+        for slot, c in enumerate((0, columns - 1))
+    ]
+    for second, target, before, pack in ((False, edge_a, pack_a_in, pack_a), (True, edge_b, pack_b_in, pack_b)):
+
+        def side(west, target=target, before=before, pack=pack):
+            mine = values[0 if west else 1]
+            for tile, value in enumerate(mine):
+                target[rows:, lanes_of(tile)] = value
+            pack_corner(half_parts(mine, west, bins), before, west, bins, rows, pack)
 
         on_each_side(second, side)
 
 
-def ordered_first_kernel(bins, second, after, corner, *refs):
-    edge_kernel(bins, second, *refs, corner=corner)
+def join_inner_kernel(bins, halo_a, halo_b, inner_in, seas_in, gains_in, inner, seas, gains):
+    columns = seas.shape[0]
+    rows = seas.shape[1] - 2 * DEPTH
+    count = columns // 2
+    for index in range(1, count):
+        for slot in range(2):
+            c = 2 * index - 1 + slot
+            values = halo_rows(bins, (halo_a, count, index), (halo_b, count - 1, index - 1), slot, seas, gains, c)
+            for tile, value in enumerate(values):
+                inner[c - 1, rows:, lanes_of(tile)] = value
 
 
 def ordered_edge_kernel(bins, second, after, *refs):
@@ -416,13 +431,13 @@
 
 
 def edge_kernel(
-    bins, second, halo, edge, inner, seas, gains, stay, go_x, go_y, wide, out, pack, adv_ref, corner=None
+    bins, second, halo, edge, inner, seas, gains, stay, go_x, go_y, wide, out, pack, adv_ref
 ):
     rows = edge.shape[0] - 2 * DEPTH
     halo_next = pack.shape[0] == pack_count(rows, True)
 
     def side(west):
-        fresh = edge_step(bins, west, halo, edge, inner, seas, gains, stay, go_x, go_y, wide, adv_ref, False, corner)
+        fresh = edge_step(bins, west, halo, edge, inner, seas, gains, stay, go_x, go_y, wide, adv_ref, False)
         for t, value in enumerate(fresh):
             out[:, lanes_of(t)] = value
         pack_half(fresh, west, bins, rows, halo_next, pack)
@@ -461,13 +476,13 @@
         copy.wait()
 
 
-def edge_step(bins, west, halo, edge, inner, seas, gains, stay, go_x, go_y, wide, adv_ref, last, corner=None):
+def edge_step(bins, west, halo, edge, inner, seas, gains, stay, go_x, go_y, wide, adv_ref, last):
     tiles = lane_tiles(bins)
     columns = inner.shape[0] + 2
     rows = edge.shape[0] - 2 * DEPTH
     used = rows if last else edge.shape[0]
     near, mine = (0, 0) if west else (columns - 3, columns - 1)
-    across = across_edge(halo, [inner[near, :, lanes_of(t)] for t in range(tiles)], west, bins, rows, not last, corner)
+    across = across_edge(halo, [inner[near, :, lanes_of(t)] for t in range(tiles)], west, bins, rows, not last)
     for t in range(tiles):
         here = lanes_of(t)
         adv = advect(edge[:, here], across[t], stay[:, here], go_x[:, here], go_y[0:1, here], bins, t)
@@ -578,22 +593,22 @@
             compiler_params=pltpu.CompilerParams(vmem_limit_bytes=24 * 1024 * 1024),
         )(*ins)
 
-    send_a, send_b = call(
+    pairs = columns // 2
+    send_a, send_b, send_c = call(
         functools.partial(first_kernel, bins),
-        (VMEM((columns // 2 * (tiles - 1) + 1, 8, LANES), f32),) * 2,
+        tuple(VMEM((halo_tiles(n, tiles), 8, LANES), f32) for n in (pairs, 1, pairs - 1)),
         [pltpu.with_memory_space_constraint(x, pltpu.HBM) for x in (spectrum, sea_mask, ice_flags, wind_forcing)],
         [hbm] * 4,
         [VMEM((2, columns, 8, bins), f32), VMEM((columns, rows), sea_mask.dtype), VMEM((columns, rows), ice_flags.dtype),
          VMEM((columns, rows), f32), pltpu.SemaphoreType.DMA((5,))],
     )
+    halo_a = lax.ppermute(send_a, "lat", lat_a)
     halo_b = lax.ppermute(send_b, "lat", lat_b)
-    halo_a = lax.ppermute(send_a, "lat", lat_a)
-    pack_own = VMEM((pack_count(rows, False), 8, LANES), f32)
+    halo_c = lax.ppermute(send_c, "lat", lat_b)
     pack_shape = VMEM((pack_count(rows, True), 8, LANES), f32)
-    corner_shape = VMEM((3, 8, LANES), f32)
     edge_a, edge_b, inner, seas, gains, pack_a, pack_b = call(
         functools.partial(load_kernel, bins),
-        (edge_shape, edge_shape, inner_shape, mask_shape, mask_shape, pack_shape, pack_own),
+        (edge_shape, edge_shape, inner_shape, mask_shape, mask_shape, pack_shape, pack_shape),
         (spectrum, sea_mask, ice_flags, wind_forcing), [vmem] * 4, flops=1 << 24,
     )
     stay, go_x, go_y, wide = call(
@@ -602,20 +617,21 @@
         (group_speed, jnp.asarray(angle_table(bins, group_speed.shape[0])), coupling),
         [smem, vmem, vmem], flops=1 << 24,
     )
-    edge_a, edge_b, inner, seas, gains, pack_a, corner_b = call(
-        functools.partial(join_kernel, bins),
-        (edge_shape, edge_shape, inner_shape, mask_shape, mask_shape, pack_shape, corner_shape),
-        (halo_a, halo_b, edge_a, edge_b, inner, seas, gains, pack_a),
-        [vmem] * 8,
+    edge_a, edge_b, seas, gains, pack_a, pack_b = call(
+        functools.partial(join_edges_kernel, bins),
+        (edge_shape, edge_shape, mask_shape, mask_shape, pack_shape, pack_shape),
+        (halo_a, halo_b, edge_a, edge_b, seas, gains, pack_a, pack_b), [vmem] * 8,
         aliases={2: 0, 3: 1, 4: 2, 5: 3, 6: 4, 7: 5},
+    )
+    inner, seas, gains = call(
+        functools.partial(join_inner_kernel, bins), (inner_shape, mask_shape, mask_shape),
+        (halo_a, halo_c, inner, seas, gains), [vmem] * 5, aliases={2: 0, 3: 1, 4: 2},
     )
     tables = (seas, gains, stay, go_x, go_y, wide)
     for step in range(STEPS):
         last = step == STEPS - 1
         halo_b = lax.ppermute(pack_b, "lon", lon_b)
         halo_a = lax.ppermute(pack_a, "lon", lon_a)
-        if step == 0:
-            corner = lax.ppermute(corner_b, "lon", lon_b)
         used = rows if last else tall
         new_inner = call(
             functools.partial(inner_kernel, bins), VMEM((columns - 2, rows, bins), f32) if last else inner_shape,
@@ -639,13 +655,9 @@
         fresh = []
         pack_next = VMEM((pack_count(rows, step < STEPS - 2), 8, LANES), f32)
         for second, halo, edge in ((False, halo_a, edge_a), (True, halo_b, edge_b)):
-            body, ins = edge_kernel, (halo, edge, inner) + tables
-            if step > 0:
-                body, ins = ordered_edge_kernel, (new_inner,) + ins
-            elif second:
-                body, ins = ordered_first_kernel, (new_inner, corner) + ins
+            ins = (new_inner, halo, edge, inner) + tables
             fresh.append(call(
-                functools.partial(body, bins, second), (edge_shape, pack_next),
+                functools.partial(ordered_edge_kernel, bins, second), (edge_shape, pack_next),
                 ins, [vmem] * len(ins), [VMEM((tall, padded), f32)], flops=1 << 26,
             ))
         inner = new_inner

time: 36.9 us -> 37.4 us (1.014)
  the two profiles are of different devices: /device:TPU:24 before, /device:TPU:16 now
where the time goes in v9:
time: 37.4 us; the launch traced here: 37.2 us
  starting transfers between devices  14.1 us (38%)
  waiting for transfers between devices  11.6 us (31%)
  Pallas kernels  11.3 us (30%)
    pallas_call x17, Pallas kernels, call(): pl.pallas_call(body, out_shape=outs, in_specs=specs, out_specs=out_specs...  11.3 us
    ppermute x4, waiting for transfers between devices, steps(): halo_b = lax.ppermute(pack_b, 'lon', lon_b)  7.28 us
    ppermute x4, starting transfers between devices, steps(): halo_a = lax.ppermute(pack_a, 'lon', lon_a)  4.74 us
    ppermute x4, starting transfers between devices, steps(): halo_b = lax.ppermute(pack_b, 'lon', lon_b)  4.63 us
    ppermute x1, starting transfers between devices, steps(): halo_b = lax.ppermute(send_b, 'lat', lat_b)  2.55 us
    ppermute x1, starting transfers between devices, steps(): halo_c = lax.ppermute(send_c, 'lat', lat_b)  2.12 us
    ppermute x1, waiting for transfers between devices, steps(): halo_b = lax.ppermute(send_b, 'lat', lat_b)  1.99 us
    ppermute x1, waiting for transfers between devices, steps(): halo_c = lax.ppermute(send_c, 'lat', lat_b)  1.96 us
  transfers between devices with their start and end apart: 11, of which 6 were waited for; matrix products, arithmetic and copies ran while one was open for 0% of the time, Pallas kernels for 23%

profile of v9, /device:TPU:16, one launch (start us, length us, event | category | flops | bytes accessed | tf_op | source)
XLA Modules:
  0.0 37.2 jit_solution(11512170846583617305)
XLA Ops:
  0.0 0.0 copy-start
  0.0 1.3 %shard_map.73 = (f32[21,8,128]{2,1,0:T(8,128)S(1)}, f32[6,8,128]{2,1,0:T(8,128)S(1)}, f32[16,8,128]{2,1,0:T(8,128)S(1)}) custom-call(f32[8,64,648]{2,1,0:T(8,128)} %spectrum.3, s32[8,64]{1,0:T(8,128)} %sea_ref.1, s32[8,64]{1,0:T(8,128)} %ice_ref.1, f32[8,64]{1,0:T(8,128)} %wind_ref.1), custom_call_target="tpu_custom_call" | custom-call | tf_op jit(solution)/shard_map/pallas_call | solution.py:585
  1.3 0.1 collective-permute-start
  1.4 0.0 copy-start.1
  1.4 0.0 copy-start.2
  1.4 0.0 copy-start.6
  1.4 2.5 %collective-permute-start.1 = (f32[6,8,128]{2,1,0:T(8,128)S(1)}, f32[6,8,128]{2,1,0:T(8,128)S(1)}, u32[]{:S(2)}, u32[]{:S(2)}) collective-permute-start(f32[6,8,128]{2,1,0:T(8,128)S(1)} %get-tuple-element.41), channel_id=1, source_target_pairs={{1,2},{2,1},{3,4},{4,3},{5,6},{6,5},{9,10},{10,9},{11,12},{12,11},... | collective-permute-start | bytes 73736 | tf_op jit(solution)/shard_map/ppermute | solution.py:606
  4.0 0.0 copy-done.5
  4.0 0.0 copy-done.4
  4.0 0.0 copy-done.3
  4.0 0.0 copy-done
  4.0 0.7 %shard_map.74 = (f32[72,768]{1,0:T(8,128)S(1)}, f32[72,768]{1,0:T(8,128)S(1)}, f32[6,72,768]{2,1,0:T(8,128)S(1)}, f32[8,72,128]{2,1,0:T(8,128)S(1)}, f32[8,72,12...) custom-call(f32[8,64,648]{2,1,0:T(8,128)S(1)} %copy-done, s32[8,64]{1,0:T(8,128)S(1)} %copy-done.3, ...), custom_call_target="tpu_custom_call" | custom-call | flops 16777216 | tf_op jit(solution)/shard_map/pallas_call | solution.py:585
  4.7 2.0 %collective-permute-done.1.halo_b = f32[6,8,128]{2,1,0:T(8,128)S(1)} collective-permute-done((f32[6,8,128]{2,1,0:T(8,128)S(1)}, f32[6,8,128]{2,1,0:T(8,128)S(1)}, u32[]{:S(2)}, u32[]{:S(2)}) %collective-permute-start.1) | collective-permute-done | bytes 24608 | tf_op jit(solution)/shard_map/ppermute | solution.py:606
  6.7 0.0 collective-permute-done.halo_a
  6.7 0.3 shard_map.75
  7.0 2.4 %collective-permute-start.4 = (f32[23,8,128]{2,1,0:T(8,128)S(1)}, f32[23,8,128]{2,1,0:T(8,128)S(1)}, u32[]{:S(2)}, u32[]{:S(2)}) collective-permute-start(f32[23,8,128]{2,1,0:T(8,128)S(1)} %get-tuple-element.63), channel_id=1, source_target_pairs={{8,16},{16,8},{24,0},{0,24},{9,17},{17,9},{25,1},{1,25},{10,18},{1... | collective-permute-start | bytes 282632 | tf_op jit(solution)/shard_map/ppermute | solution.py:633
  9.3 2.1 %collective-permute-start.2 = (f32[16,8,128]{2,1,0:T(8,128)S(1)}, f32[16,8,128]{2,1,0:T(8,128)S(1)}, u32[]{:S(2)}, u32[]{:S(2)}) collective-permute-start(f32[16,8,128]{2,1,0:T(8,128)S(1)} %get-tuple-element.50), channel_id=1, source_target_pairs={{1,2},{2,1},{3,4},{4,3},{5,6},{6,5},{9,10},{10,9},{11,12},{12,11},... | collective-permute-start | bytes 196616 | tf_op jit(solution)/shard_map/ppermute | solution.py:607
  11.5 0.7 %collective-permute-start.3 = (f32[23,8,128]{2,1,0:T(8,128)S(1)}, f32[23,8,128]{2,1,0:T(8,128)S(1)}, u32[]{:S(2)}, u32[]{:S(2)}) collective-permute-start(f32[23,8,128]{2,1,0:T(8,128)S(1)} %get-tuple-element.61), channel_id=1, source_target_pairs={{0,8},{8,0},{16,24},{24,16},{1,9},{9,1},{17,25},{25,17},{2,10},{10... | collective-permute-start | bytes 282632 | tf_op jit(solution)/shard_map/ppermute | solution.py:634
  12.2 0.0 copy-done.2
  12.2 0.8 %shard_map.77 = (f32[72,768]{1,0:T(8,128)S(1)}, f32[72,768]{1,0:T(8,128)S(1)}, f32[8,768]{1,0:T(8,128)S(1)}, bf16[768,768]{1,0:T(8,128)(2,1)S(1)}) custom-call(f32[18]{0:T(128)S(1)} %copy-done.6, f32[8,768]{1,0:T(8,128)S(1)} %copy-done.2, bf16[648,648]{1,0:T(8,128)(2,1)S(1)} %copy-done.1), custom_call_target="tpu_custom_call" | custom-call | flops 16777216 | tf_op jit(solution)/shard_map/pallas_call | solution.py:585
  13.0 2.0 %collective-permute-done.2.halo_b = f32[16,8,128]{2,1,0:T(8,128)S(1)} collective-permute-done((f32[16,8,128]{2,1,0:T(8,128)S(1)}, f32[16,8,128]{2,1,0:T(8,128)S(1)}, u32[]{:S(2)}, u32[]{:S(2)}) %collective-permute-start.2) | collective-permute-done | bytes 65568 | tf_op jit(solution)/shard_map/ppermute | solution.py:607
  14.9 0.2 shard_map.76
  15.1 0.9 %shard_map.78.after.inner.refs_2_ = f32[6,72,768]{2,1,0:T(8,128)S(1)} custom-call(f32[72,768]{1,0:T(8,128)S(1)} %get-tuple-element.48.edge_a.refs_1_, f32[72,768]{1,0:T(8,128)S(1)} %get-tuple-element.49.edge_b.refs_1_, f32[6,72,768]{2,1,0:T(8,128)S(1)} %get-tuple-element.54.inner.refs_2_, f32[8,72,128]{2,1,0:T(8,128)S(1)} %get-tuple-element.55.seas.refs_3_, ...), custom_call_target="tpu_custom_call" | custom-call | flops 268435456 | tf_op jit(solution)/shard_map/pallas_call | solution.py:585
  16.0 0.0 collective-permute-done.4.refs_0_
  16.0 0.5 %shard_map.80 = (f32[72,768]{1,0:T(8,128)S(1)}, f32[23,8,128]{2,1,0:T(8,128)S(1)}) custom-call(f32[6,72,768]{2,1,0:T(8,128)S(1)} %shard_map.78.after.inner.refs_2_, f32[23,8,128]{2,1,0:T(8,128)S(1)} %collective-permute-done.4.refs_0_, f32[72,768]{1,0:T(8,128)S(1)} %get-tuple-element.49.edge_b.refs_1_, f32[6,72,768]{2,1,0:T(8,128)S(1)} %get-tuple-element.54.inner.refs_2_, ...), custom_call_target="tpu_custom_call" | custom-call | flops 67108864 | tf_op jit(solution)/shard_map/pallas_call | solution.py:585
  16.6 0.6 %collective-permute-start.6 = (f32[23,8,128]{2,1,0:T(8,128)S(1)}, f32[23,8,128]{2,1,0:T(8,128)S(1)}, u32[]{:S(2)}, u32[]{:S(2)}) collective-permute-start(f32[23,8,128]{2,1,0:T(8,128)S(1)} %get-tuple-element.67), channel_id=1, source_target_pairs={{8,16},{16,8},{24,0},{0,24},{9,17},{17,9},{25,1},{1,25},{10,18},{1... | collective-permute-start | bytes 282632 | tf_op jit(solution)/shard_map/ppermute | solution.py:633
  17.2 0.0 collective-permute-done.3.refs_0_
  17.2 0.5 %shard_map.79 = (f32[72,768]{1,0:T(8,128)S(1)}, f32[23,8,128]{2,1,0:T(8,128)S(1)}) custom-call(f32[6,72,768]{2,1,0:T(8,128)S(1)} %shard_map.78.after.inner.refs_2_, f32[23,8,128]{2,1,0:T(8,128)S(1)} %collective-permute-done.3.refs_0_, f32[72,768]{1,0:T(8,128)S(1)} %get-tuple-element.48.edge_a.refs_1_, f32[6,72,768]{2,1,0:T(8,128)S(1)} %get-tuple-element.54.inner.refs_2_, ...), custom_call_target="tpu_custom_call" | custom-call | flops 67108864 | tf_op jit(solution)/shard_map/pallas_call | solution.py:585
  17.6 1.5 %collective-permute-start.5 = (f32[23,8,128]{2,1,0:T(8,128)S(1)}, f32[23,8,128]{2,1,0:T(8,128)S(1)}, u32[]{:S(2)}, u32[]{:S(2)}) collective-permute-start(f32[23,8,128]{2,1,0:T(8,128)S(1)} %get-tuple-element.65), channel_id=1, source_target_pairs={{0,8},{8,0},{16,24},{24,16},{1,9},{9,1},{17,25},{25,17},{2,10},{10... | collective-permute-start | bytes 282632 | tf_op jit(solution)/shard_map/ppermute | solution.py:634
  19.1 1.0 %shard_map.81.after.inner.refs_2_ = f32[6,72,768]{2,1,0:T(8,128)S(1)} custom-call(f32[72,768]{1,0:T(8,128)S(1)} %get-tuple-element.62.edge_a.refs_1_, f32[72,768]{1,0:T(8,128)S(1)} %get-tuple-element.64.edge_b.refs_1_, f32[6,72,768]{2,1,0:T(8,128)S(1)} %shard_map.78.after.inner.refs_2_, f32[8,72,128]{2,1,0:T(8,128)S(1)} %get-tuple-element.55.seas.refs_3_, ...), custom_call_target="tpu_custom_call" | custom-call | flops 268435456 | tf_op jit(solution)/shard_map/pallas_call | solution.py:585
  20.1 3.0 %collective-permute-done.6.refs_0_ = f32[23,8,128]{2,1,0:T(8,128)S(1)} collective-permute-done((f32[23,8,128]{2,1,0:T(8,128)S(1)}, f32[23,8,128]{2,1,0:T(8,128)S(1)}, u32[]{:S(2)}, u32[]{:S(2)}) %collective-permute-start.6) | collective-permute-done | bytes 94240 | tf_op jit(solution)/shard_map/ppermute | solution.py:633
  23.1 0.5 %shard_map.83 = (f32[72,768]{1,0:T(8,128)S(1)}, f32[23,8,128]{2,1,0:T(8,128)S(1)}) custom-call(f32[6,72,768]{2,1,0:T(8,128)S(1)} %shard_map.81.after.inner.refs_2_, f32[23,8,128]{2,1,0:T(8,128)S(1)} %collective-permute-done.6.refs_0_, f32[72,768]{1,0:T(8,128)S(1)} %get-tuple-element.64.edge_b.refs_1_, f32[6,72,768]{2,1,0:T(8,128)S(1)} %shard_map.78.after.inner.refs_2_, ...), custom_call_target="tpu_custom_call" | custom-call | flops 67108864 | tf_op jit(solution)/shard_map/pallas_call | solution.py:585
  23.6 0.4 %collective-permute-start.9 = (f32[23,8,128]{2,1,0:T(8,128)S(1)}, f32[23,8,128]{2,1,0:T(8,128)S(1)}, u32[]{:S(2)}, u32[]{:S(2)}) collective-permute-start(f32[23,8,128]{2,1,0:T(8,128)S(1)} %get-tuple-element.72), channel_id=1, source_target_pairs={{8,16},{16,8},{24,0},{0,24},{9,17},{17,9},{25,1},{1,25},{10,18},{1... | collective-permute-start | bytes 282632 | tf_op jit(solution)/shard_map/ppermute | solution.py:633
  24.0 0.0 collective-permute-done.5.refs_0_
  24.0 0.5 %shard_map.82 = (f32[72,768]{1,0:T(8,128)S(1)}, f32[23,8,128]{2,1,0:T(8,128)S(1)}) custom-call(f32[6,72,768]{2,1,0:T(8,128)S(1)} %shard_map.81.after.inner.refs_2_, f32[23,8,128]{2,1,0:T(8,128)S(1)} %collective-permute-done.5.refs_0_, f32[72,768]{1,0:T(8,128)S(1)} %get-tuple-element.62.edge_a.refs_1_, f32[6,72,768]{2,1,0:T(8,128)S(1)} %shard_map.78.after.inner.refs_2_, ...), custom_call_target="tpu_custom_call" | custom-call | flops 67108864 | tf_op jit(solution)/shard_map/pallas_call | solution.py:585
  24.5 1.7 %collective-permute-start.7 = (f32[23,8,128]{2,1,0:T(8,128)S(1)}, f32[23,8,128]{2,1,0:T(8,128)S(1)}, u32[]{:S(2)}, u32[]{:S(2)}) collective-permute-start(f32[23,8,128]{2,1,0:T(8,128)S(1)} %get-tuple-element.69), channel_id=1, source_target_pairs={{0,8},{8,0},{16,24},{24,16},{1,9},{9,1},{17,25},{25,17},{2,10},{10... | collective-permute-start | bytes 282632 | tf_op jit(solution)/shard_map/ppermute | solution.py:634
  26.2 0.9 %shard_map.84.after.inner.refs_2_ = f32[6,72,768]{2,1,0:T(8,128)S(1)} custom-call(f32[72,768]{1,0:T(8,128)S(1)} %get-tuple-element.66.edge_a.refs_1_, f32[72,768]{1,0:T(8,128)S(1)} %get-tuple-element.68.edge_b.refs_1_, f32[6,72,768]{2,1,0:T(8,128)S(1)} %shard_map.81.after.inner.refs_2_, f32[8,72,128]{2,1,0:T(8,128)S(1)} %get-tuple-element.55.seas.refs_3_, ...), custom_call_target="tpu_custom_call" | custom-call | flops 268435456 | tf_op jit(solution)/shard_map/pallas_call | solution.py:585
  27.1 2.3 %collective-permute-done.9.refs_0_ = f32[23,8,128]{2,1,0:T(8,128)S(1)} collective-permute-done((f32[23,8,128]{2,1,0:T(8,128)S(1)}, f32[23,8,128]{2,1,0:T(8,128)S(1)}, u32[]{:S(2)}, u32[]{:S(2)}) %collective-permute-start.9) | collective-permute-done | bytes 94240 | tf_op jit(solution)/shard_map/ppermute | solution.py:633
  29.4 0.5 %shard_map.86 = (f32[72,768]{1,0:T(8,128)S(1)}, f32[21,8,128]{2,1,0:T(8,128)S(1)}) custom-call(f32[6,72,768]{2,1,0:T(8,128)S(1)} %shard_map.84.after.inner.refs_2_, f32[23,8,128]{2,1,0:T(8,128)S(1)} %collective-permute-done.9.refs_0_, f32[72,768]{1,0:T(8,128)S(1)} %get-tuple-element.68.edge_b.refs_1_, f32[6,72,768]{2,1,0:T(8,128)S(1)} %shard_map.81.after.inner.refs_2_, ...), custom_call_target="tpu_custom_call" | custom-call | flops 67108864 | tf_op jit(solution)/shard_map/pallas_call | solution.py:585
  29.8 1.2 %collective-permute-start.10 = (f32[21,8,128]{2,1,0:T(8,128)S(1)}, f32[21,8,128]{2,1,0:T(8,128)S(1)}, u32[]{:S(2)}, u32[]{:S(2)}) collective-permute-start(f32[21,8,128]{2,1,0:T(8,128)S(1)} %get-tuple-element.74), channel_id=1, source_target_pairs={{8,16},{16,8},{24,0},{0,24},{9,17},{17,9},{25,1},{1,25},{10,18},{1... | collective-permute-start | bytes 258056 | tf_op jit(solution)/shard_map/ppermute | solution.py:633
  31.0 0.0 collective-permute-done.7.refs_0_
  31.0 0.5 %shard_map.85 = (f32[72,768]{1,0:T(8,128)S(1)}, f32[21,8,128]{2,1,0:T(8,128)S(1)}) custom-call(f32[6,72,768]{2,1,0:T(8,128)S(1)} %shard_map.84.after.inner.refs_2_, f32[23,8,128]{2,1,0:T(8,128)S(1)} %collective-permute-done.7.refs_0_, f32[72,768]{1,0:T(8,128)S(1)} %get-tuple-element.66.edge_a.refs_1_, f32[6,72,768]{2,1,0:T(8,128)S(1)} %shard_map.81.after.inner.refs_2_, ...), custom_call_target="tpu_custom_call" | custom-call | flops 67108864 | tf_op jit(solution)/shard_map/pallas_call | solution.py:585
  31.5 0.9 %collective-permute-start.8 = (f32[21,8,128]{2,1,0:T(8,128)S(1)}, f32[21,8,128]{2,1,0:T(8,128)S(1)}, u32[]{:S(2)}, u32[]{:S(2)}) collective-permute-start(f32[21,8,128]{2,1,0:T(8,128)S(1)} %get-tuple-element.70), channel_id=1, source_target_pairs={{0,8},{8,0},{16,24},{24,16},{1,9},{9,1},{17,25},{25,17},{2,10},{10... | collective-permute-start | bytes 258056 | tf_op jit(solution)/shard_map/ppermute | solution.py:634
  32.4 0.8 %shard_map.87.after.done_inner = f32[6,64,648]{2,1,0:T(8,128)S(1)} custom-call(f32[72,768]{1,0:T(8,128)S(1)} %get-tuple-element.71.edge_a.edge, f32[72,768]{1,0:T(8,128)S(1)} %get-tuple-element.73.edge_b.refs_1_, f32[6,72,768]{2,1,0:T(8,128)S(1)} %shard_map.84.after.inner.refs_2_, f32[8,72,128]{2,1,0:T(8,128)S(1)} %get-tuple-element.55.seas.refs_3_, ...), custom_call_target="tpu_custom_call" | custom-call | flops 268435456 | tf_op jit(solution)/shard_map/pallas_call | solution.py:585
  33.3 2.0 %collective-permute-done.10.refs_0_ = f32[21,8,128]{2,1,0:T(8,128)S(1)} collective-permute-done((f32[21,8,128]{2,1,0:T(8,128)S(1)}, f32[21,8,128]{2,1,0:T(8,128)S(1)}, u32[]{:S(2)}, u32[]{:S(2)}) %collective-permute-start.10) | collective-permute-done | bytes 86048 | tf_op jit(solution)/shard_map/ppermute | solution.py:633
  35.3 0.4 %shard_map.88.done_edge = f32[64,648]{1,0:T(8,128)S(1)} custom-call(f32[6,64,648]{2,1,0:T(8,128)S(1)} %shard_map.87.after.done_inner, f32[21,8,128]{2,1,0:T(8,128)S(1)} %collective-permute-done.10.refs_0_, f32[72,768]{1,0:T(8,128)S(1)} %get-tuple-element.73.edge_b.refs_1_, f32[6,72,768]{2,1,0:T(8,128)S(1)} %shard_map.84.after.inner.refs_2_, ...), custom_call_target="tpu_custom_call" | custom-call | flops 67108864 | tf_op jit(solution)/shard_map/pallas_call | solution.py:585
  35.7 0.3 collective-permute-done.8.halo
  36.1 1.2 %shard_map.89 = f32[8,64,648]{2,1,0:T(8,128)} custom-call(f32[21,8,128]{2,1,0:T(8,128)S(1)} %collective-permute-done.8.halo, f32[72,768]{1,0:T(8,128)S(1)} %get-tuple-element.71.edge_a.edge, f32[6,72,768]{2,1,0:T(8,128)S(1)} %shard_map.84.after.inner.refs_2_, f32[8,72,128]{2,1,0:T(8,128)S(1)} %get-tuple-element.55.seas.refs_3_, ...), custom_call_target="tpu_custom_call" | custom-call | flops 67108864 | tf_op jit(solution)/shard_map/pallas_call | solution.py:585
  (5 shorter events, 0.0 us)
Async XLA Ops:
  0.0 4.0 %copy-start.5 = (f32[8,64]{1,0:T(8,128)S(1)}, f32[8,64]{1,0:T(8,128)}, u32[]{:S(2)}) copy-start(f32[8,64]{1,0:T(8,128)} %wind_ref.1) | copy-start | bytes 6148
  0.0 4.0 %copy-start.4 = (s32[8,64]{1,0:T(8,128)S(1)}, s32[8,64]{1,0:T(8,128)}, u32[]{:S(2)}) copy-start(s32[8,64]{1,0:T(8,128)} %ice_ref.1) | copy-start | bytes 6148
  0.0 4.0 %copy-start.3 = (s32[8,64]{1,0:T(8,128)S(1)}, s32[8,64]{1,0:T(8,128)}, u32[]{:S(2)}) copy-start(s32[8,64]{1,0:T(8,128)} %sea_ref.1) | copy-start | bytes 6148
  0.0 4.0 %copy-start = (f32[8,64,648]{2,1,0:T(8,128)S(1)}, f32[8,64,648]{2,1,0:T(8,128)}, u32[]{:S(2)}) copy-start(f32[8,64,648]{2,1,0:T(8,128)} %spectrum.3) | copy-start | bytes 3981316
  1.3 5.4 %collective-permute-start = (f32[21,8,128]{2,1,0:T(8,128)S(1)}, f32[21,8,128]{2,1,0:T(8,128)S(1)}, u32[]{:S(2)}, u32[]{:S(2)}) collective-permute-start(f32[21,8,128]{2,1,0:T(8,128)S(1)} %get-tuple-element.40), channel_id=1, source_target_pairs={{0,1},{1,0},{2,3},{3,2},{4,5},{5,4},{6,7},{7,6},{8,9},{9,8},{10,11... | collective-permute-start | bytes 258056 | tf_op jit(solution)/shard_map/ppermute | solution.py:605
  1.4 10.8 %copy-start.1 = (bf16[648,648]{1,0:T(8,128)(2,1)S(1)}, bf16[648,648]{1,0:T(8,128)(2,1)}, u32[]{:S(2)}) copy-start(bf16[648,648]{1,0:T(8,128)(2,1)} %coupling_ref.1) | copy-start | bytes 2519428
  1.4 10.8 %copy-start.2 = (f32[8,768]{1,0:T(8,128)S(1)}, f32[8,768]{1,0:T(8,128)}, u32[]{:S(2)}) copy-start(f32[8,768]{1,0:T(8,128)} %constant.2.clone.angle_ref) | copy-start | bytes 73732
  1.4 10.8 %copy-start.6 = (f32[18]{0:T(128)S(1)}, f32[18]{0:T(128)}, u32[]{:S(2)}) copy-start(f32[18]{0:T(128)} %speed_ref.1) | copy-start | bytes 220
  1.4 5.3 %collective-permute-start.1 = (f32[6,8,128]{2,1,0:T(8,128)S(1)}, f32[6,8,128]{2,1,0:T(8,128)S(1)}, u32[]{:S(2)}, u32[]{:S(2)}) collective-permute-start(f32[6,8,128]{2,1,0:T(8,128)S(1)} %get-tuple-element.41), channel_id=1, source_target_pairs={{1,2},{2,1},{3,4},{4,3},{5,6},{6,5},{9,10},{10,9},{11,12},{12,11},... | collective-permute-start | bytes 73736 | tf_op jit(solution)/shard_map/ppermute | solution.py:606
  7.0 9.1 %collective-permute-start.4 = (f32[23,8,128]{2,1,0:T(8,128)S(1)}, f32[23,8,128]{2,1,0:T(8,128)S(1)}, u32[]{:S(2)}, u32[]{:S(2)}) collective-permute-start(f32[23,8,128]{2,1,0:T(8,128)S(1)} %get-tuple-element.63), channel_id=1, source_target_pairs={{8,16},{16,8},{24,0},{0,24},{9,17},{17,9},{25,1},{1,25},{10,18},{1... | collective-permute-start | bytes 282632 | tf_op jit(solution)/shard_map/ppermute | solution.py:633
  9.3 5.6 %collective-permute-start.2 = (f32[16,8,128]{2,1,0:T(8,128)S(1)}, f32[16,8,128]{2,1,0:T(8,128)S(1)}, u32[]{:S(2)}, u32[]{:S(2)}) collective-permute-start(f32[16,8,128]{2,1,0:T(8,128)S(1)} %get-tuple-element.50), channel_id=1, source_target_pairs={{1,2},{2,1},{3,4},{4,3},{5,6},{6,5},{9,10},{10,9},{11,12},{12,11},... | collective-permute-start | bytes 196616 | tf_op jit(solution)/shard_map/ppermute | solution.py:607
  11.5 5.7 %collective-permute-start.3 = (f32[23,8,128]{2,1,0:T(8,128)S(1)}, f32[23,8,128]{2,1,0:T(8,128)S(1)}, u32[]{:S(2)}, u32[]{:S(2)}) collective-permute-start(f32[23,8,128]{2,1,0:T(8,128)S(1)} %get-tuple-element.61), channel_id=1, source_target_pairs={{0,8},{8,0},{16,24},{24,16},{1,9},{9,1},{17,25},{25,17},{2,10},{10... | collective-permute-start | bytes 282632 | tf_op jit(solution)/shard_map/ppermute | solution.py:634
  16.6 6.5 %collective-permute-start.6 = (f32[23,8,128]{2,1,0:T(8,128)S(1)}, f32[23,8,128]{2,1,0:T(8,128)S(1)}, u32[]{:S(2)}, u32[]{:S(2)}) collective-permute-start(f32[23,8,128]{2,1,0:T(8,128)S(1)} %get-tuple-element.67), channel_id=1, source_target_pairs={{8,16},{16,8},{24,0},{0,24},{9,17},{17,9},{25,1},{1,25},{10,18},{1... | collective-permute-start | bytes 282632 | tf_op jit(solution)/shard_map/ppermute | solution.py:633
  17.6 6.4 %collective-permute-start.5 = (f32[23,8,128]{2,1,0:T(8,128)S(1)}, f32[23,8,128]{2,1,0:T(8,128)S(1)}, u32[]{:S(2)}, u32[]{:S(2)}) collective-permute-start(f32[23,8,128]{2,1,0:T(8,128)S(1)} %get-tuple-element.65), channel_id=1, source_target_pairs={{0,8},{8,0},{16,24},{24,16},{1,9},{9,1},{17,25},{25,17},{2,10},{10... | collective-permute-start | bytes 282632 | tf_op jit(solution)/shard_map/ppermute | solution.py:634
  23.6 5.8 %collective-permute-start.9 = (f32[23,8,128]{2,1,0:T(8,128)S(1)}, f32[23,8,128]{2,1,0:T(8,128)S(1)}, u32[]{:S(2)}, u32[]{:S(2)}) collective-permute-start(f32[23,8,128]{2,1,0:T(8,128)S(1)} %get-tuple-element.72), channel_id=1, source_target_pairs={{8,16},{16,8},{24,0},{0,24},{9,17},{17,9},{25,1},{1,25},{10,18},{1... | collective-permute-start | bytes 282632 | tf_op jit(solution)/shard_map/ppermute | solution.py:633
  24.5 6.5 %collective-permute-start.7 = (f32[23,8,128]{2,1,0:T(8,128)S(1)}, f32[23,8,128]{2,1,0:T(8,128)S(1)}, u32[]{:S(2)}, u32[]{:S(2)}) collective-permute-start(f32[23,8,128]{2,1,0:T(8,128)S(1)} %get-tuple-element.69), channel_id=1, source_target_pairs={{0,8},{8,0},{16,24},{24,16},{1,9},{9,1},{17,25},{25,17},{2,10},{10... | collective-permute-start | bytes 282632 | tf_op jit(solution)/shard_map/ppermute | solution.py:634
  29.8 5.5 %collective-permute-start.10 = (f32[21,8,128]{2,1,0:T(8,128)S(1)}, f32[21,8,128]{2,1,0:T(8,128)S(1)}, u32[]{:S(2)}, u32[]{:S(2)}) collective-permute-start(f32[21,8,128]{2,1,0:T(8,128)S(1)} %get-tuple-element.74), channel_id=1, source_target_pairs={{8,16},{16,8},{24,0},{0,24},{9,17},{17,9},{25,1},{1,25},{10,18},{1... | collective-permute-start | bytes 258056 | tf_op jit(solution)/shard_map/ppermute | solution.py:633
  31.5 4.6 %collective-permute-start.8 = (f32[21,8,128]{2,1,0:T(8,128)S(1)}, f32[21,8,128]{2,1,0:T(8,128)S(1)}, u32[]{:S(2)}, u32[]{:S(2)}) collective-permute-start(f32[21,8,128]{2,1,0:T(8,128)S(1)} %get-tuple-element.70), channel_id=1, source_target_pairs={{0,8},{8,0},{16,24},{24,16},{1,9},{9,1},{17,25},{25,17},{2,10},{10... | collective-permute-start | bytes 258056 | tf_op jit(solution)/shard_map/ppermute | solution.py:634
